TPU v7x, 128 devices: a whole 4x4x4 slice. The times are simulated.
128 devices in a mesh: gx: 8 (over x_lo, z), gy: 4 (over x_hi, core), gz: 4 (over y).
Axes of the slice: x: 4 (x_hi: 2, x_lo: 2; x = x_hi * 2 + x_lo), y: 4, z: 4, core: 2. Of those that a mesh axis runs over, the one named last changes fastest.
Arguments:
- field: bfloat16 [81, 64, 64, 1024], P(None, 'gx', 'gy', 'gz'), may hold values from -6 to 6
- samples: int32 [3, 8, 524288], P(None, None, ('gx', 'gy', 'gz')), may hold values from 0 to 1023, as said below
- weights: float32 [8, 524288], P(None, ('gx', 'gy', 'gz')), may hold values from 0.05 to 0.25
- destination: int32 [2, 524288], P(None, ('gx', 'gy', 'gz')), may hold values from 0 to 127, as said below
- transfer: bfloat16 [81, 524288], P(None, ('gx', 'gy', 'gz')), may hold values from -5 to 5
Outputs:
- shadowed: bfloat16 [81, 524288], P(None, ('gx', 'gy', 'gz'))
Inputs may be any that keep to these rules, and one draw needn't show every extreme that they name: Number the devices with gz fastest and gx slowest; device b holds grid cells b_x * 8 to (b_x + 1) * 8 - 1 along the first dimension and likewise along the others. Every sample of a receiver in the b-th block of 4096 receivers lies at most 2 cells, periodically along each dimension, outside device b's cells; samples[0] is below 64, samples[1] below 64, samples[2] below 1024. destination[0] is below 128 and destination[1] below 32. Of the b-th block of 4096 receivers exactly 32 have each value of destination[0], and those take each value of destination[1] once, so the columns of the output are a permutation of the receivers.
All inputs are finite; a program needn't handle non-finite values.
Results may differ from a plain program's by a relative error of at most 0.011.
Values may be sent and summed in bfloat16 or wider, within the bound.
No kernel may reach another device: no remote copies, remote signals or barrier semaphores. Data moves between devices by JAX's collectives and lax.ppermute only.
A program may use at most 128 MiB of HBM per device.

v0:
```python
import math

import jax
import jax.numpy as jnp
import numpy as np
from jax import lax
from jax.experimental import pallas as pl
from jax.experimental.pallas import tpu as pltpu
from jax.sharding import PartitionSpec as P

HALO = 2
SAMPLES = 8
DEGREES = 9
POLAR = 32
AZIMUTH = 32
LANES = 128
MIB = 1024 * 1024


def harmonic_values():
    polar = (np.arange(POLAR, dtype=np.float64) + 0.5) * (2.0 / POLAR) - 1.0
    beside = (np.arange(AZIMUTH, dtype=np.float64) + 0.5) * (2.0 * math.pi / AZIMUTH)
    cosines = np.repeat(polar, AZIMUTH)
    angles = np.tile(beside, POLAR)
    sines = np.sqrt(np.maximum(1.0 - cosines * cosines, 0.0))
    entries = {}
    for m in range(DEGREES):
        diagonal = (-1.0) ** m * float(math.prod(range(1, 2 * m, 2))) * sines**m
        legendre = {m: diagonal}
        if m + 1 < DEGREES:
            legendre[m + 1] = cosines * (2 * m + 1) * diagonal
        for l in range(m + 2, DEGREES):
            legendre[l] = (
                (2 * l - 1) * cosines * legendre[l - 1] - (l + m - 1) * legendre[l - 2]
            ) / (l - m)
        for l in range(m, DEGREES):
            factor = math.sqrt(
                (2 * l + 1) / (4.0 * math.pi) * math.factorial(l - m) / math.factorial(l + m)
            )
            if m == 0:
                entries[l, 0] = factor * legendre[l]
            else:
                entries[l, m] = math.sqrt(2.0) * factor * np.cos(m * angles) * legendre[l]
                entries[l, -m] = math.sqrt(2.0) * factor * np.sin(m * angles) * legendre[l]
    return np.stack([entries[l, m] for l in range(DEGREES) for m in range(-l, l + 1)])


def direction_tables():
    values = harmonic_values()
    basis = values.T.astype(np.float32).astype(jnp.bfloat16)
    projector = (values * (4.0 * math.pi / (POLAR * AZIMUTH))).astype(np.float32)
    return basis, projector.astype(jnp.bfloat16)


def build_planes(planes, coeffs, rows_y, cells_z, base, buf, sems, spread, eye, table):
    halves = cells_z // LANES
    keep = -(-coeffs // 16) * 16
    zeros = jnp.zeros((LANES - keep, cells_z), jnp.bfloat16)

    def one(p, _):
        pltpu.make_async_copy(planes(0), buf.at[p], sems.at[p]).wait()
        for c in range(coeffs):
            for h in range(halves):
                block = buf[p, c, :, h * LANES : (h + 1) * LANES].astype(jnp.float32)
                spread[h, pl.ds(c, rows_y, stride=coeffs), :] = block
        for y in range(0, rows_y, 2):
            parts = []
            for i in (y, y + 1):
                rows = jnp.concatenate(
                    [spread[h, i * coeffs : i * coeffs + keep, :] for h in range(halves)], axis=1
                )
                parts += [rows.astype(jnp.bfloat16), zeros]
            both = lax.dot_general(
                eye[...],
                jnp.concatenate(parts, axis=0),
                (((1,), (1,)), ((), ())),
                preferred_element_type=jnp.float32,
            )
            at = pl.multiple_of(base + (p * rows_y + y) * cells_z, 8)
            table[pl.ds(at, cells_z), :] = both[:, :LANES]
            table[pl.ds(at + cells_z, cells_z), :] = both[:, LANES:]
        return 0

    return one


def own_table(field, eye, total_rows):
    coeffs, cells_x, cells_y, cells_z = field.shape

    def kernel(field, eye, table, buf, sems, spread):
        for x in range(cells_x):
            pltpu.make_async_copy(field.at[:, x], buf.at[x], sems.at[x]).start()
        one = build_planes(
            lambda p: field.at[:, p], coeffs, cells_y, cells_z, 0, buf, sems, spread, eye, table
        )
        lax.fori_loop(0, cells_x, one, 0)

    return pl.pallas_call(
        kernel,
        out_shape=pltpu.VMEM((total_rows, LANES), jnp.float32),
        in_specs=[
            pl.BlockSpec(memory_space=pl.ANY),
            pl.BlockSpec(memory_space=pltpu.VMEM),
        ],
        out_specs=pl.BlockSpec(memory_space=pltpu.VMEM),
        scratch_shapes=[
            pltpu.VMEM((cells_x, coeffs, cells_y, cells_z), jnp.bfloat16),
            pltpu.SemaphoreType.DMA((cells_x,)),
            pltpu.VMEM((cells_z // LANES, cells_y * coeffs + 16, LANES), jnp.float32),
        ],
        compiler_params=pltpu.CompilerParams(vmem_limit_bytes=24 * MIB),
        cost_estimate=pl.CostEstimate(
            flops=2 * 10**10, transcendentals=0, bytes_accessed=2 * 10**7
        ),
        name="own_table",
    )(field, eye)


def halo_table(table, xlo, xhi, ylo, yhi, corners, eye, first_line):
    coeffs, _, cells_y, cells_z = xlo.shape
    count = 2 * HALO + 3
    lines = first_line + count * cells_y

    def kernel(_, xlo, xhi, ylo, yhi, corners, eye, table, zhi, zlo, buf, sems, spread):
        sources = [xlo.at[:, 0], xlo.at[:, 1], xhi.at[:, 0], xhi.at[:, 1], ylo, yhi, corners]
        for p, source in enumerate(sources):
            pltpu.make_async_copy(source, buf.at[p], sems.at[p]).start()
        one = build_planes(
            lambda p: ylo,
            coeffs,
            cells_y,
            cells_z,
            first_line * cells_z,
            buf,
            sems,
            spread,
            eye,
            table,
        )
        lax.fori_loop(0, count, one, 0)
        for out, start in ((zhi, 0), (zlo, cells_z - HALO)):
            for j in range(HALO):
                for line in range(0, lines, 16):
                    parts = [
                        table[pl.ds((line + i) * cells_z + start + j, 8, stride=cells_z), :]
                        for i in (0, 8)
                    ]
                    out[j * lines + line : j * lines + line + 16, :] = jnp.concatenate(
                        parts, axis=0
                    ).astype(jnp.bfloat16)

    edge = jax.ShapeDtypeStruct((HALO * lines, LANES), jnp.bfloat16)
    vmem = pl.BlockSpec(memory_space=pltpu.VMEM)
    hbm = pl.BlockSpec(memory_space=pl.ANY)
    return pl.pallas_call(
        kernel,
        out_shape=(pltpu.VMEM(table.shape, jnp.float32), edge, edge),
        in_specs=[vmem] + [hbm] * 5 + [vmem],
        out_specs=(vmem, vmem, vmem),
        scratch_shapes=[
            pltpu.VMEM((count, coeffs, cells_y, cells_z), jnp.bfloat16),
            pltpu.SemaphoreType.DMA((count,)),
            pltpu.VMEM((cells_z // LANES, cells_y * coeffs + 16, LANES), jnp.float32),
        ],
        input_output_aliases={0: 0},
        compiler_params=pltpu.CompilerParams(vmem_limit_bytes=24 * MIB),
        cost_estimate=pl.CostEstimate(
            flops=2 * 10**10, transcendentals=0, bytes_accessed=2 * 10**7
        ),
        name="halo_table",
    )(table, xlo, xhi, ylo, yhi, corners, eye)


GROUPS = 2


def gather_rows(index, slot, weights, table, zlo, zhi, first_edge, coeffs):
    receivers = slot.shape[0]
    edges = zlo.shape[0]
    steps = receivers // (8 * GROUPS)

    def kernel(index, slot, weights, zlo, zhi, table_in, table, out, rows):
        table[pl.ds(first_edge, edges), :] = zlo[...].astype(jnp.float32)
        table[pl.ds(first_edge + edges, edges), :] = zhi[...].astype(jnp.float32)
        sublane = lax.broadcasted_iota(jnp.int32, (8, LANES), 0)
        masks = [sublane == k for k in range(8)]
        used = lax.broadcasted_iota(jnp.int32, (8, LANES), 1) < coeffs

        def spread_weights(g):
            result = []
            for q in range(GROUPS):
                tile = weights[pl.ds(pl.multiple_of((g * GROUPS + q) * 8, 8), 8), :]
                for s in range(SAMPLES):
                    result.append(jnp.broadcast_to(tile[:, s : s + 1], (8, LANES)))
            return tuple(result)

        def body(g, scales):
            following = spread_weights(jnp.minimum(g + 1, steps - 1))
            index_g = index.at[pl.ds(g * (64 * GROUPS), 64 * GROUPS)]
            slot_g = slot.at[pl.ds(g * (8 * GROUPS), 8 * GROUPS)]
            for q in range(GROUPS):
                total = None
                for s in range(SAMPLES):
                    merged = None
                    for k in range(8):
                        row = table[pl.ds(index_g[q * 64 + s * 8 + k], 8, stride=0), :]
                        merged = row if merged is None else jnp.where(masks[k], row, merged)
                    term = merged * scales[q * 8 + s]
                    total = term if total is None else total + term
                total = jnp.where(used, total, 0.0)
                for k in range(8):
                    rows[pl.ds(slot_g[q * 8 + k], 1), :] = total[k : k + 1, :]
            return following

        lax.fori_loop(0, steps, body, spread_weights(0))

        def convert(i, _):
            at = pl.multiple_of(i * 256, 256)
            out[pl.ds(at, 256), :] = rows[pl.ds(at, 256), :].astype(jnp.bfloat16)
            return 0

        lax.fori_loop(0, receivers // 256, convert, 0)

    vmem = pl.BlockSpec(memory_space=pltpu.VMEM)
    smem = pl.BlockSpec(memory_space=pltpu.SMEM)
    return pl.pallas_call(
        kernel,
        out_shape=(
            pltpu.VMEM(table.shape, jnp.float32),
            jax.ShapeDtypeStruct((receivers, LANES), jnp.bfloat16),
        ),
        in_specs=[smem, smem, vmem, vmem, vmem, vmem],
        out_specs=(vmem, vmem),
        scratch_shapes=[pltpu.VMEM((receivers, LANES), jnp.float32)],
        input_output_aliases={5: 0},
        compiler_params=pltpu.CompilerParams(vmem_limit_bytes=24 * MIB),
        cost_estimate=pl.CostEstimate(
            flops=4 * 10**10, transcendentals=0, bytes_accessed=2 * 10**7
        ),
        name="gather_rows",
    )(index, slot, weights, zlo, zhi, table)[1]


def relight(transfer, routed, basis, projector):
    coeffs, count = transfer.shape
    block = 512

    def kernel(transfer, routed, basis, wide, projector, out):
        lit = jnp.dot(basis[...], transfer[...], preferred_element_type=jnp.float32)
        shade = lax.dot_general(
            wide[...],
            routed[...],
            (((1,), (1,)), ((), ())),
            preferred_element_type=jnp.float32,
        )
        product = (lit * shade).astype(jnp.bfloat16)
        out[...] = jnp.dot(projector[...], product, preferred_element_type=jnp.float32).astype(
            jnp.bfloat16
        )

    directions = basis.shape[0]
    wide = np.zeros((directions, LANES), jnp.bfloat16)
    wide[:, :coeffs] = basis
    return pl.pallas_call(
        kernel,
        out_shape=jax.ShapeDtypeStruct((coeffs, count), jnp.bfloat16),
        grid=(count // block,),
        in_specs=[
            pl.BlockSpec((coeffs, block), lambda i: (0, i)),
            pl.BlockSpec((block, LANES), lambda i: (i, 0)),
            pl.BlockSpec((directions, coeffs), lambda i: (0, 0)),
            pl.BlockSpec((directions, LANES), lambda i: (0, 0)),
            pl.BlockSpec((coeffs, directions), lambda i: (0, 0)),
        ],
        out_specs=pl.BlockSpec((coeffs, block), lambda i: (0, i)),
        compiler_params=pltpu.CompilerParams(vmem_limit_bytes=40 * MIB),
        name="relight",
    )(transfer, routed, jnp.asarray(basis), jnp.asarray(wide), jnp.asarray(projector))


def ring(axis):
    count = lax.axis_size(axis)
    forward = [(i, (i + 1) % count) for i in range(count)]
    return forward, [(target, source) for source, target in forward]


def per_device(field, samples, weights, destination, transfer):
    basis, projector = direction_tables()
    coeffs, cells_x, cells_y, cells_z = field.shape
    count = transfer.shape[1]
    along_x = lax.axis_size("gx")
    along_y = lax.axis_size("gy")
    along_z = lax.axis_size("gz")
    up_x, down_x = ring("gx")
    up_y, down_y = ring("gy")
    up_z, down_z = ring("gz")

    xlo = lax.ppermute(field[:, cells_x - HALO :], "gx", up_x)
    xhi = lax.ppermute(field[:, :HALO], "gx", down_x)
    plane = (coeffs, cells_x * HALO, cells_z)
    ylo = lax.ppermute(field[:, :, cells_y - HALO :].reshape(plane), "gy", up_y)
    yhi = lax.ppermute(field[:, :, :HALO].reshape(plane), "gy", down_y)
    half = (coeffs, 2 * HALO * HALO, cells_z)
    outer = jnp.concatenate([xlo[:, :, cells_y - HALO :], xhi[:, :, cells_y - HALO :]], axis=1)
    inner = jnp.concatenate([xlo[:, :, :HALO], xhi[:, :, :HALO]], axis=1)
    corner_lo = lax.ppermute(outer.reshape(half), "gy", up_y)
    corner_hi = lax.ppermute(inner.reshape(half), "gy", down_y)
    corners = jnp.concatenate([corner_lo, corner_hi], axis=1)

    own_lines = cells_x * cells_y
    lines = own_lines + (2 * HALO + 3) * cells_y
    rows = lines * cells_z
    total_rows = rows + 2 * HALO * lines

    near_x = (samples[0] - lax.axis_index("gx") * cells_x + HALO) % (cells_x * along_x)
    near_y = (samples[1] - lax.axis_index("gy") * cells_y + HALO) % (cells_y * along_y)
    near_z = (samples[2] - lax.axis_index("gz") * cells_z + HALO) % (cells_z * along_z)
    own_x = (near_x >= HALO) & (near_x < HALO + cells_x)
    own_y = (near_y >= HALO) & (near_y < HALO + cells_y)
    low_y = near_y < HALO
    side_x = jnp.where(near_x < HALO, near_x, near_x - cells_x)
    side_y = jnp.where(low_y, near_y, near_y - HALO - cells_y)
    line_own = jnp.where(own_x, near_x - HALO, cells_x + side_x) * cells_y + near_y - HALO
    line_y = (
        (cells_x + 2 * HALO + jnp.where(low_y, 0, 1)) * cells_y + (near_x - HALO) * HALO + side_y
    )
    line_corner = (
        (cells_x + 2 * HALO + 2) * cells_y
        + jnp.where(low_y, 0, 2 * HALO * HALO)
        + side_x * HALO
        + side_y
    )
    line = jnp.where(own_y, line_own, jnp.where(own_x, line_y, line_corner))
    inside = line * cells_z + near_z - HALO
    below = rows + near_z * lines + line
    above = rows + (HALO + near_z - HALO - cells_z) * lines + line
    position = jnp.where(
        near_z < HALO, below, jnp.where(near_z < HALO + cells_z, inside, above)
    )
    index = position.reshape(SAMPLES, count // 8, 8).transpose(1, 0, 2).reshape(-1)
    devices = along_x * along_y * along_z
    per_pair = count // devices
    slot = destination[0] * per_pair + destination[1]

    eye = jnp.asarray(np.eye(cells_z, dtype=np.float32).astype(jnp.bfloat16))
    table = own_table(field, eye, total_rows)
    table, edge_lo, edge_hi = halo_table(table, xlo, xhi, ylo, yhi, corners, eye, own_lines)
    zhi = lax.ppermute(edge_lo, "gz", down_z)
    zlo = lax.ppermute(edge_hi, "gz", up_z)
    outgoing = gather_rows(index, slot, weights.T, table, zlo, zhi, rows, coeffs)
    routed = lax.all_to_all(
        outgoing.reshape(devices, per_pair, LANES),
        ("gx", "gy", "gz"),
        split_axis=0,
        concat_axis=0,
        tiled=True,
    ).reshape(count, LANES)
    return relight(transfer, routed, basis, projector)


def solution(mesh):
    placed = (
        P(None, "gx", "gy", "gz"),
        P(None, None, ("gx", "gy", "gz")),
        P(None, ("gx", "gy", "gz")),
        P(None, ("gx", "gy", "gz")),
        P(None, ("gx", "gy", "gz")),
    )
    return jax.shard_map(
        per_device,
        mesh=mesh,
        in_specs=placed,
        out_specs=P(None, ("gx", "gy", "gz")),
        check_vma=False,
    )
```

profile of v0, /device:TPU:1, one launch (start us, length us, event | category | flops | bytes accessed | tf_op | source)
XLA Modules:
  0.0 182.0 jit_solution(5945605682957420235)
XLA Ops:
  0.0 3.1 %fusion.7 = (bf16[81,2,16,256]{3,2,1,0:T(8,128)(2,1)S(1)}, bf16[81,2,16,256]{3,2,1,0:T(8,128)(2,1)}) fusion(bf16[81,8,16,256]{3,2,1,0:T(8,128)(2,1)} %field.1), kind=kLoop, calls=%fused_computation.27 | loop fusion | bytes 5308416 | tf_op jit(solution)/shard_map/slice | solution.py:299
  3.1 2.5 %collective-permute-start = (bf16[81,2,16,256]{3,2,1,0:T(8,128)(2,1)}, bf16[81,2,16,256]{3,2,1,0:T(8,128)(2,1)}, u32[]{:S(2)}, u32[]{:S(2)}) collective-permute-start(bf16[81,2,16,256]{3,2,1,0:T(8,128)(2,1)} %get-tuple-element.16), channel_id=1, source_target_pairs={{0,16},{16,32},{32,48},{48,64},{64,80},{80,96},{96,112},{112,0},{1... | collective-permute-start | bytes 3981320 | tf_op jit(solution)/shard_map/ppermute | solution.py:298
  5.5 3.0 %collective-permute-start.1 = (bf16[81,2,16,256]{3,2,1,0:T(8,128)(2,1)S(1)}, bf16[81,2,16,256]{3,2,1,0:T(8,128)(2,1)}, u32[]{:S(2)}, u32[]{:S(2)}) collective-permute-start(bf16[81,2,16,256]{3,2,1,0:T(8,128)(2,1)S(1)} %get-tuple-element.15), channel_id=1, source_target_pairs={{16,0},{32,16},{48,32},{64,48},{80,64},{96,80},{112,96},{0,112},{1... | collective-permute-start | bytes 3981320 | tf_op jit(solution)/shard_map/ppermute | solution.py:299
  8.6 3.8 %fusion.6 = (bf16[81,8,2,256]{3,2,1,0:T(2,128)(2,1)S(1)}, bf16[81,8,2,256]{3,2,1,0:T(2,128)(2,1)S(1)}) fusion(bf16[81,8,16,256]{3,2,1,0:T(8,128)(2,1)} %field.1), kind=kLoop, calls=%fused_computation.26 | loop fusion | bytes 2654208 | tf_op jit(solution)/shard_map/slice | solution.py:302
  13.5 3.3 %collective-permute-start.2 = (bf16[81,16,256]{2,1,0:T(8,128)(2,1)}, bf16[81,16,256]{2,1,0:T(8,128)(2,1)}, u32[]{:S(2)}, u32[]{:S(2)}) collective-permute-start(bf16[81,16,256]{2,1,0:T(8,128)(2,1)} %reshape.41), channel_id=1, source_target_pairs={{0,4},{4,8},{8,12},{12,0},{1,5},{5,9},{9,13},{13,1},{2,6},{6,10},{... | collective-permute-start | bytes 1990664 | tf_op jit(solution)/shard_map/ppermute | solution.py:301
  18.6 2.0 %add.124 = s32[8,512,8]{2,1,0:T(8,128)S(1)} reshape(s32[1,8,4096]{2,1,0:T(8,128)} %get-tuple-element.21) | data formatting | bytes 262144 | tf_op jit(solution)/shard_map/add | solution.py:317
  20.7 3.4 %add.128 = s32[8,512,8]{2,1,0:T(8,128)} reshape(s32[1,8,4096]{2,1,0:T(8,128)} %get-tuple-element.23) | data formatting | bytes 262144 | tf_op jit(solution)/shard_map/add | solution.py:316
  24.0 2.5 %add.131 = s32[8,512,8]{2,1,0:T(8,128)} reshape(s32[1,8,4096]{2,1,0:T(8,128)S(1)} %get-tuple-element.22) | data formatting | bytes 262144 | tf_op jit(solution)/shard_map/add | solution.py:315
  26.5 6.2 %own_table.1._ = f32[62400,128]{1,0:T(8,128)S(1)} custom-call(bf16[81,8,16,256]{3,2,1,0:T(8,128)(2,1)} %field.1, bf16[256,256]{1,0:T(8,128)(2,1)} %constant.96.clone.eye), custom_call_target="tpu_custom_call" | custom-call | flops 20000000000 | bytes 20000000 | tf_op jit(solution)/shard_map/own_table/pallas_call | solution.py:98
  32.8 10.5 %copy-done.4 = f32[62400,128]{1,0:T(8,128)} copy-done((f32[62400,128]{1,0:T(8,128)}, f32[62400,128]{1,0:T(8,128)S(1)}, u32[]{:S(2)}) %copy-start.4) | copy-done | bytes 31948824
  43.3 2.2 %fusion.8 = (bf16[81,2,2,256]{3,2,1,0:T(2,128)(2,1)S(1)}, bf16[81,2,2,256]{3,2,1,0:T(2,128)(2,1)}) fusion(bf16[81,2,16,256]{3,2,1,0:T(8,128)(2,1)} %collective-permute-done.xlo), kind=kLoop, calls=%fused_computation.28 | loop fusion | bytes 663552 | tf_op jit(solution)/shard_map/slice | solution.py:304
  47.7 3.3 %collective-permute-start.4 = (bf16[81,8,256]{2,1,0:T(8,128)(2,1)S(1)}, bf16[81,8,256]{2,1,0:T(8,128)(2,1)}, u32[]{:S(2)}, u32[]{:S(2)}) collective-permute-start(bf16[81,8,256]{2,1,0:T(8,128)(2,1)S(1)} %reshape.43), channel_id=1, source_target_pairs={{0,4},{4,8},{8,12},{12,0},{1,5},{5,9},{9,13},{13,1},{2,6},{6,10},{... | collective-permute-start | bytes 995336 | tf_op jit(solution)/shard_map/ppermute | solution.py:306
  51.7 6.8 %select_bitcast_fusion = s32[512,8,8]{2,0,1:T(8,128)S(1)} fusion(s32[8,512,8]{2,1,0:T(8,128)} %add.131, s32[8,512,8]{2,1,0:T(8,128)} %add.128, s32[8,512,8]{2,1,0:T(8,128)S(1)} %add.124), kind=kLoop, calls=%fused_computation.14 | loop fusion | flops 2555904 | bytes 524288 | tf_op jit(solution)/shard_map/transpose | solution.py:340
  58.5 3.3 %collective-permute-done.5 = bf16[81,8,256]{2,1,0:T(8,128)(2,1)S(1)} collective-permute-done((bf16[81,8,256]{2,1,0:T(8,128)(2,1)S(1)}, bf16[81,8,256]{2,1,0:T(8,128)(2,1)S(1)}, u32[]{:S(2)}, u32[]{:S(2)}) %collective-permute-start.5) | collective-permute-done | bytes 331808 | tf_op jit(solution)/shard_map/ppermute | solution.py:307
  61.8 1.9 %pad_maximum_fusion.corners = bf16[81,16,256]{2,1,0:T(8,128)(2,1)} fusion(bf16[81,8,256]{2,1,0:T(8,128)(2,1)S(1)} %collective-permute-done.5, bf16[81,8,256]{2,1,0:T(8,128)(2,1)} %collective-permute-done.4), kind=kLoop, calls=%fused_computation.19 | loop fusion | flops 1327104 | bytes 1327104 | tf_op jit(solution)/shard_map/concatenate | solution.py:308
  63.6 10.1 %copy-done.5 = f32[62400,128]{1,0:T(8,128)S(1)} copy-done((f32[62400,128]{1,0:T(8,128)S(1)}, f32[62400,128]{1,0:T(8,128)}, u32[]{:S(2)}) %copy-start.5) | copy-done | bytes 31948824
  73.7 6.9 %halo_table.1 = (f32[62400,128]{1,0:T(8,128)S(1)}, bf16[480,128]{1,0:T(8,128)(2,1)}, bf16[480,128]{1,0:T(8,128)(2,1)}) custom-call(f32[62400,128]{1,0:T(8,128)S(1)} %copy-done.5, bf16[81,2,16,256]{3,2,1,0:T(8,128)(2,1)} %collective-permute-done.xlo, bf16[81,2,16,256]{3,2,1,0:T(8,128)(2,1)} %collective-permute-done.1.xhi, ...), custom_call_target="tpu_custom_call", output_to_operand_aliasing={{0}: (0, {})} | custom-call | flops 20000000000 | bytes 20000000 | tf_op jit(solution)/shard_map/halo_table/pallas_call | solution.py:155
  80.6 10.5 %copy-done.6 = f32[62400,128]{1,0:T(8,128)} copy-done((f32[62400,128]{1,0:T(8,128)}, f32[62400,128]{1,0:T(8,128)S(1)}, u32[]{:S(2)}) %copy-start.6) | copy-done | bytes 31948824
  95.7 1.6 reshape.40.index
  97.3 1.9 %copy.14 = f32[8,4096]{0,1:T(8,128)} copy(f32[8,4096]{1,0:T(8,128)S(1)} %copy-done.10) | data formatting | bytes 262144 | tf_op args[2]
  99.9 10.1 %copy-done.7 = f32[62400,128]{1,0:T(8,128)S(1)} copy-done((f32[62400,128]{1,0:T(8,128)S(1)}, f32[62400,128]{1,0:T(8,128)}, u32[]{:S(2)}) %copy-start.7) | copy-done | bytes 31948824
  110.0 42.3 %gather_rows.1 = (f32[62400,128]{1,0:T(8,128)S(1)}, bf16[4096,128]{1,0:T(8,128)(2,1)}) custom-call(s32[32768]{0:T(1024)} %reshape.40.index, s32[4096]{0:T(1024)} %bitcast.9, f32[4096,8]{1,0:T(8,128)} %bitcast.7, bf16[480,128]{1,0:T(8,128)(2,1)} %copy-done.12, bf16[480,128]{1,0:T(8,128)(2,1)} %copy-done.13, ...), custom_call_target="tpu_custom_call", output_to_operand_aliasing={{0}: (5, {})} | custom-call | flops 40000000000 | bytes 20000000 | tf_op jit(solution)/shard_map/gather_rows/pallas_call | solution.py:226
  152.4 22.0 %all_to_all.5 = bf16[128,32,128]{2,1,0:T(8,128)(2,1)S(1)} all-to-all(bf16[128,32,128]{2,1,0:T(8,128)(2,1)} %bitcast.8), channel_id=1, replica_groups=mesh['gx'=8,'gy'=4,'gz'=4] {'gx','gy','gz'}, dimensions={0} | all-to-all | bytes 2097152 | tf_op jit(solution)/shard_map/all_to_all | solution.py:351
  174.4 7.5 %relight.1 = bf16[81,4096]{1,0:T(8,128)(2,1)} custom-call(bf16[81,4096]{1,0:T(8,128)(2,1)S(1)} %copy-done, bf16[4096,128]{1,0:T(8,128)(2,1)S(1)} %bitcast.6, bf16[1024,81]{1,0:T(8,128)(2,1)S(1)} %copy-done.1, bf16[1024,128]{1,0:T(8,128)(2,1)S(1)} %copy-done.2, bf16[81,1024]{1,0:T(8,128)(2,1)S(1)} %copy-done.3), custom_call_target="tpu_custom_call" | custom-call | tf_op jit(solution)/shard_map/relight/pallas_call | solution.py:264
  (45 shorter events, 11.0 us)
Async XLA Ops:
  3.1 40.2 %collective-permute-start = (bf16[81,2,16,256]{3,2,1,0:T(8,128)(2,1)}, bf16[81,2,16,256]{3,2,1,0:T(8,128)(2,1)}, u32[]{:S(2)}, u32[]{:S(2)}) collective-permute-start(bf16[81,2,16,256]{3,2,1,0:T(8,128)(2,1)} %get-tuple-element.16), channel_id=1, source_target_pairs={{0,16},{16,32},{32,48},{48,64},{64,80},{80,96},{96,112},{112,0},{1... | collective-permute-start | bytes 3981320 | tf_op jit(solution)/shard_map/ppermute | solution.py:298
  5.5 12.4 %copy-start.9 = (s32[3,8,4096]{2,1,0:T(8,128)S(1)}, s32[3,8,4096]{2,1,0:T(8,128)}, u32[]{:S(2)}) copy-start(s32[3,8,4096]{2,1,0:T(8,128)} %param.10) | copy-start | bytes 1179652
  5.5 40.0 %collective-permute-start.1 = (bf16[81,2,16,256]{3,2,1,0:T(8,128)(2,1)S(1)}, bf16[81,2,16,256]{3,2,1,0:T(8,128)(2,1)}, u32[]{:S(2)}, u32[]{:S(2)}) collective-permute-start(bf16[81,2,16,256]{3,2,1,0:T(8,128)(2,1)S(1)} %get-tuple-element.15), channel_id=1, source_target_pairs={{16,0},{32,16},{48,32},{64,48},{80,64},{96,80},{112,96},{0,112},{1... | collective-permute-start | bytes 3981320 | tf_op jit(solution)/shard_map/ppermute | solution.py:299
  13.5 50.1 %collective-permute-start.2 = (bf16[81,16,256]{2,1,0:T(8,128)(2,1)}, bf16[81,16,256]{2,1,0:T(8,128)(2,1)}, u32[]{:S(2)}, u32[]{:S(2)}) collective-permute-start(bf16[81,16,256]{2,1,0:T(8,128)(2,1)} %reshape.41), channel_id=1, source_target_pairs={{0,4},{4,8},{8,12},{12,0},{1,5},{5,9},{9,13},{13,1},{2,6},{6,10},{... | collective-permute-start | bytes 1990664 | tf_op jit(solution)/shard_map/ppermute | solution.py:301
  17.9 45.7 %collective-permute-start.3 = (bf16[81,16,256]{2,1,0:T(8,128)(2,1)}, bf16[81,16,256]{2,1,0:T(8,128)(2,1)}, u32[]{:S(2)}, u32[]{:S(2)}) collective-permute-start(bf16[81,16,256]{2,1,0:T(8,128)(2,1)} %reshape.42), channel_id=1, source_target_pairs={{4,0},{8,4},{12,8},{0,12},{5,1},{9,5},{13,9},{1,13},{6,2},{10,6},{... | collective-permute-start | bytes 1990664 | tf_op jit(solution)/shard_map/ppermute | solution.py:302
  32.8 10.5 %copy-start.4 = (f32[62400,128]{1,0:T(8,128)}, f32[62400,128]{1,0:T(8,128)S(1)}, u32[]{:S(2)}) copy-start(f32[62400,128]{1,0:T(8,128)S(1)} %own_table.1._) | copy-start | bytes 95846400
  45.5 5.5 %copy-start.8 = (bf16[81,2,2,256]{3,2,1,0:T(2,128)(2,1)S(1)}, bf16[81,2,2,256]{3,2,1,0:T(2,128)(2,1)}, u32[]{:S(2)}) copy-start(bf16[81,2,2,256]{3,2,1,0:T(2,128)(2,1)} %get-tuple-element.18) | copy-start | bytes 497668
  47.7 10.8 %collective-permute-start.4 = (bf16[81,8,256]{2,1,0:T(8,128)(2,1)S(1)}, bf16[81,8,256]{2,1,0:T(8,128)(2,1)}, u32[]{:S(2)}, u32[]{:S(2)}) collective-permute-start(bf16[81,8,256]{2,1,0:T(8,128)(2,1)S(1)} %reshape.43), channel_id=1, source_target_pairs={{0,4},{4,8},{8,12},{12,0},{1,5},{5,9},{9,13},{13,1},{2,6},{6,10},{... | collective-permute-start | bytes 995336 | tf_op jit(solution)/shard_map/ppermute | solution.py:306
  51.6 10.2 %collective-permute-start.5 = (bf16[81,8,256]{2,1,0:T(8,128)(2,1)S(1)}, bf16[81,8,256]{2,1,0:T(8,128)(2,1)S(1)}, u32[]{:S(2)}, u32[]{:S(2)}) collective-permute-start(bf16[81,8,256]{2,1,0:T(8,128)(2,1)S(1)} %reshape.44), channel_id=1, source_target_pairs={{4,0},{8,4},{12,8},{0,12},{5,1},{9,5},{13,9},{1,13},{6,2},{10,6},{... | collective-permute-start | bytes 995336 | tf_op jit(solution)/shard_map/ppermute | solution.py:307
  61.8 32.1 %copy-start.11 = (s32[2,4096]{1,0:T(2,128)S(1)}, s32[2,4096]{1,0:T(2,128)}, u32[]{:S(2)}) copy-start(s32[2,4096]{1,0:T(2,128)} %param.12) | copy-start | bytes 98308
  63.6 10.1 %copy-start.5 = (f32[62400,128]{1,0:T(8,128)S(1)}, f32[62400,128]{1,0:T(8,128)}, u32[]{:S(2)}) copy-start(f32[62400,128]{1,0:T(8,128)} %copy-done.4) | copy-start | bytes 95846400
  80.6 10.5 %copy-start.6 = (f32[62400,128]{1,0:T(8,128)}, f32[62400,128]{1,0:T(8,128)S(1)}, u32[]{:S(2)}) copy-start(f32[62400,128]{1,0:T(8,128)S(1)} %get-tuple-element.11.table_in) | copy-start | bytes 95846400
  91.1 8.1 %collective-permute-start.6 = (bf16[480,128]{1,0:T(8,128)(2,1)}, bf16[480,128]{1,0:T(8,128)(2,1)S(1)}, u32[]{:S(2)}, u32[]{:S(2)}) collective-permute-start(bf16[480,128]{1,0:T(8,128)(2,1)} %get-tuple-element.9), channel_id=1, source_target_pairs={{0,1},{1,2},{2,3},{3,0},{4,5},{5,6},{6,7},{7,4},{8,9},{9,10},{10,1... | collective-permute-start | bytes 368648 | tf_op jit(solution)/shard_map/ppermute | solution.py:349
  92.4 6.8 %collective-permute-start.7 = (bf16[480,128]{1,0:T(8,128)(2,1)}, bf16[480,128]{1,0:T(8,128)(2,1)S(1)}, u32[]{:S(2)}, u32[]{:S(2)}) collective-permute-start(bf16[480,128]{1,0:T(8,128)(2,1)} %get-tuple-element.10), channel_id=1, source_target_pairs={{1,0},{2,1},{3,2},{0,3},{5,4},{6,5},{7,6},{4,7},{9,8},{10,9},{11,1... | collective-permute-start | bytes 368648 | tf_op jit(solution)/shard_map/ppermute | solution.py:348
  95.7 1.6 copy-start.10
  99.2 0.6 copy-start.12
  99.3 0.7 copy-start.13
  99.9 10.1 %copy-start.7 = (f32[62400,128]{1,0:T(8,128)S(1)}, f32[62400,128]{1,0:T(8,128)}, u32[]{:S(2)}) copy-start(f32[62400,128]{1,0:T(8,128)} %copy-done.6) | copy-start | bytes 95846400
  152.4 22.1 %copy-start = (bf16[81,4096]{1,0:T(8,128)(2,1)S(1)}, bf16[81,4096]{1,0:T(8,128)(2,1)}, u32[]{:S(2)}) copy-start(bf16[81,4096]{1,0:T(8,128)(2,1)} %transfer.1) | copy-start | bytes 1990660
  152.4 22.1 %copy-start.1 = (bf16[1024,81]{1,0:T(8,128)(2,1)S(1)}, bf16[1024,81]{1,0:T(8,128)(2,1)}, u32[]{:S(2)}) copy-start(bf16[1024,81]{1,0:T(8,128)(2,1)} %constant.97.clone.basis) | copy-start | bytes 497668
  152.4 22.1 %copy-start.2 = (bf16[1024,128]{1,0:T(8,128)(2,1)S(1)}, bf16[1024,128]{1,0:T(8,128)(2,1)}, u32[]{:S(2)}) copy-start(bf16[1024,128]{1,0:T(8,128)(2,1)} %constant.98.clone.wide) | copy-start | bytes 786436
  152.4 22.1 %copy-start.3 = (bf16[81,1024]{1,0:T(8,128)(2,1)S(1)}, bf16[81,1024]{1,0:T(8,128)(2,1)}, u32[]{:S(2)}) copy-start(bf16[81,1024]{1,0:T(8,128)(2,1)} %constant.99.clone.projector) | copy-start | bytes 497668
where the time goes:
time: 182 us
  local copies, waits for them, and re-layouts  67.7 us (37%)
  Pallas kernels  62.9 us (35%)
  blocking collectives  22 us (12%)
  starting transfers between devices  14.9 us (8%)
  other arithmetic  10.8 us (6%)
  waiting for transfers between devices  3.3 us (2%)
    unnamed x29, local copies, waits for them, and re-layouts  43.9 us
    pallas_call x1, Pallas kernels, gather_rows(): pl.pallas_call(kernel, out_shape=(pltpu.VMEM(table.shape, jnp.float32), j...  42.3 us
    all_to_all x1, blocking collectives, per_device(): lax.all_to_all(outgoing.reshape(devices, per_pair, LANES), ('gx', 'gy', '...  22 us
    pallas_call x1, Pallas kernels, relight(): pl.pallas_call(kernel, out_shape=jax.ShapeDtypeStruct((coeffs, count), jn...  7.53 us
    pallas_call x1, Pallas kernels, halo_table(): pl.pallas_call(kernel, out_shape=(pltpu.VMEM(table.shape, jnp.float32), e...  6.86 us
    transpose x1, other arithmetic, per_device(): position.reshape(SAMPLES, count // 8, 8).transpose(1, 0, 2).reshape(-1)  6.78 us
    pallas_call x1, Pallas kernels, own_table(): pl.pallas_call(kernel, out_shape=pltpu.VMEM((total_rows, LANES), jnp.floa...  6.23 us
    slice x1, local copies, waits for them, and re-layouts, per_device(): yhi = lax.ppermute(field[:, :, :HALO].reshape(plane), 'gy', down_y)  3.8 us
  transfers between devices with their start and end apart: 8, of which 1 were waited for; matrix products, arithmetic and copies ran while one was open for 18% of the time, Pallas kernels for 3%

commit v1 on v0

v1 whole, which is shorter than its diff:
```python
import math

import jax
import jax.numpy as jnp
import numpy as np
from jax import lax
from jax.experimental import pallas as pl
from jax.experimental.pallas import tpu as pltpu
from jax.sharding import PartitionSpec as P


HALO = 2
SAMPLES = 8
DEGREES = 9
POLAR = 32
AZIMUTH = 32
LANES = 128
MIB = 1024 * 1024


def harmonic_values():
    polar = (np.arange(POLAR, dtype=np.float64) + 0.5) * (2.0 / POLAR) - 1.0
    beside = (np.arange(AZIMUTH, dtype=np.float64) + 0.5) * (2.0 * math.pi / AZIMUTH)
    cosines = np.repeat(polar, AZIMUTH)
    angles = np.tile(beside, POLAR)
    sines = np.sqrt(np.maximum(1.0 - cosines * cosines, 0.0))
    entries = {}
    for m in range(DEGREES):
        diagonal = (-1.0) ** m * float(math.prod(range(1, 2 * m, 2))) * sines**m
        legendre = {m: diagonal}
        if m + 1 < DEGREES:
            legendre[m + 1] = cosines * (2 * m + 1) * diagonal
        for l in range(m + 2, DEGREES):
            legendre[l] = (
                (2 * l - 1) * cosines * legendre[l - 1] - (l + m - 1) * legendre[l - 2]
            ) / (l - m)
        for l in range(m, DEGREES):
            factor = math.sqrt(
                (2 * l + 1) / (4.0 * math.pi) * math.factorial(l - m) / math.factorial(l + m)
            )
            if m == 0:
                entries[l, 0] = factor * legendre[l]
            else:
                entries[l, m] = math.sqrt(2.0) * factor * np.cos(m * angles) * legendre[l]
                entries[l, -m] = math.sqrt(2.0) * factor * np.sin(m * angles) * legendre[l]
    return np.stack([entries[l, m] for l in range(DEGREES) for m in range(-l, l + 1)])


def direction_tables():
    values = harmonic_values()
    basis = values.T.astype(np.float32).astype(jnp.bfloat16)
    projector = (values * (4.0 * math.pi / (POLAR * AZIMUTH))).astype(np.float32)
    return basis, projector.astype(jnp.bfloat16)


def fill_rows(get, spread, coeffs, rows_y, cells_z):
    halves = cells_z // LANES
    for c in range(coeffs):
        for h in range(halves):
            block = get(c, h).astype(jnp.float32)
            spread[h, pl.ds(c, rows_y, stride=coeffs), :] = block


def turn_rows(spread, eye, coeffs, rows_y, cells_z, put):
    halves = cells_z // LANES
    keep = -(-coeffs // 16) * 16
    zeros = jnp.zeros((LANES - keep, cells_z), jnp.bfloat16)
    for y in range(0, rows_y, 2):
        parts = []
        for i in (y, y + 1):
            rows = jnp.concatenate(
                [spread[h, i * coeffs : i * coeffs + keep, :] for h in range(halves)], axis=1
            )
            parts += [rows.astype(jnp.bfloat16), zeros]
        both = lax.dot_general(
            eye[...],
            jnp.concatenate(parts, axis=0),
            (((1,), (1,)), ((), ())),
            preferred_element_type=jnp.float32,
        )
        put(y, both[:, :LANES])
        put(y + 1, both[:, LANES:])


def spread_shape(coeffs, cells_y, cells_z):
    return pltpu.VMEM((cells_z // LANES, cells_y * coeffs + 16, LANES), jnp.float32)


def own_table(field, eye):
    coeffs, cells_x, cells_y, cells_z = field.shape
    plane = cells_y * cells_z

    def kernel(field, eye, out, spread):
        fill_rows(
            lambda c, h: field[c, 0, :, h * LANES : (h + 1) * LANES],
            spread,
            coeffs,
            cells_y,
            cells_z,
        )

        def put(y, block):
            out[y * cells_z : (y + 1) * cells_z, :] = block

        turn_rows(spread, eye, coeffs, cells_y, cells_z, put)

    return pl.pallas_call(
        kernel,
        out_shape=pltpu.HBM((cells_x * plane, LANES), jnp.float32),
        grid=(cells_x,),
        in_specs=[
            pl.BlockSpec((coeffs, 1, cells_y, cells_z), lambda x: (0, x, 0, 0)),
            pl.BlockSpec((cells_z, cells_z), lambda x: (0, 0)),
        ],
        out_specs=pl.BlockSpec((plane, LANES), lambda x: (x, 0)),
        scratch_shapes=[spread_shape(coeffs, cells_y, cells_z)],
        compiler_params=pltpu.CompilerParams(vmem_limit_bytes=16 * MIB),
        cost_estimate=pl.CostEstimate(
            flops=2 * 10**10, transcendentals=0, bytes_accessed=2 * 10**7
        ),
        name="own_table",
    )(field, eye)


def full_table(own, xlo, xhi, ylo, yhi, corners, eye, total_rows):
    coeffs, _, cells_y, cells_z = xlo.shape
    count = 2 * HALO + 3
    own_rows = own.shape[0]
    lines = own_rows // cells_z + count * cells_y
    halves = range(cells_z // LANES)

    def kernel(own, xlo, xhi, ylo, yhi, corners, eye, table, zhi, zlo, buf, sems, spread, done):
        sources = [xlo.at[:, 0], xlo.at[:, 1], xhi.at[:, 0], xhi.at[:, 1], ylo, yhi, corners]
        for p, source in enumerate(sources):
            pltpu.make_async_copy(source, buf.at[p], sems.at[p]).start()
        inherit = pltpu.make_async_copy(own, table.at[pl.ds(0, own_rows), :], done)
        inherit.start()

        def one(p, _):
            pltpu.make_async_copy(ylo, buf.at[p], sems.at[p]).wait()
            fill_rows(
                lambda c, h: buf[p, c, :, h * LANES : (h + 1) * LANES],
                spread,
                coeffs,
                cells_y,
                cells_z,
            )

            def put(y, block):
                at = pl.multiple_of(own_rows + (p * cells_y + y) * cells_z, 8)
                table[pl.ds(at, cells_z), :] = block

            turn_rows(spread, eye, coeffs, cells_y, cells_z, put)
            return 0

        lax.fori_loop(0, count, one, 0)
        inherit.wait()
        for out, start in ((zhi, 0), (zlo, cells_z - HALO)):
            for j in range(HALO):
                for line in range(0, lines, 16):
                    parts = [
                        table[pl.ds((line + i) * cells_z + start + j, 8, stride=cells_z), :]
                        for i in (0, 8)
                    ]
                    out[j * lines + line : j * lines + line + 16, :] = jnp.concatenate(
                        parts, axis=0
                    ).astype(jnp.bfloat16)

    del halves
    edge = jax.ShapeDtypeStruct((HALO * lines, LANES), jnp.bfloat16)
    vmem = pl.BlockSpec(memory_space=pltpu.VMEM)
    hbm = pl.BlockSpec(memory_space=pl.ANY)
    return pl.pallas_call(
        kernel,
        out_shape=(pltpu.VMEM((total_rows, LANES), jnp.float32), edge, edge),
        in_specs=[hbm] * 6 + [vmem],
        out_specs=(vmem, vmem, vmem),
        scratch_shapes=[
            pltpu.VMEM((count, coeffs, cells_y, cells_z), jnp.bfloat16),
            pltpu.SemaphoreType.DMA((count,)),
            spread_shape(coeffs, cells_y, cells_z),
            pltpu.SemaphoreType.DMA(()),
        ],
        compiler_params=pltpu.CompilerParams(vmem_limit_bytes=12 * MIB),
        cost_estimate=pl.CostEstimate(
            flops=2 * 10**10, transcendentals=0, bytes_accessed=2 * 10**7
        ),
        name="full_table",
    )(own, xlo, xhi, ylo, yhi, corners, eye)


GROUP = 8


def prepare(samples, weights, slot, origin, cells, total):
    count = slot.shape[0]
    cells_x, cells_y, cells_z = cells
    own_lines = cells_x * cells_y
    lines = own_lines + (2 * HALO + 3) * cells_y
    rows = lines * cells_z
    per_row = LANES // SAMPLES

    def locate(near_x, near_y, near_z):
        own_x = (near_x >= HALO) & (near_x < HALO + cells_x)
        own_y = (near_y >= HALO) & (near_y < HALO + cells_y)
        low_y = near_y < HALO
        side_x = jnp.where(near_x < HALO, near_x, near_x - cells_x)
        side_y = jnp.where(low_y, near_y, near_y - HALO - cells_y)
        line_own = jnp.where(own_x, near_x - HALO, cells_x + side_x) * cells_y + near_y - HALO
        line_y = (
            (cells_x + 2 * HALO) * cells_y
            + jnp.where(low_y, 0, cells_y)
            + (near_x - HALO) * HALO
            + side_y
        )
        line_corner = (
            (cells_x + 2 * HALO + 2) * cells_y
            + jnp.where(low_y, 0, 2 * HALO * HALO)
            + side_x * HALO
            + side_y
        )
        line = jnp.where(own_y, line_own, jnp.where(own_x, line_y, line_corner))
        inside = line * cells_z + near_z - HALO
        below = rows + near_z * lines + line
        above = rows + (near_z - cells_z) * lines + line
        return jnp.where(near_z < HALO, below, jnp.where(near_z < HALO + cells_z, inside, above))

    def kernel(origin, slot, samples, weights, index, ordered):
        def scatter(j, _):
            at = pl.multiple_of(j * LANES, LANES)
            near = []
            for d in range(3):
                shift = samples[d, :, pl.ds(at, LANES)] - origin[d] + HALO
                shift = jnp.where(shift < 0, shift + total[d], shift)
                near.append(jnp.where(shift >= total[d], shift - total[d], shift))
            block = jnp.concatenate(
                [
                    locate(*near).astype(jnp.float32),
                    weights[:, pl.ds(at, LANES)],
                    jnp.zeros((LANES - 2 * SAMPLES, LANES), jnp.float32),
                ],
                axis=0,
            ).T
            mine = slot.at[pl.ds(at, LANES)]
            for r in range(LANES):
                ordered[pl.ds(mine[r], 1), :] = block[r : r + 1, :]
            return 0

        lax.fori_loop(0, count // LANES, scatter, 0)
        sub = lax.broadcasted_iota(jnp.int32, (SAMPLES, LANES), 0)
        group = lax.broadcasted_iota(jnp.int32, (SAMPLES, LANES), 1) // per_row

        def turn(j, _):
            block = ordered[pl.ds(pl.multiple_of(j * LANES, LANES), LANES), :].T
            tile = block[:SAMPLES, :].astype(jnp.int32)
            for b in (1, 2, 4):
                up = pltpu.roll(pltpu.roll(tile, b, 0), LANES - b * per_row, 1)
                down = pltpu.roll(pltpu.roll(tile, SAMPLES - b, 0), b * per_row, 1)
                row_bit = (sub & b) != 0
                lane_bit = (group & b) != 0
                tile = jnp.where(row_bit == lane_bit, tile, jnp.where(row_bit, up, down))
            index[pl.ds(pl.multiple_of(j * SAMPLES, SAMPLES), SAMPLES), :] = tile
            return 0

        lax.fori_loop(0, count // LANES, turn, 0)

    vmem = pl.BlockSpec(memory_space=pltpu.VMEM)
    smem = pl.BlockSpec(memory_space=pltpu.SMEM)
    return pl.pallas_call(
        kernel,
        out_shape=(
            jax.ShapeDtypeStruct((count * SAMPLES // LANES, LANES), jnp.int32),
            jax.ShapeDtypeStruct((count, LANES), jnp.float32),
        ),
        in_specs=[smem, smem, vmem, vmem],
        out_specs=(vmem, vmem),
        compiler_params=pltpu.CompilerParams(vmem_limit_bytes=12 * MIB),
        cost_estimate=pl.CostEstimate(
            flops=2 * 10**10, transcendentals=0, bytes_accessed=3 * 10**6
        ),
        name="prepare",
    )(origin, slot, samples, weights)


def spread_weights(ordered):
    count = ordered.shape[0]
    step = 4

    def kernel(ordered, wide):
        def body(i, _):
            for q in range(step):
                g = i * step + q
                tile = ordered[pl.ds(pl.multiple_of(g * GROUP, GROUP), GROUP), :]
                for s in range(SAMPLES):
                    at = pl.multiple_of((g * SAMPLES + s) * GROUP, GROUP)
                    wide[pl.ds(at, GROUP), :] = jnp.broadcast_to(
                        tile[:, SAMPLES + s : SAMPLES + s + 1], (GROUP, LANES)
                    )
            return 0

        lax.fori_loop(0, count // (GROUP * step), body, 0)

    vmem = pl.BlockSpec(memory_space=pltpu.VMEM)
    return pl.pallas_call(
        kernel,
        out_shape=pltpu.VMEM((count * SAMPLES, LANES), jnp.float32),
        in_specs=[vmem],
        out_specs=vmem,
        compiler_params=pltpu.CompilerParams(vmem_limit_bytes=4 * MIB),
        cost_estimate=pl.CostEstimate(
            flops=10**10, transcendentals=0, bytes_accessed=3 * 10**6
        ),
        name="spread_weights",
    )(ordered)


RING = 8
CHUNK = 256


def gather_rows(index, wide, table, zlo, zhi, first_edge, coeffs):
    edges = zlo.shape[0]
    chunks = index.shape[0] // CHUNK
    per_chunk = CHUNK // SAMPLES
    packed = per_chunk * 3 // 4
    groups = per_chunk // GROUP

    def kernel(index, zlo, zhi, table_in, wide_in, table, wide, out, local, sems):
        table[pl.ds(first_edge, edges), :] = zlo[...].astype(jnp.float32)
        table[pl.ds(first_edge + edges, edges), :] = zhi[...].astype(jnp.float32)
        sublane = lax.broadcasted_iota(jnp.int32, (GROUP, LANES), 0)
        masks = [sublane == k for k in range(GROUP)]
        lane = lax.broadcasted_iota(jnp.int32, (GROUP, LANES), 1)
        used = lane < coeffs
        low = lane < 64
        quarters = [lane < 32, lane < 64, lane < 96]

        def fetch(n, slot):
            return pltpu.make_async_copy(
                index.at[pl.ds(pl.multiple_of(n * CHUNK, CHUNK), CHUNK)],
                local.at[slot],
                sems.at[slot],
            )

        for b in range(RING - 1):
            fetch(b, b).start()

        def body(i, _):
            for b in range(RING):
                n = i * RING + b
                fetch(n, b).wait()
                ahead = n + RING - 1

                @pl.when(ahead < chunks)
                def _():
                    fetch(ahead, (b + RING - 1) % RING).start()

                sums = []
                for q in range(groups):
                    total = None
                    for s in range(SAMPLES):
                        merged = None
                        for k in range(GROUP):
                            place = (q // 2) * LANES + s * 16 + (q % 2) * GROUP + k
                            row = table[pl.ds(local[b, place], GROUP, stride=0), :]
                            merged = row if merged is None else jnp.where(masks[k], row, merged)
                        at = pl.multiple_of(n * CHUNK + (q * SAMPLES + s) * GROUP, GROUP)
                        term = merged * wide[pl.ds(at, GROUP), :]
                        total = term if total is None else total + term
                    sums.append(jnp.where(used, total, 0.0))
                first = jnp.where(low, sums[0], pltpu.roll(sums[2], 64, 1))
                second = jnp.where(low, sums[1], pltpu.roll(sums[3], 64, 1))
                third = jnp.where(
                    quarters[0],
                    pltpu.roll(sums[0], 64, 1),
                    jnp.where(
                        quarters[1],
                        pltpu.roll(sums[1], 96, 1),
                        jnp.where(quarters[2], sums[2], pltpu.roll(sums[3], 32, 1)),
                    ),
                )
                out[n, :16, :] = jnp.concatenate([first, second], axis=0).astype(jnp.bfloat16)
                out[n, 16:, :] = third.astype(jnp.bfloat16)
            return 0

        lax.fori_loop(0, chunks // RING, body, 0)

    vmem = pl.BlockSpec(memory_space=pltpu.VMEM)
    return pl.pallas_call(
        kernel,
        out_shape=(
            pltpu.VMEM(table.shape, jnp.float32),
            pltpu.VMEM(wide.shape, jnp.float32),
            jax.ShapeDtypeStruct((chunks, packed, LANES), jnp.bfloat16),
        ),
        in_specs=[vmem] * 5,
        out_specs=(vmem, vmem, vmem),
        scratch_shapes=[
            pltpu.SMEM((RING, CHUNK), jnp.int32),
            pltpu.SemaphoreType.DMA((RING,)),
        ],
        input_output_aliases={3: 0, 4: 1},
        compiler_params=pltpu.CompilerParams(vmem_limit_bytes=8 * MIB),
        cost_estimate=pl.CostEstimate(
            flops=4 * 10**10, transcendentals=0, bytes_accessed=2 * 10**7
        ),
        name="gather_rows",
    )(index, zlo, zhi, table, wide)[2]


def relight(transfer, routed, basis, projector):
    coeffs, count = transfer.shape
    sources, packed, _ = routed.shape
    per_pair = count // sources
    block = 512
    step = block // per_pair

    def kernel(transfer, routed, basis, wide, projector, out):
        low = lax.broadcasted_iota(jnp.int32, (GROUP, LANES), 1) < 64
        parts = []
        for i in range(step):
            head = routed[i, :16, :].astype(jnp.float32)
            first, second = head[:GROUP], head[GROUP:]
            third = routed[i, 16:, :].astype(jnp.float32)
            parts += [
                jnp.where(low, first, pltpu.roll(third, 64, 1)),
                jnp.where(low, second, pltpu.roll(third, 32, 1)),
                jnp.where(low, pltpu.roll(first, 64, 1), third),
                jnp.where(low, pltpu.roll(second, 64, 1), pltpu.roll(third, 96, 1)),
            ]
        rows = jnp.concatenate(parts, axis=0).astype(jnp.bfloat16)
        lit = jnp.dot(basis[...], transfer[...], preferred_element_type=jnp.float32)
        shade = lax.dot_general(
            wide[...], rows, (((1,), (1,)), ((), ())), preferred_element_type=jnp.float32
        )
        product = (lit * shade).astype(jnp.bfloat16)
        out[...] = jnp.dot(projector[...], product, preferred_element_type=jnp.float32).astype(
            jnp.bfloat16
        )

    directions = basis.shape[0]
    wide = np.zeros((directions, LANES), jnp.bfloat16)
    wide[:, :coeffs] = basis
    return pl.pallas_call(
        kernel,
        out_shape=jax.ShapeDtypeStruct((coeffs, count), jnp.bfloat16),
        grid=(count // block,),
        in_specs=[
            pl.BlockSpec((coeffs, block), lambda i: (0, i)),
            pl.BlockSpec((step, packed, LANES), lambda i: (i, 0, 0)),
            pl.BlockSpec((directions, coeffs), lambda i: (0, 0)),
            pl.BlockSpec((directions, LANES), lambda i: (0, 0)),
            pl.BlockSpec((coeffs, directions), lambda i: (0, 0)),
        ],
        out_specs=pl.BlockSpec((coeffs, block), lambda i: (0, i)),
        compiler_params=pltpu.CompilerParams(vmem_limit_bytes=40 * MIB),
        name="relight",
    )(transfer, routed, jnp.asarray(basis), jnp.asarray(wide), jnp.asarray(projector))


def moves(sizes, steps):
    pairs = []
    for x in range(sizes[0]):
        for y in range(sizes[1]):
            to_x, to_y = (x + steps[0]) % sizes[0], (y + steps[1]) % sizes[1]
            pairs.append((x * sizes[1] + y, to_x * sizes[1] + to_y))
    return pairs


def halo_step(field, samples, weights, destination, transfer):
    basis, projector = direction_tables()
    coeffs, cells_x, cells_y, cells_z = field.shape
    count = transfer.shape[1]
    along = tuple(lax.axis_size(axis) for axis in ("gx", "gy", "gz"))
    ups = [moves((n, 1), (1, 0)) for n in along]
    downs = [moves((n, 1), (-1, 0)) for n in along]

    last, first, cut = lax.optimization_barrier(
        (field[:, cells_x - HALO :], field[:, :HALO], field)
    )
    xlo = lax.ppermute(last, "gx", ups[0])
    xhi = lax.ppermute(first, "gx", downs[0])
    plane = (coeffs, cells_x * HALO, cells_z)
    top = cut[:, :, cells_y - HALO :]
    bottom = cut[:, :, :HALO]
    ylo = lax.ppermute(top.reshape(plane), "gy", ups[1])
    yhi = lax.ppermute(bottom.reshape(plane), "gy", downs[1])
    corners = []
    for edge, step_y in ((top, 1), (bottom, -1)):
        for piece, step_x in ((edge[:, cells_x - HALO :], 1), (edge[:, :HALO], -1)):
            piece = piece.reshape(coeffs, HALO * HALO, cells_z)
            corners.append(lax.ppermute(piece, ("gx", "gy"), moves(along[:2], (step_x, step_y))))
    corners = jnp.concatenate(corners, axis=1)

    lines = cells_x * cells_y + (2 * HALO + 3) * cells_y
    rows = lines * cells_z
    cells = (cells_x, cells_y, cells_z)
    total = tuple(c * n for c, n in zip(cells, along))
    origin = jnp.stack(
        [lax.axis_index(axis) * c for axis, c in zip(("gx", "gy", "gz"), cells)]
    ).astype(jnp.int32)
    devices = math.prod(along)
    per_pair = count // devices
    slot = destination[0] * per_pair + destination[1]

    eye = jnp.asarray(np.eye(cells_z, dtype=np.float32).astype(jnp.bfloat16))
    own = own_table(field, eye)
    index, ordered = prepare(samples, weights, slot, origin, cells, total)
    own, index, ordered, corners = lax.optimization_barrier((own, index, ordered, corners))
    table, edge_lo, edge_hi = full_table(
        own, xlo, xhi, ylo, yhi, corners, eye, rows + 2 * HALO * lines
    )
    zhi = lax.ppermute(edge_lo, "gz", downs[2])
    zlo = lax.ppermute(edge_hi, "gz", ups[2])
    wide = spread_weights(ordered)
    outgoing = gather_rows(index.reshape(-1), wide, table, zlo, zhi, rows, coeffs)
    routed = lax.all_to_all(
        outgoing, ("gx", "gy", "gz"), split_axis=0, concat_axis=0, tiled=True
    )
    return relight(transfer, routed, basis, projector)


def solution(mesh):
    placed = (
        P(None, "gx", "gy", "gz"),
        P(None, None, ("gx", "gy", "gz")),
        P(None, ("gx", "gy", "gz")),
        P(None, ("gx", "gy", "gz")),
        P(None, ("gx", "gy", "gz")),
    )
    return jax.shard_map(
        halo_step,
        mesh=mesh,
        in_specs=placed,
        out_specs=P(None, ("gx", "gy", "gz")),
        check_vma=False,
    )
```

time: 182 us -> 169 us (0.929)
  local copies, waits for them, and re-layouts: 67.7 us -> 18.9 us
  Pallas kernels: 62.9 us -> 88.7 us
  other arithmetic: 10.8 us -> 1.72 us
  blocking collectives: 22 us -> 30.2 us
  waiting for transfers between devices: 3.3 us -> 10.2 us
  starting transfers between devices: 14.9 us -> 18.5 us
    unnamed x29 -> x28, local copies, waits for them, and re-layouts: 43.9 us -> 5.22 us
    pallas_call x3 -> x5, Pallas kernels: 55.4 us -> 81.2 us  [the longest x1 33.9 us: gather_rows(): pl.pallas_call(kernel, out_shape=(pltpu.VMEM(table.shape, jnp.float32), p...]
    all_to_all x1, blocking collectives: 22 us -> 30.2 us  [halo_step(): lax.all_to_all(outgoing, ('gx', 'gy', 'gz'), split_axis=0, concat_axis=0,...]
    add x3 -> x0, local copies, waits for them, and re-layouts: 7.88 us -> none  [the longest x1 3.36 us: per_device(): samples[1] - lax.axis_index('gy') * cells_y + HALO]
    ppermute x8 -> x10, waiting for transfers between devices: 3.3 us -> 10.2 us  [the longest x1 10.2 us: halo_step(): xlo = lax.ppermute(last, 'gx', ups[0])]
    transpose x1 -> x0, other arithmetic: 6.78 us -> none  [per_device(): position.reshape(SAMPLES, count // 8, 8).transpose(1, 0, 2).reshape(-1)]
    ppermute x8 -> x10, starting transfers between devices: 14.9 us -> 18.5 us  [the longest x4 11.6 us: halo_step(): lax.ppermute(piece, ('gx', 'gy'), moves(along[:2], (step_x, step_y)))]
    slice x4 -> x7, local copies, waits for them, and re-layouts: 10.7 us -> 9.22 us  [the longest x1 3.79 us: halo_step(): bottom = cut[:, :, :HALO]]
  transfers between devices with their start and end apart: 8 -> 10, of which waited for: 1 -> 1; matrix products, arithmetic and copies ran while one was open for 18% -> 6% of each run, Pallas kernels for 3% -> 24%
where the time goes in v1:
time: 169 us
  Pallas kernels  88.7 us (52%)
  blocking collectives  30.2 us (18%)
  local copies, waits for them, and re-layouts  18.9 us (11%)
  starting transfers between devices  18.5 us (11%)
  waiting for transfers between devices  10.2 us (6%)
  other arithmetic  1.72 us (1%)
    pallas_call x1, Pallas kernels, gather_rows(): pl.pallas_call(kernel, out_shape=(pltpu.VMEM(table.shape, jnp.float32), p...  33.9 us
    all_to_all x1, blocking collectives, halo_step(): lax.all_to_all(outgoing, ('gx', 'gy', 'gz'), split_axis=0, concat_axis=0,...  30.2 us
    pallas_call x1, Pallas kernels, prepare(): pl.pallas_call(kernel, out_shape=(jax.ShapeDtypeStruct((count * SAMPLES /...  16 us
    pallas_call x1, Pallas kernels, spread_weights(): pl.pallas_call(kernel, out_shape=pltpu.VMEM((count * SAMPLES, LANES), jnp...  15.6 us
    ppermute x4, starting transfers between devices, halo_step(): lax.ppermute(piece, ('gx', 'gy'), moves(along[:2], (step_x, step_y)))  11.6 us
    ppermute x1, waiting for transfers between devices, halo_step(): xlo = lax.ppermute(last, 'gx', ups[0])  10.2 us
    pallas_call x1, Pallas kernels, own_table(): pl.pallas_call(kernel, out_shape=pltpu.HBM((cells_x * plane, LANES), jnp....  8.35 us
    pallas_call x1, Pallas kernels, relight(): pl.pallas_call(kernel, out_shape=jax.ShapeDtypeStruct((coeffs, count), jn...  7.55 us
  transfers between devices with their start and end apart: 10, of which 1 were waited for; matrix products, arithmetic and copies ran while one was open for 6% of the time, Pallas kernels for 24%

profile of v1, /device:TPU:1, one launch (start us, length us, event | category | flops | bytes accessed | tf_op | source)
XLA Modules:
  0.0 168.5 jit_solution(17318192319298360319)
XLA Ops:
  0.0 3.1 %fusion.2 = (bf16[81,2,16,256]{3,2,1,0:T(8,128)(2,1)S(1)}, bf16[81,2,16,256]{3,2,1,0:T(8,128)(2,1)}) fusion(bf16[81,8,16,256]{3,2,1,0:T(8,128)(2,1)} %field.1), kind=kLoop, calls=%fused_computation.5 | loop fusion | bytes 5308416 | tf_op jit(solution)/shard_map/slice | solution.py:479
  3.1 2.3 %fusion.1 = (bf16[81,2,2,256]{3,2,1,0:T(2,128)(2,1)S(1)}, bf16[81,2,2,256]{3,2,1,0:T(2,128)(2,1)S(1)}, bf16[81,2,2,256]{3,2,1,0:T(2,128)(2,1)S(1)}, bf16[81,2,2,256]{3,2,1,0:T(2,128)(2,1)S(1)}) fusion(bf16[81,8,16,256]{3,2,1,0:T(8,128)(2,1)} %field.1), kind=kLoop, calls=%fused_computation.4 | loop fusion | bytes 1327104 | tf_op jit(solution)/shard_map/slice | solution.py:490
  5.4 0.7 copy.13
  6.1 5.5 %collective-permute-start = (bf16[81,4,256]{2,1,0:T(4,128)(2,1)}, bf16[81,4,256]{2,1,0:T(4,128)(2,1)}, u32[]{:S(2)}, u32[]{:S(2)}) collective-permute-start(bf16[81,4,256]{2,1,0:T(4,128)(2,1)} %copy.13), channel_id=1, source_target_pairs={{0,20},{4,24},{8,28},{12,16},{16,36},{20,40},{24,44},{28,32},{32,5... | collective-permute-start | bytes 497672 | tf_op jit(solution)/shard_map/ppermute | solution.py:492
  12.9 0.7 copy.17
  13.7 1.1 collective-permute-start.2
  14.9 4.4 %collective-permute-start.1 = (bf16[81,4,256]{2,1,0:T(4,128)(2,1)S(1)}, bf16[81,4,256]{2,1,0:T(4,128)(2,1)}, u32[]{:S(2)}, u32[]{:S(2)}) collective-permute-start(bf16[81,4,256]{2,1,0:T(4,128)(2,1)S(1)} %copy.15), channel_id=1, source_target_pairs={{0,116},{4,120},{8,124},{12,112},{16,4},{20,8},{24,12},{28,0},{32,... | collective-permute-start | bytes 497672 | tf_op jit(solution)/shard_map/ppermute | solution.py:492
  19.3 3.8 %fusion = (bf16[81,8,2,256]{3,2,1,0:T(2,128)(2,1)S(1)}, bf16[81,8,2,256]{3,2,1,0:T(2,128)(2,1)S(1)}) fusion(bf16[81,8,16,256]{3,2,1,0:T(8,128)(2,1)} %field.1), kind=kLoop, calls=%fused_computation.3 | loop fusion | bytes 2654208 | tf_op jit(solution)/shard_map/slice | solution.py:485
  23.1 1.1 reshape.29
  24.5 2.5 %copy-done = bf16[81,8,16,256]{3,2,1,0:T(8,128)(2,1)S(1)} copy-done((bf16[81,8,16,256]{3,2,1,0:T(8,128)(2,1)S(1)}, bf16[81,8,16,256]{3,2,1,0:T(8,128)(2,1)}, u32[]{:S(2)}) %copy-start) | copy-done | bytes 5308440
  27.0 8.4 %own_table.1.own = f32[32768,128]{1,0:T(8,128)} custom-call(bf16[81,8,16,256]{3,2,1,0:T(8,128)(2,1)S(1)} %copy-done, bf16[256,256]{1,0:T(8,128)(2,1)S(1)} %copy-done.7), custom_call_target="tpu_custom_call" | custom-call | flops 20000000000 | bytes 20000000 | tf_op jit(solution)/shard_map/own_table/pallas_call | solution.py:107
  35.4 1.1 reshape.30
  36.8 3.6 %collective-permute-start.5 = (bf16[81,2,16,256]{3,2,1,0:T(8,128)(2,1)S(1)}, bf16[81,2,16,256]{3,2,1,0:T(8,128)(2,1)S(1)}, u32[]{:S(2)}, u32[]{:S(2)}) collective-permute-start(bf16[81,2,16,256]{3,2,1,0:T(8,128)(2,1)S(1)} %get-tuple-element.24), channel_id=1, source_target_pairs={{0,112},{16,0},{32,16},{48,32},{64,48},{80,64},{96,80},{112,96},{1... | collective-permute-start | bytes 3981320 | tf_op jit(solution)/shard_map/ppermute | solution.py:482
  40.4 16.0 %prepare.1 = (s32[256,128]{1,0:T(8,128)S(1)}, f32[4096,128]{1,0:T(8,128)S(1)}) custom-call(s32[3]{0:T(128)S(1)} %pad_add_fusion.origin, s32[4096]{0:T(1024)S(1)} %bitcast.9, s32[3,8,4096]{2,1,0:T(8,128)S(1)} %copy-done.5, f32[8,4096]{1,0:T(8,128)S(1)} %copy-done.6), custom_call_target="tpu_custom_call" | custom-call | flops 20000000000 | bytes 3000000 | tf_op jit(solution)/shard_map/prepare/pallas_call | solution.py:269
  57.0 1.3 copy-done.9
  58.4 1.6 pad_maximum_fusion.corners
  60.0 10.2 %collective-permute-done.4.xlo = bf16[81,2,16,256]{3,2,1,0:T(8,128)(2,1)S(1)} collective-permute-done((bf16[81,2,16,256]{3,2,1,0:T(8,128)(2,1)}, bf16[81,2,16,256]{3,2,1,0:T(8,128)(2,1)S(1)}, u32[]{:S(2)}, u32[]{:S(2)}) %collective-permute-start.4) | collective-permute-done | bytes 1327136 | tf_op jit(solution)/shard_map/ppermute | solution.py:481
  70.2 7.3 %full_table.1 = (f32[62400,128]{1,0:T(8,128)S(1)}, bf16[480,128]{1,0:T(8,128)(2,1)S(1)}, bf16[480,128]{1,0:T(8,128)(2,1)S(1)}) custom-call(f32[32768,128]{1,0:T(8,128)} %own_table.1.own, bf16[81,2,16,256]{3,2,1,0:T(8,128)(2,1)S(1)} %collective-permute-done.4.xlo, bf16[81,2,16,256]{3,2,1,0:T(8,128)(2,1)S(1)} %collective-permute-done.5.xhi, ...), custom_call_target="tpu_custom_call" | custom-call | flops 20000000000 | bytes 20000000 | tf_op jit(solution)/shard_map/full_table/pallas_call | solution.py:173
  77.5 1.4 collective-permute-start.8
  78.9 1.5 collective-permute-start.9
  80.4 15.6 %spread_weights.1.wide_in = f32[32768,128]{1,0:T(8,128)S(1)} custom-call(f32[4096,128]{1,0:T(8,128)S(1)} %copy-done.10), custom_call_target="tpu_custom_call" | custom-call | flops 10000000000 | bytes 3000000 | tf_op jit(solution)/shard_map/spread_weights/pallas_call | solution.py:304
  96.7 33.9 %gather_rows.1 = (f32[62400,128]{1,0:T(8,128)S(1)}, f32[32768,128]{1,0:T(8,128)S(1)}, bf16[128,24,128]{2,1,0:T(8,128)(2,1)}) custom-call(s32[32768]{0:T(1024)} %bitcast.10, bf16[480,128]{1,0:T(8,128)(2,1)} %copy-done.12, bf16[480,128]{1,0:T(8,128)(2,1)} %copy-done.13, ...), custom_call_target="tpu_custom_call", output_to_operand_aliasing={{0}: (3, {}), {1}: (4, {})} | custom-call | flops 40000000000 | bytes 20000000 | tf_op jit(solution)/shard_map/gather_rows/pallas_call | solution.py:389
  130.7 30.2 %all_to_all.5.routed = bf16[128,24,128]{2,1,0:T(8,128)(2,1)S(1)} all-to-all(bf16[128,24,128]{2,1,0:T(8,128)(2,1)} %get-tuple-element.30), channel_id=1, replica_groups=mesh['gx'=8,'gy'=4,'gz'=4] {'gx','gy','gz'}, dimensions={0} | all-to-all | bytes 1572864 | tf_op jit(solution)/shard_map/all_to_all | solution.py:517
  161.0 7.6 %relight.1 = bf16[81,4096]{1,0:T(8,128)(2,1)} custom-call(bf16[81,4096]{1,0:T(8,128)(2,1)S(1)} %copy-done.1, bf16[128,24,128]{2,1,0:T(8,128)(2,1)S(1)} %all_to_all.5.routed, bf16[1024,81]{1,0:T(8,128)(2,1)S(1)} %copy-done.3, bf16[1024,128]{1,0:T(8,128)(2,1)S(1)} %copy-done.2, bf16[81,1024]{1,0:T(8,128)(2,1)S(1)} %copy-done.4), custom_call_target="tpu_custom_call" | custom-call | tf_op jit(solution)/shard_map/relight/pallas_call | solution.py:444
  (47 shorter events, 3.5 us)
Async XLA Ops:
  6.1 30.5 %collective-permute-start = (bf16[81,4,256]{2,1,0:T(4,128)(2,1)}, bf16[81,4,256]{2,1,0:T(4,128)(2,1)}, u32[]{:S(2)}, u32[]{:S(2)}) collective-permute-start(bf16[81,4,256]{2,1,0:T(4,128)(2,1)} %copy.13), channel_id=1, source_target_pairs={{0,20},{4,24},{8,28},{12,16},{16,36},{20,40},{24,44},{28,32},{32,5... | collective-permute-start | bytes 497672 | tf_op jit(solution)/shard_map/ppermute | solution.py:492
  12.3 24.4 %collective-permute-start.3 = (bf16[81,4,256]{2,1,0:T(4,128)(2,1)}, bf16[81,4,256]{2,1,0:T(4,128)(2,1)}, u32[]{:S(2)}, u32[]{:S(2)}) collective-permute-start(bf16[81,4,256]{2,1,0:T(4,128)(2,1)} %copy.19), channel_id=1, source_target_pairs={{0,124},{4,112},{8,116},{12,120},{16,12},{20,0},{24,4},{28,8},{32,... | collective-permute-start | bytes 497672 | tf_op jit(solution)/shard_map/ppermute | solution.py:492
  13.7 23.1 %collective-permute-start.2 = (bf16[81,4,256]{2,1,0:T(4,128)(2,1)}, bf16[81,4,256]{2,1,0:T(4,128)(2,1)}, u32[]{:S(2)}, u32[]{:S(2)}) collective-permute-start(bf16[81,4,256]{2,1,0:T(4,128)(2,1)} %copy.17), channel_id=1, source_target_pairs={{0,28},{4,16},{8,20},{12,24},{16,44},{20,32},{24,36},{28,40},{32,6... | collective-permute-start | bytes 497672 | tf_op jit(solution)/shard_map/ppermute | solution.py:492
  14.9 43.5 %collective-permute-start.1 = (bf16[81,4,256]{2,1,0:T(4,128)(2,1)S(1)}, bf16[81,4,256]{2,1,0:T(4,128)(2,1)}, u32[]{:S(2)}, u32[]{:S(2)}) collective-permute-start(bf16[81,4,256]{2,1,0:T(4,128)(2,1)S(1)} %copy.15), channel_id=1, source_target_pairs={{0,116},{4,120},{8,124},{12,112},{16,4},{20,8},{24,12},{28,0},{32,... | collective-permute-start | bytes 497672 | tf_op jit(solution)/shard_map/ppermute | solution.py:492
  23.1 1.5 copy-start.7
  24.2 35.9 %collective-permute-start.6 = (bf16[81,16,256]{2,1,0:T(8,128)(2,1)}, bf16[81,16,256]{2,1,0:T(8,128)(2,1)S(1)}, u32[]{:S(2)}, u32[]{:S(2)}) collective-permute-start(bf16[81,16,256]{2,1,0:T(8,128)(2,1)} %reshape.29), channel_id=1, source_target_pairs={{0,4},{4,8},{8,12},{12,0},{1,5},{5,9},{9,13},{13,1},{2,6},{6,10},{... | collective-permute-start | bytes 1990664 | tf_op jit(solution)/shard_map/ppermute | solution.py:486
  24.5 2.5 %copy-start = (bf16[81,8,16,256]{3,2,1,0:T(8,128)(2,1)S(1)}, bf16[81,8,16,256]{3,2,1,0:T(8,128)(2,1)}, u32[]{:S(2)}) copy-start(bf16[81,8,16,256]{3,2,1,0:T(8,128)(2,1)} %field.1) | copy-start | bytes 15925252
  27.0 8.4 %copy-start.11 = (s32[2,4096]{1,0:T(2,128)S(1)}, s32[2,4096]{1,0:T(2,128)}, u32[]{:S(2)}) copy-start(s32[2,4096]{1,0:T(2,128)} %param.12) | copy-start | bytes 98308
  35.4 5.0 %copy-start.5 = (s32[3,8,4096]{2,1,0:T(8,128)S(1)}, s32[3,8,4096]{2,1,0:T(8,128)}, u32[]{:S(2)}) copy-start(s32[3,8,4096]{2,1,0:T(8,128)} %samples.1) | copy-start | bytes 1179652
  35.4 5.0 %copy-start.6 = (f32[8,4096]{1,0:T(8,128)S(1)}, f32[8,4096]{1,0:T(8,128)}, u32[]{:S(2)}) copy-start(f32[8,4096]{1,0:T(8,128)} %weights.1) | copy-start | bytes 393220
  36.6 23.4 %collective-permute-start.7 = (bf16[81,16,256]{2,1,0:T(8,128)(2,1)}, bf16[81,16,256]{2,1,0:T(8,128)(2,1)S(1)}, u32[]{:S(2)}, u32[]{:S(2)}) collective-permute-start(bf16[81,16,256]{2,1,0:T(8,128)(2,1)} %reshape.30), channel_id=1, source_target_pairs={{0,12},{4,0},{8,4},{12,8},{1,13},{5,1},{9,5},{13,9},{2,14},{6,2},{... | collective-permute-start | bytes 1990664 | tf_op jit(solution)/shard_map/ppermute | solution.py:487
  36.8 33.5 %collective-permute-start.4 = (bf16[81,2,16,256]{3,2,1,0:T(8,128)(2,1)}, bf16[81,2,16,256]{3,2,1,0:T(8,128)(2,1)S(1)}, u32[]{:S(2)}, u32[]{:S(2)}) collective-permute-start(bf16[81,2,16,256]{3,2,1,0:T(8,128)(2,1)} %get-tuple-element.23), channel_id=1, source_target_pairs={{0,16},{16,32},{32,48},{48,64},{64,80},{80,96},{96,112},{112,0},{1... | collective-permute-start | bytes 3981320 | tf_op jit(solution)/shard_map/ppermute | solution.py:481
  36.8 33.5 %collective-permute-start.5 = (bf16[81,2,16,256]{3,2,1,0:T(8,128)(2,1)S(1)}, bf16[81,2,16,256]{3,2,1,0:T(8,128)(2,1)S(1)}, u32[]{:S(2)}, u32[]{:S(2)}) collective-permute-start(bf16[81,2,16,256]{3,2,1,0:T(8,128)(2,1)S(1)} %get-tuple-element.24), channel_id=1, source_target_pairs={{0,112},{16,0},{32,16},{48,32},{64,48},{80,64},{96,80},{112,96},{1... | collective-permute-start | bytes 3981320 | tf_op jit(solution)/shard_map/ppermute | solution.py:482
  56.4 0.7 copy-start.8
  57.0 1.3 copy-start.9
  60.0 20.4 %copy-start.10 = (f32[4096,128]{1,0:T(8,128)S(1)}, f32[4096,128]{1,0:T(8,128)}, u32[]{:S(2)}) copy-start(f32[4096,128]{1,0:T(8,128)} %copy-done.9) | copy-start | bytes 6291460
  77.5 18.5 %collective-permute-start.8 = (bf16[480,128]{1,0:T(8,128)(2,1)S(1)}, bf16[480,128]{1,0:T(8,128)(2,1)S(1)}, u32[]{:S(2)}, u32[]{:S(2)}) collective-permute-start(bf16[480,128]{1,0:T(8,128)(2,1)S(1)} %get-tuple-element.26), channel_id=1, source_target_pairs={{0,1},{1,2},{2,3},{3,0},{4,5},{5,6},{6,7},{7,4},{8,9},{9,10},{10,1... | collective-permute-start | bytes 368648 | tf_op jit(solution)/shard_map/ppermute | solution.py:514
  78.9 17.2 %collective-permute-start.9 = (bf16[480,128]{1,0:T(8,128)(2,1)S(1)}, bf16[480,128]{1,0:T(8,128)(2,1)S(1)}, u32[]{:S(2)}, u32[]{:S(2)}) collective-permute-start(bf16[480,128]{1,0:T(8,128)(2,1)S(1)} %get-tuple-element.27), channel_id=1, source_target_pairs={{0,3},{1,0},{2,1},{3,2},{4,7},{5,4},{6,5},{7,6},{8,11},{9,8},{10,9... | collective-permute-start | bytes 368648 | tf_op jit(solution)/shard_map/ppermute | solution.py:513
  96.1 0.7 copy-start.12
  96.1 0.7 copy-start.13
  130.7 30.3 %copy-start.1 = (bf16[81,4096]{1,0:T(8,128)(2,1)S(1)}, bf16[81,4096]{1,0:T(8,128)(2,1)}, u32[]{:S(2)}) copy-start(bf16[81,4096]{1,0:T(8,128)(2,1)} %transfer.1) | copy-start | bytes 1990660
  130.7 30.3 %copy-start.2 = (bf16[1024,128]{1,0:T(8,128)(2,1)S(1)}, bf16[1024,128]{1,0:T(8,128)(2,1)}, u32[]{:S(2)}) copy-start(bf16[1024,128]{1,0:T(8,128)(2,1)} %constant.31.clone.wide) | copy-start | bytes 786436
  130.7 30.3 %copy-start.3 = (bf16[1024,81]{1,0:T(8,128)(2,1)S(1)}, bf16[1024,81]{1,0:T(8,128)(2,1)}, u32[]{:S(2)}) copy-start(bf16[1024,81]{1,0:T(8,128)(2,1)} %constant.30.clone.basis) | copy-start | bytes 497668
  130.7 30.3 %copy-start.4 = (bf16[81,1024]{1,0:T(8,128)(2,1)S(1)}, bf16[81,1024]{1,0:T(8,128)(2,1)}, u32[]{:S(2)}) copy-start(bf16[81,1024]{1,0:T(8,128)(2,1)} %constant.32.clone.projector) | copy-start | bytes 497668

commit v2 on v1

--- a/solution.py
+++ b/solution.py
@@ -190,6 +190,7 @@
 
 
 GROUP = 8
+PARTS = 3
 
 
 def prepare(samples, weights, slot, origin, cells, total):
@@ -198,7 +199,9 @@
     own_lines = cells_x * cells_y
     lines = own_lines + (2 * HALO + 3) * cells_y
     rows = lines * cells_z
-    per_row = LANES // SAMPLES
+    block = 256
+    burst = 32
+    kinds = (2 + PARTS) * SAMPLES
 
     def locate(near_x, near_y, near_z):
         own_x = (near_x >= HALO) & (near_x < HALO + cells_x)
@@ -225,45 +228,62 @@
         above = rows + (near_z - cells_z) * lines + line
         return jnp.where(near_z < HALO, below, jnp.where(near_z < HALO + cells_z, inside, above))
 
-    def kernel(origin, slot, samples, weights, index, ordered):
-        def scatter(j, _):
-            at = pl.multiple_of(j * LANES, LANES)
+    def kernel(origin, slot, samples, weights, eye, join, index, ordered, natural):
+        def turn(j, _):
+            at = pl.multiple_of(j * block, block)
             near = []
             for d in range(3):
-                shift = samples[d, :, pl.ds(at, LANES)] - origin[d] + HALO
+                shift = samples[d, :, pl.ds(at, block)] - origin[d] + HALO
                 shift = jnp.where(shift < 0, shift + total[d], shift)
                 near.append(jnp.where(shift >= total[d], shift - total[d], shift))
-            block = jnp.concatenate(
-                [
-                    locate(*near).astype(jnp.float32),
-                    weights[:, pl.ds(at, LANES)],
-                    jnp.zeros((LANES - 2 * SAMPLES, LANES), jnp.float32),
-                ],
-                axis=0,
-            ).T
-            mine = slot.at[pl.ds(at, LANES)]
-            for r in range(LANES):
-                ordered[pl.ds(mine[r], 1), :] = block[r : r + 1, :]
-            return 0
-
-        lax.fori_loop(0, count // LANES, scatter, 0)
-        sub = lax.broadcasted_iota(jnp.int32, (SAMPLES, LANES), 0)
-        group = lax.broadcasted_iota(jnp.int32, (SAMPLES, LANES), 1) // per_row
-
-        def turn(j, _):
-            block = ordered[pl.ds(pl.multiple_of(j * LANES, LANES), LANES), :].T
-            tile = block[:SAMPLES, :].astype(jnp.int32)
-            for b in (1, 2, 4):
-                up = pltpu.roll(pltpu.roll(tile, b, 0), LANES - b * per_row, 1)
-                down = pltpu.roll(pltpu.roll(tile, SAMPLES - b, 0), b * per_row, 1)
-                row_bit = (sub & b) != 0
-                lane_bit = (group & b) != 0
-                tile = jnp.where(row_bit == lane_bit, tile, jnp.where(row_bit, up, down))
-            index[pl.ds(pl.multiple_of(j * SAMPLES, SAMPLES), SAMPLES), :] = tile
-            return 0
-
-        lax.fori_loop(0, count // LANES, turn, 0)
-
+            row = locate(*near)
+            pieces = [(row >> 8).astype(jnp.float32), (row & 255).astype(jnp.float32)]
+            rest = weights[:, pl.ds(at, block)]
+            for _ in range(PARTS):
+                piece = rest.astype(jnp.bfloat16).astype(jnp.float32)
+                pieces.append(piece)
+                rest = rest - piece
+            pieces.append(jnp.zeros((LANES - kinds, block), jnp.float32))
+            natural[pl.ds(at, block), :] = lax.dot_general(
+                eye[...],
+                jnp.concatenate(pieces, axis=0).astype(jnp.bfloat16),
+                (((1,), (1,)), ((), ())),
+                preferred_element_type=jnp.float32,
+            )
+            return 0
+
+        lax.fori_loop(0, count // block, turn, 0)
+
+        def scatter(j, _):
+            at = pl.multiple_of(j * burst, burst)
+            mine = slot.at[pl.ds(at, burst)]
+            for g in range(0, burst, GROUP):
+                tile = natural[pl.ds(at + g, GROUP), :]
+                for k in range(GROUP):
+                    ordered[pl.ds(mine[g + k], 1), :] = tile[k : k + 1, :]
+            return 0
+
+        lax.fori_loop(0, count // burst, scatter, 0)
+
+        def collect(j, _):
+            at = pl.multiple_of(j * 4 * LANES, 4 * LANES)
+            wide = lax.dot_general(
+                join[...],
+                ordered[pl.ds(at, 4 * LANES), :].astype(jnp.bfloat16),
+                (((1,), (1,)), ((), ())),
+                preferred_element_type=jnp.float32,
+            ).astype(jnp.int32)
+            for i in range(4):
+                to = pl.multiple_of((j * 4 + i) * SAMPLES, SAMPLES)
+                index[pl.ds(to, SAMPLES), :] = wide[:SAMPLES, i * LANES : (i + 1) * LANES]
+            return 0
+
+        lax.fori_loop(0, count // (4 * LANES), collect, 0)
+
+    join = np.zeros((16, LANES), np.float32)
+    for s in range(SAMPLES):
+        join[s, s] = 256.0
+        join[s, SAMPLES + s] = 1.0
     vmem = pl.BlockSpec(memory_space=pltpu.VMEM)
     smem = pl.BlockSpec(memory_space=pltpu.SMEM)
     return pl.pallas_call(
@@ -272,68 +292,84 @@
             jax.ShapeDtypeStruct((count * SAMPLES // LANES, LANES), jnp.int32),
             jax.ShapeDtypeStruct((count, LANES), jnp.float32),
         ),
-        in_specs=[smem, smem, vmem, vmem],
+        in_specs=[smem, smem, vmem, vmem, vmem, vmem],
         out_specs=(vmem, vmem),
+        scratch_shapes=[pltpu.VMEM((count, LANES), jnp.float32)],
         compiler_params=pltpu.CompilerParams(vmem_limit_bytes=12 * MIB),
         cost_estimate=pl.CostEstimate(
             flops=2 * 10**10, transcendentals=0, bytes_accessed=3 * 10**6
         ),
         name="prepare",
-    )(origin, slot, samples, weights)
+    )(
+        origin,
+        slot,
+        samples,
+        weights,
+        jnp.asarray(np.eye(block, dtype=np.float32).astype(jnp.bfloat16)),
+        jnp.asarray(join.astype(jnp.bfloat16)),
+    )
 
 
 def spread_weights(ordered):
     count = ordered.shape[0]
-    step = 4
-
-    def kernel(ordered, wide):
+    block = 128
+
+    def kernel(ordered, ones, wide):
         def body(i, _):
-            for q in range(step):
-                g = i * step + q
-                tile = ordered[pl.ds(pl.multiple_of(g * GROUP, GROUP), GROUP), :]
-                for s in range(SAMPLES):
-                    at = pl.multiple_of((g * SAMPLES + s) * GROUP, GROUP)
-                    wide[pl.ds(at, GROUP), :] = jnp.broadcast_to(
-                        tile[:, SAMPLES + s : SAMPLES + s + 1], (GROUP, LANES)
-                    )
-            return 0
-
-        lax.fori_loop(0, count // (GROUP * step), body, 0)
-
+            at = pl.multiple_of(i * block, block)
+            rows = ordered[pl.ds(at, block), :].astype(jnp.bfloat16)
+            for h in range(0, SAMPLES, 2):
+                both = jnp.dot(
+                    rows,
+                    ones[:, h * LANES : (h + 2) * LANES],
+                    preferred_element_type=jnp.float32,
+                )
+                for s in range(2):
+                    for g in range(block // GROUP):
+                        to = (i * (block // GROUP) + g) * SAMPLES + h + s
+                        wide[pl.ds(pl.multiple_of(to * GROUP, GROUP), GROUP), :] = both[
+                            g * GROUP : (g + 1) * GROUP, s * LANES : (s + 1) * LANES
+                        ]
+            return 0
+
+        lax.fori_loop(0, count // block, body, 0)
+
+    ones = np.zeros((LANES, SAMPLES * LANES), np.float32)
+    for s in range(SAMPLES):
+        for p in range(PARTS):
+            ones[(2 + p) * SAMPLES + s, s * LANES : (s + 1) * LANES] = 1.0
     vmem = pl.BlockSpec(memory_space=pltpu.VMEM)
     return pl.pallas_call(
         kernel,
         out_shape=pltpu.VMEM((count * SAMPLES, LANES), jnp.float32),
-        in_specs=[vmem],
+        in_specs=[vmem, vmem],
         out_specs=vmem,
         compiler_params=pltpu.CompilerParams(vmem_limit_bytes=4 * MIB),
         cost_estimate=pl.CostEstimate(
             flops=10**10, transcendentals=0, bytes_accessed=3 * 10**6
         ),
         name="spread_weights",
-    )(ordered)
-
-
-RING = 8
-CHUNK = 256
-
-
-def gather_rows(index, wide, table, zlo, zhi, first_edge, coeffs):
+    )(ordered, jnp.asarray(ones.astype(jnp.bfloat16)))
+
+
+RING = 2
+CHUNK = 1024
+
+
+def gather_rows(index, wide, table, zlo, zhi, first_edge, count, coeffs):
     edges = zlo.shape[0]
     chunks = index.shape[0] // CHUNK
     per_chunk = CHUNK // SAMPLES
-    packed = per_chunk * 3 // 4
     groups = per_chunk // GROUP
-
-    def kernel(index, zlo, zhi, table_in, wide_in, table, wide, out, local, sems):
+    pairs = count // 32
+    half = LANES // 2
+
+    def kernel(index, zlo, zhi, pick, table_in, wide_in, table, wide, out, local, sems, rows):
         table[pl.ds(first_edge, edges), :] = zlo[...].astype(jnp.float32)
         table[pl.ds(first_edge + edges, edges), :] = zhi[...].astype(jnp.float32)
         sublane = lax.broadcasted_iota(jnp.int32, (GROUP, LANES), 0)
         masks = [sublane == k for k in range(GROUP)]
-        lane = lax.broadcasted_iota(jnp.int32, (GROUP, LANES), 1)
-        used = lane < coeffs
-        low = lane < 64
-        quarters = [lane < 32, lane < 64, lane < 96]
+        used = lax.broadcasted_iota(jnp.int32, (GROUP, LANES), 1) < coeffs
 
         def fetch(n, slot):
             return pltpu.make_async_copy(
@@ -355,57 +391,73 @@
                 def _():
                     fetch(ahead, (b + RING - 1) % RING).start()
 
-                sums = []
                 for q in range(groups):
                     total = None
                     for s in range(SAMPLES):
                         merged = None
                         for k in range(GROUP):
-                            place = (q // 2) * LANES + s * 16 + (q % 2) * GROUP + k
+                            place = s * per_chunk + q * GROUP + k
                             row = table[pl.ds(local[b, place], GROUP, stride=0), :]
                             merged = row if merged is None else jnp.where(masks[k], row, merged)
                         at = pl.multiple_of(n * CHUNK + (q * SAMPLES + s) * GROUP, GROUP)
                         term = merged * wide[pl.ds(at, GROUP), :]
                         total = term if total is None else total + term
-                    sums.append(jnp.where(used, total, 0.0))
-                first = jnp.where(low, sums[0], pltpu.roll(sums[2], 64, 1))
-                second = jnp.where(low, sums[1], pltpu.roll(sums[3], 64, 1))
-                third = jnp.where(
-                    quarters[0],
-                    pltpu.roll(sums[0], 64, 1),
-                    jnp.where(
-                        quarters[1],
-                        pltpu.roll(sums[1], 96, 1),
-                        jnp.where(quarters[2], sums[2], pltpu.roll(sums[3], 32, 1)),
-                    ),
-                )
-                out[n, :16, :] = jnp.concatenate([first, second], axis=0).astype(jnp.bfloat16)
-                out[n, 16:, :] = third.astype(jnp.bfloat16)
+                    to = pl.multiple_of((n * (groups // 4) + q // 4) * GROUP, GROUP)
+                    rows[q % 4, pl.ds(to, GROUP), :] = jnp.where(used, total, 0.0)
             return 0
 
         lax.fori_loop(0, chunks // RING, body, 0)
 
+        def pack(i, _):
+            at = pl.multiple_of(i * 128, 128)
+            part = [rows[q, pl.ds(at, 128), :].astype(jnp.bfloat16) for q in range(4)]
+            outer = [jnp.concatenate([part[0], part[2]], axis=1)]
+            outer.append(jnp.concatenate([part[1], part[3]], axis=1))
+            first = jnp.dot(outer[0], pick[0], preferred_element_type=jnp.float32)
+            second = jnp.dot(outer[1], pick[0], preferred_element_type=jnp.float32)
+            third = jnp.dot(outer[0], pick[1], preferred_element_type=jnp.float32)
+            third += jnp.dot(outer[1], pick[2], preferred_element_type=jnp.float32)
+            for d in range(128 // GROUP):
+                here = slice(d * GROUP, (d + 1) * GROUP)
+                out[i * (128 // GROUP) + d, :16, :] = jnp.concatenate(
+                    [first[here], second[here]], axis=0
+                ).astype(jnp.bfloat16)
+                out[i * (128 // GROUP) + d, 16:, :] = third[here].astype(jnp.bfloat16)
+            return 0
+
+        lax.fori_loop(0, pairs * GROUP // 128, pack, 0)
+
+    pick = np.zeros((3, 2 * LANES, LANES), np.float32)
+    for c in range(half):
+        pick[0, c, c] = 1.0
+        pick[0, LANES + c, half + c] = 1.0
+    for c in range(32):
+        pick[1, half + c, c] = 1.0
+        pick[1, LANES + half + c, 64 + c] = 1.0
+        pick[2, half + c, 32 + c] = 1.0
+        pick[2, LANES + half + c, 96 + c] = 1.0
     vmem = pl.BlockSpec(memory_space=pltpu.VMEM)
     return pl.pallas_call(
         kernel,
         out_shape=(
             pltpu.VMEM(table.shape, jnp.float32),
             pltpu.VMEM(wide.shape, jnp.float32),
-            jax.ShapeDtypeStruct((chunks, packed, LANES), jnp.bfloat16),
-        ),
-        in_specs=[vmem] * 5,
+            jax.ShapeDtypeStruct((pairs, 24, LANES), jnp.bfloat16),
+        ),
+        in_specs=[vmem] * 6,
         out_specs=(vmem, vmem, vmem),
         scratch_shapes=[
             pltpu.SMEM((RING, CHUNK), jnp.int32),
             pltpu.SemaphoreType.DMA((RING,)),
+            pltpu.VMEM((4, pairs * GROUP, LANES), jnp.float32),
         ],
-        input_output_aliases={3: 0, 4: 1},
+        input_output_aliases={4: 0, 5: 1},
         compiler_params=pltpu.CompilerParams(vmem_limit_bytes=8 * MIB),
         cost_estimate=pl.CostEstimate(
             flops=4 * 10**10, transcendentals=0, bytes_accessed=2 * 10**7
         ),
         name="gather_rows",
-    )(index, zlo, zhi, table, wide)[2]
+    )(index, zlo, zhi, jnp.asarray(pick.astype(jnp.bfloat16)), table, wide)[2]
 
 
 def relight(transfer, routed, basis, projector):
@@ -513,7 +565,7 @@
     zhi = lax.ppermute(edge_lo, "gz", downs[2])
     zlo = lax.ppermute(edge_hi, "gz", ups[2])
     wide = spread_weights(ordered)
-    outgoing = gather_rows(index.reshape(-1), wide, table, zlo, zhi, rows, coeffs)
+    outgoing = gather_rows(index.reshape(-1), wide, table, zlo, zhi, rows, count, coeffs)
     routed = lax.all_to_all(
         outgoing, ("gx", "gy", "gz"), split_axis=0, concat_axis=0, tiled=True
     )

time: 169 us -> 183 us (1.083)
  local copies, waits for them, and re-layouts: 18.9 us -> 49.7 us
  Pallas kernels: 88.7 us -> 63.4 us
  waiting for transfers between devices: 10.2 us -> 18.6 us
    unnamed x28 -> x36, local copies, waits for them, and re-layouts: 5.22 us -> 36.1 us
    pallas_call x1, Pallas kernels: 33.9 us -> 24.2 us  [gather_rows(): pl.pallas_call(kernel, out_shape=(pltpu.VMEM(table.shape, jnp.float32), p...]
    pallas_call x1, Pallas kernels: 15.6 us -> 7 us  [spread_weights(): pl.pallas_call(kernel, out_shape=pltpu.VMEM((count * SAMPLES, LANES), jnp...]
    pallas_call x1, Pallas kernels: 16 us -> 9.01 us  [prepare(): pl.pallas_call(kernel, out_shape=(jax.ShapeDtypeStruct((count * SAMPLES /...]
    ppermute x1, waiting for transfers between devices: 10.2 us -> 16.7 us  [halo_step(): xlo = lax.ppermute(last, 'gx', ups[0])]
    ppermute x1, waiting for transfers between devices: 0.01 us -> 1.87 us  [halo_step(): yhi = lax.ppermute(bottom.reshape(plane), 'gy', downs[1])]
  transfers between devices with their start and end apart: 10 -> 10, of which waited for: 1 -> 2; matrix products, arithmetic and copies ran while one was open for 6% -> 5% of each run, Pallas kernels for 24% -> 13%
where the time goes in v2:
time: 183 us; the launch traced here: 182 us
  Pallas kernels  63.4 us (35%)
  local copies, waits for them, and re-layouts  49.7 us (27%)
  blocking collectives  30.3 us (17%)
  waiting for transfers between devices  18.6 us (10%)
  starting transfers between devices  18.4 us (10%)
    unnamed x36, local copies, waits for them, and re-layouts  36.1 us
    all_to_all x1, blocking collectives, halo_step(): lax.all_to_all(outgoing, ('gx', 'gy', 'gz'), split_axis=0, concat_axis=0,...  30.3 us
    pallas_call x1, Pallas kernels, gather_rows(): pl.pallas_call(kernel, out_shape=(pltpu.VMEM(table.shape, jnp.float32), p...  24.2 us
    ppermute x1, waiting for transfers between devices, halo_step(): xlo = lax.ppermute(last, 'gx', ups[0])  16.7 us
    ppermute x4, starting transfers between devices, halo_step(): lax.ppermute(piece, ('gx', 'gy'), moves(along[:2], (step_x, step_y)))  11.6 us
    pallas_call x1, Pallas kernels, prepare(): pl.pallas_call(kernel, out_shape=(jax.ShapeDtypeStruct((count * SAMPLES /...  9.01 us
    pallas_call x1, Pallas kernels, own_table(): pl.pallas_call(kernel, out_shape=pltpu.HBM((cells_x * plane, LANES), jnp....  8.35 us
    pallas_call x1, Pallas kernels, relight(): pl.pallas_call(kernel, out_shape=jax.ShapeDtypeStruct((coeffs, count), jn...  7.53 us
  transfers between devices with their start and end apart: 10, of which 2 were waited for; matrix products, arithmetic and copies ran while one was open for 5% of the time, Pallas kernels for 13%

profile of v2, /device:TPU:1, one launch (start us, length us, event | category | flops | bytes accessed | tf_op | source)
XLA Modules:
  0.0 182.3 jit_solution(18009405172363581498)
XLA Ops:
  0.0 3.1 %fusion.2 = (bf16[81,2,16,256]{3,2,1,0:T(8,128)(2,1)S(1)}, bf16[81,2,16,256]{3,2,1,0:T(8,128)(2,1)}) fusion(bf16[81,8,16,256]{3,2,1,0:T(8,128)(2,1)} %field.1), kind=kLoop, calls=%fused_computation.5 | loop fusion | bytes 5308416 | tf_op jit(solution)/shard_map/slice | solution.py:531
  3.1 2.3 %fusion.1 = (bf16[81,2,2,256]{3,2,1,0:T(2,128)(2,1)S(1)}, bf16[81,2,2,256]{3,2,1,0:T(2,128)(2,1)S(1)}, bf16[81,2,2,256]{3,2,1,0:T(2,128)(2,1)S(1)}, bf16[81,2,2,256]{3,2,1,0:T(2,128)(2,1)S(1)}) fusion(bf16[81,8,16,256]{3,2,1,0:T(8,128)(2,1)} %field.1), kind=kLoop, calls=%fused_computation.4 | loop fusion | bytes 1327104 | tf_op jit(solution)/shard_map/slice | solution.py:542
  6.1 5.5 %collective-permute-start = (bf16[81,4,256]{2,1,0:T(4,128)(2,1)}, bf16[81,4,256]{2,1,0:T(4,128)(2,1)}, u32[]{:S(2)}, u32[]{:S(2)}) collective-permute-start(bf16[81,4,256]{2,1,0:T(4,128)(2,1)} %copy.17), channel_id=1, source_target_pairs={{0,20},{4,24},{8,28},{12,16},{16,36},{20,40},{24,44},{28,32},{32,5... | collective-permute-start | bytes 497672 | tf_op jit(solution)/shard_map/ppermute | solution.py:544
  13.7 1.1 collective-permute-start.2
  14.9 4.4 %collective-permute-start.1 = (bf16[81,4,256]{2,1,0:T(4,128)(2,1)S(1)}, bf16[81,4,256]{2,1,0:T(4,128)(2,1)}, u32[]{:S(2)}, u32[]{:S(2)}) collective-permute-start(bf16[81,4,256]{2,1,0:T(4,128)(2,1)S(1)} %copy.19), channel_id=1, source_target_pairs={{0,116},{4,120},{8,124},{12,112},{16,4},{20,8},{24,12},{28,0},{32,... | collective-permute-start | bytes 497672 | tf_op jit(solution)/shard_map/ppermute | solution.py:544
  19.2 3.8 %fusion = (bf16[81,8,2,256]{3,2,1,0:T(2,128)(2,1)S(1)}, bf16[81,8,2,256]{3,2,1,0:T(2,128)(2,1)S(1)}) fusion(bf16[81,8,16,256]{3,2,1,0:T(8,128)(2,1)} %field.1), kind=kLoop, calls=%fused_computation.3 | loop fusion | bytes 2654208 | tf_op jit(solution)/shard_map/slice | solution.py:537
  24.5 2.5 %copy-done = bf16[81,8,16,256]{3,2,1,0:T(8,128)(2,1)S(1)} copy-done((bf16[81,8,16,256]{3,2,1,0:T(8,128)(2,1)S(1)}, bf16[81,8,16,256]{3,2,1,0:T(8,128)(2,1)}, u32[]{:S(2)}) %copy-start) | copy-done | bytes 5308440
  27.0 8.4 %own_table.1.own = f32[32768,128]{1,0:T(8,128)} custom-call(bf16[81,8,16,256]{3,2,1,0:T(8,128)(2,1)S(1)} %copy-done, bf16[256,256]{1,0:T(8,128)(2,1)S(1)} %copy-done.8), custom_call_target="tpu_custom_call" | custom-call | flops 20000000000 | bytes 20000000 | tf_op jit(solution)/shard_map/own_table/pallas_call | solution.py:107
  36.7 3.6 %collective-permute-start.5 = (bf16[81,2,16,256]{3,2,1,0:T(8,128)(2,1)S(1)}, bf16[81,2,16,256]{3,2,1,0:T(8,128)(2,1)S(1)}, u32[]{:S(2)}, u32[]{:S(2)}) collective-permute-start(bf16[81,2,16,256]{3,2,1,0:T(8,128)(2,1)S(1)} %get-tuple-element.24), channel_id=1, source_target_pairs={{0,112},{16,0},{32,16},{48,32},{64,48},{80,64},{96,80},{112,96},{1... | collective-permute-start | bytes 3981320 | tf_op jit(solution)/shard_map/ppermute | solution.py:534
  40.3 9.0 %prepare.1 = (s32[256,128]{1,0:T(8,128)S(1)}, f32[4096,128]{1,0:T(8,128)S(1)}) custom-call(s32[3]{0:T(128)S(1)} %pad_add_fusion.origin, s32[4096]{0:T(1024)S(1)} %bitcast.9, s32[3,8,4096]{2,1,0:T(8,128)S(1)} %copy-done.5, f32[8,4096]{1,0:T(8,128)S(1)} %copy-done.6, bf16[256,256]{1,0:T(8,128)(2,1)S(1)} %copy-done.8, bf16[16,128]{1,0:T(8,128)(2,1)S(1)} %copy-done.10), custom_call_target="tpu_custom_call" | custom-call | flops 20000000000 | bytes 3000000 | tf_op jit(solution)/shard_map/prepare/pallas_call | solution.py:289
  50.0 1.6 pad_maximum_fusion.corners
  51.6 1.9 %collective-permute-done.7.yhi = bf16[81,16,256]{2,1,0:T(8,128)(2,1)S(1)} collective-permute-done((bf16[81,16,256]{2,1,0:T(8,128)(2,1)}, bf16[81,16,256]{2,1,0:T(8,128)(2,1)S(1)}, u32[]{:S(2)}, u32[]{:S(2)}) %collective-permute-start.7) | collective-permute-done | bytes 663584 | tf_op jit(solution)/shard_map/ppermute | solution.py:539
  53.5 16.7 %collective-permute-done.4.xlo = bf16[81,2,16,256]{3,2,1,0:T(8,128)(2,1)S(1)} collective-permute-done((bf16[81,2,16,256]{3,2,1,0:T(8,128)(2,1)}, bf16[81,2,16,256]{3,2,1,0:T(8,128)(2,1)S(1)}, u32[]{:S(2)}, u32[]{:S(2)}) %collective-permute-start.4) | collective-permute-done | bytes 1327136 | tf_op jit(solution)/shard_map/ppermute | solution.py:533
  70.2 7.3 %full_table.1 = (f32[62400,128]{1,0:T(8,128)S(1)}, bf16[480,128]{1,0:T(8,128)(2,1)S(1)}, bf16[480,128]{1,0:T(8,128)(2,1)S(1)}) custom-call(f32[32768,128]{1,0:T(8,128)} %own_table.1.own, bf16[81,2,16,256]{3,2,1,0:T(8,128)(2,1)S(1)} %collective-permute-done.4.xlo, bf16[81,2,16,256]{3,2,1,0:T(8,128)(2,1)S(1)} %collective-permute-done.5.xhi, ...), custom_call_target="tpu_custom_call" | custom-call | flops 20000000000 | bytes 20000000 | tf_op jit(solution)/shard_map/full_table/pallas_call | solution.py:173
  77.5 10.5 %copy-done.13 = f32[62400,128]{1,0:T(8,128)} copy-done((f32[62400,128]{1,0:T(8,128)}, f32[62400,128]{1,0:T(8,128)S(1)}, u32[]{:S(2)}) %copy-start.13) | copy-done | bytes 31948824
  88.0 1.3 collective-permute-start.8
  89.3 1.4 collective-permute-start.9
  90.8 7.0 %spread_weights.1.wide_in = f32[32768,128]{1,0:T(8,128)S(1)} custom-call(f32[4096,128]{1,0:T(8,128)S(1)} %get-tuple-element.29.ordered, bf16[128,1024]{1,0:T(8,128)(2,1)S(1)} %copy-done.7), custom_call_target="tpu_custom_call" | custom-call | flops 10000000000 | bytes 3000000 | tf_op jit(solution)/shard_map/spread_weights/pallas_call | solution.py:342
  97.8 5.8 %copy-done.11 = f32[32768,128]{1,0:T(8,128)} copy-done((f32[32768,128]{1,0:T(8,128)}, f32[32768,128]{1,0:T(8,128)S(1)}, u32[]{:S(2)}) %copy-start.11) | copy-done | bytes 16777240
  104.3 5.8 %copy-done.12 = f32[32768,128]{1,0:T(8,128)S(1)} copy-done((f32[32768,128]{1,0:T(8,128)S(1)}, f32[32768,128]{1,0:T(8,128)}, u32[]{:S(2)}) %copy-start.12) | copy-done | bytes 16777240
  110.0 10.1 %copy-done.14 = f32[62400,128]{1,0:T(8,128)S(1)} copy-done((f32[62400,128]{1,0:T(8,128)S(1)}, f32[62400,128]{1,0:T(8,128)}, u32[]{:S(2)}) %copy-start.14) | copy-done | bytes 31948824
  120.1 24.2 %gather_rows.1 = (f32[62400,128]{1,0:T(8,128)S(1)}, f32[32768,128]{1,0:T(8,128)S(1)}, bf16[128,24,128]{2,1,0:T(8,128)(2,1)}) custom-call(s32[32768]{0:T(1024)} %bitcast.10, bf16[480,128]{1,0:T(8,128)(2,1)} %copy-done.16, bf16[480,128]{1,0:T(8,128)(2,1)} %copy-done.17, ...), custom_call_target="tpu_custom_call", output_to_operand_aliasing={{0}: (4, {}), {1}: (5, {})} | custom-call | flops 40000000000 | bytes 20000000 | tf_op jit(solution)/shard_map/gather_rows/pallas_call | solution.py:440
  144.4 30.3 %all_to_all.5.routed = bf16[128,24,128]{2,1,0:T(8,128)(2,1)S(1)} all-to-all(bf16[128,24,128]{2,1,0:T(8,128)(2,1)} %get-tuple-element.30), channel_id=1, replica_groups=mesh['gx'=8,'gy'=4,'gz'=4] {'gx','gy','gz'}, dimensions={0} | all-to-all | bytes 1572864 | tf_op jit(solution)/shard_map/all_to_all | solution.py:569
  174.7 7.5 %relight.1 = bf16[81,4096]{1,0:T(8,128)(2,1)} custom-call(bf16[81,4096]{1,0:T(8,128)(2,1)S(1)} %copy-done.1, bf16[128,24,128]{2,1,0:T(8,128)(2,1)S(1)} %all_to_all.5.routed, bf16[1024,81]{1,0:T(8,128)(2,1)S(1)} %copy-done.3, bf16[1024,128]{1,0:T(8,128)(2,1)S(1)} %copy-done.2, bf16[81,1024]{1,0:T(8,128)(2,1)S(1)} %copy-done.4), custom_call_target="tpu_custom_call" | custom-call | tf_op jit(solution)/shard_map/relight/pallas_call | solution.py:496
  (55 shorter events, 7.2 us)
Async XLA Ops:
  6.1 30.5 %collective-permute-start = (bf16[81,4,256]{2,1,0:T(4,128)(2,1)}, bf16[81,4,256]{2,1,0:T(4,128)(2,1)}, u32[]{:S(2)}, u32[]{:S(2)}) collective-permute-start(bf16[81,4,256]{2,1,0:T(4,128)(2,1)} %copy.17), channel_id=1, source_target_pairs={{0,20},{4,24},{8,28},{12,16},{16,36},{20,40},{24,44},{28,32},{32,5... | collective-permute-start | bytes 497672 | tf_op jit(solution)/shard_map/ppermute | solution.py:544
  12.3 24.4 %collective-permute-start.3 = (bf16[81,4,256]{2,1,0:T(4,128)(2,1)}, bf16[81,4,256]{2,1,0:T(4,128)(2,1)}, u32[]{:S(2)}, u32[]{:S(2)}) collective-permute-start(bf16[81,4,256]{2,1,0:T(4,128)(2,1)} %copy.23), channel_id=1, source_target_pairs={{0,124},{4,112},{8,116},{12,120},{16,12},{20,0},{24,4},{28,8},{32,... | collective-permute-start | bytes 497672 | tf_op jit(solution)/shard_map/ppermute | solution.py:544
  13.7 23.1 %collective-permute-start.2 = (bf16[81,4,256]{2,1,0:T(4,128)(2,1)}, bf16[81,4,256]{2,1,0:T(4,128)(2,1)}, u32[]{:S(2)}, u32[]{:S(2)}) collective-permute-start(bf16[81,4,256]{2,1,0:T(4,128)(2,1)} %copy.21), channel_id=1, source_target_pairs={{0,28},{4,16},{8,20},{12,24},{16,44},{20,32},{24,36},{28,40},{32,6... | collective-permute-start | bytes 497672 | tf_op jit(solution)/shard_map/ppermute | solution.py:544
  14.9 35.1 %collective-permute-start.1 = (bf16[81,4,256]{2,1,0:T(4,128)(2,1)S(1)}, bf16[81,4,256]{2,1,0:T(4,128)(2,1)}, u32[]{:S(2)}, u32[]{:S(2)}) collective-permute-start(bf16[81,4,256]{2,1,0:T(4,128)(2,1)S(1)} %copy.19), channel_id=1, source_target_pairs={{0,116},{4,120},{8,124},{12,112},{16,4},{20,8},{24,12},{28,0},{32,... | collective-permute-start | bytes 497672 | tf_op jit(solution)/shard_map/ppermute | solution.py:544
  24.1 27.5 %collective-permute-start.6 = (bf16[81,16,256]{2,1,0:T(8,128)(2,1)}, bf16[81,16,256]{2,1,0:T(8,128)(2,1)S(1)}, u32[]{:S(2)}, u32[]{:S(2)}) collective-permute-start(bf16[81,16,256]{2,1,0:T(8,128)(2,1)} %reshape.29), channel_id=1, source_target_pairs={{0,4},{4,8},{8,12},{12,0},{1,5},{5,9},{9,13},{13,1},{2,6},{6,10},{... | collective-permute-start | bytes 1990664 | tf_op jit(solution)/shard_map/ppermute | solution.py:538
  24.5 2.5 %copy-start = (bf16[81,8,16,256]{3,2,1,0:T(8,128)(2,1)S(1)}, bf16[81,8,16,256]{3,2,1,0:T(8,128)(2,1)}, u32[]{:S(2)}) copy-start(bf16[81,8,16,256]{3,2,1,0:T(8,128)(2,1)} %field.1) | copy-start | bytes 15925252
  27.0 8.4 %copy-start.15 = (s32[2,4096]{1,0:T(2,128)S(1)}, s32[2,4096]{1,0:T(2,128)}, u32[]{:S(2)}) copy-start(s32[2,4096]{1,0:T(2,128)} %param.16) | copy-start | bytes 98308
  35.3 5.0 %copy-start.5 = (s32[3,8,4096]{2,1,0:T(8,128)S(1)}, s32[3,8,4096]{2,1,0:T(8,128)}, u32[]{:S(2)}) copy-start(s32[3,8,4096]{2,1,0:T(8,128)} %samples.1) | copy-start | bytes 1179652
  35.3 5.0 %copy-start.6 = (f32[8,4096]{1,0:T(8,128)S(1)}, f32[8,4096]{1,0:T(8,128)}, u32[]{:S(2)}) copy-start(f32[8,4096]{1,0:T(8,128)} %weights.1) | copy-start | bytes 393220
  35.3 5.0 %copy-start.10 = (bf16[16,128]{1,0:T(8,128)(2,1)S(1)}, bf16[16,128]{1,0:T(8,128)(2,1)}, u32[]{:S(2)}) copy-start(bf16[16,128]{1,0:T(8,128)(2,1)} %constant.36.clone.join) | copy-start | bytes 12292
  36.5 17.0 %collective-permute-start.7 = (bf16[81,16,256]{2,1,0:T(8,128)(2,1)}, bf16[81,16,256]{2,1,0:T(8,128)(2,1)S(1)}, u32[]{:S(2)}, u32[]{:S(2)}) collective-permute-start(bf16[81,16,256]{2,1,0:T(8,128)(2,1)} %reshape.30), channel_id=1, source_target_pairs={{0,12},{4,0},{8,4},{12,8},{1,13},{5,1},{9,5},{13,9},{2,14},{6,2},{... | collective-permute-start | bytes 1990664 | tf_op jit(solution)/shard_map/ppermute | solution.py:539
  36.7 33.5 %collective-permute-start.4 = (bf16[81,2,16,256]{3,2,1,0:T(8,128)(2,1)}, bf16[81,2,16,256]{3,2,1,0:T(8,128)(2,1)S(1)}, u32[]{:S(2)}, u32[]{:S(2)}) collective-permute-start(bf16[81,2,16,256]{3,2,1,0:T(8,128)(2,1)} %get-tuple-element.23), channel_id=1, source_target_pairs={{0,16},{16,32},{32,48},{48,64},{64,80},{80,96},{96,112},{112,0},{1... | collective-permute-start | bytes 3981320 | tf_op jit(solution)/shard_map/ppermute | solution.py:533
  36.7 33.5 %collective-permute-start.5 = (bf16[81,2,16,256]{3,2,1,0:T(8,128)(2,1)S(1)}, bf16[81,2,16,256]{3,2,1,0:T(8,128)(2,1)S(1)}, u32[]{:S(2)}, u32[]{:S(2)}) collective-permute-start(bf16[81,2,16,256]{3,2,1,0:T(8,128)(2,1)S(1)} %get-tuple-element.24), channel_id=1, source_target_pairs={{0,112},{16,0},{32,16},{48,32},{64,48},{80,64},{96,80},{112,96},{1... | collective-permute-start | bytes 3981320 | tf_op jit(solution)/shard_map/ppermute | solution.py:534
  51.6 39.1 %copy-start.7 = (bf16[128,1024]{1,0:T(8,128)(2,1)S(1)}, bf16[128,1024]{1,0:T(8,128)(2,1)}, u32[]{:S(2)}) copy-start(bf16[128,1024]{1,0:T(8,128)(2,1)} %constant.37.clone.ones) | copy-start | bytes 786436
  77.5 10.5 %copy-start.13 = (f32[62400,128]{1,0:T(8,128)}, f32[62400,128]{1,0:T(8,128)S(1)}, u32[]{:S(2)}) copy-start(f32[62400,128]{1,0:T(8,128)S(1)} %get-tuple-element.28.table_in) | copy-start | bytes 95846400
  88.0 15.6 %collective-permute-start.8 = (bf16[480,128]{1,0:T(8,128)(2,1)S(1)}, bf16[480,128]{1,0:T(8,128)(2,1)S(1)}, u32[]{:S(2)}, u32[]{:S(2)}) collective-permute-start(bf16[480,128]{1,0:T(8,128)(2,1)S(1)} %get-tuple-element.26), channel_id=1, source_target_pairs={{0,1},{1,2},{2,3},{3,0},{4,5},{5,6},{6,7},{7,4},{8,9},{9,10},{10,1... | collective-permute-start | bytes 368648 | tf_op jit(solution)/shard_map/ppermute | solution.py:566
  89.3 14.3 %collective-permute-start.9 = (bf16[480,128]{1,0:T(8,128)(2,1)S(1)}, bf16[480,128]{1,0:T(8,128)(2,1)S(1)}, u32[]{:S(2)}, u32[]{:S(2)}) collective-permute-start(bf16[480,128]{1,0:T(8,128)(2,1)S(1)} %get-tuple-element.27), channel_id=1, source_target_pairs={{0,3},{1,0},{2,1},{3,2},{4,7},{5,4},{6,5},{7,6},{8,11},{9,8},{10,9... | collective-permute-start | bytes 368648 | tf_op jit(solution)/shard_map/ppermute | solution.py:565
  97.8 5.8 %copy-start.11 = (f32[32768,128]{1,0:T(8,128)}, f32[32768,128]{1,0:T(8,128)S(1)}, u32[]{:S(2)}) copy-start(f32[32768,128]{1,0:T(8,128)S(1)} %spread_weights.1.wide_in) | copy-start | bytes 50331652
  104.3 5.8 %copy-start.12 = (f32[32768,128]{1,0:T(8,128)S(1)}, f32[32768,128]{1,0:T(8,128)}, u32[]{:S(2)}) copy-start(f32[32768,128]{1,0:T(8,128)} %copy-done.11) | copy-start | bytes 50331652
  110.0 10.1 %copy-start.14 = (f32[62400,128]{1,0:T(8,128)S(1)}, f32[62400,128]{1,0:T(8,128)}, u32[]{:S(2)}) copy-start(f32[62400,128]{1,0:T(8,128)} %copy-done.13) | copy-start | bytes 95846400
  144.3 30.4 %copy-start.1 = (bf16[81,4096]{1,0:T(8,128)(2,1)S(1)}, bf16[81,4096]{1,0:T(8,128)(2,1)}, u32[]{:S(2)}) copy-start(bf16[81,4096]{1,0:T(8,128)(2,1)} %transfer.1) | copy-start | bytes 1990660
  144.4 30.4 %copy-start.2 = (bf16[1024,128]{1,0:T(8,128)(2,1)S(1)}, bf16[1024,128]{1,0:T(8,128)(2,1)}, u32[]{:S(2)}) copy-start(bf16[1024,128]{1,0:T(8,128)(2,1)} %constant.40.clone.wide) | copy-start | bytes 786436
  144.4 30.4 %copy-start.3 = (bf16[1024,81]{1,0:T(8,128)(2,1)S(1)}, bf16[1024,81]{1,0:T(8,128)(2,1)}, u32[]{:S(2)}) copy-start(bf16[1024,81]{1,0:T(8,128)(2,1)} %constant.39.clone.basis) | copy-start | bytes 497668
  144.4 30.3 %copy-start.4 = (bf16[81,1024]{1,0:T(8,128)(2,1)S(1)}, bf16[81,1024]{1,0:T(8,128)(2,1)}, u32[]{:S(2)}) copy-start(bf16[81,1024]{1,0:T(8,128)(2,1)} %constant.41.clone.projector) | copy-start | bytes 497668
  (4 other events, 3.5 us)

commit v3 on v2

--- a/solution.py
+++ b/solution.py
@@ -86,6 +86,56 @@
     return pltpu.VMEM((cells_z // LANES, cells_y * coeffs + 16, LANES), jnp.float32)
 
 
+def cut_faces(field):
+    coeffs, cells_x, cells_y, cells_z = field.shape
+    per_step = 9
+    rows = cells_x * HALO
+    corner = HALO * HALO
+
+    def kernel(field, pick, last, first, top, bottom, *corners):
+        for c in range(per_step):
+            last[c] = field[c, cells_x - HALO :]
+            first[c] = field[c, :HALO]
+            chosen = jnp.dot(
+                pick[...],
+                field[c].reshape(cells_x * cells_y, cells_z),
+                preferred_element_type=jnp.float32,
+            ).astype(jnp.bfloat16)
+            top[c] = chosen[:rows]
+            bottom[c] = chosen[rows : 2 * rows]
+            for q in range(4):
+                at = 2 * rows + q * 16
+                corners[q][c] = chosen[at : at + corner]
+
+    pick = np.zeros((2 * rows + 64, cells_x * cells_y), np.float32)
+    for x in range(cells_x):
+        for j in range(HALO):
+            pick[x * HALO + j, x * cells_y + cells_y - HALO + j] = 1.0
+            pick[rows + x * HALO + j, x * cells_y + j] = 1.0
+    for q in range(4):
+        start_y = cells_y - HALO if q < 2 else 0
+        start_x = cells_x - HALO if q % 2 == 0 else 0
+        for i in range(HALO):
+            for j in range(HALO):
+                pick[2 * rows + q * 16 + i * HALO + j, (start_x + i) * cells_y + start_y + j] = 1.0
+    shapes = [(coeffs, HALO, cells_y, cells_z)] * 2
+    shapes += [(coeffs, rows, cells_z)] * 2 + [(coeffs, corner, cells_z)] * 4
+
+    def whole(shape):
+        zeros = (0,) * (len(shape) - 1)
+        return pl.BlockSpec((per_step,) + shape[1:], lambda i: (i,) + zeros)
+
+    return pl.pallas_call(
+        kernel,
+        out_shape=[pltpu.HBM(shape, jnp.bfloat16) for shape in shapes],
+        grid=(coeffs // per_step,),
+        in_specs=[whole(field.shape), pl.BlockSpec(pick.shape, lambda i: (0, 0))],
+        out_specs=[whole(shape) for shape in shapes],
+        compiler_params=pltpu.CompilerParams(vmem_limit_bytes=24 * MIB),
+        name="cut_faces",
+    )(field, jnp.asarray(pick.astype(jnp.bfloat16)))
+
+
 def own_table(field, eye):
     coeffs, cells_x, cells_y, cells_z = field.shape
     plane = cells_y * cells_z
@@ -127,14 +177,27 @@
     count = 2 * HALO + 3
     own_rows = own.shape[0]
     lines = own_rows // cells_z + count * cells_y
-    halves = range(cells_z // LANES)
-
-    def kernel(own, xlo, xhi, ylo, yhi, corners, eye, table, zhi, zlo, buf, sems, spread, done):
-        sources = [xlo.at[:, 0], xlo.at[:, 1], xhi.at[:, 0], xhi.at[:, 1], ylo, yhi, corners]
+
+    def kernel(own, xlo, xhi, ylo, yhi, c0, c1, c2, c3, eye, table, zhi, zlo, *scratch):
+        buf, sems, small, small_sems, spread, done = scratch
+        inherit = pltpu.make_async_copy(own, table.at[pl.ds(0, own_rows), :], done)
+        sources = [xlo.at[:, 0], xlo.at[:, 1], xhi.at[:, 0], xhi.at[:, 1], ylo, yhi]
         for p, source in enumerate(sources):
             pltpu.make_async_copy(source, buf.at[p], sems.at[p]).start()
-        inherit = pltpu.make_async_copy(own, table.at[pl.ds(0, own_rows), :], done)
+        pieces = [
+            pltpu.make_async_copy(corner, small.at[q], small_sems.at[q])
+            for q, corner in enumerate((c0, c1, c2, c3))
+        ]
+        for piece in pieces:
+            piece.start()
         inherit.start()
+
+        def turn(p):
+            def put(y, block):
+                at = pl.multiple_of(own_rows + (p * cells_y + y) * cells_z, 8)
+                table[pl.ds(at, cells_z), :] = block
+
+            turn_rows(spread, eye, coeffs, cells_y, cells_z, put)
 
         def one(p, _):
             pltpu.make_async_copy(ylo, buf.at[p], sems.at[p]).wait()
@@ -145,15 +208,26 @@
                 cells_y,
                 cells_z,
             )
-
-            def put(y, block):
-                at = pl.multiple_of(own_rows + (p * cells_y + y) * cells_z, 8)
-                table[pl.ds(at, cells_z), :] = block
-
-            turn_rows(spread, eye, coeffs, cells_y, cells_z, put)
+            turn(p)
             return 0
 
-        lax.fori_loop(0, count, one, 0)
+        lax.fori_loop(0, count - 1, one, 0)
+        for piece in pieces:
+            piece.wait()
+        fill_rows(
+            lambda c, h: jnp.concatenate(
+                [
+                    small[q, c, :, h * LANES : (h + 1) * LANES].astype(jnp.float32)
+                    for q in range(4)
+                ],
+                axis=0,
+            ),
+            spread,
+            coeffs,
+            cells_y,
+            cells_z,
+        )
+        turn(count - 1)
         inherit.wait()
         for out, start in ((zhi, 0), (zlo, cells_z - HALO)):
             for j in range(HALO):
@@ -166,27 +240,28 @@
                         parts, axis=0
                     ).astype(jnp.bfloat16)
 
-    del halves
     edge = jax.ShapeDtypeStruct((HALO * lines, LANES), jnp.bfloat16)
     vmem = pl.BlockSpec(memory_space=pltpu.VMEM)
     hbm = pl.BlockSpec(memory_space=pl.ANY)
     return pl.pallas_call(
         kernel,
         out_shape=(pltpu.VMEM((total_rows, LANES), jnp.float32), edge, edge),
-        in_specs=[hbm] * 6 + [vmem],
+        in_specs=[hbm] * 9 + [vmem],
         out_specs=(vmem, vmem, vmem),
         scratch_shapes=[
-            pltpu.VMEM((count, coeffs, cells_y, cells_z), jnp.bfloat16),
-            pltpu.SemaphoreType.DMA((count,)),
+            pltpu.VMEM((count - 1, coeffs, cells_y, cells_z), jnp.bfloat16),
+            pltpu.SemaphoreType.DMA((count - 1,)),
+            pltpu.VMEM((4, coeffs, HALO * HALO, cells_z), jnp.bfloat16),
+            pltpu.SemaphoreType.DMA((4,)),
             spread_shape(coeffs, cells_y, cells_z),
             pltpu.SemaphoreType.DMA(()),
         ],
-        compiler_params=pltpu.CompilerParams(vmem_limit_bytes=12 * MIB),
+        compiler_params=pltpu.CompilerParams(vmem_limit_bytes=24 * MIB),
         cost_estimate=pl.CostEstimate(
             flops=2 * 10**10, transcendentals=0, bytes_accessed=2 * 10**7
         ),
         name="full_table",
-    )(own, xlo, xhi, ylo, yhi, corners, eye)
+    )(own, xlo, xhi, ylo, yhi, *corners, eye)
 
 
 GROUP = 8
@@ -312,39 +387,35 @@
 
 def spread_weights(ordered):
     count = ordered.shape[0]
-    block = 128
+    block = 512
 
     def kernel(ordered, ones, wide):
-        def body(i, _):
-            at = pl.multiple_of(i * block, block)
-            rows = ordered[pl.ds(at, block), :].astype(jnp.bfloat16)
-            for h in range(0, SAMPLES, 2):
-                both = jnp.dot(
-                    rows,
-                    ones[:, h * LANES : (h + 2) * LANES],
-                    preferred_element_type=jnp.float32,
-                )
-                for s in range(2):
-                    for g in range(block // GROUP):
-                        to = (i * (block // GROUP) + g) * SAMPLES + h + s
-                        wide[pl.ds(pl.multiple_of(to * GROUP, GROUP), GROUP), :] = both[
-                            g * GROUP : (g + 1) * GROUP, s * LANES : (s + 1) * LANES
-                        ]
-            return 0
-
-        lax.fori_loop(0, count // block, body, 0)
+        rows = ordered[...].astype(jnp.bfloat16)
+        for h in range(0, SAMPLES, 2):
+            both = jnp.dot(
+                rows, ones[:, h * LANES : (h + 2) * LANES], preferred_element_type=jnp.float32
+            )
+            for s in range(2):
+                for g in range(block // GROUP):
+                    to = (g * SAMPLES + h + s) * GROUP
+                    wide[to : to + GROUP, :] = both[
+                        g * GROUP : (g + 1) * GROUP, s * LANES : (s + 1) * LANES
+                    ]
 
     ones = np.zeros((LANES, SAMPLES * LANES), np.float32)
     for s in range(SAMPLES):
         for p in range(PARTS):
             ones[(2 + p) * SAMPLES + s, s * LANES : (s + 1) * LANES] = 1.0
-    vmem = pl.BlockSpec(memory_space=pltpu.VMEM)
     return pl.pallas_call(
         kernel,
-        out_shape=pltpu.VMEM((count * SAMPLES, LANES), jnp.float32),
-        in_specs=[vmem, vmem],
-        out_specs=vmem,
-        compiler_params=pltpu.CompilerParams(vmem_limit_bytes=4 * MIB),
+        out_shape=pltpu.HBM((count * SAMPLES, LANES), jnp.float32),
+        grid=(count // block,),
+        in_specs=[
+            pl.BlockSpec((block, LANES), lambda i: (i, 0)),
+            pl.BlockSpec(ones.shape, lambda i: (0, 0)),
+        ],
+        out_specs=pl.BlockSpec((block * SAMPLES, LANES), lambda i: (i, 0)),
+        compiler_params=pltpu.CompilerParams(vmem_limit_bytes=12 * MIB),
         cost_estimate=pl.CostEstimate(
             flops=10**10, transcendentals=0, bytes_accessed=3 * 10**6
         ),
@@ -364,7 +435,8 @@
     pairs = count // 32
     half = LANES // 2
 
-    def kernel(index, zlo, zhi, pick, table_in, wide_in, table, wide, out, local, sems, rows):
+    def kernel(index, zlo, zhi, pick, wide, table_in, table, out, *scratch):
+        local, sems, near, near_sems, rows = scratch
         table[pl.ds(first_edge, edges), :] = zlo[...].astype(jnp.float32)
         table[pl.ds(first_edge + edges, edges), :] = zhi[...].astype(jnp.float32)
         sublane = lax.broadcasted_iota(jnp.int32, (GROUP, LANES), 0)
@@ -378,18 +450,28 @@
                 sems.at[slot],
             )
 
+        def stream(n, slot):
+            return pltpu.make_async_copy(
+                wide.at[pl.ds(pl.multiple_of(n * CHUNK, CHUNK), CHUNK), :],
+                near.at[slot],
+                near_sems.at[slot],
+            )
+
         for b in range(RING - 1):
             fetch(b, b).start()
+            stream(b, b).start()
 
         def body(i, _):
             for b in range(RING):
                 n = i * RING + b
                 fetch(n, b).wait()
+                stream(n, b).wait()
                 ahead = n + RING - 1
 
                 @pl.when(ahead < chunks)
                 def _():
                     fetch(ahead, (b + RING - 1) % RING).start()
+                    stream(ahead, (b + RING - 1) % RING).start()
 
                 for q in range(groups):
                     total = None
@@ -399,8 +481,8 @@
                             place = s * per_chunk + q * GROUP + k
                             row = table[pl.ds(local[b, place], GROUP, stride=0), :]
                             merged = row if merged is None else jnp.where(masks[k], row, merged)
-                        at = pl.multiple_of(n * CHUNK + (q * SAMPLES + s) * GROUP, GROUP)
-                        term = merged * wide[pl.ds(at, GROUP), :]
+                        at = (q * SAMPLES + s) * GROUP
+                        term = merged * near[b, at : at + GROUP, :]
                         total = term if total is None else total + term
                     to = pl.multiple_of((n * (groups // 4) + q // 4) * GROUP, GROUP)
                     rows[q % 4, pl.ds(to, GROUP), :] = jnp.where(used, total, 0.0)
@@ -441,23 +523,24 @@
         kernel,
         out_shape=(
             pltpu.VMEM(table.shape, jnp.float32),
-            pltpu.VMEM(wide.shape, jnp.float32),
             jax.ShapeDtypeStruct((pairs, 24, LANES), jnp.bfloat16),
         ),
-        in_specs=[vmem] * 6,
-        out_specs=(vmem, vmem, vmem),
+        in_specs=[vmem] * 4 + [pl.BlockSpec(memory_space=pl.ANY), vmem],
+        out_specs=(vmem, vmem),
         scratch_shapes=[
             pltpu.SMEM((RING, CHUNK), jnp.int32),
             pltpu.SemaphoreType.DMA((RING,)),
+            pltpu.VMEM((RING, CHUNK, LANES), jnp.float32),
+            pltpu.SemaphoreType.DMA((RING,)),
             pltpu.VMEM((4, pairs * GROUP, LANES), jnp.float32),
         ],
-        input_output_aliases={4: 0, 5: 1},
-        compiler_params=pltpu.CompilerParams(vmem_limit_bytes=8 * MIB),
+        input_output_aliases={5: 0},
+        compiler_params=pltpu.CompilerParams(vmem_limit_bytes=24 * MIB),
         cost_estimate=pl.CostEstimate(
             flops=4 * 10**10, transcendentals=0, bytes_accessed=2 * 10**7
         ),
         name="gather_rows",
-    )(index, zlo, zhi, jnp.asarray(pick.astype(jnp.bfloat16)), table, wide)[2]
+    )(index, zlo, zhi, jnp.asarray(pick.astype(jnp.bfloat16)), wide, table)[1]
 
 
 def relight(transfer, routed, basis, projector):
@@ -527,22 +610,14 @@
     ups = [moves((n, 1), (1, 0)) for n in along]
     downs = [moves((n, 1), (-1, 0)) for n in along]
 
-    last, first, cut = lax.optimization_barrier(
-        (field[:, cells_x - HALO :], field[:, :HALO], field)
-    )
+    last, first, top, bottom, *pieces = cut_faces(field)
     xlo = lax.ppermute(last, "gx", ups[0])
     xhi = lax.ppermute(first, "gx", downs[0])
-    plane = (coeffs, cells_x * HALO, cells_z)
-    top = cut[:, :, cells_y - HALO :]
-    bottom = cut[:, :, :HALO]
-    ylo = lax.ppermute(top.reshape(plane), "gy", ups[1])
-    yhi = lax.ppermute(bottom.reshape(plane), "gy", downs[1])
+    ylo = lax.ppermute(top, "gy", ups[1])
+    yhi = lax.ppermute(bottom, "gy", downs[1])
     corners = []
-    for edge, step_y in ((top, 1), (bottom, -1)):
-        for piece, step_x in ((edge[:, cells_x - HALO :], 1), (edge[:, :HALO], -1)):
-            piece = piece.reshape(coeffs, HALO * HALO, cells_z)
-            corners.append(lax.ppermute(piece, ("gx", "gy"), moves(along[:2], (step_x, step_y))))
-    corners = jnp.concatenate(corners, axis=1)
+    for piece, step in zip(pieces, ((1, 1), (-1, 1), (1, -1), (-1, -1))):
+        corners.append(lax.ppermute(piece, ("gx", "gy"), moves(along[:2], step)))
 
     lines = cells_x * cells_y + (2 * HALO + 3) * cells_y
     rows = lines * cells_z
@@ -558,13 +633,13 @@
     eye = jnp.asarray(np.eye(cells_z, dtype=np.float32).astype(jnp.bfloat16))
     own = own_table(field, eye)
     index, ordered = prepare(samples, weights, slot, origin, cells, total)
-    own, index, ordered, corners = lax.optimization_barrier((own, index, ordered, corners))
+    wide = spread_weights(ordered)
+    own, index, wide = lax.optimization_barrier((own, index, wide))
     table, edge_lo, edge_hi = full_table(
         own, xlo, xhi, ylo, yhi, corners, eye, rows + 2 * HALO * lines
     )
     zhi = lax.ppermute(edge_lo, "gz", downs[2])
     zlo = lax.ppermute(edge_hi, "gz", ups[2])
-    wide = spread_weights(ordered)
     outgoing = gather_rows(index.reshape(-1), wide, table, zlo, zhi, rows, count, coeffs)
     routed = lax.all_to_all(
         outgoing, ("gx", "gy", "gz"), split_axis=0, concat_axis=0, tiled=True

time: 183 us -> 157 us (0.86)
  local copies, waits for them, and re-layouts: 49.7 us -> 9.48 us
  Pallas kernels: 63.4 us -> 84.7 us
  blocking collectives: 30.3 us -> 23.2 us
    unnamed x36 -> x50, local copies, waits for them, and re-layouts: 36.1 us -> 9.48 us
    pallas_call x2 -> x3, Pallas kernels: 31.2 us -> 50.4 us  [the longest x1 37.8 us: gather_rows(): pl.pallas_call(kernel, out_shape=(pltpu.VMEM(table.shape, jnp.float32), j...]
    ppermute x1, waiting for transfers between devices: 16.7 us -> 0.01 us  [halo_step(): xlo = lax.ppermute(last, 'gx', ups[0])]
    ppermute x6, waiting for transfers between devices: 1.88 us -> 16.5 us  [the longest x1 13 us: halo_step(): ylo = lax.ppermute(top, 'gy', ups[1])]
    slice x7 -> x0, local copies, waits for them, and re-layouts: 9.17 us -> none  [the longest x1 3.76 us: halo_step(): bottom = cut[:, :, :HALO]]
    all_to_all x1, blocking collectives: 30.3 us -> 23.2 us  [halo_step(): lax.all_to_all(outgoing, ('gx', 'gy', 'gz'), split_axis=0, concat_axis=0,...]
    reshape x6 -> x0, local copies, waits for them, and re-layouts: 4.42 us -> none  [the longest x4 2.25 us: halo_step(): piece = piece.reshape(coeffs, HALO * HALO, cells_z)]
    ppermute x1, waiting for transfers between devices: 0.01 us -> 3.3 us  [halo_step(): zlo = lax.ppermute(edge_hi, 'gz', ups[2])]
  transfers between devices with their start and end apart: 10 -> 10, of which waited for: 2 -> 4; matrix products, arithmetic and copies ran while one was open for 5% -> 0% of each run, Pallas kernels for 13% -> 16%
where the time goes in v3:
time: 157 us; the launch traced here: 155 us
  Pallas kernels  84.7 us (54%)
  blocking collectives  23.2 us (15%)
  waiting for transfers between devices  19.8 us (13%)
  starting transfers between devices  17.3 us (11%)
  local copies, waits for them, and re-layouts  9.48 us (6%)
    pallas_call x1, Pallas kernels, gather_rows(): pl.pallas_call(kernel, out_shape=(pltpu.VMEM(table.shape, jnp.float32), j...  37.8 us
    all_to_all x1, blocking collectives, halo_step(): lax.all_to_all(outgoing, ('gx', 'gy', 'gz'), split_axis=0, concat_axis=0,...  23.2 us
    ppermute x1, waiting for transfers between devices, halo_step(): ylo = lax.ppermute(top, 'gy', ups[1])  13 us
    unnamed x50, local copies, waits for them, and re-layouts  9.48 us
    pallas_call x1, Pallas kernels, full_table(): pl.pallas_call(kernel, out_shape=(pltpu.VMEM((total_rows, LANES), jnp.flo...  9.35 us
    pallas_call x1, Pallas kernels, prepare(): pl.pallas_call(kernel, out_shape=(jax.ShapeDtypeStruct((count * SAMPLES /...  9.02 us
    ppermute x4, starting transfers between devices, halo_step(): corners.append(lax.ppermute(piece, ('gx', 'gy'), moves(along[:2], step)))  8.58 us
    pallas_call x1, Pallas kernels, own_table(): pl.pallas_call(kernel, out_shape=pltpu.HBM((cells_x * plane, LANES), jnp....  8.38 us
  transfers between devices with their start and end apart: 10, of which 4 were waited for; matrix products, arithmetic and copies ran while one was open for 0% of the time, Pallas kernels for 16%

profile of v3, /device:TPU:1, one launch (start us, length us, event | category | flops | bytes accessed | tf_op | source)
XLA Modules:
  0.0 154.8 jit_solution(17890470474191739653)
XLA Ops:
  0.0 2.5 %copy-done = bf16[81,8,16,256]{3,2,1,0:T(8,128)(2,1)S(1)} copy-done((bf16[81,8,16,256]{3,2,1,0:T(8,128)(2,1)S(1)}, bf16[81,8,16,256]{3,2,1,0:T(8,128)(2,1)}, u32[]{:S(2)}) %copy-start) | copy-done | bytes 5308440
  3.2 4.9 %cut_faces.1 = (bf16[81,2,16,256]{3,2,1,0:T(8,128)(2,1)}, bf16[81,2,16,256]{3,2,1,0:T(8,128)(2,1)}, bf16[81,16,256]{2,1,0:T(8,128)(2,1)}, bf16[81,16,256]{2,1,0:...) custom-call(bf16[81,8,16,256]{3,2,1,0:T(8,128)(2,1)S(1)} %copy-done,, ...), custom_call_target="tpu_custom_call" | custom-call | tf_op jit(solution)/shard_map/cut_faces/pallas_call | solution.py:128
  8.1 5.6 %collective-permute-start.4 = (bf16[81,4,256]{2,1,0:T(4,128)(2,1)}, bf16[81,4,256]{2,1,0:T(4,128)(2,1)S(1)}, u32[]{:S(2)}, u32[]{:S(2)}) collective-permute-start(bf16[81,4,256]{2,1,0:T(4,128)(2,1)} %get-tuple-element.30), channel_id=1, source_target_pairs={{0,20},{4,24},{8,28},{12,16},{16,36},{20,40},{24,44},{28,32},{32,5... | collective-permute-start | bytes 497672 | tf_op jit(solution)/shard_map/ppermute | solution.py:620
  13.7 1.9 %collective-permute-start.5 = (bf16[81,4,256]{2,1,0:T(4,128)(2,1)}, bf16[81,4,256]{2,1,0:T(4,128)(2,1)}, u32[]{:S(2)}, u32[]{:S(2)}) collective-permute-start(bf16[81,4,256]{2,1,0:T(4,128)(2,1)} %get-tuple-element.31), channel_id=1, source_target_pairs={{0,116},{4,120},{8,124},{12,112},{16,4},{20,8},{24,12},{28,0},{32,... | collective-permute-start | bytes 497672 | tf_op jit(solution)/shard_map/ppermute | solution.py:620
  15.6 1.4 collective-permute-start
  17.1 2.1 %collective-permute-start.1 = (bf16[81,2,16,256]{3,2,1,0:T(8,128)(2,1)}, bf16[81,2,16,256]{3,2,1,0:T(8,128)(2,1)S(1)}, u32[]{:S(2)}, u32[]{:S(2)}) collective-permute-start(bf16[81,2,16,256]{3,2,1,0:T(8,128)(2,1)} %get-tuple-element.27), channel_id=1, source_target_pairs={{0,112},{16,0},{32,16},{48,32},{64,48},{80,64},{96,80},{112,96},{1... | collective-permute-start | bytes 3981320 | tf_op jit(solution)/shard_map/ppermute | solution.py:615
  19.3 2.5 %copy-done.1 = bf16[81,8,16,256]{3,2,1,0:T(8,128)(2,1)S(1)} copy-done((bf16[81,8,16,256]{3,2,1,0:T(8,128)(2,1)S(1)}, bf16[81,8,16,256]{3,2,1,0:T(8,128)(2,1)}, u32[]{:S(2)}) %copy-start.1) | copy-done | bytes 5308440
  21.8 8.4 %own_table.1.own = f32[32768,128]{1,0:T(8,128)} custom-call(bf16[81,8,16,256]{3,2,1,0:T(8,128)(2,1)S(1)} %copy-done.1, bf16[256,256]{1,0:T(8,128)(2,1)S(1)} %copy-done.10), custom_call_target="tpu_custom_call" | custom-call | flops 20000000000 | bytes 20000000 | tf_op jit(solution)/shard_map/own_table/pallas_call | solution.py:157
  30.3 9.0 %prepare.1 = (s32[256,128]{1,0:T(8,128)S(1)}, f32[4096,128]{1,0:T(8,128)S(1)}) custom-call(s32[3]{0:T(128)S(1)} %pad_add_fusion.origin, s32[4096]{0:T(1024)S(1)} %bitcast.5, s32[3,8,4096]{2,1,0:T(8,128)S(1)} %copy-done.7, f32[8,4096]{1,0:T(8,128)S(1)} %copy-done.8, bf16[256,256]{1,0:T(8,128)(2,1)S(1)} %copy-done.10, bf16[16,128]{1,0:T(8,128)(2,1)S(1)} %copy-done.12), custom_call_target="tpu_custom_call" | custom-call | flops 20000000000 | bytes 3000000 | tf_op jit(solution)/shard_map/prepare/pallas_call | solution.py:364
  40.0 1.1 collective-permute-start.7
  41.1 2.3 %collective-permute-start.2 = (bf16[81,16,256]{2,1,0:T(8,128)(2,1)S(1)}, bf16[81,16,256]{2,1,0:T(8,128)(2,1)S(1)}, u32[]{:S(2)}, u32[]{:S(2)}) collective-permute-start(bf16[81,16,256]{2,1,0:T(8,128)(2,1)S(1)} %copy-done.17), channel_id=1, source_target_pairs={{0,4},{4,8},{8,12},{12,0},{1,5},{5,9},{9,13},{13,1},{2,6},{6,10},{... | collective-permute-start | bytes 1990664 | tf_op jit(solution)/shard_map/ppermute | solution.py:616
  43.4 7.8 %spread_weights.1.wide = f32[32768,128]{1,0:T(8,128)} custom-call(f32[4096,128]{1,0:T(8,128)S(1)} %get-tuple-element.23.ordered, bf16[128,1024]{1,0:T(8,128)(2,1)S(1)} %copy-done.9), custom_call_target="tpu_custom_call" | custom-call | flops 10000000000 | bytes 3000000 | tf_op jit(solution)/shard_map/spread_weights/pallas_call | solution.py:409
  51.2 2.1 %collective-permute-done.7.c3 = bf16[81,4,256]{2,1,0:T(4,128)(2,1)S(1)} collective-permute-done((bf16[81,4,256]{2,1,0:T(4,128)(2,1)S(1)}, bf16[81,4,256]{2,1,0:T(4,128)(2,1)S(1)}, u32[]{:S(2)}, u32[]{:S(2)}) %collective-permute-start.7) | collective-permute-done | bytes 165920 | tf_op jit(solution)/shard_map/ppermute | solution.py:620
  53.2 13.0 %collective-permute-done.2.ylo = bf16[81,16,256]{2,1,0:T(8,128)(2,1)S(1)} collective-permute-done((bf16[81,16,256]{2,1,0:T(8,128)(2,1)S(1)}, bf16[81,16,256]{2,1,0:T(8,128)(2,1)S(1)}, u32[]{:S(2)}, u32[]{:S(2)}) %collective-permute-start.2) | collective-permute-done | bytes 663584 | tf_op jit(solution)/shard_map/ppermute | solution.py:616
  66.3 1.4 collective-permute-done.3.yhi
  67.7 0.8 copy-done.19
  69.0 1.1 copy-done.15
  70.0 9.3 %full_table.1 = (f32[62400,128]{1,0:T(8,128)S(1)}, bf16[480,128]{1,0:T(8,128)(2,1)}, bf16[480,128]{1,0:T(8,128)(2,1)}) custom-call(f32[32768,128]{1,0:T(8,128)} %own_table.1.own, bf16[81,2,16,256]{3,2,1,0:T(8,128)(2,1)} %copy-done.14, bf16[81,2,16,256]{3,2,1,0:T(8,128)(2,1)} %copy-done.15, bf16[81,16,256]{2,1,0:T(8,128)(2,1)} %copy-done.18, ...), custom_call_target="tpu_custom_call" | custom-call | flops 20000000000 | bytes 20000000 | tf_op jit(solution)/shard_map/full_table/pallas_call | solution.py:246
  79.4 1.4 collective-permute-start.8
  80.8 1.5 collective-permute-start.9
  82.3 3.3 %collective-permute-done.8.zlo = bf16[480,128]{1,0:T(8,128)(2,1)S(1)} collective-permute-done((bf16[480,128]{1,0:T(8,128)(2,1)}, bf16[480,128]{1,0:T(8,128)(2,1)S(1)}, u32[]{:S(2)}, u32[]{:S(2)}) %collective-permute-start.8) | collective-permute-done | bytes 122912 | tf_op jit(solution)/shard_map/ppermute | solution.py:642
  86.3 37.8 %gather_rows.1 = (f32[62400,128]{1,0:T(8,128)S(1)}, bf16[128,24,128]{2,1,0:T(8,128)(2,1)}) custom-call(s32[32768]{0:T(1024)} %bitcast.6, bf16[480,128]{1,0:T(8,128)(2,1)} %copy-done.23, bf16[480,128]{1,0:T(8,128)(2,1)} %copy-done.24, bf16[3,256,128]{2,1,0:T(8,128)(2,1)} %constant.41.clone.pick, ...), custom_call_target="tpu_custom_call", output_to_operand_aliasing={{0}: (5, {})} | custom-call | flops 40000000000 | bytes 20000000 | tf_op jit(solution)/shard_map/gather_rows/pallas_call | solution.py:522
  124.0 23.2 %all_to_all.5.routed = bf16[128,24,128]{2,1,0:T(8,128)(2,1)S(1)} all-to-all(bf16[128,24,128]{2,1,0:T(8,128)(2,1)} %get-tuple-element.38), channel_id=1, replica_groups=mesh['gx'=8,'gy'=4,'gz'=4] {'gx','gy','gz'}, dimensions={0} | all-to-all | bytes 1572864 | tf_op jit(solution)/shard_map/all_to_all | solution.py:644
  147.3 7.6 %relight.1 = bf16[81,4096]{1,0:T(8,128)(2,1)} custom-call(bf16[81,4096]{1,0:T(8,128)(2,1)S(1)} %copy-done.2, bf16[128,24,128]{2,1,0:T(8,128)(2,1)S(1)} %all_to_all.5.routed, bf16[1024,81]{1,0:T(8,128)(2,1)S(1)} %copy-done.4, bf16[1024,128]{1,0:T(8,128)(2,1)S(1)} %copy-done.3, bf16[81,1024]{1,0:T(8,128)(2,1)S(1)} %copy-done.5), custom_call_target="tpu_custom_call" | custom-call | tf_op jit(solution)/shard_map/relight/pallas_call | solution.py:579
  (56 shorter events, 2.7 us)
Async XLA Ops:
  3.2 16.0 %copy-start.13 = (s32[2,4096]{1,0:T(2,128)S(1)}, s32[2,4096]{1,0:T(2,128)}, u32[]{:S(2)}) copy-start(s32[2,4096]{1,0:T(2,128)} %param.17) | copy-start | bytes 98308
  3.2 16.0 %copy-start.10 = (bf16[256,256]{1,0:T(8,128)(2,1)S(1)}, bf16[256,256]{1,0:T(8,128)(2,1)}, u32[]{:S(2)}) copy-start(bf16[256,256]{1,0:T(8,128)(2,1)} %constant.38.clone.eye) | copy-start | bytes 393220
  8.1 31.8 %collective-permute-start.4 = (bf16[81,4,256]{2,1,0:T(4,128)(2,1)}, bf16[81,4,256]{2,1,0:T(4,128)(2,1)S(1)}, u32[]{:S(2)}, u32[]{:S(2)}) collective-permute-start(bf16[81,4,256]{2,1,0:T(4,128)(2,1)} %get-tuple-element.30), channel_id=1, source_target_pairs={{0,20},{4,24},{8,28},{12,16},{16,36},{20,40},{24,44},{28,32},{32,5... | collective-permute-start | bytes 497672 | tf_op jit(solution)/shard_map/ppermute | solution.py:620
  13.7 27.4 %collective-permute-start.5 = (bf16[81,4,256]{2,1,0:T(4,128)(2,1)}, bf16[81,4,256]{2,1,0:T(4,128)(2,1)}, u32[]{:S(2)}, u32[]{:S(2)}) collective-permute-start(bf16[81,4,256]{2,1,0:T(4,128)(2,1)} %get-tuple-element.31), channel_id=1, source_target_pairs={{0,116},{4,120},{8,124},{12,112},{16,4},{20,8},{24,12},{28,0},{32,... | collective-permute-start | bytes 497672 | tf_op jit(solution)/shard_map/ppermute | solution.py:620
  15.6 27.7 %collective-permute-start.6 = (bf16[81,4,256]{2,1,0:T(4,128)(2,1)}, bf16[81,4,256]{2,1,0:T(4,128)(2,1)}, u32[]{:S(2)}, u32[]{:S(2)}) collective-permute-start(bf16[81,4,256]{2,1,0:T(4,128)(2,1)} %get-tuple-element.32), channel_id=1, source_target_pairs={{0,28},{4,16},{8,20},{12,24},{16,44},{20,32},{24,36},{28,40},{32,6... | collective-permute-start | bytes 497672 | tf_op jit(solution)/shard_map/ppermute | solution.py:620
  15.6 52.1 %collective-permute-start = (bf16[81,2,16,256]{3,2,1,0:T(8,128)(2,1)}, bf16[81,2,16,256]{3,2,1,0:T(8,128)(2,1)S(1)}, u32[]{:S(2)}, u32[]{:S(2)}) collective-permute-start(bf16[81,2,16,256]{3,2,1,0:T(8,128)(2,1)} %get-tuple-element.26), channel_id=1, source_target_pairs={{0,16},{16,32},{32,48},{48,64},{64,80},{80,96},{96,112},{112,0},{1... | collective-permute-start | bytes 3981320 | tf_op jit(solution)/shard_map/ppermute | solution.py:614
  17.1 50.6 %collective-permute-start.1 = (bf16[81,2,16,256]{3,2,1,0:T(8,128)(2,1)}, bf16[81,2,16,256]{3,2,1,0:T(8,128)(2,1)S(1)}, u32[]{:S(2)}, u32[]{:S(2)}) collective-permute-start(bf16[81,2,16,256]{3,2,1,0:T(8,128)(2,1)} %get-tuple-element.27), channel_id=1, source_target_pairs={{0,112},{16,0},{32,16},{48,32},{64,48},{80,64},{96,80},{112,96},{1... | collective-permute-start | bytes 3981320 | tf_op jit(solution)/shard_map/ppermute | solution.py:615
  21.7 8.5 %copy-start.8 = (f32[8,4096]{1,0:T(8,128)S(1)}, f32[8,4096]{1,0:T(8,128)}, u32[]{:S(2)}) copy-start(f32[8,4096]{1,0:T(8,128)} %weights.1) | copy-start | bytes 393220
  21.8 8.5 %copy-start.12 = (bf16[16,128]{1,0:T(8,128)(2,1)S(1)}, bf16[16,128]{1,0:T(8,128)(2,1)}, u32[]{:S(2)}) copy-start(bf16[16,128]{1,0:T(8,128)(2,1)} %constant.39.clone.join) | copy-start | bytes 12292
  30.2 9.7 %copy-start.21 = (bf16[81,4,256]{2,1,0:T(4,128)(2,1)S(1)}, bf16[81,4,256]{2,1,0:T(4,128)(2,1)}, u32[]{:S(2)}) copy-start(bf16[81,4,256]{2,1,0:T(4,128)(2,1)} %get-tuple-element.33) | copy-start | bytes 497668
  30.2 10.8 %copy-start.17 = (bf16[81,16,256]{2,1,0:T(8,128)(2,1)S(1)}, bf16[81,16,256]{2,1,0:T(8,128)(2,1)}, u32[]{:S(2)}) copy-start(bf16[81,16,256]{2,1,0:T(8,128)(2,1)} %get-tuple-element.28) | copy-start | bytes 1990660
  30.2 13.1 %copy-start.16 = (bf16[81,16,256]{2,1,0:T(8,128)(2,1)S(1)}, bf16[81,16,256]{2,1,0:T(8,128)(2,1)}, u32[]{:S(2)}) copy-start(bf16[81,16,256]{2,1,0:T(8,128)(2,1)} %get-tuple-element.29) | copy-start | bytes 1990660
  30.2 13.1 %copy-start.9 = (bf16[128,1024]{1,0:T(8,128)(2,1)S(1)}, bf16[128,1024]{1,0:T(8,128)(2,1)}, u32[]{:S(2)}) copy-start(bf16[128,1024]{1,0:T(8,128)(2,1)} %constant.40.clone.ones) | copy-start | bytes 786436
  39.9 11.2 %copy-start.20 = (bf16[81,4,256]{2,1,0:T(4,128)(2,1)}, bf16[81,4,256]{2,1,0:T(4,128)(2,1)S(1)}, u32[]{:S(2)}) copy-start(bf16[81,4,256]{2,1,0:T(4,128)(2,1)S(1)} %collective-permute-done.4.c0) | copy-start | bytes 497668
  40.0 13.3 %collective-permute-start.7 = (bf16[81,4,256]{2,1,0:T(4,128)(2,1)S(1)}, bf16[81,4,256]{2,1,0:T(4,128)(2,1)S(1)}, u32[]{:S(2)}, u32[]{:S(2)}) collective-permute-start(bf16[81,4,256]{2,1,0:T(4,128)(2,1)S(1)} %copy-done.21), channel_id=1, source_target_pairs={{0,124},{4,112},{8,116},{12,120},{16,12},{20,0},{24,4},{28,8},{32,... | collective-permute-start | bytes 497672 | tf_op jit(solution)/shard_map/ppermute | solution.py:620
  41.1 25.2 %collective-permute-start.2 = (bf16[81,16,256]{2,1,0:T(8,128)(2,1)S(1)}, bf16[81,16,256]{2,1,0:T(8,128)(2,1)S(1)}, u32[]{:S(2)}, u32[]{:S(2)}) collective-permute-start(bf16[81,16,256]{2,1,0:T(8,128)(2,1)S(1)} %copy-done.17), channel_id=1, source_target_pairs={{0,4},{4,8},{8,12},{12,0},{1,5},{5,9},{9,13},{13,1},{2,6},{6,10},{... | collective-permute-start | bytes 1990664 | tf_op jit(solution)/shard_map/ppermute | solution.py:616
  43.4 24.3 %collective-permute-start.3 = (bf16[81,16,256]{2,1,0:T(8,128)(2,1)S(1)}, bf16[81,16,256]{2,1,0:T(8,128)(2,1)S(1)}, u32[]{:S(2)}, u32[]{:S(2)}) collective-permute-start(bf16[81,16,256]{2,1,0:T(8,128)(2,1)S(1)} %copy-done.16), channel_id=1, source_target_pairs={{0,12},{4,0},{8,4},{12,8},{1,13},{5,1},{9,5},{13,9},{2,14},{6,2},{... | collective-permute-start | bytes 1990664 | tf_op jit(solution)/shard_map/ppermute | solution.py:617
  53.2 14.5 %copy-start.22 = (bf16[81,4,256]{2,1,0:T(4,128)(2,1)}, bf16[81,4,256]{2,1,0:T(4,128)(2,1)S(1)}, u32[]{:S(2)}) copy-start(bf16[81,4,256]{2,1,0:T(4,128)(2,1)S(1)} %collective-permute-done.7.c3) | copy-start | bytes 497668
  79.4 6.2 %collective-permute-start.8 = (bf16[480,128]{1,0:T(8,128)(2,1)}, bf16[480,128]{1,0:T(8,128)(2,1)S(1)}, u32[]{:S(2)}, u32[]{:S(2)}) collective-permute-start(bf16[480,128]{1,0:T(8,128)(2,1)} %get-tuple-element.34), channel_id=1, source_target_pairs={{0,1},{1,2},{2,3},{3,0},{4,5},{5,6},{6,7},{7,4},{8,9},{9,10},{10,1... | collective-permute-start | bytes 368648 | tf_op jit(solution)/shard_map/ppermute | solution.py:642
  80.8 4.8 %collective-permute-start.9 = (bf16[480,128]{1,0:T(8,128)(2,1)}, bf16[480,128]{1,0:T(8,128)(2,1)S(1)}, u32[]{:S(2)}, u32[]{:S(2)}) collective-permute-start(bf16[480,128]{1,0:T(8,128)(2,1)} %get-tuple-element.35), channel_id=1, source_target_pairs={{0,3},{1,0},{2,1},{3,2},{4,7},{5,4},{6,5},{7,6},{8,11},{9,8},{10,9... | collective-permute-start | bytes 368648 | tf_op jit(solution)/shard_map/ppermute | solution.py:641
  86.3 61.0 %copy-start.2 = (bf16[81,4096]{1,0:T(8,128)(2,1)S(1)}, bf16[81,4096]{1,0:T(8,128)(2,1)}, u32[]{:S(2)}) copy-start(bf16[81,4096]{1,0:T(8,128)(2,1)} %transfer.1) | copy-start | bytes 1990660
  86.3 61.0 %copy-start.3 = (bf16[1024,128]{1,0:T(8,128)(2,1)S(1)}, bf16[1024,128]{1,0:T(8,128)(2,1)}, u32[]{:S(2)}) copy-start(bf16[1024,128]{1,0:T(8,128)(2,1)} %constant.43.clone.wide) | copy-start | bytes 786436
  86.3 61.0 %copy-start.4 = (bf16[1024,81]{1,0:T(8,128)(2,1)S(1)}, bf16[1024,81]{1,0:T(8,128)(2,1)}, u32[]{:S(2)}) copy-start(bf16[1024,81]{1,0:T(8,128)(2,1)} %constant.42.clone.basis) | copy-start | bytes 497668
  86.3 61.0 %copy-start.5 = (bf16[81,1024]{1,0:T(8,128)(2,1)S(1)}, bf16[81,1024]{1,0:T(8,128)(2,1)}, u32[]{:S(2)}) copy-start(bf16[81,1024]{1,0:T(8,128)(2,1)} %constant.44.clone.projector) | copy-start | bytes 497668
  (11 other events, 20.9 us)

commit v4 on v3

--- a/solution.py
+++ b/solution.py
@@ -90,9 +90,8 @@
     coeffs, cells_x, cells_y, cells_z = field.shape
     per_step = 9
     rows = cells_x * HALO
-    corner = HALO * HALO
-
-    def kernel(field, pick, last, first, top, bottom, *corners):
+
+    def kernel(field, pick, last, first, top, bottom):
         for c in range(per_step):
             last[c] = field[c, cells_x - HALO :]
             first[c] = field[c, :HALO]
@@ -102,24 +101,15 @@
                 preferred_element_type=jnp.float32,
             ).astype(jnp.bfloat16)
             top[c] = chosen[:rows]
-            bottom[c] = chosen[rows : 2 * rows]
-            for q in range(4):
-                at = 2 * rows + q * 16
-                corners[q][c] = chosen[at : at + corner]
-
-    pick = np.zeros((2 * rows + 64, cells_x * cells_y), np.float32)
+            bottom[c] = chosen[rows:]
+
+    pick = np.zeros((2 * rows, cells_x * cells_y), np.float32)
     for x in range(cells_x):
         for j in range(HALO):
             pick[x * HALO + j, x * cells_y + cells_y - HALO + j] = 1.0
             pick[rows + x * HALO + j, x * cells_y + j] = 1.0
-    for q in range(4):
-        start_y = cells_y - HALO if q < 2 else 0
-        start_x = cells_x - HALO if q % 2 == 0 else 0
-        for i in range(HALO):
-            for j in range(HALO):
-                pick[2 * rows + q * 16 + i * HALO + j, (start_x + i) * cells_y + start_y + j] = 1.0
     shapes = [(coeffs, HALO, cells_y, cells_z)] * 2
-    shapes += [(coeffs, rows, cells_z)] * 2 + [(coeffs, corner, cells_z)] * 4
+    shapes += [(coeffs, rows, cells_z)] * 2
 
     def whole(shape):
         zeros = (0,) * (len(shape) - 1)
@@ -134,6 +124,40 @@
         compiler_params=pltpu.CompilerParams(vmem_limit_bytes=24 * MIB),
         name="cut_faces",
     )(field, jnp.asarray(pick.astype(jnp.bfloat16)))
+
+
+def cut_corners(ylo, yhi):
+    coeffs, rows, cells_z = ylo.shape
+    per_step = 27
+    corner = HALO * HALO
+
+    def kernel(ylo, yhi, pick, up, down):
+        for c in range(per_step):
+            chosen = jnp.dot(
+                pick[...],
+                jnp.concatenate([ylo[c], yhi[c]], axis=0),
+                preferred_element_type=jnp.float32,
+            )
+            up[c] = chosen[: 2 * corner].astype(jnp.bfloat16)
+            down[c] = chosen[2 * corner :].astype(jnp.bfloat16)
+
+    pick = np.zeros((4 * corner, 2 * rows), np.float32)
+    for side in range(2):
+        for i in range(corner):
+            pick[side * corner + i, side * rows + rows - corner + i] = 1.0
+            pick[2 * corner + side * corner + i, side * rows + i] = 1.0
+    shape = (coeffs, 2 * corner, cells_z)
+    face = pl.BlockSpec((per_step, rows, cells_z), lambda i: (i, 0, 0))
+    piece = pl.BlockSpec((per_step,) + shape[1:], lambda i: (i, 0, 0))
+    return pl.pallas_call(
+        kernel,
+        out_shape=[pltpu.HBM(shape, jnp.bfloat16)] * 2,
+        grid=(coeffs // per_step,),
+        in_specs=[face, face, pl.BlockSpec(pick.shape, lambda i: (0, 0))],
+        out_specs=[piece, piece],
+        compiler_params=pltpu.CompilerParams(vmem_limit_bytes=24 * MIB),
+        name="cut_corners",
+    )(ylo, yhi, jnp.asarray(pick.astype(jnp.bfloat16)))
 
 
 def own_table(field, eye):
@@ -178,7 +202,7 @@
     own_rows = own.shape[0]
     lines = own_rows // cells_z + count * cells_y
 
-    def kernel(own, xlo, xhi, ylo, yhi, c0, c1, c2, c3, eye, table, zhi, zlo, *scratch):
+    def kernel(own, xlo, xhi, ylo, yhi, clo, chi, eye, table, zhi, zlo, *scratch):
         buf, sems, small, small_sems, spread, done = scratch
         inherit = pltpu.make_async_copy(own, table.at[pl.ds(0, own_rows), :], done)
         sources = [xlo.at[:, 0], xlo.at[:, 1], xhi.at[:, 0], xhi.at[:, 1], ylo, yhi]
@@ -186,7 +210,7 @@
             pltpu.make_async_copy(source, buf.at[p], sems.at[p]).start()
         pieces = [
             pltpu.make_async_copy(corner, small.at[q], small_sems.at[q])
-            for q, corner in enumerate((c0, c1, c2, c3))
+            for q, corner in enumerate((clo, chi))
         ]
         for piece in pieces:
             piece.start()
@@ -218,7 +242,7 @@
             lambda c, h: jnp.concatenate(
                 [
                     small[q, c, :, h * LANES : (h + 1) * LANES].astype(jnp.float32)
-                    for q in range(4)
+                    for q in range(2)
                 ],
                 axis=0,
             ),
@@ -246,13 +270,13 @@
     return pl.pallas_call(
         kernel,
         out_shape=(pltpu.VMEM((total_rows, LANES), jnp.float32), edge, edge),
-        in_specs=[hbm] * 9 + [vmem],
+        in_specs=[hbm] * 7 + [vmem],
         out_specs=(vmem, vmem, vmem),
         scratch_shapes=[
             pltpu.VMEM((count - 1, coeffs, cells_y, cells_z), jnp.bfloat16),
             pltpu.SemaphoreType.DMA((count - 1,)),
-            pltpu.VMEM((4, coeffs, HALO * HALO, cells_z), jnp.bfloat16),
-            pltpu.SemaphoreType.DMA((4,)),
+            pltpu.VMEM((2, coeffs, 2 * HALO * HALO, cells_z), jnp.bfloat16),
+            pltpu.SemaphoreType.DMA((2,)),
             spread_shape(coeffs, cells_y, cells_z),
             pltpu.SemaphoreType.DMA(()),
         ],
@@ -293,7 +317,8 @@
         )
         line_corner = (
             (cells_x + 2 * HALO + 2) * cells_y
-            + jnp.where(low_y, 0, 2 * HALO * HALO)
+            + jnp.where(near_x < HALO, 0, HALO * HALO)
+            + jnp.where(low_y, 0, HALO * HALO)
             + side_x * HALO
             + side_y
         )
@@ -424,6 +449,7 @@
 
 
 RING = 2
+STREAM = 8
 CHUNK = 1024
 
 
@@ -459,19 +485,25 @@
 
         for b in range(RING - 1):
             fetch(b, b).start()
+        for b in range(STREAM - 1):
             stream(b, b).start()
 
         def body(i, _):
             for b in range(RING):
                 n = i * RING + b
+                slot = n % STREAM
                 fetch(n, b).wait()
-                stream(n, b).wait()
+                stream(n, slot).wait()
                 ahead = n + RING - 1
+                later = n + STREAM - 1
 
                 @pl.when(ahead < chunks)
                 def _():
                     fetch(ahead, (b + RING - 1) % RING).start()
-                    stream(ahead, (b + RING - 1) % RING).start()
+
+                @pl.when(later < chunks)
+                def _():
+                    stream(later, later % STREAM).start()
 
                 for q in range(groups):
                     total = None
@@ -482,7 +514,7 @@
                             row = table[pl.ds(local[b, place], GROUP, stride=0), :]
                             merged = row if merged is None else jnp.where(masks[k], row, merged)
                         at = (q * SAMPLES + s) * GROUP
-                        term = merged * near[b, at : at + GROUP, :]
+                        term = merged * near[slot, at : at + GROUP, :]
                         total = term if total is None else total + term
                     to = pl.multiple_of((n * (groups // 4) + q // 4) * GROUP, GROUP)
                     rows[q % 4, pl.ds(to, GROUP), :] = jnp.where(used, total, 0.0)
@@ -530,8 +562,8 @@
         scratch_shapes=[
             pltpu.SMEM((RING, CHUNK), jnp.int32),
             pltpu.SemaphoreType.DMA((RING,)),
-            pltpu.VMEM((RING, CHUNK, LANES), jnp.float32),
-            pltpu.SemaphoreType.DMA((RING,)),
+            pltpu.VMEM((STREAM, CHUNK, LANES), jnp.float32),
+            pltpu.SemaphoreType.DMA((STREAM,)),
             pltpu.VMEM((4, pairs * GROUP, LANES), jnp.float32),
         ],
         input_output_aliases={5: 0},
@@ -610,14 +642,17 @@
     ups = [moves((n, 1), (1, 0)) for n in along]
     downs = [moves((n, 1), (-1, 0)) for n in along]
 
-    last, first, top, bottom, *pieces = cut_faces(field)
+    field = pltpu.with_memory_space_constraint(field, pltpu.HBM)
+    last, first, top, bottom = cut_faces(field)
+    ylo = lax.ppermute(top, "gy", ups[1])
+    yhi = lax.ppermute(bottom, "gy", downs[1])
     xlo = lax.ppermute(last, "gx", ups[0])
     xhi = lax.ppermute(first, "gx", downs[0])
-    ylo = lax.ppermute(top, "gy", ups[1])
-    yhi = lax.ppermute(bottom, "gy", downs[1])
-    corners = []
-    for piece, step in zip(pieces, ((1, 1), (-1, 1), (1, -1), (-1, -1))):
-        corners.append(lax.ppermute(piece, ("gx", "gy"), moves(along[:2], step)))
+    eye = jnp.asarray(np.eye(cells_z, dtype=np.float32).astype(jnp.bfloat16))
+    own = own_table(field, eye)
+    ylo, yhi, own = lax.optimization_barrier((ylo, yhi, own))
+    ends = cut_corners(ylo, yhi)
+    corners = [lax.ppermute(ends[0], "gx", ups[0]), lax.ppermute(ends[1], "gx", downs[0])]
 
     lines = cells_x * cells_y + (2 * HALO + 3) * cells_y
     rows = lines * cells_z
@@ -630,8 +665,6 @@
     per_pair = count // devices
     slot = destination[0] * per_pair + destination[1]
 
-    eye = jnp.asarray(np.eye(cells_z, dtype=np.float32).astype(jnp.bfloat16))
-    own = own_table(field, eye)
     index, ordered = prepare(samples, weights, slot, origin, cells, total)
     wide = spread_weights(ordered)
     own, index, wide = lax.optimization_barrier((own, index, wide))

time: 157 us -> 141 us (0.90)
  local copies, waits for them, and re-layouts: 9.48 us -> 3.41 us
  Pallas kernels: 84.7 us -> 79.6 us
  starting transfers between devices: 17.3 us -> 14.4 us
  waiting for transfers between devices: 19.8 us -> 18 us
    ppermute x4 -> x2, waiting for transfers between devices: 2.08 us -> 15.5 us  [the longest x1 15.5 us: halo_step(): lax.ppermute(ends[0], 'gx', ups[0])]
    ppermute x1, waiting for transfers between devices: 13 us -> 0.01 us  [halo_step(): ylo = lax.ppermute(top, 'gy', ups[1])]
    pallas_call x1, Pallas kernels: 37.8 us -> 25.5 us  [gather_rows(): pl.pallas_call(kernel, out_shape=(pltpu.VMEM(table.shape, jnp.float32), j...]
    unnamed x50 -> x40, local copies, waits for them, and re-layouts: 9.48 us -> 3.41 us
    ppermute x4 -> x2, starting transfers between devices: 8.58 us -> 3.58 us  [the longest x1 3.57 us: halo_step(): lax.ppermute(ends[1], 'gx', downs[0])]
    pallas_call x1, Pallas kernels: 4.88 us -> 7.67 us  [cut_faces(): pl.pallas_call(kernel, out_shape=[pltpu.HBM(shape, jnp.bfloat16) for shap...]
    pallas_call x1, Pallas kernels: 8.38 us -> 10.8 us  [own_table(): pl.pallas_call(kernel, out_shape=pltpu.HBM((cells_x * plane, LANES), jnp....]
    pallas_call x0 -> x1, Pallas kernels: none -> 1.98 us  [cut_corners(): pl.pallas_call(kernel, out_shape=[pltpu.HBM(shape, jnp.bfloat16)] * 2, gr...]
  transfers between devices with their start and end apart: 10 -> 8, of which waited for: 4 -> 2; matrix products, arithmetic and copies ran while one was open for 0% -> 0% of each run, Pallas kernels for 16% -> 21%
where the time goes in v4:
time: 141 us; the launch traced here: 140 us
  Pallas kernels  79.6 us (56%)
  blocking collectives  24.4 us (17%)
  waiting for transfers between devices  18 us (13%)
  starting transfers between devices  14.4 us (10%)
  local copies, waits for them, and re-layouts  3.41 us (2%)
    pallas_call x1, Pallas kernels, gather_rows(): pl.pallas_call(kernel, out_shape=(pltpu.VMEM(table.shape, jnp.float32), j...  25.5 us
    all_to_all x1, blocking collectives, halo_step(): lax.all_to_all(outgoing, ('gx', 'gy', 'gz'), split_axis=0, concat_axis=0,...  24.4 us
    ppermute x1, waiting for transfers between devices, halo_step(): lax.ppermute(ends[0], 'gx', ups[0])  15.5 us
    pallas_call x1, Pallas kernels, own_table(): pl.pallas_call(kernel, out_shape=pltpu.HBM((cells_x * plane, LANES), jnp....  10.8 us
    pallas_call x1, Pallas kernels, full_table(): pl.pallas_call(kernel, out_shape=(pltpu.VMEM((total_rows, LANES), jnp.flo...  9.32 us
    pallas_call x1, Pallas kernels, prepare(): pl.pallas_call(kernel, out_shape=(jax.ShapeDtypeStruct((count * SAMPLES /...  9.01 us
    pallas_call x1, Pallas kernels, spread_weights(): pl.pallas_call(kernel, out_shape=pltpu.HBM((count * SAMPLES, LANES), jnp....  7.71 us
    pallas_call x1, Pallas kernels, cut_faces(): pl.pallas_call(kernel, out_shape=[pltpu.HBM(shape, jnp.bfloat16) for shap...  7.67 us
  transfers between devices with their start and end apart: 8, of which 2 were waited for; matrix products, arithmetic and copies ran while one was open for 0% of the time, Pallas kernels for 21%

profile of v4, /device:TPU:1, one launch (start us, length us, event | category | flops | bytes accessed | tf_op | source)
XLA Modules:
  0.0 140.0 jit_solution(5045966964283113289)
XLA Ops:
  0.0 0.7 copy-done.6
  0.7 7.7 %cut_faces.1 = (bf16[81,2,16,256]{3,2,1,0:T(8,128)(2,1)}, bf16[81,2,16,256]{3,2,1,0:T(8,128)(2,1)}, bf16[81,16,256]{2,1,0:T(8,128)(2,1)}, bf16[81,16,256]{2,1,0:T(8,128)(2,1)}) custom-call(bf16[81,8,16,256]{3,2,1,0:T(8,128)(2,1)} %field.3, bf16[32,128]{1,0:T(8,128)(2,1)S(1)} %copy-done.6), custom_call_target="tpu_custom_call" | custom-call | tf_op jit(solution)/shard_map/cut_faces/pallas_call | solution.py:118
  8.4 4.1 %collective-permute-start = (bf16[81,16,256]{2,1,0:T(8,128)(2,1)}, bf16[81,16,256]{2,1,0:T(8,128)(2,1)S(1)}, u32[]{:S(2)}, u32[]{:S(2)}) collective-permute-start(bf16[81,16,256]{2,1,0:T(8,128)(2,1)} %get-tuple-element.23), channel_id=1, source_target_pairs={{0,4},{4,8},{8,12},{12,0},{1,5},{5,9},{9,13},{13,1},{2,6},{6,10},{... | collective-permute-start | bytes 1990664 | tf_op jit(solution)/shard_map/ppermute | solution.py:647
  12.5 1.6 %collective-permute-start.2 = (bf16[81,2,16,256]{3,2,1,0:T(8,128)(2,1)}, bf16[81,2,16,256]{3,2,1,0:T(8,128)(2,1)S(1)}, u32[]{:S(2)}, u32[]{:S(2)}) collective-permute-start(bf16[81,2,16,256]{3,2,1,0:T(8,128)(2,1)} %get-tuple-element.30), channel_id=1, source_target_pairs={{0,16},{16,32},{32,48},{48,64},{64,80},{80,96},{96,112},{112,0},{1... | collective-permute-start | bytes 3981320 | tf_op jit(solution)/shard_map/ppermute | solution.py:649
  14.1 2.2 %collective-permute-start.3 = (bf16[81,2,16,256]{3,2,1,0:T(8,128)(2,1)}, bf16[81,2,16,256]{3,2,1,0:T(8,128)(2,1)}, u32[]{:S(2)}, u32[]{:S(2)}) collective-permute-start(bf16[81,2,16,256]{3,2,1,0:T(8,128)(2,1)} %get-tuple-element.31), channel_id=1, source_target_pairs={{0,112},{16,0},{32,16},{48,32},{64,48},{80,64},{96,80},{112,96},{1... | collective-permute-start | bytes 3981320 | tf_op jit(solution)/shard_map/ppermute | solution.py:650
  16.4 10.8 %own_table.1.own = f32[32768,128]{1,0:T(8,128)} custom-call(bf16[81,8,16,256]{3,2,1,0:T(8,128)(2,1)} %field.3, bf16[256,256]{1,0:T(8,128)(2,1)S(1)} %copy-done.11), custom_call_target="tpu_custom_call" | custom-call | flops 20000000000 | bytes 20000000 | tf_op jit(solution)/shard_map/own_table/pallas_call | solution.py:181
  27.2 0.1 pad_add_fusion.origin
  27.3 9.0 %prepare.1 = (s32[256,128]{1,0:T(8,128)S(1)}, f32[4096,128]{1,0:T(8,128)S(1)}) custom-call(s32[3]{0:T(128)S(1)} %pad_add_fusion.origin, s32[4096]{0:T(1024)S(1)} %bitcast.5, s32[3,8,4096]{2,1,0:T(8,128)S(1)} %copy-done.8, f32[8,4096]{1,0:T(8,128)S(1)} %copy-done.9, bf16[256,256]{1,0:T(8,128)(2,1)S(1)} %copy-done.11, bf16[16,128]{1,0:T(8,128)(2,1)S(1)} %copy-done.13), custom_call_target="tpu_custom_call" | custom-call | flops 20000000000 | bytes 3000000 | tf_op jit(solution)/shard_map/prepare/pallas_call | solution.py:389
  36.3 0.7 copy-done.12
  37.0 2.0 %cut_corners.1 = (bf16[81,8,256]{2,1,0:T(8,128)(2,1)}, bf16[81,8,256]{2,1,0:T(8,128)(2,1)}) custom-call(bf16[81,16,256]{2,1,0:T(8,128)(2,1)S(1)} %collective-permute-done.ylo, bf16[81,16,256]{2,1,0:T(8,128)(2,1)S(1)} %collective-permute-done.1.yhi, bf16[16,32]{1,0:T(8,128)(2,1)S(1)} %copy-done.7), custom_call_target="tpu_custom_call" | custom-call | tf_op jit(solution)/shard_map/cut_corners/pallas_call | solution.py:152
  39.0 3.6 %collective-permute-start.5 = (bf16[81,8,256]{2,1,0:T(8,128)(2,1)}, bf16[81,8,256]{2,1,0:T(8,128)(2,1)S(1)}, u32[]{:S(2)}, u32[]{:S(2)}) collective-permute-start(bf16[81,8,256]{2,1,0:T(8,128)(2,1)} %get-tuple-element.35), channel_id=1, source_target_pairs={{0,112},{16,0},{32,16},{48,32},{64,48},{80,64},{96,80},{112,96},{1... | collective-permute-start | bytes 995336 | tf_op jit(solution)/shard_map/ppermute | solution.py:655
  42.6 7.7 %spread_weights.1.wide = f32[32768,128]{1,0:T(8,128)} custom-call(f32[4096,128]{1,0:T(8,128)S(1)} %get-tuple-element.27.ordered, bf16[128,1024]{1,0:T(8,128)(2,1)S(1)} %copy-done.10), custom_call_target="tpu_custom_call" | custom-call | flops 10000000000 | bytes 3000000 | tf_op jit(solution)/shard_map/spread_weights/pallas_call | solution.py:434
  50.3 15.5 %collective-permute-done.4.clo = bf16[81,8,256]{2,1,0:T(8,128)(2,1)S(1)} collective-permute-done((bf16[81,8,256]{2,1,0:T(8,128)(2,1)}, bf16[81,8,256]{2,1,0:T(8,128)(2,1)S(1)}, u32[]{:S(2)}, u32[]{:S(2)}) %collective-permute-start.4) | collective-permute-done | bytes 331808 | tf_op jit(solution)/shard_map/ppermute | solution.py:655
  65.8 0.7 copy-done.16
  66.5 0.1 copy-done.17
  66.7 0.5 copy-done.15
  67.1 9.3 %full_table.1 = (f32[62400,128]{1,0:T(8,128)S(1)}, bf16[480,128]{1,0:T(8,128)(2,1)}, bf16[480,128]{1,0:T(8,128)(2,1)}) custom-call(f32[32768,128]{1,0:T(8,128)} %own_table.1.own, bf16[81,2,16,256]{3,2,1,0:T(8,128)(2,1)} %copy-done.15, bf16[81,2,16,256]{3,2,1,0:T(8,128)(2,1)} %collective-permute-done.3.xhi, bf16[81,16,256]{2,1,0:T(8,128)(2,1)} %copy-done.1, ...), custom_call_target="tpu_custom_call" | custom-call | flops 20000000000 | bytes 20000000 | tf_op jit(solution)/shard_map/full_table/pallas_call | solution.py:270
  76.5 1.3 collective-permute-start.6
  77.8 1.5 %collective-permute-start.7 = (bf16[480,128]{1,0:T(8,128)(2,1)}, bf16[480,128]{1,0:T(8,128)(2,1)S(1)}, u32[]{:S(2)}, u32[]{:S(2)}) collective-permute-start(bf16[480,128]{1,0:T(8,128)(2,1)} %get-tuple-element.37), channel_id=1, source_target_pairs={{0,3},{1,0},{2,1},{3,2},{4,7},{5,4},{6,5},{7,6},{8,11},{9,8},{10,9... | collective-permute-start | bytes 368648 | tf_op jit(solution)/shard_map/ppermute | solution.py:674
  79.3 2.4 %collective-permute-done.6.zlo = bf16[480,128]{1,0:T(8,128)(2,1)S(1)} collective-permute-done((bf16[480,128]{1,0:T(8,128)(2,1)}, bf16[480,128]{1,0:T(8,128)(2,1)S(1)}, u32[]{:S(2)}, u32[]{:S(2)}) %collective-permute-start.6) | collective-permute-done | bytes 122912 | tf_op jit(solution)/shard_map/ppermute | solution.py:675
  81.8 0.6 copy-done.18
  82.4 25.5 %gather_rows.1 = (f32[62400,128]{1,0:T(8,128)S(1)}, bf16[128,24,128]{2,1,0:T(8,128)(2,1)}) custom-call(s32[32768]{0:T(1024)} %bitcast.6, bf16[480,128]{1,0:T(8,128)(2,1)} %copy-done.18, bf16[480,128]{1,0:T(8,128)(2,1)} %copy-done.19, bf16[3,256,128]{2,1,0:T(8,128)(2,1)} %constant.44.clone.pick, ...), custom_call_target="tpu_custom_call", output_to_operand_aliasing={{0}: (5, {})} | custom-call | flops 40000000000 | bytes 20000000 | tf_op jit(solution)/shard_map/gather_rows/pallas_call | solution.py:554
  108.0 24.4 %all_to_all.5.routed = bf16[128,24,128]{2,1,0:T(8,128)(2,1)S(1)} all-to-all(bf16[128,24,128]{2,1,0:T(8,128)(2,1)} %get-tuple-element.40), channel_id=1, replica_groups=mesh['gx'=8,'gy'=4,'gz'=4] {'gx','gy','gz'}, dimensions={0} | all-to-all | bytes 1572864 | tf_op jit(solution)/shard_map/all_to_all | solution.py:677
  132.4 7.5 %relight.1 = bf16[81,4096]{1,0:T(8,128)(2,1)} custom-call(bf16[81,4096]{1,0:T(8,128)(2,1)S(1)} %copy-done, bf16[128,24,128]{2,1,0:T(8,128)(2,1)S(1)} %all_to_all.5.routed, bf16[1024,81]{1,0:T(8,128)(2,1)S(1)} %copy-done.4, bf16[1024,128]{1,0:T(8,128)(2,1)S(1)} %copy-done.3, bf16[81,1024]{1,0:T(8,128)(2,1)S(1)} %copy-done.5), custom_call_target="tpu_custom_call" | custom-call | tf_op jit(solution)/shard_map/relight/pallas_call | solution.py:611
  (43 shorter events, 0.2 us)
Async XLA Ops:
  0.7 15.6 %copy-start.14 = (s32[2,4096]{1,0:T(2,128)S(1)}, s32[2,4096]{1,0:T(2,128)}, u32[]{:S(2)}) copy-start(s32[2,4096]{1,0:T(2,128)} %param.18) | copy-start | bytes 98308
  0.7 15.6 %copy-start.11 = (bf16[256,256]{1,0:T(8,128)(2,1)S(1)}, bf16[256,256]{1,0:T(8,128)(2,1)}, u32[]{:S(2)}) copy-start(bf16[256,256]{1,0:T(8,128)(2,1)} %constant.40.clone.eye) | copy-start | bytes 393220
  8.4 28.6 %collective-permute-start = (bf16[81,16,256]{2,1,0:T(8,128)(2,1)}, bf16[81,16,256]{2,1,0:T(8,128)(2,1)S(1)}, u32[]{:S(2)}, u32[]{:S(2)}) collective-permute-start(bf16[81,16,256]{2,1,0:T(8,128)(2,1)} %get-tuple-element.23), channel_id=1, source_target_pairs={{0,4},{4,8},{8,12},{12,0},{1,5},{5,9},{9,13},{13,1},{2,6},{6,10},{... | collective-permute-start | bytes 1990664 | tf_op jit(solution)/shard_map/ppermute | solution.py:647
  12.5 24.5 %collective-permute-start.1 = (bf16[81,16,256]{2,1,0:T(8,128)(2,1)}, bf16[81,16,256]{2,1,0:T(8,128)(2,1)S(1)}, u32[]{:S(2)}, u32[]{:S(2)}) collective-permute-start(bf16[81,16,256]{2,1,0:T(8,128)(2,1)} %get-tuple-element.24), channel_id=1, source_target_pairs={{0,12},{4,0},{8,4},{12,8},{1,13},{5,1},{9,5},{13,9},{2,14},{6,2},{... | collective-permute-start | bytes 1990664 | tf_op jit(solution)/shard_map/ppermute | solution.py:648
  12.5 53.3 %collective-permute-start.2 = (bf16[81,2,16,256]{3,2,1,0:T(8,128)(2,1)}, bf16[81,2,16,256]{3,2,1,0:T(8,128)(2,1)S(1)}, u32[]{:S(2)}, u32[]{:S(2)}) collective-permute-start(bf16[81,2,16,256]{3,2,1,0:T(8,128)(2,1)} %get-tuple-element.30), channel_id=1, source_target_pairs={{0,16},{16,32},{32,48},{48,64},{64,80},{80,96},{96,112},{112,0},{1... | collective-permute-start | bytes 3981320 | tf_op jit(solution)/shard_map/ppermute | solution.py:649
  14.1 51.7 %collective-permute-start.3 = (bf16[81,2,16,256]{3,2,1,0:T(8,128)(2,1)}, bf16[81,2,16,256]{3,2,1,0:T(8,128)(2,1)}, u32[]{:S(2)}, u32[]{:S(2)}) collective-permute-start(bf16[81,2,16,256]{3,2,1,0:T(8,128)(2,1)} %get-tuple-element.31), channel_id=1, source_target_pairs={{0,112},{16,0},{32,16},{48,32},{64,48},{80,64},{96,80},{112,96},{1... | collective-permute-start | bytes 3981320 | tf_op jit(solution)/shard_map/ppermute | solution.py:650
  16.3 10.9 %copy-start.8 = (s32[3,8,4096]{2,1,0:T(8,128)S(1)}, s32[3,8,4096]{2,1,0:T(8,128)}, u32[]{:S(2)}) copy-start(s32[3,8,4096]{2,1,0:T(8,128)} %samples.1) | copy-start | bytes 1179652
  16.3 10.9 %copy-start.9 = (f32[8,4096]{1,0:T(8,128)S(1)}, f32[8,4096]{1,0:T(8,128)}, u32[]{:S(2)}) copy-start(f32[8,4096]{1,0:T(8,128)} %weights.1) | copy-start | bytes 393220
  16.4 10.9 %copy-start.13 = (bf16[16,128]{1,0:T(8,128)(2,1)S(1)}, bf16[16,128]{1,0:T(8,128)(2,1)}, u32[]{:S(2)}) copy-start(bf16[16,128]{1,0:T(8,128)(2,1)} %constant.42.clone.join) | copy-start | bytes 12292
  27.3 9.7 %copy-start.7 = (bf16[16,32]{1,0:T(8,128)(2,1)S(1)}, bf16[16,32]{1,0:T(8,128)(2,1)}, u32[]{:S(2)}) copy-start(bf16[16,32]{1,0:T(8,128)(2,1)} %constant.41.clone.pick) | copy-start | bytes 3076
  27.3 15.3 %copy-start.10 = (bf16[128,1024]{1,0:T(8,128)(2,1)S(1)}, bf16[128,1024]{1,0:T(8,128)(2,1)}, u32[]{:S(2)}) copy-start(bf16[128,1024]{1,0:T(8,128)(2,1)} %constant.43.clone.ones) | copy-start | bytes 786436
  37.0 13.3 %copy-start.1 = (bf16[81,16,256]{2,1,0:T(8,128)(2,1)}, bf16[81,16,256]{2,1,0:T(8,128)(2,1)S(1)}, u32[]{:S(2)}) copy-start(bf16[81,16,256]{2,1,0:T(8,128)(2,1)S(1)} %collective-permute-done.ylo) | copy-start | bytes 1990660
  37.0 13.3 %copy-start.2 = (bf16[81,16,256]{2,1,0:T(8,128)(2,1)}, bf16[81,16,256]{2,1,0:T(8,128)(2,1)S(1)}, u32[]{:S(2)}) copy-start(bf16[81,16,256]{2,1,0:T(8,128)(2,1)S(1)} %collective-permute-done.1.yhi) | copy-start | bytes 1990660
  39.0 26.8 %collective-permute-start.4 = (bf16[81,8,256]{2,1,0:T(8,128)(2,1)}, bf16[81,8,256]{2,1,0:T(8,128)(2,1)S(1)}, u32[]{:S(2)}, u32[]{:S(2)}) collective-permute-start(bf16[81,8,256]{2,1,0:T(8,128)(2,1)} %get-tuple-element.34), channel_id=1, source_target_pairs={{0,16},{16,32},{32,48},{48,64},{64,80},{80,96},{96,112},{112,0},{1... | collective-permute-start | bytes 995336 | tf_op jit(solution)/shard_map/ppermute | solution.py:655
  39.0 26.8 %collective-permute-start.5 = (bf16[81,8,256]{2,1,0:T(8,128)(2,1)}, bf16[81,8,256]{2,1,0:T(8,128)(2,1)S(1)}, u32[]{:S(2)}, u32[]{:S(2)}) collective-permute-start(bf16[81,8,256]{2,1,0:T(8,128)(2,1)} %get-tuple-element.35), channel_id=1, source_target_pairs={{0,112},{16,0},{32,16},{48,32},{64,48},{80,64},{96,80},{112,96},{1... | collective-permute-start | bytes 995336 | tf_op jit(solution)/shard_map/ppermute | solution.py:655
  65.8 0.7 copy-start.16
  65.8 0.9 copy-start.17
  65.8 1.3 copy-start.15
  76.5 5.3 %collective-permute-start.6 = (bf16[480,128]{1,0:T(8,128)(2,1)}, bf16[480,128]{1,0:T(8,128)(2,1)S(1)}, u32[]{:S(2)}, u32[]{:S(2)}) collective-permute-start(bf16[480,128]{1,0:T(8,128)(2,1)} %get-tuple-element.36), channel_id=1, source_target_pairs={{0,1},{1,2},{2,3},{3,0},{4,5},{5,6},{6,7},{7,4},{8,9},{9,10},{10,1... | collective-permute-start | bytes 368648 | tf_op jit(solution)/shard_map/ppermute | solution.py:675
  77.8 3.9 %collective-permute-start.7 = (bf16[480,128]{1,0:T(8,128)(2,1)}, bf16[480,128]{1,0:T(8,128)(2,1)S(1)}, u32[]{:S(2)}, u32[]{:S(2)}) collective-permute-start(bf16[480,128]{1,0:T(8,128)(2,1)} %get-tuple-element.37), channel_id=1, source_target_pairs={{0,3},{1,0},{2,1},{3,2},{4,7},{5,4},{6,5},{7,6},{8,11},{9,8},{10,9... | collective-permute-start | bytes 368648 | tf_op jit(solution)/shard_map/ppermute | solution.py:674
  82.4 50.0 %copy-start = (bf16[81,4096]{1,0:T(8,128)(2,1)S(1)}, bf16[81,4096]{1,0:T(8,128)(2,1)}, u32[]{:S(2)}) copy-start(bf16[81,4096]{1,0:T(8,128)(2,1)} %transfer.1) | copy-start | bytes 1990660
  82.4 50.0 %copy-start.3 = (bf16[1024,128]{1,0:T(8,128)(2,1)S(1)}, bf16[1024,128]{1,0:T(8,128)(2,1)}, u32[]{:S(2)}) copy-start(bf16[1024,128]{1,0:T(8,128)(2,1)} %constant.46.clone.wide) | copy-start | bytes 786436
  82.4 50.0 %copy-start.4 = (bf16[1024,81]{1,0:T(8,128)(2,1)S(1)}, bf16[1024,81]{1,0:T(8,128)(2,1)}, u32[]{:S(2)}) copy-start(bf16[1024,81]{1,0:T(8,128)(2,1)} %constant.45.clone.basis) | copy-start | bytes 497668
  82.4 50.0 %copy-start.5 = (bf16[81,1024]{1,0:T(8,128)(2,1)S(1)}, bf16[81,1024]{1,0:T(8,128)(2,1)}, u32[]{:S(2)}) copy-start(bf16[81,1024]{1,0:T(8,128)(2,1)} %constant.47.clone.projector) | copy-start | bytes 497668
  (4 other events, 2.7 us)

commit v5 on v4

--- a/solution.py
+++ b/solution.py
@@ -86,15 +86,38 @@
     return pltpu.VMEM((cells_z // LANES, cells_y * coeffs + 16, LANES), jnp.float32)
 
 
-def cut_faces(field):
+def cut_x(field):
+    coeffs, cells_x, cells_y, cells_z = field.shape
+
+    def kernel(field, last, first, sems):
+        copies = [
+            pltpu.make_async_copy(field.at[:, pl.ds(cells_x - HALO, HALO)], last, sems.at[0]),
+            pltpu.make_async_copy(field.at[:, pl.ds(0, HALO)], first, sems.at[1]),
+        ]
+        for copy in copies:
+            copy.start()
+        for copy in copies:
+            copy.wait()
+
+    hbm = pl.BlockSpec(memory_space=pl.ANY)
+    return pl.pallas_call(
+        kernel,
+        out_shape=[pltpu.HBM((coeffs, HALO, cells_y, cells_z), jnp.bfloat16)] * 2,
+        in_specs=[hbm],
+        out_specs=[hbm, hbm],
+        scratch_shapes=[pltpu.SemaphoreType.DMA((2,))],
+        compiler_params=pltpu.CompilerParams(vmem_limit_bytes=4 * MIB),
+        name="cut_x",
+    )(field)
+
+
+def cut_y(field):
     coeffs, cells_x, cells_y, cells_z = field.shape
     per_step = 9
     rows = cells_x * HALO
 
-    def kernel(field, pick, last, first, top, bottom):
+    def kernel(field, pick, top, bottom):
         for c in range(per_step):
-            last[c] = field[c, cells_x - HALO :]
-            first[c] = field[c, :HALO]
             chosen = jnp.dot(
                 pick[...],
                 field[c].reshape(cells_x * cells_y, cells_z),
@@ -108,21 +131,18 @@
         for j in range(HALO):
             pick[x * HALO + j, x * cells_y + cells_y - HALO + j] = 1.0
             pick[rows + x * HALO + j, x * cells_y + j] = 1.0
-    shapes = [(coeffs, HALO, cells_y, cells_z)] * 2
-    shapes += [(coeffs, rows, cells_z)] * 2
-
-    def whole(shape):
-        zeros = (0,) * (len(shape) - 1)
-        return pl.BlockSpec((per_step,) + shape[1:], lambda i: (i,) + zeros)
-
+    face = pl.BlockSpec((per_step, rows, cells_z), lambda i: (i, 0, 0))
     return pl.pallas_call(
         kernel,
-        out_shape=[pltpu.HBM(shape, jnp.bfloat16) for shape in shapes],
+        out_shape=[pltpu.HBM((coeffs, rows, cells_z), jnp.bfloat16)] * 2,
         grid=(coeffs // per_step,),
-        in_specs=[whole(field.shape), pl.BlockSpec(pick.shape, lambda i: (0, 0))],
-        out_specs=[whole(shape) for shape in shapes],
-        compiler_params=pltpu.CompilerParams(vmem_limit_bytes=24 * MIB),
-        name="cut_faces",
+        in_specs=[
+            pl.BlockSpec((per_step, cells_x, cells_y, cells_z), lambda i: (i, 0, 0, 0)),
+            pl.BlockSpec(pick.shape, lambda i: (0, 0)),
+        ],
+        out_specs=[face, face],
+        compiler_params=pltpu.CompilerParams(vmem_limit_bytes=16 * MIB),
+        name="cut_y",
     )(field, jnp.asarray(pick.astype(jnp.bfloat16)))
 
 
@@ -155,76 +175,51 @@
         grid=(coeffs // per_step,),
         in_specs=[face, face, pl.BlockSpec(pick.shape, lambda i: (0, 0))],
         out_specs=[piece, piece],
-        compiler_params=pltpu.CompilerParams(vmem_limit_bytes=24 * MIB),
+        compiler_params=pltpu.CompilerParams(vmem_limit_bytes=16 * MIB),
         name="cut_corners",
     )(ylo, yhi, jnp.asarray(pick.astype(jnp.bfloat16)))
 
 
-def own_table(field, eye):
-    coeffs, cells_x, cells_y, cells_z = field.shape
-    plane = cells_y * cells_z
-
-    def kernel(field, eye, out, spread):
-        fill_rows(
-            lambda c, h: field[c, 0, :, h * LANES : (h + 1) * LANES],
-            spread,
-            coeffs,
-            cells_y,
-            cells_z,
-        )
-
-        def put(y, block):
-            out[y * cells_z : (y + 1) * cells_z, :] = block
-
-        turn_rows(spread, eye, coeffs, cells_y, cells_z, put)
-
-    return pl.pallas_call(
-        kernel,
-        out_shape=pltpu.HBM((cells_x * plane, LANES), jnp.float32),
-        grid=(cells_x,),
-        in_specs=[
-            pl.BlockSpec((coeffs, 1, cells_y, cells_z), lambda x: (0, x, 0, 0)),
-            pl.BlockSpec((cells_z, cells_z), lambda x: (0, 0)),
-        ],
-        out_specs=pl.BlockSpec((plane, LANES), lambda x: (x, 0)),
-        scratch_shapes=[spread_shape(coeffs, cells_y, cells_z)],
-        compiler_params=pltpu.CompilerParams(vmem_limit_bytes=16 * MIB),
-        cost_estimate=pl.CostEstimate(
-            flops=2 * 10**10, transcendentals=0, bytes_accessed=2 * 10**7
-        ),
-        name="own_table",
-    )(field, eye)
-
-
-def full_table(own, xlo, xhi, ylo, yhi, corners, eye, total_rows):
-    coeffs, _, cells_y, cells_z = xlo.shape
-    count = 2 * HALO + 3
-    own_rows = own.shape[0]
-    lines = own_rows // cells_z + count * cells_y
-
-    def kernel(own, xlo, xhi, ylo, yhi, clo, chi, eye, table, zhi, zlo, *scratch):
-        buf, sems, small, small_sems, spread, done = scratch
-        inherit = pltpu.make_async_copy(own, table.at[pl.ds(0, own_rows), :], done)
-        sources = [xlo.at[:, 0], xlo.at[:, 1], xhi.at[:, 0], xhi.at[:, 1], ylo, yhi]
-        for p, source in enumerate(sources):
-            pltpu.make_async_copy(source, buf.at[p], sems.at[p]).start()
-        pieces = [
-            pltpu.make_async_copy(corner, small.at[q], small_sems.at[q])
-            for q, corner in enumerate((clo, chi))
-        ]
-        for piece in pieces:
-            piece.start()
-        inherit.start()
+def add_planes(table, planes, halves, eye, first_plane, total_rows, edge_lines):
+    source = planes[0][0]
+    coeffs, cells_y, cells_z = source.shape[0], source.shape[-2], source.shape[-1]
+    count = len(planes)
+    arrays = []
+    for array, _ in planes:
+        if not any(array is other for other in arrays):
+            arrays.append(array)
+    places = [next(i for i, o in enumerate(arrays) if o is array) for array, _ in planes]
+    new = table is None
+
+    def kernel(*refs):
+        refs = list(refs)
+        if not new:
+            refs.pop(0)
+        inputs = [refs.pop(0) for _ in arrays]
+        shared = [refs.pop(0) for _ in halves]
+        eye = refs.pop(0)
+        table = refs.pop(0)
+        edges = [refs.pop(0) for _ in range(2)] if edge_lines else []
+        buf, sems, spread = refs[:3]
+        copies = []
+        for p, ((_, at), place) in enumerate(zip(planes, places)):
+            ref = inputs[place] if at is None else inputs[place].at[:, at]
+            copies.append(pltpu.make_async_copy(ref, buf.at[p], sems.at[p]))
+        for q, piece in enumerate(shared):
+            copies.append(pltpu.make_async_copy(piece, refs[3].at[q], refs[4].at[q]))
+        for copy in copies:
+            copy.start()
 
         def turn(p):
             def put(y, block):
-                at = pl.multiple_of(own_rows + (p * cells_y + y) * cells_z, 8)
+                at = pl.multiple_of(((first_plane + p) * cells_y + y) * cells_z, 8)
                 table[pl.ds(at, cells_z), :] = block
 
             turn_rows(spread, eye, coeffs, cells_y, cells_z, put)
 
         def one(p, _):
-            pltpu.make_async_copy(ylo, buf.at[p], sems.at[p]).wait()
+            first = inputs[0] if planes[0][1] is None else inputs[0].at[:, 0]
+            pltpu.make_async_copy(first, buf.at[p], sems.at[p]).wait()
             fill_rows(
                 lambda c, h: buf[p, c, :, h * LANES : (h + 1) * LANES],
                 spread,
@@ -235,59 +230,97 @@
             turn(p)
             return 0
 
-        lax.fori_loop(0, count - 1, one, 0)
-        for piece in pieces:
-            piece.wait()
-        fill_rows(
-            lambda c, h: jnp.concatenate(
-                [
-                    small[q, c, :, h * LANES : (h + 1) * LANES].astype(jnp.float32)
-                    for q in range(2)
-                ],
-                axis=0,
-            ),
-            spread,
-            coeffs,
-            cells_y,
-            cells_z,
-        )
-        turn(count - 1)
-        inherit.wait()
-        for out, start in ((zhi, 0), (zlo, cells_z - HALO)):
+        lax.fori_loop(0, count, one, 0)
+        if halves:
+            for copy in copies[count:]:
+                copy.wait()
+            fill_rows(
+                lambda c, h: jnp.concatenate(
+                    [
+                        refs[3][q, c, :, h * LANES : (h + 1) * LANES].astype(jnp.float32)
+                        for q in range(2)
+                    ],
+                    axis=0,
+                ),
+                spread,
+                coeffs,
+                cells_y,
+                cells_z,
+            )
+            turn(count)
+        for out, start in zip(edges, (0, cells_z - HALO)):
             for j in range(HALO):
-                for line in range(0, lines, 16):
+                for line in range(0, edge_lines, 16):
                     parts = [
                         table[pl.ds((line + i) * cells_z + start + j, 8, stride=cells_z), :]
                         for i in (0, 8)
                     ]
-                    out[j * lines + line : j * lines + line + 16, :] = jnp.concatenate(
-                        parts, axis=0
-                    ).astype(jnp.bfloat16)
-
-    edge = jax.ShapeDtypeStruct((HALO * lines, LANES), jnp.bfloat16)
+                    at = j * edge_lines + line
+                    out[at : at + 16, :] = jnp.concatenate(parts, axis=0).astype(jnp.bfloat16)
+
     vmem = pl.BlockSpec(memory_space=pltpu.VMEM)
     hbm = pl.BlockSpec(memory_space=pl.ANY)
+    shapes = [pltpu.VMEM((total_rows, LANES), jnp.float32)]
+    if edge_lines:
+        shapes += [jax.ShapeDtypeStruct((HALO * edge_lines, LANES), jnp.bfloat16)] * 2
+    scratch = [
+        pltpu.VMEM((count, coeffs, cells_y, cells_z), jnp.bfloat16),
+        pltpu.SemaphoreType.DMA((count,)),
+        spread_shape(coeffs, cells_y, cells_z),
+    ]
+    if halves:
+        scratch += [
+            pltpu.VMEM((2, coeffs, cells_y // 2, cells_z), jnp.bfloat16),
+            pltpu.SemaphoreType.DMA((2,)),
+        ]
+    held = [] if new else [table]
     return pl.pallas_call(
         kernel,
-        out_shape=(pltpu.VMEM((total_rows, LANES), jnp.float32), edge, edge),
-        in_specs=[hbm] * 7 + [vmem],
-        out_specs=(vmem, vmem, vmem),
-        scratch_shapes=[
-            pltpu.VMEM((count - 1, coeffs, cells_y, cells_z), jnp.bfloat16),
-            pltpu.SemaphoreType.DMA((count - 1,)),
-            pltpu.VMEM((2, coeffs, 2 * HALO * HALO, cells_z), jnp.bfloat16),
-            pltpu.SemaphoreType.DMA((2,)),
-            spread_shape(coeffs, cells_y, cells_z),
-            pltpu.SemaphoreType.DMA(()),
-        ],
-        compiler_params=pltpu.CompilerParams(vmem_limit_bytes=24 * MIB),
+        out_shape=shapes,
+        in_specs=[vmem] * len(held) + [hbm] * (len(arrays) + len(halves)) + [vmem],
+        out_specs=[vmem] * len(shapes),
+        scratch_shapes=scratch,
+        input_output_aliases={} if new else {0: 0},
+        compiler_params=pltpu.CompilerParams(vmem_limit_bytes=TABLE_LIMIT * MIB),
         cost_estimate=pl.CostEstimate(
             flops=2 * 10**10, transcendentals=0, bytes_accessed=2 * 10**7
         ),
-        name="full_table",
-    )(own, xlo, xhi, ylo, yhi, *corners, eye)
-
-
+    )(*held, *arrays, *halves, eye)
+
+
+def cut_ends(zlo, zhi, lines, cells_x, cells_y):
+    own = cells_x * cells_y
+    half = HALO * cells_y + 2 * HALO * HALO
+    rows = 2 * HALO * half
+
+    def kernel(zlo, zhi, pick, up, down):
+        both = jnp.concatenate([zlo[...], zhi[...]], axis=0)
+        chosen = jnp.dot(pick[...], both, preferred_element_type=jnp.float32)
+        up[...] = chosen[:rows].astype(jnp.bfloat16)
+        down[...] = chosen[rows:].astype(jnp.bfloat16)
+
+    pick = np.zeros((2 * rows, 2 * HALO * lines), np.float32)
+    for side in range(2):
+        x = cells_x - HALO if side == 0 else 0
+        places = [x * cells_y + i for i in range(HALO * cells_y)]
+        for face in range(2):
+            at = own + face * cells_y + x * HALO
+            places += [at + i for i in range(HALO * HALO)]
+        for z in range(2 * HALO):
+            for i, place in enumerate(places):
+                pick[side * rows + z * half + i, z * lines + place] = 1.0
+    vmem = pl.BlockSpec(memory_space=pltpu.VMEM)
+    return pl.pallas_call(
+        kernel,
+        out_shape=[jax.ShapeDtypeStruct((rows, LANES), jnp.bfloat16)] * 2,
+        in_specs=[vmem] * 3,
+        out_specs=[vmem] * 2,
+        compiler_params=pltpu.CompilerParams(vmem_limit_bytes=8 * MIB),
+        name="cut_ends",
+    )(zlo, zhi, jnp.asarray(pick.astype(jnp.bfloat16)))
+
+
+TABLE_LIMIT = 24
 GROUP = 8
 PARTS = 3
 
@@ -296,37 +329,41 @@
     count = slot.shape[0]
     cells_x, cells_y, cells_z = cells
     own_lines = cells_x * cells_y
-    lines = own_lines + (2 * HALO + 3) * cells_y
-    rows = lines * cells_z
+    early = own_lines + 2 * cells_y
+    rows = (early + (2 * HALO + 1) * cells_y) * cells_z
     block = 256
     burst = 32
     kinds = (2 + PARTS) * SAMPLES
+    corner = HALO * HALO
+    end = HALO * cells_y + 2 * corner
 
     def locate(near_x, near_y, near_z):
         own_x = (near_x >= HALO) & (near_x < HALO + cells_x)
         own_y = (near_y >= HALO) & (near_y < HALO + cells_y)
+        low_x = near_x < HALO
         low_y = near_y < HALO
-        side_x = jnp.where(near_x < HALO, near_x, near_x - cells_x)
+        side_x = jnp.where(low_x, near_x, near_x - HALO - cells_x)
         side_y = jnp.where(low_y, near_y, near_y - HALO - cells_y)
-        line_own = jnp.where(own_x, near_x - HALO, cells_x + side_x) * cells_y + near_y - HALO
-        line_y = (
-            (cells_x + 2 * HALO) * cells_y
-            + jnp.where(low_y, 0, cells_y)
-            + (near_x - HALO) * HALO
-            + side_y
+        line_own = (near_x - HALO) * cells_y + near_y - HALO
+        line_y = own_lines + jnp.where(low_y, 0, cells_y) + (near_x - HALO) * HALO + side_y
+        line_early = jnp.where(own_y, line_own, line_y)
+        in_face = side_x * cells_y + near_y - HALO
+        in_corner = jnp.where(low_y, 0, corner) + side_x * HALO + side_y
+        line_late = early + jnp.where(
+            own_y,
+            jnp.where(low_x, 0, HALO * cells_y) + in_face,
+            2 * HALO * cells_y + jnp.where(low_x, 0, 2 * corner) + in_corner,
         )
-        line_corner = (
-            (cells_x + 2 * HALO + 2) * cells_y
-            + jnp.where(near_x < HALO, 0, HALO * HALO)
-            + jnp.where(low_y, 0, HALO * HALO)
-            + side_x * HALO
-            + side_y
+        line = jnp.where(own_x, line_early, line_late)
+        edge = jnp.where(near_z < HALO, near_z, near_z - cells_z)
+        at_end = jnp.where(own_y, in_face, HALO * cells_y + in_corner)
+        beyond = jnp.where(
+            own_x,
+            edge * early + line_early,
+            2 * HALO * early + jnp.where(low_x, 0, 2 * HALO * end) + edge * end + at_end,
         )
-        line = jnp.where(own_y, line_own, jnp.where(own_x, line_y, line_corner))
-        inside = line * cells_z + near_z - HALO
-        below = rows + near_z * lines + line
-        above = rows + (near_z - cells_z) * lines + line
-        return jnp.where(near_z < HALO, below, jnp.where(near_z < HALO + cells_z, inside, above))
+        inside = (near_z >= HALO) & (near_z < HALO + cells_z)
+        return jnp.where(inside, line * cells_z + near_z - HALO, rows + beyond)
 
     def kernel(origin, slot, samples, weights, eye, join, index, ordered, natural):
         def turn(j, _):
@@ -410,61 +447,24 @@
     )
 
 
-def spread_weights(ordered):
+RING = 2
+CHUNK = 1024
+
+
+def gather_rows(index, ordered, table, edges, first_edge, coeffs):
     count = ordered.shape[0]
-    block = 512
-
-    def kernel(ordered, ones, wide):
-        rows = ordered[...].astype(jnp.bfloat16)
-        for h in range(0, SAMPLES, 2):
-            both = jnp.dot(
-                rows, ones[:, h * LANES : (h + 2) * LANES], preferred_element_type=jnp.float32
-            )
-            for s in range(2):
-                for g in range(block // GROUP):
-                    to = (g * SAMPLES + h + s) * GROUP
-                    wide[to : to + GROUP, :] = both[
-                        g * GROUP : (g + 1) * GROUP, s * LANES : (s + 1) * LANES
-                    ]
-
-    ones = np.zeros((LANES, SAMPLES * LANES), np.float32)
-    for s in range(SAMPLES):
-        for p in range(PARTS):
-            ones[(2 + p) * SAMPLES + s, s * LANES : (s + 1) * LANES] = 1.0
-    return pl.pallas_call(
-        kernel,
-        out_shape=pltpu.HBM((count * SAMPLES, LANES), jnp.float32),
-        grid=(count // block,),
-        in_specs=[
-            pl.BlockSpec((block, LANES), lambda i: (i, 0)),
-            pl.BlockSpec(ones.shape, lambda i: (0, 0)),
-        ],
-        out_specs=pl.BlockSpec((block * SAMPLES, LANES), lambda i: (i, 0)),
-        compiler_params=pltpu.CompilerParams(vmem_limit_bytes=12 * MIB),
-        cost_estimate=pl.CostEstimate(
-            flops=10**10, transcendentals=0, bytes_accessed=3 * 10**6
-        ),
-        name="spread_weights",
-    )(ordered, jnp.asarray(ones.astype(jnp.bfloat16)))
-
-
-RING = 2
-STREAM = 8
-CHUNK = 1024
-
-
-def gather_rows(index, wide, table, zlo, zhi, first_edge, count, coeffs):
-    edges = zlo.shape[0]
     chunks = index.shape[0] // CHUNK
     per_chunk = CHUNK // SAMPLES
     groups = per_chunk // GROUP
     pairs = count // 32
     half = LANES // 2
 
-    def kernel(index, zlo, zhi, pick, wide, table_in, table, out, *scratch):
-        local, sems, near, near_sems, rows = scratch
-        table[pl.ds(first_edge, edges), :] = zlo[...].astype(jnp.float32)
-        table[pl.ds(first_edge + edges, edges), :] = zhi[...].astype(jnp.float32)
+    def kernel(index, ordered, ones, pick, *refs):
+        table, out, local, sems, near, rows = refs[len(edges) + 1 :]
+        at = first_edge
+        for edge in refs[: len(edges)]:
+            table[pl.ds(at, edge.shape[0]), :] = edge[...].astype(jnp.float32)
+            at += edge.shape[0]
         sublane = lax.broadcasted_iota(jnp.int32, (GROUP, LANES), 0)
         masks = [sublane == k for k in range(GROUP)]
         used = lax.broadcasted_iota(jnp.int32, (GROUP, LANES), 1) < coeffs
@@ -476,34 +476,35 @@
                 sems.at[slot],
             )
 
-        def stream(n, slot):
-            return pltpu.make_async_copy(
-                wide.at[pl.ds(pl.multiple_of(n * CHUNK, CHUNK), CHUNK), :],
-                near.at[slot],
-                near_sems.at[slot],
-            )
+        def spread(n, slot):
+            at = pl.multiple_of(n * per_chunk, per_chunk)
+            parts = ordered[pl.ds(at, per_chunk), :].astype(jnp.bfloat16)
+            for h in range(0, SAMPLES, 2):
+                both = jnp.dot(
+                    parts, ones[:, h * LANES : (h + 2) * LANES], preferred_element_type=jnp.float32
+                )
+                for s in range(2):
+                    for q in range(groups):
+                        to = (q * SAMPLES + h + s) * GROUP
+                        near[slot, to : to + GROUP, :] = both[
+                            q * GROUP : (q + 1) * GROUP, s * LANES : (s + 1) * LANES
+                        ]
 
         for b in range(RING - 1):
             fetch(b, b).start()
-        for b in range(STREAM - 1):
-            stream(b, b).start()
+        spread(0, 0)
 
         def body(i, _):
             for b in range(RING):
                 n = i * RING + b
-                slot = n % STREAM
                 fetch(n, b).wait()
-                stream(n, slot).wait()
                 ahead = n + RING - 1
-                later = n + STREAM - 1
 
                 @pl.when(ahead < chunks)
                 def _():
                     fetch(ahead, (b + RING - 1) % RING).start()
 
-                @pl.when(later < chunks)
-                def _():
-                    stream(later, later % STREAM).start()
+                spread(jnp.minimum(n + 1, chunks - 1), 1 - b)
 
                 for q in range(groups):
                     total = None
@@ -514,7 +515,7 @@
                             row = table[pl.ds(local[b, place], GROUP, stride=0), :]
                             merged = row if merged is None else jnp.where(masks[k], row, merged)
                         at = (q * SAMPLES + s) * GROUP
-                        term = merged * near[slot, at : at + GROUP, :]
+                        term = merged * near[b, at : at + GROUP, :]
                         total = term if total is None else total + term
                     to = pl.multiple_of((n * (groups // 4) + q // 4) * GROUP, GROUP)
                     rows[q % 4, pl.ds(to, GROUP), :] = jnp.where(used, total, 0.0)
@@ -541,6 +542,10 @@
 
         lax.fori_loop(0, pairs * GROUP // 128, pack, 0)
 
+    ones = np.zeros((LANES, SAMPLES * LANES), np.float32)
+    for s in range(SAMPLES):
+        for p in range(PARTS):
+            ones[(2 + p) * SAMPLES + s, s * LANES : (s + 1) * LANES] = 1.0
     pick = np.zeros((3, 2 * LANES, LANES), np.float32)
     for c in range(half):
         pick[0, c, c] = 1.0
@@ -557,22 +562,28 @@
             pltpu.VMEM(table.shape, jnp.float32),
             jax.ShapeDtypeStruct((pairs, 24, LANES), jnp.bfloat16),
         ),
-        in_specs=[vmem] * 4 + [pl.BlockSpec(memory_space=pl.ANY), vmem],
+        in_specs=[vmem] * (5 + len(edges)),
         out_specs=(vmem, vmem),
         scratch_shapes=[
             pltpu.SMEM((RING, CHUNK), jnp.int32),
             pltpu.SemaphoreType.DMA((RING,)),
-            pltpu.VMEM((STREAM, CHUNK, LANES), jnp.float32),
-            pltpu.SemaphoreType.DMA((STREAM,)),
+            pltpu.VMEM((RING, CHUNK, LANES), jnp.float32),
             pltpu.VMEM((4, pairs * GROUP, LANES), jnp.float32),
         ],
-        input_output_aliases={5: 0},
+        input_output_aliases={4 + len(edges): 0},
         compiler_params=pltpu.CompilerParams(vmem_limit_bytes=24 * MIB),
         cost_estimate=pl.CostEstimate(
             flops=4 * 10**10, transcendentals=0, bytes_accessed=2 * 10**7
         ),
         name="gather_rows",
-    )(index, zlo, zhi, jnp.asarray(pick.astype(jnp.bfloat16)), wide, table)[1]
+    )(
+        index,
+        ordered,
+        jnp.asarray(ones.astype(jnp.bfloat16)),
+        jnp.asarray(pick.astype(jnp.bfloat16)),
+        *edges,
+        table,
+    )[1]
 
 
 def relight(transfer, routed, basis, projector):
@@ -642,20 +653,6 @@
     ups = [moves((n, 1), (1, 0)) for n in along]
     downs = [moves((n, 1), (-1, 0)) for n in along]
 
-    field = pltpu.with_memory_space_constraint(field, pltpu.HBM)
-    last, first, top, bottom = cut_faces(field)
-    ylo = lax.ppermute(top, "gy", ups[1])
-    yhi = lax.ppermute(bottom, "gy", downs[1])
-    xlo = lax.ppermute(last, "gx", ups[0])
-    xhi = lax.ppermute(first, "gx", downs[0])
-    eye = jnp.asarray(np.eye(cells_z, dtype=np.float32).astype(jnp.bfloat16))
-    own = own_table(field, eye)
-    ylo, yhi, own = lax.optimization_barrier((ylo, yhi, own))
-    ends = cut_corners(ylo, yhi)
-    corners = [lax.ppermute(ends[0], "gx", ups[0]), lax.ppermute(ends[1], "gx", downs[0])]
-
-    lines = cells_x * cells_y + (2 * HALO + 3) * cells_y
-    rows = lines * cells_z
     cells = (cells_x, cells_y, cells_z)
     total = tuple(c * n for c, n in zip(cells, along))
     origin = jnp.stack(
@@ -665,15 +662,40 @@
     per_pair = count // devices
     slot = destination[0] * per_pair + destination[1]
 
+    field = pltpu.with_memory_space_constraint(field, pltpu.HBM)
+    last, first = cut_x(field)
+    xlo = lax.ppermute(last, "gx", ups[0])
+    xhi = lax.ppermute(first, "gx", downs[0])
+    top, bottom = cut_y(field)
+    ylo = lax.ppermute(top, "gy", ups[1])
+    yhi = lax.ppermute(bottom, "gy", downs[1])
+    field, slot, origin = lax.optimization_barrier((field, slot, origin))
+
+    eye = jnp.asarray(np.eye(cells_z, dtype=np.float32).astype(jnp.bfloat16))
+    early = (cells_x + 2) * cells_y
+    rows = (early + (2 * HALO + 1) * cells_y) * cells_z
+    ends = HALO * cells_y + 2 * HALO * HALO
+    total_rows = rows + 2 * HALO * (early + 2 * ends)
+    own = [(field, x) for x in range(cells_x)]
+    table = add_planes(None, own, (), eye, 0, total_rows, 0)[0]
     index, ordered = prepare(samples, weights, slot, origin, cells, total)
-    wide = spread_weights(ordered)
-    own, index, wide = lax.optimization_barrier((own, index, wide))
-    table, edge_lo, edge_hi = full_table(
-        own, xlo, xhi, ylo, yhi, corners, eye, rows + 2 * HALO * lines
+    table, index, ordered, ylo, yhi = lax.optimization_barrier((table, index, ordered, ylo, yhi))
+    up, down = cut_corners(ylo, yhi)
+    clo = lax.ppermute(up, "gx", ups[0])
+    chi = lax.ppermute(down, "gx", downs[0])
+    table, bottoms, tops = add_planes(
+        table, [(ylo, None), (yhi, None)], (), eye, cells_x, total_rows, early
     )
-    zhi = lax.ppermute(edge_lo, "gz", downs[2])
-    zlo = lax.ppermute(edge_hi, "gz", ups[2])
-    outgoing = gather_rows(index.reshape(-1), wide, table, zlo, zhi, rows, count, coeffs)
+    zhi = lax.ppermute(bottoms, "gz", downs[2])
+    zlo = lax.ppermute(tops, "gz", ups[2])
+    up, down = cut_ends(zlo, zhi, early, cells_x, cells_y)
+    elo = lax.ppermute(up, "gx", ups[0])
+    ehi = lax.ppermute(down, "gx", downs[0])
+    sides = [(xlo, 0), (xlo, 1), (xhi, 0), (xhi, 1)]
+    table = add_planes(table, sides, (clo, chi), eye, cells_x + 2, total_rows, 0)[0]
+    outgoing = gather_rows(
+        index.reshape(-1), ordered, table, (zlo, zhi, elo, ehi), rows, coeffs
+    )
     routed = lax.all_to_all(
         outgoing, ("gx", "gy", "gz"), split_axis=0, concat_axis=0, tiled=True
     )

time: 141 us -> 207 us (1.47)
  Pallas kernels: 79.6 us -> 151 us
  waiting for transfers between devices: 18 us -> 6.13 us
  starting transfers between devices: 14.4 us -> 18.1 us
    pallas_call x4 -> x6, Pallas kernels: 35.5 us -> 104 us  [the longest x1 81.5 us: cut_x(): pl.pallas_call(kernel, out_shape=[pltpu.HBM((coeffs, HALO, cells_y, cells...]
    ppermute x4 -> x6, waiting for transfers between devices: 17.9 us -> 6.12 us  [the longest x1 3.77 us: halo_step(): zlo = lax.ppermute(tops, 'gz', ups[2])]
    ppermute x4 -> x6, starting transfers between devices: 6.45 us -> 10 us  [the longest x1 3.57 us: halo_step(): chi = lax.ppermute(down, 'gx', downs[0])]
    pallas_call x1, Pallas kernels: 25.5 us -> 28.4 us  [gather_rows(): pl.pallas_call(kernel, out_shape=(pltpu.VMEM(table.shape, jnp.float32), j...]
    unnamed x40 -> x46, local copies, waits for them, and re-layouts: 3.41 us -> 4.56 us
  transfers between devices with their start and end apart: 8 -> 10, of which waited for: 2 -> 2; matrix products, arithmetic and copies ran while one was open for 0% -> 0% of each run, Pallas kernels for 21% -> 52%
where the time goes in v5:
time: 207 us
  Pallas kernels  151 us (73%)
  blocking collectives  26.3 us (13%)
  starting transfers between devices  18.1 us (9%)
  waiting for transfers between devices  6.13 us (3%)
  local copies, waits for them, and re-layouts  4.56 us (2%)
    pallas_call x1, Pallas kernels, cut_x(): pl.pallas_call(kernel, out_shape=[pltpu.HBM((coeffs, HALO, cells_y, cells...  81.5 us
    pallas_call x1, Pallas kernels, gather_rows(): pl.pallas_call(kernel, out_shape=(pltpu.VMEM(table.shape, jnp.float32), j...  28.4 us
    all_to_all x1, blocking collectives, halo_step(): lax.all_to_all(outgoing, ('gx', 'gy', 'gz'), split_axis=0, concat_axis=0,...  26.3 us
    pallas_call x3, Pallas kernels, add_planes(): pl.pallas_call(kernel, out_shape=shapes, in_specs=[vmem] * len(held) + [h...  15 us
    pallas_call x1, Pallas kernels, prepare(): pl.pallas_call(kernel, out_shape=(jax.ShapeDtypeStruct((count * SAMPLES /...  9.08 us
    pallas_call x1, Pallas kernels, relight(): pl.pallas_call(kernel, out_shape=jax.ShapeDtypeStruct((coeffs, count), jn...  7.55 us
    pallas_call x1, Pallas kernels, cut_y(): pl.pallas_call(kernel, out_shape=[pltpu.HBM((coeffs, rows, cells_z), jnp....  7.44 us
    unnamed x46, local copies, waits for them, and re-layouts  4.56 us
  transfers between devices with their start and end apart: 10, of which 2 were waited for; matrix products, arithmetic and copies ran while one was open for 0% of the time, Pallas kernels for 52%

profile of v5, /device:TPU:1, one launch (start us, length us, event | category | flops | bytes accessed | tf_op | source)
XLA Modules:
  0.0 206.7 jit_solution(6373435744359760199)
XLA Ops:
  0.0 0.7 copy-done.9
  0.7 7.4 %cut_y.1 = (bf16[81,16,256]{2,1,0:T(8,128)(2,1)}, bf16[81,16,256]{2,1,0:T(8,128)(2,1)}) custom-call(bf16[81,8,16,256]{3,2,1,0:T(8,128)(2,1)} %field.3, bf16[32,128]{1,0:T(8,128)(2,1)S(1)} %copy-done.9), custom_call_target="tpu_custom_call" | custom-call | tf_op jit(solution)/shard_map/cut_y/pallas_call | solution.py:135
  8.1 4.1 %collective-permute-start = (bf16[81,16,256]{2,1,0:T(8,128)(2,1)}, bf16[81,16,256]{2,1,0:T(8,128)(2,1)S(1)}, u32[]{:S(2)}, u32[]{:S(2)}) collective-permute-start(bf16[81,16,256]{2,1,0:T(8,128)(2,1)} %get-tuple-element.32), channel_id=1, source_target_pairs={{0,4},{4,8},{8,12},{12,0},{1,5},{5,9},{9,13},{13,1},{2,6},{6,10},{... | collective-permute-start | bytes 1990664 | tf_op jit(solution)/shard_map/ppermute | solution.py:670
  12.3 81.5 %cut_x.1 = (bf16[81,2,16,256]{3,2,1,0:T(8,128)(2,1)}, bf16[81,2,16,256]{3,2,1,0:T(8,128)(2,1)}) custom-call(bf16[81,8,16,256]{3,2,1,0:T(8,128)(2,1)} %field.3), custom_call_target="tpu_custom_call" | custom-call | tf_op jit(solution)/shard_map/cut_x/pallas_call | solution.py:103
  93.8 1.7 collective-permute-start.6
  95.5 2.2 %collective-permute-start.7 = (bf16[81,2,16,256]{3,2,1,0:T(8,128)(2,1)}, bf16[81,2,16,256]{3,2,1,0:T(8,128)(2,1)}, u32[]{:S(2)}, u32[]{:S(2)}) collective-permute-start(bf16[81,2,16,256]{3,2,1,0:T(8,128)(2,1)} %get-tuple-element.45), channel_id=1, source_target_pairs={{0,112},{16,0},{32,16},{48,32},{64,48},{80,64},{96,80},{112,96},{1... | collective-permute-start | bytes 3981320 | tf_op jit(solution)/shard_map/ppermute | solution.py:668
  97.9 6.3 %shard_map.154.refs_0_ = f32[62400,128]{1,0:T(8,128)S(1)} custom-call(bf16[81,8,16,256]{3,2,1,0:T(8,128)(2,1)} %field.3, bf16[256,256]{1,0:T(8,128)(2,1)} %constant.42.clone.refs_1_.eye.refs_3_.refs_5_), custom_call_target="tpu_custom_call" | custom-call | flops 20000000000 | bytes 20000000 | tf_op jit(solution)/shard_map/pallas_call | solution.py:277
  104.2 9.1 %prepare.1 = (s32[256,128]{1,0:T(8,128)S(1)}, f32[4096,128]{1,0:T(8,128)S(1)}) custom-call(s32[3]{0:T(128)S(1)} %pad_add_fusion.origin, s32[4096]{0:T(1024)S(1)} %bitcast.5, s32[3,8,4096]{2,1,0:T(8,128)S(1)} %copy-done.11, f32[8,4096]{1,0:T(8,128)S(1)} %copy-done.12, bf16[256,256]{1,0:T(8,128)(2,1)S(1)} %copy-done.13, bf16[16,128]{1,0:T(8,128)(2,1)S(1)} %copy-done.15), custom_call_target="tpu_custom_call" | custom-call | flops 20000000000 | bytes 3000000 | tf_op jit(solution)/shard_map/prepare/pallas_call | solution.py:426
  113.3 0.7 copy-done.14
  114.0 1.4 copy-done.16
  115.4 2.0 cut_corners.1
  117.4 3.6 %collective-permute-start.9 = (bf16[81,8,256]{2,1,0:T(8,128)(2,1)}, bf16[81,8,256]{2,1,0:T(8,128)(2,1)S(1)}, u32[]{:S(2)}, u32[]{:S(2)}) collective-permute-start(bf16[81,8,256]{2,1,0:T(8,128)(2,1)} %get-tuple-element.47), channel_id=1, source_target_pairs={{0,112},{16,0},{32,16},{48,32},{64,48},{80,64},{96,80},{112,96},{1... | collective-permute-start | bytes 995336 | tf_op jit(solution)/shard_map/ppermute | solution.py:685
  121.0 4.0 %shard_map.155 = (f32[62400,128]{1,0:T(8,128)S(1)}, bf16[320,128]{1,0:T(8,128)(2,1)}, bf16[320,128]{1,0:T(8,128)(2,1)}) custom-call(f32[62400,128]{1,0:T(8,128)S(1)} %shard_map.154.refs_0_, bf16[81,16,256]{2,1,0:T(8,128)(2,1)} %copy-done.1, bf16[81,16,256]{2,1,0:T(8,128)(2,1)} %copy-done.2, ...), custom_call_target="tpu_custom_call", output_to_operand_aliasing={{0}: (0, {})} | custom-call | flops 20000000000 | bytes 20000000 | tf_op jit(solution)/shard_map/pallas_call | solution.py:277
  125.0 1.4 collective-permute-start.2
  126.4 3.8 %collective-permute-done.2.zlo.refs_0_ = bf16[320,128]{1,0:T(8,128)(2,1)S(1)} collective-permute-done((bf16[320,128]{1,0:T(8,128)(2,1)}, bf16[320,128]{1,0:T(8,128)(2,1)S(1)}, u32[]{:S(2)}, u32[]{:S(2)}) %collective-permute-start.2) | collective-permute-done | bytes 81952 | tf_op jit(solution)/shard_map/ppermute | solution.py:690
  130.1 1.5 collective-permute-start.3
  131.6 2.3 %collective-permute-done.3.zhi.refs_1_ = bf16[320,128]{1,0:T(8,128)(2,1)S(1)} collective-permute-done((bf16[320,128]{1,0:T(8,128)(2,1)}, bf16[320,128]{1,0:T(8,128)(2,1)S(1)}, u32[]{:S(2)}, u32[]{:S(2)}) %collective-permute-start.3) | collective-permute-done | bytes 81952 | tf_op jit(solution)/shard_map/ppermute | solution.py:689
  134.3 3.5 %collective-permute-start.5 = (bf16[160,128]{1,0:T(8,128)(2,1)S(1)}, bf16[160,128]{1,0:T(8,128)(2,1)S(1)}, u32[]{:S(2)}, u32[]{:S(2)}) collective-permute-start(bf16[160,128]{1,0:T(8,128)(2,1)S(1)} %get-tuple-element.42), channel_id=1, source_target_pairs={{0,112},{16,0},{32,16},{48,32},{64,48},{80,64},{96,80},{112,96},{1... | collective-permute-start | bytes 122888 | tf_op jit(solution)/shard_map/ppermute | solution.py:693
  137.9 0.7 copy-done.20
  139.1 4.7 %shard_map.156.refs_4_ = f32[62400,128]{1,0:T(8,128)S(1)} custom-call(f32[62400,128]{1,0:T(8,128)S(1)} %get-tuple-element.43.refs_0_, bf16[81,2,16,256]{3,2,1,0:T(8,128)(2,1)} %copy-done.18, bf16[81,2,16,256]{3,2,1,0:T(8,128)(2,1)} %collective-permute-done.7.refs_2_, bf16[81,8,256]{2,1,0:T(8,128)(2,1)} %copy-done.19, ...), custom_call_target="tpu_custom_call", output_to_operand_aliasing={{}: (0, {})} | custom-call | flops 20000000000 | bytes 20000000 | tf_op jit(solution)/shard_map/pallas_call | solution.py:277
  143.8 0.6 copy-done.21
  144.4 28.4 %gather_rows.1 = (f32[62400,128]{1,0:T(8,128)S(1)}, bf16[128,24,128]{2,1,0:T(8,128)(2,1)}) custom-call(s32[32768]{0:T(1024)} %bitcast.6, f32[4096,128]{1,0:T(8,128)} %copy-done.16, bf16[128,1024]{1,0:T(8,128)(2,1)} %constant.46.clone.ones, bf16[3,256,128]{2,1,0:T(8,128)(2,1)} %constant.47.clone.pick, ...), custom_call_target="tpu_custom_call", output_to_operand_aliasing={{0}: (8, {})} | custom-call | flops 40000000000 | bytes 20000000 | tf_op jit(solution)/shard_map/gather_rows/pallas_call | solution.py:559
  172.8 26.3 %all_to_all.5.routed = bf16[128,24,128]{2,1,0:T(8,128)(2,1)S(1)} all-to-all(bf16[128,24,128]{2,1,0:T(8,128)(2,1)} %get-tuple-element.48), channel_id=1, replica_groups=mesh['gx'=8,'gy'=4,'gz'=4] {'gx','gy','gz'}, dimensions={0} | all-to-all | bytes 1572864 | tf_op jit(solution)/shard_map/all_to_all | solution.py:699
  199.1 7.5 %relight.1 = bf16[81,4096]{1,0:T(8,128)(2,1)} custom-call(bf16[81,4096]{1,0:T(8,128)(2,1)S(1)} %copy-done, bf16[128,24,128]{2,1,0:T(8,128)(2,1)S(1)} %all_to_all.5.routed, bf16[1024,81]{1,0:T(8,128)(2,1)S(1)} %copy-done.4, bf16[1024,128]{1,0:T(8,128)(2,1)S(1)} %copy-done.5, bf16[81,1024]{1,0:T(8,128)(2,1)S(1)} %copy-done.6), custom_call_target="tpu_custom_call" | custom-call | tf_op jit(solution)/shard_map/relight/pallas_call | solution.py:622
  (55 shorter events, 1.0 us)
Async XLA Ops:
  0.7 97.0 %copy-start.17 = (s32[2,4096]{1,0:T(2,128)S(1)}, s32[2,4096]{1,0:T(2,128)}, u32[]{:S(2)}) copy-start(s32[2,4096]{1,0:T(2,128)} %param.19) | copy-start | bytes 98308
  8.1 107.2 %collective-permute-start = (bf16[81,16,256]{2,1,0:T(8,128)(2,1)}, bf16[81,16,256]{2,1,0:T(8,128)(2,1)S(1)}, u32[]{:S(2)}, u32[]{:S(2)}) collective-permute-start(bf16[81,16,256]{2,1,0:T(8,128)(2,1)} %get-tuple-element.32), channel_id=1, source_target_pairs={{0,4},{4,8},{8,12},{12,0},{1,5},{5,9},{9,13},{13,1},{2,6},{6,10},{... | collective-permute-start | bytes 1990664 | tf_op jit(solution)/shard_map/ppermute | solution.py:670
  12.3 103.1 %collective-permute-start.1 = (bf16[81,16,256]{2,1,0:T(8,128)(2,1)}, bf16[81,16,256]{2,1,0:T(8,128)(2,1)S(1)}, u32[]{:S(2)}, u32[]{:S(2)}) collective-permute-start(bf16[81,16,256]{2,1,0:T(8,128)(2,1)} %get-tuple-element.33), channel_id=1, source_target_pairs={{0,12},{4,0},{8,4},{12,8},{1,13},{5,1},{9,5},{13,9},{2,14},{6,2},{... | collective-permute-start | bytes 1990664 | tf_op jit(solution)/shard_map/ppermute | solution.py:671
  93.8 44.1 %collective-permute-start.6 = (bf16[81,2,16,256]{3,2,1,0:T(8,128)(2,1)}, bf16[81,2,16,256]{3,2,1,0:T(8,128)(2,1)S(1)}, u32[]{:S(2)}, u32[]{:S(2)}) collective-permute-start(bf16[81,2,16,256]{3,2,1,0:T(8,128)(2,1)} %get-tuple-element.44), channel_id=1, source_target_pairs={{0,16},{16,32},{32,48},{48,64},{64,80},{80,96},{96,112},{112,0},{1... | collective-permute-start | bytes 3981320 | tf_op jit(solution)/shard_map/ppermute | solution.py:667
  95.5 42.4 %collective-permute-start.7 = (bf16[81,2,16,256]{3,2,1,0:T(8,128)(2,1)}, bf16[81,2,16,256]{3,2,1,0:T(8,128)(2,1)}, u32[]{:S(2)}, u32[]{:S(2)}) collective-permute-start(bf16[81,2,16,256]{3,2,1,0:T(8,128)(2,1)} %get-tuple-element.45), channel_id=1, source_target_pairs={{0,112},{16,0},{32,16},{48,32},{64,48},{80,64},{96,80},{112,96},{1... | collective-permute-start | bytes 3981320 | tf_op jit(solution)/shard_map/ppermute | solution.py:668
  97.8 6.3 %copy-start.11 = (s32[3,8,4096]{2,1,0:T(8,128)S(1)}, s32[3,8,4096]{2,1,0:T(8,128)}, u32[]{:S(2)}) copy-start(s32[3,8,4096]{2,1,0:T(8,128)} %samples.1) | copy-start | bytes 1179652
  97.8 6.4 %copy-start.12 = (f32[8,4096]{1,0:T(8,128)S(1)}, f32[8,4096]{1,0:T(8,128)}, u32[]{:S(2)}) copy-start(f32[8,4096]{1,0:T(8,128)} %weights.1) | copy-start | bytes 393220
  97.9 6.4 %copy-start.13 = (bf16[256,256]{1,0:T(8,128)(2,1)S(1)}, bf16[256,256]{1,0:T(8,128)(2,1)}, u32[]{:S(2)}) copy-start(bf16[256,256]{1,0:T(8,128)(2,1)} %constant.42.clone.refs_1_.eye.refs_3_.refs_5_) | copy-start | bytes 393220
  97.9 6.4 %copy-start.15 = (bf16[16,128]{1,0:T(8,128)(2,1)S(1)}, bf16[16,128]{1,0:T(8,128)(2,1)}, u32[]{:S(2)}) copy-start(bf16[16,128]{1,0:T(8,128)(2,1)} %constant.43.clone.join) | copy-start | bytes 12292
  104.2 11.2 %copy-start.10 = (bf16[16,32]{1,0:T(8,128)(2,1)S(1)}, bf16[16,32]{1,0:T(8,128)(2,1)}, u32[]{:S(2)}) copy-start(bf16[16,32]{1,0:T(8,128)(2,1)} %constant.44.clone.pick) | copy-start | bytes 3076
  115.4 5.6 %copy-start.1 = (bf16[81,16,256]{2,1,0:T(8,128)(2,1)}, bf16[81,16,256]{2,1,0:T(8,128)(2,1)S(1)}, u32[]{:S(2)}) copy-start(bf16[81,16,256]{2,1,0:T(8,128)(2,1)S(1)} %collective-permute-done.refs_1_.ylo) | copy-start | bytes 1990660
  117.4 16.9 %collective-permute-start.8 = (bf16[81,8,256]{2,1,0:T(8,128)(2,1)}, bf16[81,8,256]{2,1,0:T(8,128)(2,1)S(1)}, u32[]{:S(2)}, u32[]{:S(2)}) collective-permute-start(bf16[81,8,256]{2,1,0:T(8,128)(2,1)} %get-tuple-element.46), channel_id=1, source_target_pairs={{0,16},{16,32},{32,48},{48,64},{64,80},{80,96},{96,112},{112,0},{1... | collective-permute-start | bytes 995336 | tf_op jit(solution)/shard_map/ppermute | solution.py:684
  117.4 16.5 %copy-start.3 = (bf16[320,640]{1,0:T(8,128)(2,1)S(1)}, bf16[320,640]{1,0:T(8,128)(2,1)}, u32[]{:S(2)}) copy-start(bf16[320,640]{1,0:T(8,128)(2,1)} %constant.45.clone.pick) | copy-start | bytes 1228804
  117.4 20.5 %collective-permute-start.9 = (bf16[81,8,256]{2,1,0:T(8,128)(2,1)}, bf16[81,8,256]{2,1,0:T(8,128)(2,1)S(1)}, u32[]{:S(2)}, u32[]{:S(2)}) collective-permute-start(bf16[81,8,256]{2,1,0:T(8,128)(2,1)} %get-tuple-element.47), channel_id=1, source_target_pairs={{0,112},{16,0},{32,16},{48,32},{64,48},{80,64},{96,80},{112,96},{1... | collective-permute-start | bytes 995336 | tf_op jit(solution)/shard_map/ppermute | solution.py:685
  125.0 5.1 %collective-permute-start.2 = (bf16[320,128]{1,0:T(8,128)(2,1)}, bf16[320,128]{1,0:T(8,128)(2,1)S(1)}, u32[]{:S(2)}, u32[]{:S(2)}) collective-permute-start(bf16[320,128]{1,0:T(8,128)(2,1)} %get-tuple-element.39), channel_id=1, source_target_pairs={{0,1},{1,2},{2,3},{3,0},{4,5},{5,6},{6,7},{7,4},{8,9},{9,10},{10,1... | collective-permute-start | bytes 245768 | tf_op jit(solution)/shard_map/ppermute | solution.py:690
  130.1 13.6 %copy-start.7 = (bf16[320,128]{1,0:T(8,128)(2,1)}, bf16[320,128]{1,0:T(8,128)(2,1)S(1)}, u32[]{:S(2)}) copy-start(bf16[320,128]{1,0:T(8,128)(2,1)S(1)} %collective-permute-done.2.zlo.refs_0_) | copy-start | bytes 245764
  130.1 3.8 %collective-permute-start.3 = (bf16[320,128]{1,0:T(8,128)(2,1)}, bf16[320,128]{1,0:T(8,128)(2,1)S(1)}, u32[]{:S(2)}, u32[]{:S(2)}) collective-permute-start(bf16[320,128]{1,0:T(8,128)(2,1)} %get-tuple-element.40), channel_id=1, source_target_pairs={{0,3},{1,0},{2,1},{3,2},{4,7},{5,4},{6,5},{7,6},{8,11},{9,8},{10,9... | collective-permute-start | bytes 245768 | tf_op jit(solution)/shard_map/ppermute | solution.py:689
  133.9 9.8 %copy-start.8 = (bf16[320,128]{1,0:T(8,128)(2,1)}, bf16[320,128]{1,0:T(8,128)(2,1)S(1)}, u32[]{:S(2)}) copy-start(bf16[320,128]{1,0:T(8,128)(2,1)S(1)} %collective-permute-done.3.zhi.refs_1_) | copy-start | bytes 245764
  134.2 9.5 %collective-permute-start.4 = (bf16[160,128]{1,0:T(8,128)(2,1)S(1)}, bf16[160,128]{1,0:T(8,128)(2,1)S(1)}, u32[]{:S(2)}, u32[]{:S(2)}) collective-permute-start(bf16[160,128]{1,0:T(8,128)(2,1)S(1)} %get-tuple-element.41), channel_id=1, source_target_pairs={{0,16},{16,32},{32,48},{48,64},{64,80},{80,96},{96,112},{112,0},{1... | collective-permute-start | bytes 122888 | tf_op jit(solution)/shard_map/ppermute | solution.py:692
  134.3 9.5 %collective-permute-start.5 = (bf16[160,128]{1,0:T(8,128)(2,1)S(1)}, bf16[160,128]{1,0:T(8,128)(2,1)S(1)}, u32[]{:S(2)}, u32[]{:S(2)}) collective-permute-start(bf16[160,128]{1,0:T(8,128)(2,1)S(1)} %get-tuple-element.42), channel_id=1, source_target_pairs={{0,112},{16,0},{32,16},{48,32},{64,48},{80,64},{96,80},{112,96},{1... | collective-permute-start | bytes 122888 | tf_op jit(solution)/shard_map/ppermute | solution.py:693
  144.4 54.7 %copy-start = (bf16[81,4096]{1,0:T(8,128)(2,1)S(1)}, bf16[81,4096]{1,0:T(8,128)(2,1)}, u32[]{:S(2)}) copy-start(bf16[81,4096]{1,0:T(8,128)(2,1)} %transfer.1) | copy-start | bytes 1990660
  144.4 54.7 %copy-start.4 = (bf16[1024,81]{1,0:T(8,128)(2,1)S(1)}, bf16[1024,81]{1,0:T(8,128)(2,1)}, u32[]{:S(2)}) copy-start(bf16[1024,81]{1,0:T(8,128)(2,1)} %constant.48.clone.basis) | copy-start | bytes 497668
  144.4 54.7 %copy-start.5 = (bf16[1024,128]{1,0:T(8,128)(2,1)S(1)}, bf16[1024,128]{1,0:T(8,128)(2,1)}, u32[]{:S(2)}) copy-start(bf16[1024,128]{1,0:T(8,128)(2,1)} %constant.49.clone.wide) | copy-start | bytes 786436
  144.4 54.7 %copy-start.6 = (bf16[81,1024]{1,0:T(8,128)(2,1)S(1)}, bf16[81,1024]{1,0:T(8,128)(2,1)}, u32[]{:S(2)}) copy-start(bf16[81,1024]{1,0:T(8,128)(2,1)} %constant.50.clone.projector) | copy-start | bytes 497668
  (9 other events, 15.1 us)

commit v6 on v5

--- a/solution.py
+++ b/solution.py
@@ -86,38 +86,15 @@
     return pltpu.VMEM((cells_z // LANES, cells_y * coeffs + 16, LANES), jnp.float32)
 
 
-def cut_x(field):
-    coeffs, cells_x, cells_y, cells_z = field.shape
-
-    def kernel(field, last, first, sems):
-        copies = [
-            pltpu.make_async_copy(field.at[:, pl.ds(cells_x - HALO, HALO)], last, sems.at[0]),
-            pltpu.make_async_copy(field.at[:, pl.ds(0, HALO)], first, sems.at[1]),
-        ]
-        for copy in copies:
-            copy.start()
-        for copy in copies:
-            copy.wait()
-
-    hbm = pl.BlockSpec(memory_space=pl.ANY)
-    return pl.pallas_call(
-        kernel,
-        out_shape=[pltpu.HBM((coeffs, HALO, cells_y, cells_z), jnp.bfloat16)] * 2,
-        in_specs=[hbm],
-        out_specs=[hbm, hbm],
-        scratch_shapes=[pltpu.SemaphoreType.DMA((2,))],
-        compiler_params=pltpu.CompilerParams(vmem_limit_bytes=4 * MIB),
-        name="cut_x",
-    )(field)
-
-
-def cut_y(field):
+def cut_faces(field):
     coeffs, cells_x, cells_y, cells_z = field.shape
     per_step = 9
     rows = cells_x * HALO
 
-    def kernel(field, pick, top, bottom):
+    def kernel(field, pick, last, first, top, bottom):
         for c in range(per_step):
+            last[c] = field[c, cells_x - HALO :]
+            first[c] = field[c, :HALO]
             chosen = jnp.dot(
                 pick[...],
                 field[c].reshape(cells_x * cells_y, cells_z),
@@ -131,18 +108,21 @@
         for j in range(HALO):
             pick[x * HALO + j, x * cells_y + cells_y - HALO + j] = 1.0
             pick[rows + x * HALO + j, x * cells_y + j] = 1.0
-    face = pl.BlockSpec((per_step, rows, cells_z), lambda i: (i, 0, 0))
+    shapes = [(coeffs, HALO, cells_y, cells_z)] * 2
+    shapes += [(coeffs, rows, cells_z)] * 2
+
+    def whole(shape):
+        zeros = (0,) * (len(shape) - 1)
+        return pl.BlockSpec((per_step,) + shape[1:], lambda i: (i,) + zeros)
+
     return pl.pallas_call(
         kernel,
-        out_shape=[pltpu.HBM((coeffs, rows, cells_z), jnp.bfloat16)] * 2,
+        out_shape=[pltpu.HBM(shape, jnp.bfloat16) for shape in shapes],
         grid=(coeffs // per_step,),
-        in_specs=[
-            pl.BlockSpec((per_step, cells_x, cells_y, cells_z), lambda i: (i, 0, 0, 0)),
-            pl.BlockSpec(pick.shape, lambda i: (0, 0)),
-        ],
-        out_specs=[face, face],
-        compiler_params=pltpu.CompilerParams(vmem_limit_bytes=16 * MIB),
-        name="cut_y",
+        in_specs=[whole(field.shape), pl.BlockSpec(pick.shape, lambda i: (0, 0))],
+        out_specs=[whole(shape) for shape in shapes],
+        compiler_params=pltpu.CompilerParams(vmem_limit_bytes=24 * MIB),
+        name="cut_faces",
     )(field, jnp.asarray(pick.astype(jnp.bfloat16)))
 
 
@@ -447,20 +427,59 @@
     )
 
 
+def spread_weights(ordered):
+    count = ordered.shape[0]
+    block = 512
+
+    def kernel(ordered, ones, wide):
+        rows = ordered[...].astype(jnp.bfloat16)
+        for h in range(0, SAMPLES, 2):
+            both = jnp.dot(
+                rows, ones[:, h * LANES : (h + 2) * LANES], preferred_element_type=jnp.float32
+            )
+            for s in range(2):
+                for g in range(block // GROUP):
+                    to = (g * SAMPLES + h + s) * GROUP
+                    wide[to : to + GROUP, :] = both[
+                        g * GROUP : (g + 1) * GROUP, s * LANES : (s + 1) * LANES
+                    ]
+
+    ones = np.zeros((LANES, SAMPLES * LANES), np.float32)
+    for s in range(SAMPLES):
+        for p in range(PARTS):
+            ones[(2 + p) * SAMPLES + s, s * LANES : (s + 1) * LANES] = 1.0
+    return pl.pallas_call(
+        kernel,
+        out_shape=pltpu.HBM((count * SAMPLES, LANES), jnp.float32),
+        grid=(count // block,),
+        in_specs=[
+            pl.BlockSpec((block, LANES), lambda i: (i, 0)),
+            pl.BlockSpec(ones.shape, lambda i: (0, 0)),
+        ],
+        out_specs=pl.BlockSpec((block * SAMPLES, LANES), lambda i: (i, 0)),
+        compiler_params=pltpu.CompilerParams(vmem_limit_bytes=12 * MIB),
+        cost_estimate=pl.CostEstimate(
+            flops=10**10, transcendentals=0, bytes_accessed=3 * 10**6
+        ),
+        name="spread_weights",
+    )(ordered, jnp.asarray(ones.astype(jnp.bfloat16)))
+
+
 RING = 2
+STREAM = 8
 CHUNK = 1024
 
 
-def gather_rows(index, ordered, table, edges, first_edge, coeffs):
-    count = ordered.shape[0]
+def gather_rows(index, wide, table, edges, first_edge, coeffs):
+    count = wide.shape[0] // SAMPLES
     chunks = index.shape[0] // CHUNK
     per_chunk = CHUNK // SAMPLES
     groups = per_chunk // GROUP
     pairs = count // 32
     half = LANES // 2
 
-    def kernel(index, ordered, ones, pick, *refs):
-        table, out, local, sems, near, rows = refs[len(edges) + 1 :]
+    def kernel(index, wide, pick, *refs):
+        table, out, local, sems, near, near_sems, rows = refs[len(edges) + 1 :]
         at = first_edge
         for edge in refs[: len(edges)]:
             table[pl.ds(at, edge.shape[0]), :] = edge[...].astype(jnp.float32)
@@ -476,35 +495,34 @@
                 sems.at[slot],
             )
 
-        def spread(n, slot):
-            at = pl.multiple_of(n * per_chunk, per_chunk)
-            parts = ordered[pl.ds(at, per_chunk), :].astype(jnp.bfloat16)
-            for h in range(0, SAMPLES, 2):
-                both = jnp.dot(
-                    parts, ones[:, h * LANES : (h + 2) * LANES], preferred_element_type=jnp.float32
-                )
-                for s in range(2):
-                    for q in range(groups):
-                        to = (q * SAMPLES + h + s) * GROUP
-                        near[slot, to : to + GROUP, :] = both[
-                            q * GROUP : (q + 1) * GROUP, s * LANES : (s + 1) * LANES
-                        ]
+        def stream(n, slot):
+            return pltpu.make_async_copy(
+                wide.at[pl.ds(pl.multiple_of(n * CHUNK, CHUNK), CHUNK), :],
+                near.at[slot],
+                near_sems.at[slot],
+            )
 
         for b in range(RING - 1):
             fetch(b, b).start()
-        spread(0, 0)
+        for b in range(STREAM - 1):
+            stream(b, b).start()
 
         def body(i, _):
             for b in range(RING):
                 n = i * RING + b
+                slot = n % STREAM
                 fetch(n, b).wait()
+                stream(n, slot).wait()
                 ahead = n + RING - 1
+                later = n + STREAM - 1
 
                 @pl.when(ahead < chunks)
                 def _():
                     fetch(ahead, (b + RING - 1) % RING).start()
 
-                spread(jnp.minimum(n + 1, chunks - 1), 1 - b)
+                @pl.when(later < chunks)
+                def _():
+                    stream(later, later % STREAM).start()
 
                 for q in range(groups):
                     total = None
@@ -515,7 +533,7 @@
                             row = table[pl.ds(local[b, place], GROUP, stride=0), :]
                             merged = row if merged is None else jnp.where(masks[k], row, merged)
                         at = (q * SAMPLES + s) * GROUP
-                        term = merged * near[b, at : at + GROUP, :]
+                        term = merged * near[slot, at : at + GROUP, :]
                         total = term if total is None else total + term
                     to = pl.multiple_of((n * (groups // 4) + q // 4) * GROUP, GROUP)
                     rows[q % 4, pl.ds(to, GROUP), :] = jnp.where(used, total, 0.0)
@@ -542,10 +560,6 @@
 
         lax.fori_loop(0, pairs * GROUP // 128, pack, 0)
 
-    ones = np.zeros((LANES, SAMPLES * LANES), np.float32)
-    for s in range(SAMPLES):
-        for p in range(PARTS):
-            ones[(2 + p) * SAMPLES + s, s * LANES : (s + 1) * LANES] = 1.0
     pick = np.zeros((3, 2 * LANES, LANES), np.float32)
     for c in range(half):
         pick[0, c, c] = 1.0
@@ -562,28 +576,22 @@
             pltpu.VMEM(table.shape, jnp.float32),
             jax.ShapeDtypeStruct((pairs, 24, LANES), jnp.bfloat16),
         ),
-        in_specs=[vmem] * (5 + len(edges)),
+        in_specs=[vmem, pl.BlockSpec(memory_space=pl.ANY)] + [vmem] * (2 + len(edges)),
         out_specs=(vmem, vmem),
         scratch_shapes=[
             pltpu.SMEM((RING, CHUNK), jnp.int32),
             pltpu.SemaphoreType.DMA((RING,)),
-            pltpu.VMEM((RING, CHUNK, LANES), jnp.float32),
+            pltpu.VMEM((STREAM, CHUNK, LANES), jnp.float32),
+            pltpu.SemaphoreType.DMA((STREAM,)),
             pltpu.VMEM((4, pairs * GROUP, LANES), jnp.float32),
         ],
-        input_output_aliases={4 + len(edges): 0},
+        input_output_aliases={3 + len(edges): 0},
         compiler_params=pltpu.CompilerParams(vmem_limit_bytes=24 * MIB),
         cost_estimate=pl.CostEstimate(
             flops=4 * 10**10, transcendentals=0, bytes_accessed=2 * 10**7
         ),
         name="gather_rows",
-    )(
-        index,
-        ordered,
-        jnp.asarray(ones.astype(jnp.bfloat16)),
-        jnp.asarray(pick.astype(jnp.bfloat16)),
-        *edges,
-        table,
-    )[1]
+    )(index, wide, jnp.asarray(pick.astype(jnp.bfloat16)), *edges, table)[1]
 
 
 def relight(transfer, routed, basis, projector):
@@ -663,12 +671,11 @@
     slot = destination[0] * per_pair + destination[1]
 
     field = pltpu.with_memory_space_constraint(field, pltpu.HBM)
-    last, first = cut_x(field)
+    last, first, top, bottom = cut_faces(field)
+    ylo = lax.ppermute(top, "gy", ups[1])
+    yhi = lax.ppermute(bottom, "gy", downs[1])
     xlo = lax.ppermute(last, "gx", ups[0])
     xhi = lax.ppermute(first, "gx", downs[0])
-    top, bottom = cut_y(field)
-    ylo = lax.ppermute(top, "gy", ups[1])
-    yhi = lax.ppermute(bottom, "gy", downs[1])
     field, slot, origin = lax.optimization_barrier((field, slot, origin))
 
     eye = jnp.asarray(np.eye(cells_z, dtype=np.float32).astype(jnp.bfloat16))
@@ -689,12 +696,15 @@
     zhi = lax.ppermute(bottoms, "gz", downs[2])
     zlo = lax.ppermute(tops, "gz", ups[2])
     up, down = cut_ends(zlo, zhi, early, cells_x, cells_y)
+    up, down, ordered = lax.optimization_barrier((up, down, ordered))
     elo = lax.ppermute(up, "gx", ups[0])
     ehi = lax.ppermute(down, "gx", downs[0])
+    wide = spread_weights(ordered)
+    table, wide = lax.optimization_barrier((table, wide))
     sides = [(xlo, 0), (xlo, 1), (xhi, 0), (xhi, 1)]
     table = add_planes(table, sides, (clo, chi), eye, cells_x + 2, total_rows, 0)[0]
     outgoing = gather_rows(
-        index.reshape(-1), ordered, table, (zlo, zhi, elo, ehi), rows, coeffs
+        index.reshape(-1), wide, table, (zlo, zhi, elo, ehi), rows, coeffs
     )
     routed = lax.all_to_all(
         outgoing, ("gx", "gy", "gz"), split_axis=0, concat_axis=0, tiled=True

time: 207 us -> 131 us (0.63)
  Pallas kernels: 151 us -> 74.6 us
  starting transfers between devices: 18.1 us -> 14.4 us
  waiting for transfers between devices: 6.13 us -> 9.56 us
    pallas_call x2, Pallas kernels: 89 us -> 15.4 us  [the longest x1 7.76 us: spread_weights(): pl.pallas_call(kernel, out_shape=pltpu.HBM((count * SAMPLES, LANES), jnp....]
    ppermute x1, waiting for transfers between devices: 0.01 us -> 9.53 us  [halo_step(): clo = lax.ppermute(up, 'gx', ups[0])]
    ppermute x1, waiting for transfers between devices: 3.77 us -> 0.01 us  [halo_step(): zlo = lax.ppermute(tops, 'gz', ups[2])]
    ppermute x1, starting transfers between devices: 3.55 us -> 0.01 us  [halo_step(): ehi = lax.ppermute(down, 'gx', downs[0])]
    pallas_call x1, Pallas kernels: 28.4 us -> 25.5 us  [gather_rows(): pl.pallas_call(kernel, out_shape=(pltpu.VMEM(table.shape, jnp.float32), j...]
    ppermute x1, waiting for transfers between devices: 2.34 us -> 0.01 us  [halo_step(): zhi = lax.ppermute(bottoms, 'gz', downs[2])]
    unnamed x46 -> x50, local copies, waits for them, and re-layouts: 4.56 us -> 6.5 us
  transfers between devices with their start and end apart: 10 -> 10, of which waited for: 2 -> 1; matrix products, arithmetic and copies ran while one was open for 0% -> 0% of each run, Pallas kernels for 52% -> 26%
where the time goes in v6:
time: 131 us
  Pallas kernels  74.6 us (57%)
  blocking collectives  25.1 us (19%)
  starting transfers between devices  14.4 us (11%)
  waiting for transfers between devices  9.56 us (7%)
  local copies, waits for them, and re-layouts  6.5 us (5%)
    pallas_call x1, Pallas kernels, gather_rows(): pl.pallas_call(kernel, out_shape=(pltpu.VMEM(table.shape, jnp.float32), j...  25.5 us
    all_to_all x1, blocking collectives, halo_step(): lax.all_to_all(outgoing, ('gx', 'gy', 'gz'), split_axis=0, concat_axis=0,...  25.1 us
    pallas_call x3, Pallas kernels, add_planes(): pl.pallas_call(kernel, out_shape=shapes, in_specs=[vmem] * len(held) + [h...  15.1 us
    ppermute x1, waiting for transfers between devices, halo_step(): clo = lax.ppermute(up, 'gx', ups[0])  9.53 us
    pallas_call x1, Pallas kernels, prepare(): pl.pallas_call(kernel, out_shape=(jax.ShapeDtypeStruct((count * SAMPLES /...  9.1 us
    pallas_call x1, Pallas kernels, spread_weights(): pl.pallas_call(kernel, out_shape=pltpu.HBM((count * SAMPLES, LANES), jnp....  7.76 us
    pallas_call x1, Pallas kernels, cut_faces(): pl.pallas_call(kernel, out_shape=[pltpu.HBM(shape, jnp.bfloat16) for shap...  7.62 us
    pallas_call x1, Pallas kernels, relight(): pl.pallas_call(kernel, out_shape=jax.ShapeDtypeStruct((coeffs, count), jn...  7.53 us
  transfers between devices with their start and end apart: 10, of which 1 were waited for; matrix products, arithmetic and copies ran while one was open for 0% of the time, Pallas kernels for 26%

profile of v6, /device:TPU:1, one launch (start us, length us, event | category | flops | bytes accessed | tf_op | source)
XLA Modules:
  0.0 130.6 jit_solution(1614439296476573389)
XLA Ops:
  0.0 0.7 copy-done.11
  0.7 7.6 %cut_faces.1 = (bf16[81,2,16,256]{3,2,1,0:T(8,128)(2,1)}, bf16[81,2,16,256]{3,2,1,0:T(8,128)(2,1)}, bf16[81,16,256]{2,1,0:T(8,128)(2,1)}, bf16[81,16,256]{2,1,0:T(8,128)(2,1)}) custom-call(bf16[81,8,16,256]{3,2,1,0:T(8,128)(2,1)} %field.1, bf16[32,128]{1,0:T(8,128)(2,1)S(1)} %copy-done.11), custom_call_target="tpu_custom_call" | custom-call | tf_op jit(solution)/shard_map/cut_faces/pallas_call | solution.py:118
  8.3 4.1 %collective-permute-start = (bf16[81,16,256]{2,1,0:T(8,128)(2,1)}, bf16[81,16,256]{2,1,0:T(8,128)(2,1)S(1)}, u32[]{:S(2)}, u32[]{:S(2)}) collective-permute-start(bf16[81,16,256]{2,1,0:T(8,128)(2,1)} %get-tuple-element.37), channel_id=1, source_target_pairs={{0,4},{4,8},{8,12},{12,0},{1,5},{5,9},{9,13},{13,1},{2,6},{6,10},{... | collective-permute-start | bytes 1990664 | tf_op jit(solution)/shard_map/ppermute | solution.py:675
  12.4 1.6 %collective-permute-start.6 = (bf16[81,2,16,256]{3,2,1,0:T(8,128)(2,1)}, bf16[81,2,16,256]{3,2,1,0:T(8,128)(2,1)S(1)}, u32[]{:S(2)}, u32[]{:S(2)}) collective-permute-start(bf16[81,2,16,256]{3,2,1,0:T(8,128)(2,1)} %get-tuple-element.54), channel_id=1, source_target_pairs={{0,16},{16,32},{32,48},{48,64},{64,80},{80,96},{96,112},{112,0},{1... | collective-permute-start | bytes 3981320 | tf_op jit(solution)/shard_map/ppermute | solution.py:677
  14.1 2.2 %collective-permute-start.7 = (bf16[81,2,16,256]{3,2,1,0:T(8,128)(2,1)}, bf16[81,2,16,256]{3,2,1,0:T(8,128)(2,1)}, u32[]{:S(2)}, u32[]{:S(2)}) collective-permute-start(bf16[81,2,16,256]{3,2,1,0:T(8,128)(2,1)} %get-tuple-element.55), channel_id=1, source_target_pairs={{0,112},{16,0},{32,16},{48,32},{64,48},{80,64},{96,80},{112,96},{1... | collective-permute-start | bytes 3981320 | tf_op jit(solution)/shard_map/ppermute | solution.py:678
  16.4 6.3 %shard_map.154.refs_0_ = f32[62400,128]{1,0:T(8,128)S(1)} custom-call(bf16[81,8,16,256]{3,2,1,0:T(8,128)(2,1)} %field.1, bf16[256,256]{1,0:T(8,128)(2,1)} %constant.42.clone.refs_1_.eye.refs_3_.refs_5_), custom_call_target="tpu_custom_call" | custom-call | flops 20000000000 | bytes 20000000 | tf_op jit(solution)/shard_map/pallas_call | solution.py:257
  22.7 9.1 %prepare.1 = (s32[256,128]{1,0:T(8,128)S(1)}, f32[4096,128]{1,0:T(8,128)S(1)}) custom-call(s32[3]{0:T(128)S(1)} %pad_add_fusion.origin, s32[4096]{0:T(1024)S(1)} %bitcast.5, s32[3,8,4096]{2,1,0:T(8,128)S(1)} %copy-done.13, f32[8,4096]{1,0:T(8,128)S(1)} %copy-done.14, bf16[256,256]{1,0:T(8,128)(2,1)S(1)} %copy-done.16, bf16[16,128]{1,0:T(8,128)(2,1)S(1)} %copy-done.18), custom_call_target="tpu_custom_call" | custom-call | flops 20000000000 | bytes 3000000 | tf_op jit(solution)/shard_map/prepare/pallas_call | solution.py:406
  31.8 0.7 copy-done.17
  32.5 0.8 copy-done.1
  33.6 4.1 %shard_map.155 = (f32[62400,128]{1,0:T(8,128)S(1)}, bf16[320,128]{1,0:T(8,128)(2,1)}, bf16[320,128]{1,0:T(8,128)(2,1)}) custom-call(f32[62400,128]{1,0:T(8,128)S(1)} %shard_map.154.refs_0_, bf16[81,16,256]{2,1,0:T(8,128)(2,1)} %copy-done.1, bf16[81,16,256]{2,1,0:T(8,128)(2,1)} %copy-done.3, ...), custom_call_target="tpu_custom_call", output_to_operand_aliasing={{0}: (0, {})} | custom-call | flops 20000000000 | bytes 20000000 | tf_op jit(solution)/shard_map/pallas_call | solution.py:257
  37.7 1.4 %collective-permute-start.2 = (bf16[320,128]{1,0:T(8,128)(2,1)}, bf16[320,128]{1,0:T(8,128)(2,1)S(1)}, u32[]{:S(2)}, u32[]{:S(2)}) collective-permute-start(bf16[320,128]{1,0:T(8,128)(2,1)} %get-tuple-element.44), channel_id=1, source_target_pairs={{0,1},{1,2},{2,3},{3,0},{4,5},{5,6},{6,7},{7,4},{8,9},{9,10},{10,1... | collective-permute-start | bytes 245768 | tf_op jit(solution)/shard_map/ppermute | solution.py:697
  39.0 1.5 %collective-permute-start.3 = (bf16[320,128]{1,0:T(8,128)(2,1)}, bf16[320,128]{1,0:T(8,128)(2,1)S(1)}, u32[]{:S(2)}, u32[]{:S(2)}) collective-permute-start(bf16[320,128]{1,0:T(8,128)(2,1)} %get-tuple-element.45), channel_id=1, source_target_pairs={{0,3},{1,0},{2,1},{3,2},{4,7},{5,4},{6,5},{7,6},{8,11},{9,8},{10,9... | collective-permute-start | bytes 245768 | tf_op jit(solution)/shard_map/ppermute | solution.py:696
  40.5 1.1 copy-done.2
  41.6 1.1 copy-done.4
  42.7 1.8 %cut_corners.1 = (bf16[81,8,256]{2,1,0:T(8,128)(2,1)}, bf16[81,8,256]{2,1,0:T(8,128)(2,1)}) custom-call(bf16[81,16,256]{2,1,0:T(8,128)(2,1)S(1)} %copy-done.2, bf16[81,16,256]{2,1,0:T(8,128)(2,1)S(1)} %copy-done.4, bf16[16,32]{1,0:T(8,128)(2,1)S(1)} %copy-done.12), custom_call_target="tpu_custom_call" | custom-call | tf_op jit(solution)/shard_map/cut_corners/pallas_call | solution.py:152
  44.5 3.6 %collective-permute-start.9 = (bf16[81,8,256]{2,1,0:T(8,128)(2,1)}, bf16[81,8,256]{2,1,0:T(8,128)(2,1)S(1)}, u32[]{:S(2)}, u32[]{:S(2)}) collective-permute-start(bf16[81,8,256]{2,1,0:T(8,128)(2,1)} %get-tuple-element.57), channel_id=1, source_target_pairs={{0,112},{16,0},{32,16},{48,32},{64,48},{80,64},{96,80},{112,96},{1... | collective-permute-start | bytes 995336 | tf_op jit(solution)/shard_map/ppermute | solution.py:692
  48.4 7.8 %spread_weights.1.wide = f32[32768,128]{1,0:T(8,128)} custom-call(f32[4096,128]{1,0:T(8,128)S(1)} %get-tuple-element.49.ordered, bf16[128,1024]{1,0:T(8,128)(2,1)S(1)} %copy-done.15), custom_call_target="tpu_custom_call" | custom-call | flops 10000000000 | bytes 3000000 | tf_op jit(solution)/shard_map/spread_weights/pallas_call | solution.py:451
  56.2 9.5 %collective-permute-done.8.refs_3_ = bf16[81,8,256]{2,1,0:T(8,128)(2,1)S(1)} collective-permute-done((bf16[81,8,256]{2,1,0:T(8,128)(2,1)}, bf16[81,8,256]{2,1,0:T(8,128)(2,1)S(1)}, u32[]{:S(2)}, u32[]{:S(2)}) %collective-permute-start.8) | collective-permute-done | bytes 331808 | tf_op jit(solution)/shard_map/ppermute | solution.py:691
  65.8 0.7 copy-done.21
  67.0 4.7 %shard_map.156.refs_4_ = f32[62400,128]{1,0:T(8,128)S(1)} custom-call(f32[62400,128]{1,0:T(8,128)S(1)} %get-tuple-element.53.refs_0_, bf16[81,2,16,256]{3,2,1,0:T(8,128)(2,1)} %copy-done.20, bf16[81,2,16,256]{3,2,1,0:T(8,128)(2,1)} %collective-permute-done.7.refs_2_, bf16[81,8,256]{2,1,0:T(8,128)(2,1)} %copy-done.21, ...), custom_call_target="tpu_custom_call", output_to_operand_aliasing={{}: (0, {})} | custom-call | flops 20000000000 | bytes 20000000 | tf_op jit(solution)/shard_map/pallas_call | solution.py:257
  71.7 0.6 copy-done.23
  72.4 25.5 %gather_rows.1 = (f32[62400,128]{1,0:T(8,128)S(1)}, bf16[128,24,128]{2,1,0:T(8,128)(2,1)}) custom-call(s32[32768]{0:T(1024)} %bitcast.6, f32[32768,128]{1,0:T(8,128)} %spread_weights.1.wide, bf16[3,256,128]{2,1,0:T(8,128)(2,1)} %constant.47.clone.pick, bf16[320,128]{1,0:T(8,128)(2,1)} %copy-done.9, ...), custom_call_target="tpu_custom_call", output_to_operand_aliasing={{0}: (7, {})} | custom-call | flops 40000000000 | bytes 20000000 | tf_op jit(solution)/shard_map/gather_rows/pallas_call | solution.py:573
  97.9 25.1 %all_to_all.5.routed = bf16[128,24,128]{2,1,0:T(8,128)(2,1)S(1)} all-to-all(bf16[128,24,128]{2,1,0:T(8,128)(2,1)} %get-tuple-element.58), channel_id=1, replica_groups=mesh['gx'=8,'gy'=4,'gz'=4] {'gx','gy','gz'}, dimensions={0} | all-to-all | bytes 1572864 | tf_op jit(solution)/shard_map/all_to_all | solution.py:709
  123.0 7.5 %relight.1 = bf16[81,4096]{1,0:T(8,128)(2,1)} custom-call(bf16[81,4096]{1,0:T(8,128)(2,1)S(1)} %copy-done, bf16[128,24,128]{2,1,0:T(8,128)(2,1)S(1)} %all_to_all.5.routed, bf16[1024,81]{1,0:T(8,128)(2,1)S(1)} %copy-done.7, bf16[1024,128]{1,0:T(8,128)(2,1)S(1)} %copy-done.6, bf16[81,1024]{1,0:T(8,128)(2,1)S(1)} %copy-done.8), custom_call_target="tpu_custom_call" | custom-call | tf_op jit(solution)/shard_map/relight/pallas_call | solution.py:630
  (59 shorter events, 1.3 us)
Async XLA Ops:
  0.7 15.5 %copy-start.19 = (s32[2,4096]{1,0:T(2,128)S(1)}, s32[2,4096]{1,0:T(2,128)}, u32[]{:S(2)}) copy-start(s32[2,4096]{1,0:T(2,128)} %param.19) | copy-start | bytes 98308
  8.3 24.2 %collective-permute-start = (bf16[81,16,256]{2,1,0:T(8,128)(2,1)}, bf16[81,16,256]{2,1,0:T(8,128)(2,1)S(1)}, u32[]{:S(2)}, u32[]{:S(2)}) collective-permute-start(bf16[81,16,256]{2,1,0:T(8,128)(2,1)} %get-tuple-element.37), channel_id=1, source_target_pairs={{0,4},{4,8},{8,12},{12,0},{1,5},{5,9},{9,13},{13,1},{2,6},{6,10},{... | collective-permute-start | bytes 1990664 | tf_op jit(solution)/shard_map/ppermute | solution.py:675
  12.4 20.1 %collective-permute-start.1 = (bf16[81,16,256]{2,1,0:T(8,128)(2,1)}, bf16[81,16,256]{2,1,0:T(8,128)(2,1)S(1)}, u32[]{:S(2)}, u32[]{:S(2)}) collective-permute-start(bf16[81,16,256]{2,1,0:T(8,128)(2,1)} %get-tuple-element.38), channel_id=1, source_target_pairs={{0,12},{4,0},{8,4},{12,8},{1,13},{5,1},{9,5},{13,9},{2,14},{6,2},{... | collective-permute-start | bytes 1990664 | tf_op jit(solution)/shard_map/ppermute | solution.py:676
  12.4 53.3 %collective-permute-start.6 = (bf16[81,2,16,256]{3,2,1,0:T(8,128)(2,1)}, bf16[81,2,16,256]{3,2,1,0:T(8,128)(2,1)S(1)}, u32[]{:S(2)}, u32[]{:S(2)}) collective-permute-start(bf16[81,2,16,256]{3,2,1,0:T(8,128)(2,1)} %get-tuple-element.54), channel_id=1, source_target_pairs={{0,16},{16,32},{32,48},{48,64},{64,80},{80,96},{96,112},{112,0},{1... | collective-permute-start | bytes 3981320 | tf_op jit(solution)/shard_map/ppermute | solution.py:677
  14.1 51.7 %collective-permute-start.7 = (bf16[81,2,16,256]{3,2,1,0:T(8,128)(2,1)}, bf16[81,2,16,256]{3,2,1,0:T(8,128)(2,1)}, u32[]{:S(2)}, u32[]{:S(2)}) collective-permute-start(bf16[81,2,16,256]{3,2,1,0:T(8,128)(2,1)} %get-tuple-element.55), channel_id=1, source_target_pairs={{0,112},{16,0},{32,16},{48,32},{64,48},{80,64},{96,80},{112,96},{1... | collective-permute-start | bytes 3981320 | tf_op jit(solution)/shard_map/ppermute | solution.py:678
  16.3 6.3 %copy-start.13 = (s32[3,8,4096]{2,1,0:T(8,128)S(1)}, s32[3,8,4096]{2,1,0:T(8,128)}, u32[]{:S(2)}) copy-start(s32[3,8,4096]{2,1,0:T(8,128)} %samples.1) | copy-start | bytes 1179652
  16.4 6.4 %copy-start.14 = (f32[8,4096]{1,0:T(8,128)S(1)}, f32[8,4096]{1,0:T(8,128)}, u32[]{:S(2)}) copy-start(f32[8,4096]{1,0:T(8,128)} %weights.1) | copy-start | bytes 393220
  16.4 6.4 %copy-start.16 = (bf16[256,256]{1,0:T(8,128)(2,1)S(1)}, bf16[256,256]{1,0:T(8,128)(2,1)}, u32[]{:S(2)}) copy-start(bf16[256,256]{1,0:T(8,128)(2,1)} %constant.42.clone.refs_1_.eye.refs_3_.refs_5_) | copy-start | bytes 393220
  16.4 6.4 %copy-start.18 = (bf16[16,128]{1,0:T(8,128)(2,1)S(1)}, bf16[16,128]{1,0:T(8,128)(2,1)}, u32[]{:S(2)}) copy-start(bf16[16,128]{1,0:T(8,128)(2,1)} %constant.43.clone.join) | copy-start | bytes 12292
  33.6 7.0 %copy-start.12 = (bf16[16,32]{1,0:T(8,128)(2,1)S(1)}, bf16[16,32]{1,0:T(8,128)(2,1)}, u32[]{:S(2)}) copy-start(bf16[16,32]{1,0:T(8,128)(2,1)} %constant.44.clone.pick) | copy-start | bytes 3076
  33.6 14.5 %copy-start.5 = (bf16[320,640]{1,0:T(8,128)(2,1)S(1)}, bf16[320,640]{1,0:T(8,128)(2,1)}, u32[]{:S(2)}) copy-start(bf16[320,640]{1,0:T(8,128)(2,1)} %constant.45.clone.pick) | copy-start | bytes 1228804
  33.6 14.9 %copy-start.15 = (bf16[128,1024]{1,0:T(8,128)(2,1)S(1)}, bf16[128,1024]{1,0:T(8,128)(2,1)}, u32[]{:S(2)}) copy-start(bf16[128,1024]{1,0:T(8,128)(2,1)} %constant.46.clone.ones) | copy-start | bytes 786436
  37.7 6.8 %collective-permute-start.2 = (bf16[320,128]{1,0:T(8,128)(2,1)}, bf16[320,128]{1,0:T(8,128)(2,1)S(1)}, u32[]{:S(2)}, u32[]{:S(2)}) collective-permute-start(bf16[320,128]{1,0:T(8,128)(2,1)} %get-tuple-element.44), channel_id=1, source_target_pairs={{0,1},{1,2},{2,3},{3,0},{4,5},{5,6},{6,7},{7,4},{8,9},{9,10},{10,1... | collective-permute-start | bytes 245768 | tf_op jit(solution)/shard_map/ppermute | solution.py:697
  39.0 9.0 %collective-permute-start.3 = (bf16[320,128]{1,0:T(8,128)(2,1)}, bf16[320,128]{1,0:T(8,128)(2,1)S(1)}, u32[]{:S(2)}, u32[]{:S(2)}) collective-permute-start(bf16[320,128]{1,0:T(8,128)(2,1)} %get-tuple-element.45), channel_id=1, source_target_pairs={{0,3},{1,0},{2,1},{3,2},{4,7},{5,4},{6,5},{7,6},{8,11},{9,8},{10,9... | collective-permute-start | bytes 245768 | tf_op jit(solution)/shard_map/ppermute | solution.py:696
  44.5 21.3 %collective-permute-start.8 = (bf16[81,8,256]{2,1,0:T(8,128)(2,1)}, bf16[81,8,256]{2,1,0:T(8,128)(2,1)S(1)}, u32[]{:S(2)}, u32[]{:S(2)}) collective-permute-start(bf16[81,8,256]{2,1,0:T(8,128)(2,1)} %get-tuple-element.56), channel_id=1, source_target_pairs={{0,16},{16,32},{32,48},{48,64},{64,80},{80,96},{96,112},{112,0},{1... | collective-permute-start | bytes 995336 | tf_op jit(solution)/shard_map/ppermute | solution.py:691
  44.5 11.7 %copy-start.9 = (bf16[320,128]{1,0:T(8,128)(2,1)}, bf16[320,128]{1,0:T(8,128)(2,1)S(1)}, u32[]{:S(2)}) copy-start(bf16[320,128]{1,0:T(8,128)(2,1)S(1)} %collective-permute-done.2.zlo.refs_0_) | copy-start | bytes 245764
  44.5 21.3 %collective-permute-start.9 = (bf16[81,8,256]{2,1,0:T(8,128)(2,1)}, bf16[81,8,256]{2,1,0:T(8,128)(2,1)S(1)}, u32[]{:S(2)}, u32[]{:S(2)}) collective-permute-start(bf16[81,8,256]{2,1,0:T(8,128)(2,1)} %get-tuple-element.57), channel_id=1, source_target_pairs={{0,112},{16,0},{32,16},{48,32},{64,48},{80,64},{96,80},{112,96},{1... | collective-permute-start | bytes 995336 | tf_op jit(solution)/shard_map/ppermute | solution.py:692
  48.1 8.1 %copy-start.10 = (bf16[320,128]{1,0:T(8,128)(2,1)}, bf16[320,128]{1,0:T(8,128)(2,1)S(1)}, u32[]{:S(2)}) copy-start(bf16[320,128]{1,0:T(8,128)(2,1)S(1)} %collective-permute-done.3.zhi.refs_1_) | copy-start | bytes 245764
  48.4 23.4 %collective-permute-start.4 = (bf16[160,128]{1,0:T(8,128)(2,1)S(1)}, bf16[160,128]{1,0:T(8,128)(2,1)S(1)}, u32[]{:S(2)}, u32[]{:S(2)}) collective-permute-start(bf16[160,128]{1,0:T(8,128)(2,1)S(1)} %get-tuple-element.51), channel_id=1, source_target_pairs={{0,16},{16,32},{32,48},{48,64},{64,80},{80,96},{96,112},{112,0},{1... | collective-permute-start | bytes 122888 | tf_op jit(solution)/shard_map/ppermute | solution.py:700
  65.7 6.0 %collective-permute-start.5 = (bf16[160,128]{1,0:T(8,128)(2,1)S(1)}, bf16[160,128]{1,0:T(8,128)(2,1)S(1)}, u32[]{:S(2)}, u32[]{:S(2)}) collective-permute-start(bf16[160,128]{1,0:T(8,128)(2,1)S(1)} %get-tuple-element.52), channel_id=1, source_target_pairs={{0,112},{16,0},{32,16},{48,32},{64,48},{80,64},{96,80},{112,96},{1... | collective-permute-start | bytes 122888 | tf_op jit(solution)/shard_map/ppermute | solution.py:701
  72.3 50.7 %copy-start = (bf16[81,4096]{1,0:T(8,128)(2,1)S(1)}, bf16[81,4096]{1,0:T(8,128)(2,1)}, u32[]{:S(2)}) copy-start(bf16[81,4096]{1,0:T(8,128)(2,1)} %transfer.1) | copy-start | bytes 1990660
  72.4 50.7 %copy-start.6 = (bf16[1024,128]{1,0:T(8,128)(2,1)S(1)}, bf16[1024,128]{1,0:T(8,128)(2,1)}, u32[]{:S(2)}) copy-start(bf16[1024,128]{1,0:T(8,128)(2,1)} %constant.49.clone.wide) | copy-start | bytes 786436
  72.4 50.7 %copy-start.7 = (bf16[1024,81]{1,0:T(8,128)(2,1)S(1)}, bf16[1024,81]{1,0:T(8,128)(2,1)}, u32[]{:S(2)}) copy-start(bf16[1024,81]{1,0:T(8,128)(2,1)} %constant.48.clone.basis) | copy-start | bytes 497668
  72.4 50.7 %copy-start.8 = (bf16[81,1024]{1,0:T(8,128)(2,1)S(1)}, bf16[81,1024]{1,0:T(8,128)(2,1)}, u32[]{:S(2)}) copy-start(bf16[81,1024]{1,0:T(8,128)(2,1)} %constant.50.clone.projector) | copy-start | bytes 497668
  (11 other events, 9.5 us)

commit v7 on v6

--- a/solution.py
+++ b/solution.py
@@ -88,40 +88,71 @@
 
 def cut_faces(field):
     coeffs, cells_x, cells_y, cells_z = field.shape
-    per_step = 9
+    parts = 9
+    per_part = coeffs // parts
     rows = cells_x * HALO
 
-    def kernel(field, pick, last, first, top, bottom):
-        for c in range(per_step):
-            last[c] = field[c, cells_x - HALO :]
-            first[c] = field[c, :HALO]
-            chosen = jnp.dot(
-                pick[...],
-                field[c].reshape(cells_x * cells_y, cells_z),
-                preferred_element_type=jnp.float32,
-            ).astype(jnp.bfloat16)
-            top[c] = chosen[:rows]
-            bottom[c] = chosen[rows:]
+    def kernel(field, pick, last, first, top, bottom, buf, high, low, sems, out_sems):
+        def load(i):
+            here = pl.ds(i * per_part, per_part)
+            return pltpu.make_async_copy(field.at[here], buf.at[here], sems.at[i])
+
+        def saves(i):
+            here = pl.ds(i * per_part, per_part)
+            return [
+                pltpu.make_async_copy(high.at[here], top.at[here], out_sems.at[0, i]),
+                pltpu.make_async_copy(low.at[here], bottom.at[here], out_sems.at[1, i]),
+                pltpu.make_async_copy(
+                    buf.at[here, pl.ds(cells_x - HALO, HALO)], last.at[here], out_sems.at[2, i]
+                ),
+                pltpu.make_async_copy(
+                    buf.at[here, pl.ds(0, HALO)], first.at[here], out_sems.at[3, i]
+                ),
+            ]
+
+        for i in range(parts):
+            load(i).start()
+
+        def body(i, _):
+            load(i).wait()
+            for k in range(per_part):
+                c = i * per_part + k
+                chosen = jnp.dot(
+                    pick[...],
+                    buf[c].reshape(cells_x * cells_y, cells_z),
+                    preferred_element_type=jnp.float32,
+                ).astype(jnp.bfloat16)
+                high[c] = chosen[:rows]
+                low[c] = chosen[rows:]
+            for save in saves(i):
+                save.start()
+            return 0
+
+        lax.fori_loop(0, parts, body, 0)
+        for i in range(parts):
+            for save in saves(i):
+                save.wait()
 
     pick = np.zeros((2 * rows, cells_x * cells_y), np.float32)
     for x in range(cells_x):
         for j in range(HALO):
             pick[x * HALO + j, x * cells_y + cells_y - HALO + j] = 1.0
             pick[rows + x * HALO + j, x * cells_y + j] = 1.0
-    shapes = [(coeffs, HALO, cells_y, cells_z)] * 2
-    shapes += [(coeffs, rows, cells_z)] * 2
-
-    def whole(shape):
-        zeros = (0,) * (len(shape) - 1)
-        return pl.BlockSpec((per_step,) + shape[1:], lambda i: (i,) + zeros)
-
+    shapes = [(coeffs, HALO, cells_y, cells_z)] * 2 + [(coeffs, rows, cells_z)] * 2
+    hbm = pl.BlockSpec(memory_space=pl.ANY)
     return pl.pallas_call(
         kernel,
         out_shape=[pltpu.HBM(shape, jnp.bfloat16) for shape in shapes],
-        grid=(coeffs // per_step,),
-        in_specs=[whole(field.shape), pl.BlockSpec(pick.shape, lambda i: (0, 0))],
-        out_specs=[whole(shape) for shape in shapes],
-        compiler_params=pltpu.CompilerParams(vmem_limit_bytes=24 * MIB),
+        in_specs=[hbm, pl.BlockSpec(memory_space=pltpu.VMEM)],
+        out_specs=[hbm] * 4,
+        scratch_shapes=[
+            pltpu.VMEM(field.shape, jnp.bfloat16),
+            pltpu.VMEM((coeffs, rows, cells_z), jnp.bfloat16),
+            pltpu.VMEM((coeffs, rows, cells_z), jnp.bfloat16),
+            pltpu.SemaphoreType.DMA((parts,)),
+            pltpu.SemaphoreType.DMA((4, parts)),
+        ],
+        compiler_params=pltpu.CompilerParams(vmem_limit_bytes=16 * MIB),
         name="cut_faces",
     )(field, jnp.asarray(pick.astype(jnp.bfloat16)))
 
@@ -465,7 +496,7 @@
     )(ordered, jnp.asarray(ones.astype(jnp.bfloat16)))
 
 
-RING = 2
+RING = 4
 STREAM = 8
 CHUNK = 1024
 
@@ -480,10 +511,6 @@
 
     def kernel(index, wide, pick, *refs):
         table, out, local, sems, near, near_sems, rows = refs[len(edges) + 1 :]
-        at = first_edge
-        for edge in refs[: len(edges)]:
-            table[pl.ds(at, edge.shape[0]), :] = edge[...].astype(jnp.float32)
-            at += edge.shape[0]
         sublane = lax.broadcasted_iota(jnp.int32, (GROUP, LANES), 0)
         masks = [sublane == k for k in range(GROUP)]
         used = lax.broadcasted_iota(jnp.int32, (GROUP, LANES), 1) < coeffs
@@ -506,6 +533,11 @@
             fetch(b, b).start()
         for b in range(STREAM - 1):
             stream(b, b).start()
+
+        at = first_edge
+        for edge in refs[: len(edges)]:
+            table[pl.ds(at, edge.shape[0]), :] = edge[...].astype(jnp.float32)
+            at += edge.shape[0]
 
         def body(i, _):
             for b in range(RING):
@@ -576,7 +608,7 @@
             pltpu.VMEM(table.shape, jnp.float32),
             jax.ShapeDtypeStruct((pairs, 24, LANES), jnp.bfloat16),
         ),
-        in_specs=[vmem, pl.BlockSpec(memory_space=pl.ANY)] + [vmem] * (2 + len(edges)),
+        in_specs=[pl.BlockSpec(memory_space=pl.ANY)] * 2 + [vmem] * (2 + len(edges)),
         out_specs=(vmem, vmem),
         scratch_shapes=[
             pltpu.SMEM((RING, CHUNK), jnp.int32),
@@ -601,19 +633,19 @@
     block = 512
     step = block // per_pair
 
-    def kernel(transfer, routed, basis, wide, projector, out):
-        low = lax.broadcasted_iota(jnp.int32, (GROUP, LANES), 1) < 64
+    def kernel(transfer, routed, basis, wide, projector, unpick, out):
+        heads = [
+            routed[:, i * GROUP : (i + 1) * GROUP, :].astype(jnp.float32).reshape(-1, LANES)
+            for i in range(3)
+        ]
+        heads = [head.astype(jnp.bfloat16) for head in heads]
+        pairs = [jnp.concatenate([heads[i], heads[2]], axis=1) for i in range(2)]
+        quarters = [
+            jnp.dot(pairs[q % 2], unpick[q], preferred_element_type=jnp.float32) for q in range(4)
+        ]
         parts = []
         for i in range(step):
-            head = routed[i, :16, :].astype(jnp.float32)
-            first, second = head[:GROUP], head[GROUP:]
-            third = routed[i, 16:, :].astype(jnp.float32)
-            parts += [
-                jnp.where(low, first, pltpu.roll(third, 64, 1)),
-                jnp.where(low, second, pltpu.roll(third, 32, 1)),
-                jnp.where(low, pltpu.roll(first, 64, 1), third),
-                jnp.where(low, pltpu.roll(second, 64, 1), pltpu.roll(third, 96, 1)),
-            ]
+            parts += [quarter[i * GROUP : (i + 1) * GROUP] for quarter in quarters]
         rows = jnp.concatenate(parts, axis=0).astype(jnp.bfloat16)
         lit = jnp.dot(basis[...], transfer[...], preferred_element_type=jnp.float32)
         shade = lax.dot_general(
@@ -627,6 +659,13 @@
     directions = basis.shape[0]
     wide = np.zeros((directions, LANES), jnp.bfloat16)
     wide[:, :coeffs] = basis
+    half = LANES // 2
+    unpick = np.zeros((4, 2 * LANES, LANES), np.float32)
+    for q in range(4):
+        for c in range(half):
+            unpick[q, (q // 2) * half + c, c] = 1.0
+        for c in range(32):
+            unpick[q, LANES + q * 32 + c, half + c] = 1.0
     return pl.pallas_call(
         kernel,
         out_shape=jax.ShapeDtypeStruct((coeffs, count), jnp.bfloat16),
@@ -637,11 +676,19 @@
             pl.BlockSpec((directions, coeffs), lambda i: (0, 0)),
             pl.BlockSpec((directions, LANES), lambda i: (0, 0)),
             pl.BlockSpec((coeffs, directions), lambda i: (0, 0)),
+            pl.BlockSpec(unpick.shape, lambda i: (0, 0, 0)),
         ],
         out_specs=pl.BlockSpec((coeffs, block), lambda i: (0, i)),
         compiler_params=pltpu.CompilerParams(vmem_limit_bytes=40 * MIB),
         name="relight",
-    )(transfer, routed, jnp.asarray(basis), jnp.asarray(wide), jnp.asarray(projector))
+    )(
+        transfer,
+        routed,
+        jnp.asarray(basis),
+        jnp.asarray(wide),
+        jnp.asarray(projector),
+        jnp.asarray(unpick.astype(jnp.bfloat16)),
+    )
 
 
 def moves(sizes, steps):
@@ -651,6 +698,10 @@
             to_x, to_y = (x + steps[0]) % sizes[0], (y + steps[1]) % sizes[1]
             pairs.append((x * sizes[1] + y, to_x * sizes[1] + to_y))
     return pairs
+
+
+def shift(array, axis, pairs):
+    return pltpu.with_memory_space_constraint(lax.ppermute(array, axis, pairs), pltpu.HBM)
 
 
 def halo_step(field, samples, weights, destination, transfer):
@@ -672,10 +723,10 @@
 
     field = pltpu.with_memory_space_constraint(field, pltpu.HBM)
     last, first, top, bottom = cut_faces(field)
-    ylo = lax.ppermute(top, "gy", ups[1])
-    yhi = lax.ppermute(bottom, "gy", downs[1])
-    xlo = lax.ppermute(last, "gx", ups[0])
-    xhi = lax.ppermute(first, "gx", downs[0])
+    ylo = shift(top, "gy", ups[1])
+    yhi = shift(bottom, "gy", downs[1])
+    xlo = shift(last, "gx", ups[0])
+    xhi = shift(first, "gx", downs[0])
     field, slot, origin = lax.optimization_barrier((field, slot, origin))
 
     eye = jnp.asarray(np.eye(cells_z, dtype=np.float32).astype(jnp.bfloat16))
@@ -688,8 +739,8 @@
     index, ordered = prepare(samples, weights, slot, origin, cells, total)
     table, index, ordered, ylo, yhi = lax.optimization_barrier((table, index, ordered, ylo, yhi))
     up, down = cut_corners(ylo, yhi)
-    clo = lax.ppermute(up, "gx", ups[0])
-    chi = lax.ppermute(down, "gx", downs[0])
+    clo = shift(up, "gx", ups[0])
+    chi = shift(down, "gx", downs[0])
     table, bottoms, tops = add_planes(
         table, [(ylo, None), (yhi, None)], (), eye, cells_x, total_rows, early
     )

time: 131 us -> 129 us (0.985)
  local copies, waits for them, and re-layouts: 6.5 us -> 4.34 us
    pallas_call x1, Pallas kernels: 7.62 us -> 4.62 us  [cut_faces(): pl.pallas_call(kernel, out_shape=[pltpu.HBM(shape, jnp.bfloat16) for shap...]
    unnamed x50 -> x48, local copies, waits for them, and re-layouts: 6.5 us -> 4.34 us
    pallas_call x1, Pallas kernels: 1.76 us -> 3.34 us  [cut_corners(): pl.pallas_call(kernel, out_shape=[pltpu.HBM(shape, jnp.bfloat16)] * 2, gr...]
  transfers between devices with their start and end apart: 10 -> 10, of which waited for: 1 -> 1; matrix products, arithmetic and copies ran while one was open for 0% -> 0% of each run, Pallas kernels for 26% -> 28%
where the time goes in v7:
time: 129 us; the launch traced here: 128 us
  Pallas kernels  73.7 us (57%)
  blocking collectives  25.1 us (19%)
  starting transfers between devices  14.5 us (11%)
  waiting for transfers between devices  10.2 us (8%)
  local copies, waits for them, and re-layouts  4.34 us (3%)
    pallas_call x1, Pallas kernels, gather_rows(): pl.pallas_call(kernel, out_shape=(pltpu.VMEM(table.shape, jnp.float32), j...  25.4 us
    all_to_all x1, blocking collectives, halo_step(): lax.all_to_all(outgoing, ('gx', 'gy', 'gz'), split_axis=0, concat_axis=0,...  25.1 us
    pallas_call x3, Pallas kernels, add_planes(): pl.pallas_call(kernel, out_shape=shapes, in_specs=[vmem] * len(held) + [h...  15 us
    ppermute x6, starting transfers between devices, shift(): lax.ppermute(array, axis, pairs)  11.5 us
    ppermute x6, waiting for transfers between devices, shift(): lax.ppermute(array, axis, pairs)  10.2 us
    pallas_call x1, Pallas kernels, prepare(): pl.pallas_call(kernel, out_shape=(jax.ShapeDtypeStruct((count * SAMPLES /...  9.09 us
    pallas_call x1, Pallas kernels, relight(): pl.pallas_call(kernel, out_shape=jax.ShapeDtypeStruct((coeffs, count), jn...  8.19 us
    pallas_call x1, Pallas kernels, spread_weights(): pl.pallas_call(kernel, out_shape=pltpu.HBM((count * SAMPLES, LANES), jnp....  7.74 us
  transfers between devices with their start and end apart: 10, of which 1 were waited for; matrix products, arithmetic and copies ran while one was open for 0% of the time, Pallas kernels for 28%

profile of v7, /device:TPU:1, one launch (start us, length us, event | category | flops | bytes accessed | tf_op | source)
XLA Modules:
  0.0 128.2 jit_solution(9324738144836270967)
XLA Ops:
  0.0 0.7 copy-done.8
  0.7 4.6 %cut_faces.1 = (bf16[81,2,16,256]{3,2,1,0:T(8,128)(2,1)}, bf16[81,2,16,256]{3,2,1,0:T(8,128)(2,1)}, bf16[81,16,256]{2,1,0:T(8,128)(2,1)}, bf16[81,16,256]{2,1,0:T(8,128)(2,1)}) custom-call(bf16[81,8,16,256]{3,2,1,0:T(8,128)(2,1)} %field.1, bf16[32,128]{1,0:T(8,128)(2,1)S(1)} %copy-done.8), custom_call_target="tpu_custom_call" | custom-call | tf_op jit(solution)/shard_map/cut_faces/pallas_call | solution.py:143
  5.3 4.2 %collective-permute-start = (bf16[81,16,256]{2,1,0:T(8,128)(2,1)}, bf16[81,16,256]{2,1,0:T(8,128)(2,1)S(1)}, u32[]{:S(2)}, u32[]{:S(2)}) collective-permute-start(bf16[81,16,256]{2,1,0:T(8,128)(2,1)} %get-tuple-element.37), channel_id=1, source_target_pairs={{0,4},{4,8},{8,12},{12,0},{1,5},{5,9},{9,13},{13,1},{2,6},{6,10},{... | collective-permute-start | bytes 1990664 | tf_op jit(solution)/shard_map/ppermute | solution.py:704
  9.5 1.6 %collective-permute-start.6 = (bf16[81,2,16,256]{3,2,1,0:T(8,128)(2,1)}, bf16[81,2,16,256]{3,2,1,0:T(8,128)(2,1)S(1)}, u32[]{:S(2)}, u32[]{:S(2)}) collective-permute-start(bf16[81,2,16,256]{3,2,1,0:T(8,128)(2,1)} %get-tuple-element.54), channel_id=1, source_target_pairs={{0,16},{16,32},{32,48},{48,64},{64,80},{80,96},{96,112},{112,0},{1... | collective-permute-start | bytes 3981320 | tf_op jit(solution)/shard_map/ppermute | solution.py:704
  11.2 2.2 %collective-permute-start.7 = (bf16[81,2,16,256]{3,2,1,0:T(8,128)(2,1)}, bf16[81,2,16,256]{3,2,1,0:T(8,128)(2,1)}, u32[]{:S(2)}, u32[]{:S(2)}) collective-permute-start(bf16[81,2,16,256]{3,2,1,0:T(8,128)(2,1)} %get-tuple-element.55), channel_id=1, source_target_pairs={{0,112},{16,0},{32,16},{48,32},{64,48},{80,64},{96,80},{112,96},{1... | collective-permute-start | bytes 3981320 | tf_op jit(solution)/shard_map/ppermute | solution.py:704
  13.4 6.3 %shard_map.163.refs_0_ = f32[62400,128]{1,0:T(8,128)S(1)} custom-call(bf16[81,8,16,256]{3,2,1,0:T(8,128)(2,1)} %field.1, bf16[256,256]{1,0:T(8,128)(2,1)} %constant.44.clone.refs_1_.eye.refs_3_.refs_5_), custom_call_target="tpu_custom_call" | custom-call | flops 20000000000 | bytes 20000000 | tf_op jit(solution)/shard_map/pallas_call | solution.py:288
  19.8 9.1 %prepare.1 = (s32[256,128]{1,0:T(8,128)S(1)}, f32[4096,128]{1,0:T(8,128)S(1)}) custom-call(s32[3]{0:T(128)S(1)} %pad_add_fusion.origin, s32[4096]{0:T(1024)S(1)} %bitcast.5, s32[3,8,4096]{2,1,0:T(8,128)S(1)} %copy-done.10, f32[8,4096]{1,0:T(8,128)S(1)} %copy-done.11, bf16[256,256]{1,0:T(8,128)(2,1)S(1)} %copy-done.13, bf16[16,128]{1,0:T(8,128)(2,1)S(1)} %copy-done.15), custom_call_target="tpu_custom_call" | custom-call | flops 20000000000 | bytes 3000000 | tf_op jit(solution)/shard_map/prepare/pallas_call | solution.py:437
  28.9 0.7 copy-done.14
  29.6 0.8 copy-done.16
  30.7 4.1 %shard_map.164 = (f32[62400,128]{1,0:T(8,128)S(1)}, bf16[320,128]{1,0:T(8,128)(2,1)}, bf16[320,128]{1,0:T(8,128)(2,1)}) custom-call(f32[62400,128]{1,0:T(8,128)S(1)} %shard_map.163.refs_0_, bf16[81,16,256]{2,1,0:T(8,128)(2,1)} %copy-done.16, bf16[81,16,256]{2,1,0:T(8,128)(2,1)} %copy-done.17, ...), custom_call_target="tpu_custom_call", output_to_operand_aliasing={{0}: (0, {})} | custom-call | flops 20000000000 | bytes 20000000 | tf_op jit(solution)/shard_map/pallas_call | solution.py:288
  34.7 1.4 %collective-permute-start.2 = (bf16[320,128]{1,0:T(8,128)(2,1)}, bf16[320,128]{1,0:T(8,128)(2,1)S(1)}, u32[]{:S(2)}, u32[]{:S(2)}) collective-permute-start(bf16[320,128]{1,0:T(8,128)(2,1)} %get-tuple-element.44), channel_id=1, source_target_pairs={{0,1},{1,2},{2,3},{3,0},{4,5},{5,6},{6,7},{7,4},{8,9},{9,10},{10,1... | collective-permute-start | bytes 245768 | tf_op jit(solution)/shard_map/ppermute | solution.py:748
  36.1 1.5 %collective-permute-start.3 = (bf16[320,128]{1,0:T(8,128)(2,1)}, bf16[320,128]{1,0:T(8,128)(2,1)S(1)}, u32[]{:S(2)}, u32[]{:S(2)}) collective-permute-start(bf16[320,128]{1,0:T(8,128)(2,1)} %get-tuple-element.45), channel_id=1, source_target_pairs={{0,3},{1,0},{2,1},{3,2},{4,7},{5,4},{6,5},{7,6},{8,11},{9,8},{10,9... | collective-permute-start | bytes 245768 | tf_op jit(solution)/shard_map/ppermute | solution.py:747
  37.6 3.3 %cut_corners.1 = (bf16[81,8,256]{2,1,0:T(8,128)(2,1)}, bf16[81,8,256]{2,1,0:T(8,128)(2,1)}) custom-call(bf16[81,16,256]{2,1,0:T(8,128)(2,1)} %copy-done.16, bf16[81,16,256]{2,1,0:T(8,128)(2,1)} %copy-done.17, bf16[16,32]{1,0:T(8,128)(2,1)S(1)} %copy-done.9), custom_call_target="tpu_custom_call" | custom-call | tf_op jit(solution)/shard_map/cut_corners/pallas_call | solution.py:183
  41.0 3.6 %collective-permute-start.9 = (bf16[81,8,256]{2,1,0:T(8,128)(2,1)}, bf16[81,8,256]{2,1,0:T(8,128)(2,1)S(1)}, u32[]{:S(2)}, u32[]{:S(2)}) collective-permute-start(bf16[81,8,256]{2,1,0:T(8,128)(2,1)} %get-tuple-element.57), channel_id=1, source_target_pairs={{0,112},{16,0},{32,16},{48,32},{64,48},{80,64},{96,80},{112,96},{1... | collective-permute-start | bytes 995336 | tf_op jit(solution)/shard_map/ppermute | solution.py:704
  44.6 0.3 cut_ends.1
  44.9 7.7 %spread_weights.1.wide = f32[32768,128]{1,0:T(8,128)} custom-call(f32[4096,128]{1,0:T(8,128)S(1)} %get-tuple-element.49.ordered, bf16[128,1024]{1,0:T(8,128)(2,1)S(1)} %copy-done.12), custom_call_target="tpu_custom_call" | custom-call | flops 10000000000 | bytes 3000000 | tf_op jit(solution)/shard_map/spread_weights/pallas_call | solution.py:482
  52.7 10.2 %collective-permute-done.8.refs_3_ = bf16[81,8,256]{2,1,0:T(8,128)(2,1)S(1)} collective-permute-done((bf16[81,8,256]{2,1,0:T(8,128)(2,1)}, bf16[81,8,256]{2,1,0:T(8,128)(2,1)S(1)}, u32[]{:S(2)}, u32[]{:S(2)}) %collective-permute-start.8) | collective-permute-done | bytes 331808 | tf_op jit(solution)/shard_map/ppermute | solution.py:704
  62.9 0.7 copy-done.20
  63.7 0.4 copy-done.19
  64.1 4.7 %shard_map.165.refs_4_ = f32[62400,128]{1,0:T(8,128)S(1)} custom-call(f32[62400,128]{1,0:T(8,128)S(1)} %get-tuple-element.53.refs_0_, bf16[81,2,16,256]{3,2,1,0:T(8,128)(2,1)} %copy-done.19, bf16[81,2,16,256]{3,2,1,0:T(8,128)(2,1)} %collective-permute-done.7.refs_2_, bf16[81,8,256]{2,1,0:T(8,128)(2,1)} %copy-done.20, ...), custom_call_target="tpu_custom_call", output_to_operand_aliasing={{}: (0, {})} | custom-call | flops 20000000000 | bytes 20000000 | tf_op jit(solution)/shard_map/pallas_call | solution.py:288
  68.8 0.6 copy-done.22
  69.5 25.4 %gather_rows.1 = (f32[62400,128]{1,0:T(8,128)S(1)}, bf16[128,24,128]{2,1,0:T(8,128)(2,1)}) custom-call(s32[32768]{0:T(1024)} %bitcast.6, f32[32768,128]{1,0:T(8,128)} %spread_weights.1.wide, bf16[3,256,128]{2,1,0:T(8,128)(2,1)} %constant.49.clone.pick, bf16[320,128]{1,0:T(8,128)(2,1)} %copy-done.6, ...), custom_call_target="tpu_custom_call", output_to_operand_aliasing={{0}: (7, {})} | custom-call | flops 40000000000 | bytes 20000000 | tf_op jit(solution)/shard_map/gather_rows/pallas_call | solution.py:605
  94.9 25.1 %all_to_all.5.routed = bf16[128,24,128]{2,1,0:T(8,128)(2,1)S(1)} all-to-all(bf16[128,24,128]{2,1,0:T(8,128)(2,1)} %get-tuple-element.58), channel_id=1, replica_groups=mesh['gx'=8,'gy'=4,'gz'=4] {'gx','gy','gz'}, dimensions={0} | all-to-all | bytes 1572864 | tf_op jit(solution)/shard_map/all_to_all | solution.py:760
  120.0 8.2 %relight.1 = bf16[81,4096]{1,0:T(8,128)(2,1)} custom-call(bf16[81,4096]{1,0:T(8,128)(2,1)S(1)} %copy-done, bf16[128,24,128]{2,1,0:T(8,128)(2,1)S(1)} %all_to_all.5.routed, bf16[1024,81]{1,0:T(8,128)(2,1)S(1)} %copy-done.4, bf16[1024,128]{1,0:T(8,128)(2,1)S(1)} %copy-done.3, bf16[81,1024]{1,0:T(8,128)(2,1)S(1)} %copy-done.5, bf16[4,256,128]{2,1,0:T(8,128)(2,1)S(1)} %copy-done.2), custom_call_target="tpu_custom_call" | custom-call | tf_op jit(solution)/shard_map/relight/pallas_call | solution.py:669
  (57 shorter events, 0.7 us)
Async XLA Ops:
  0.7 12.6 %copy-start.18 = (s32[2,4096]{1,0:T(2,128)S(1)}, s32[2,4096]{1,0:T(2,128)}, u32[]{:S(2)}) copy-start(s32[2,4096]{1,0:T(2,128)} %param.20) | copy-start | bytes 98308
  5.3 24.3 %collective-permute-start = (bf16[81,16,256]{2,1,0:T(8,128)(2,1)}, bf16[81,16,256]{2,1,0:T(8,128)(2,1)S(1)}, u32[]{:S(2)}, u32[]{:S(2)}) collective-permute-start(bf16[81,16,256]{2,1,0:T(8,128)(2,1)} %get-tuple-element.37), channel_id=1, source_target_pairs={{0,4},{4,8},{8,12},{12,0},{1,5},{5,9},{9,13},{13,1},{2,6},{6,10},{... | collective-permute-start | bytes 1990664 | tf_op jit(solution)/shard_map/ppermute | solution.py:704
  9.5 20.1 %collective-permute-start.1 = (bf16[81,16,256]{2,1,0:T(8,128)(2,1)}, bf16[81,16,256]{2,1,0:T(8,128)(2,1)S(1)}, u32[]{:S(2)}, u32[]{:S(2)}) collective-permute-start(bf16[81,16,256]{2,1,0:T(8,128)(2,1)} %get-tuple-element.38), channel_id=1, source_target_pairs={{0,12},{4,0},{8,4},{12,8},{1,13},{5,1},{9,5},{13,9},{2,14},{6,2},{... | collective-permute-start | bytes 1990664 | tf_op jit(solution)/shard_map/ppermute | solution.py:704
  9.5 53.3 %collective-permute-start.6 = (bf16[81,2,16,256]{3,2,1,0:T(8,128)(2,1)}, bf16[81,2,16,256]{3,2,1,0:T(8,128)(2,1)S(1)}, u32[]{:S(2)}, u32[]{:S(2)}) collective-permute-start(bf16[81,2,16,256]{3,2,1,0:T(8,128)(2,1)} %get-tuple-element.54), channel_id=1, source_target_pairs={{0,16},{16,32},{32,48},{48,64},{64,80},{80,96},{96,112},{112,0},{1... | collective-permute-start | bytes 3981320 | tf_op jit(solution)/shard_map/ppermute | solution.py:704
  11.2 51.7 %collective-permute-start.7 = (bf16[81,2,16,256]{3,2,1,0:T(8,128)(2,1)}, bf16[81,2,16,256]{3,2,1,0:T(8,128)(2,1)}, u32[]{:S(2)}, u32[]{:S(2)}) collective-permute-start(bf16[81,2,16,256]{3,2,1,0:T(8,128)(2,1)} %get-tuple-element.55), channel_id=1, source_target_pairs={{0,112},{16,0},{32,16},{48,32},{64,48},{80,64},{96,80},{112,96},{1... | collective-permute-start | bytes 3981320 | tf_op jit(solution)/shard_map/ppermute | solution.py:704
  13.4 6.3 %copy-start.11 = (f32[8,4096]{1,0:T(8,128)S(1)}, f32[8,4096]{1,0:T(8,128)}, u32[]{:S(2)}) copy-start(f32[8,4096]{1,0:T(8,128)} %weights.1) | copy-start | bytes 393220
  13.4 6.4 %copy-start.13 = (bf16[256,256]{1,0:T(8,128)(2,1)S(1)}, bf16[256,256]{1,0:T(8,128)(2,1)}, u32[]{:S(2)}) copy-start(bf16[256,256]{1,0:T(8,128)(2,1)} %constant.44.clone.refs_1_.eye.refs_3_.refs_5_) | copy-start | bytes 393220
  13.4 6.4 %copy-start.15 = (bf16[16,128]{1,0:T(8,128)(2,1)S(1)}, bf16[16,128]{1,0:T(8,128)(2,1)}, u32[]{:S(2)}) copy-start(bf16[16,128]{1,0:T(8,128)(2,1)} %constant.45.clone.join) | copy-start | bytes 12292
  30.7 7.0 %copy-start.9 = (bf16[16,32]{1,0:T(8,128)(2,1)S(1)}, bf16[16,32]{1,0:T(8,128)(2,1)}, u32[]{:S(2)}) copy-start(bf16[16,32]{1,0:T(8,128)(2,1)} %constant.46.clone.pick) | copy-start | bytes 3076
  30.7 13.9 %copy-start.1 = (bf16[320,640]{1,0:T(8,128)(2,1)S(1)}, bf16[320,640]{1,0:T(8,128)(2,1)}, u32[]{:S(2)}) copy-start(bf16[320,640]{1,0:T(8,128)(2,1)} %constant.47.clone.pick) | copy-start | bytes 1228804
  30.7 14.3 %copy-start.12 = (bf16[128,1024]{1,0:T(8,128)(2,1)S(1)}, bf16[128,1024]{1,0:T(8,128)(2,1)}, u32[]{:S(2)}) copy-start(bf16[128,1024]{1,0:T(8,128)(2,1)} %constant.48.clone.ones) | copy-start | bytes 786436
  34.7 6.2 %collective-permute-start.2 = (bf16[320,128]{1,0:T(8,128)(2,1)}, bf16[320,128]{1,0:T(8,128)(2,1)S(1)}, u32[]{:S(2)}, u32[]{:S(2)}) collective-permute-start(bf16[320,128]{1,0:T(8,128)(2,1)} %get-tuple-element.44), channel_id=1, source_target_pairs={{0,1},{1,2},{2,3},{3,0},{4,5},{5,6},{6,7},{7,4},{8,9},{9,10},{10,1... | collective-permute-start | bytes 245768 | tf_op jit(solution)/shard_map/ppermute | solution.py:748
  36.1 8.4 %collective-permute-start.3 = (bf16[320,128]{1,0:T(8,128)(2,1)}, bf16[320,128]{1,0:T(8,128)(2,1)S(1)}, u32[]{:S(2)}, u32[]{:S(2)}) collective-permute-start(bf16[320,128]{1,0:T(8,128)(2,1)} %get-tuple-element.45), channel_id=1, source_target_pairs={{0,3},{1,0},{2,1},{3,2},{4,7},{5,4},{6,5},{7,6},{8,11},{9,8},{10,9... | collective-permute-start | bytes 245768 | tf_op jit(solution)/shard_map/ppermute | solution.py:747
  41.0 21.9 %collective-permute-start.8 = (bf16[81,8,256]{2,1,0:T(8,128)(2,1)}, bf16[81,8,256]{2,1,0:T(8,128)(2,1)S(1)}, u32[]{:S(2)}, u32[]{:S(2)}) collective-permute-start(bf16[81,8,256]{2,1,0:T(8,128)(2,1)} %get-tuple-element.56), channel_id=1, source_target_pairs={{0,16},{16,32},{32,48},{48,64},{64,80},{80,96},{96,112},{112,0},{1... | collective-permute-start | bytes 995336 | tf_op jit(solution)/shard_map/ppermute | solution.py:704
  41.0 11.7 %copy-start.6 = (bf16[320,128]{1,0:T(8,128)(2,1)}, bf16[320,128]{1,0:T(8,128)(2,1)S(1)}, u32[]{:S(2)}) copy-start(bf16[320,128]{1,0:T(8,128)(2,1)S(1)} %collective-permute-done.2.zlo.refs_0_) | copy-start | bytes 245764
  41.0 21.9 %collective-permute-start.9 = (bf16[81,8,256]{2,1,0:T(8,128)(2,1)}, bf16[81,8,256]{2,1,0:T(8,128)(2,1)S(1)}, u32[]{:S(2)}, u32[]{:S(2)}) collective-permute-start(bf16[81,8,256]{2,1,0:T(8,128)(2,1)} %get-tuple-element.57), channel_id=1, source_target_pairs={{0,112},{16,0},{32,16},{48,32},{64,48},{80,64},{96,80},{112,96},{1... | collective-permute-start | bytes 995336 | tf_op jit(solution)/shard_map/ppermute | solution.py:704
  44.6 8.1 %copy-start.7 = (bf16[320,128]{1,0:T(8,128)(2,1)}, bf16[320,128]{1,0:T(8,128)(2,1)S(1)}, u32[]{:S(2)}) copy-start(bf16[320,128]{1,0:T(8,128)(2,1)S(1)} %collective-permute-done.3.zhi.refs_1_) | copy-start | bytes 245764
  44.8 24.0 %collective-permute-start.4 = (bf16[160,128]{1,0:T(8,128)(2,1)S(1)}, bf16[160,128]{1,0:T(8,128)(2,1)S(1)}, u32[]{:S(2)}, u32[]{:S(2)}) collective-permute-start(bf16[160,128]{1,0:T(8,128)(2,1)S(1)} %get-tuple-element.51), channel_id=1, source_target_pairs={{0,16},{16,32},{32,48},{48,64},{64,80},{80,96},{96,112},{112,0},{1... | collective-permute-start | bytes 122888 | tf_op jit(solution)/shard_map/ppermute | solution.py:751
  62.8 6.0 %collective-permute-start.5 = (bf16[160,128]{1,0:T(8,128)(2,1)S(1)}, bf16[160,128]{1,0:T(8,128)(2,1)S(1)}, u32[]{:S(2)}, u32[]{:S(2)}) collective-permute-start(bf16[160,128]{1,0:T(8,128)(2,1)S(1)} %get-tuple-element.52), channel_id=1, source_target_pairs={{0,112},{16,0},{32,16},{48,32},{64,48},{80,64},{96,80},{112,96},{1... | collective-permute-start | bytes 122888 | tf_op jit(solution)/shard_map/ppermute | solution.py:752
  69.4 50.5 %copy-start = (bf16[81,4096]{1,0:T(8,128)(2,1)S(1)}, bf16[81,4096]{1,0:T(8,128)(2,1)}, u32[]{:S(2)}) copy-start(bf16[81,4096]{1,0:T(8,128)(2,1)} %transfer.1) | copy-start | bytes 1990660
  69.5 50.5 %copy-start.2 = (bf16[4,256,128]{2,1,0:T(8,128)(2,1)S(1)}, bf16[4,256,128]{2,1,0:T(8,128)(2,1)}, u32[]{:S(2)}) copy-start(bf16[4,256,128]{2,1,0:T(8,128)(2,1)} %constant.53.clone.unpick) | copy-start | bytes 786436
  69.5 50.5 %copy-start.3 = (bf16[1024,128]{1,0:T(8,128)(2,1)S(1)}, bf16[1024,128]{1,0:T(8,128)(2,1)}, u32[]{:S(2)}) copy-start(bf16[1024,128]{1,0:T(8,128)(2,1)} %constant.51.clone.wide) | copy-start | bytes 786436
  69.5 50.5 %copy-start.4 = (bf16[1024,81]{1,0:T(8,128)(2,1)S(1)}, bf16[1024,81]{1,0:T(8,128)(2,1)}, u32[]{:S(2)}) copy-start(bf16[1024,81]{1,0:T(8,128)(2,1)} %constant.50.clone.basis) | copy-start | bytes 497668
  69.5 50.5 %copy-start.5 = (bf16[81,1024]{1,0:T(8,128)(2,1)S(1)}, bf16[81,1024]{1,0:T(8,128)(2,1)}, u32[]{:S(2)}) copy-start(bf16[81,1024]{1,0:T(8,128)(2,1)} %constant.52.clone.projector) | copy-start | bytes 497668
  (10 other events, 13.7 us)

commit v8 on v7

--- a/solution.py
+++ b/solution.py
@@ -510,7 +510,7 @@
     half = LANES // 2
 
     def kernel(index, wide, pick, *refs):
-        table, out, local, sems, near, near_sems, rows = refs[len(edges) + 1 :]
+        table, out, local, sems, near, near_sems, rows, staged, out_sems = refs[len(edges) + 1 :]
         sublane = lax.broadcasted_iota(jnp.int32, (GROUP, LANES), 0)
         masks = [sublane == k for k in range(GROUP)]
         used = lax.broadcasted_iota(jnp.int32, (GROUP, LANES), 1) < coeffs
@@ -528,6 +528,29 @@
                 near.at[slot],
                 near_sems.at[slot],
             )
+
+        dests = groups // 4
+
+        def save(n):
+            here = pl.ds(n * dests, dests)
+            return pltpu.make_async_copy(staged.at[here], out.at[here], out_sems.at[n])
+
+        def pack(n):
+            span = dests * GROUP
+            at = pl.multiple_of(n * span, span)
+            part = [rows[q, pl.ds(at, span), :].astype(jnp.bfloat16) for q in range(4)]
+            even = jnp.concatenate([part[0], part[2]], axis=1)
+            odd = jnp.concatenate([part[1], part[3]], axis=1)
+            first = jnp.dot(even, pick[0], preferred_element_type=jnp.float32)
+            second = jnp.dot(odd, pick[0], preferred_element_type=jnp.float32)
+            third = jnp.dot(even, pick[1], preferred_element_type=jnp.float32)
+            third += jnp.dot(odd, pick[2], preferred_element_type=jnp.float32)
+            for d in range(dests):
+                here = slice(d * GROUP, (d + 1) * GROUP)
+                staged[n * dests + d, :16, :] = jnp.concatenate(
+                    [first[here], second[here]], axis=0
+                ).astype(jnp.bfloat16)
+                staged[n * dests + d, 16:, :] = third[here].astype(jnp.bfloat16)
 
         for b in range(RING - 1):
             fetch(b, b).start()
@@ -555,6 +578,12 @@
                 @pl.when(later < chunks)
                 def _():
                     stream(later, later % STREAM).start()
+
+                @pl.when(n > 1)
+                def _():
+                    save(n - 2).start()
+
+                pack(jnp.maximum(n - 1, 0))
 
                 for q in range(groups):
                     total = None
@@ -573,24 +602,11 @@
 
         lax.fori_loop(0, chunks // RING, body, 0)
 
-        def pack(i, _):
-            at = pl.multiple_of(i * 128, 128)
-            part = [rows[q, pl.ds(at, 128), :].astype(jnp.bfloat16) for q in range(4)]
-            outer = [jnp.concatenate([part[0], part[2]], axis=1)]
-            outer.append(jnp.concatenate([part[1], part[3]], axis=1))
-            first = jnp.dot(outer[0], pick[0], preferred_element_type=jnp.float32)
-            second = jnp.dot(outer[1], pick[0], preferred_element_type=jnp.float32)
-            third = jnp.dot(outer[0], pick[1], preferred_element_type=jnp.float32)
-            third += jnp.dot(outer[1], pick[2], preferred_element_type=jnp.float32)
-            for d in range(128 // GROUP):
-                here = slice(d * GROUP, (d + 1) * GROUP)
-                out[i * (128 // GROUP) + d, :16, :] = jnp.concatenate(
-                    [first[here], second[here]], axis=0
-                ).astype(jnp.bfloat16)
-                out[i * (128 // GROUP) + d, 16:, :] = third[here].astype(jnp.bfloat16)
-            return 0
-
-        lax.fori_loop(0, pairs * GROUP // 128, pack, 0)
+        save(chunks - 2).start()
+        pack(chunks - 1)
+        save(chunks - 1).start()
+        for n in range(chunks):
+            save(n).wait()
 
     pick = np.zeros((3, 2 * LANES, LANES), np.float32)
     for c in range(half):
@@ -606,16 +622,18 @@
         kernel,
         out_shape=(
             pltpu.VMEM(table.shape, jnp.float32),
-            jax.ShapeDtypeStruct((pairs, 24, LANES), jnp.bfloat16),
+            pltpu.HBM((pairs, 24, LANES), jnp.bfloat16),
         ),
         in_specs=[pl.BlockSpec(memory_space=pl.ANY)] * 2 + [vmem] * (2 + len(edges)),
-        out_specs=(vmem, vmem),
+        out_specs=(vmem, pl.BlockSpec(memory_space=pl.ANY)),
         scratch_shapes=[
             pltpu.SMEM((RING, CHUNK), jnp.int32),
             pltpu.SemaphoreType.DMA((RING,)),
             pltpu.VMEM((STREAM, CHUNK, LANES), jnp.float32),
             pltpu.SemaphoreType.DMA((STREAM,)),
             pltpu.VMEM((4, pairs * GROUP, LANES), jnp.float32),
+            pltpu.VMEM((pairs, 24, LANES), jnp.bfloat16),
+            pltpu.SemaphoreType.DMA((chunks,)),
         ],
         input_output_aliases={3 + len(edges): 0},
         compiler_params=pltpu.CompilerParams(vmem_limit_bytes=24 * MIB),
@@ -633,19 +651,19 @@
     block = 512
     step = block // per_pair
 
-    def kernel(transfer, routed, basis, wide, projector, unpick, out):
-        heads = [
-            routed[:, i * GROUP : (i + 1) * GROUP, :].astype(jnp.float32).reshape(-1, LANES)
-            for i in range(3)
-        ]
-        heads = [head.astype(jnp.bfloat16) for head in heads]
-        pairs = [jnp.concatenate([heads[i], heads[2]], axis=1) for i in range(2)]
-        quarters = [
-            jnp.dot(pairs[q % 2], unpick[q], preferred_element_type=jnp.float32) for q in range(4)
-        ]
+    def kernel(transfer, routed, basis, wide, projector, out):
+        low = lax.broadcasted_iota(jnp.int32, (GROUP, LANES), 1) < 64
         parts = []
         for i in range(step):
-            parts += [quarter[i * GROUP : (i + 1) * GROUP] for quarter in quarters]
+            head = routed[i, :16, :].astype(jnp.float32)
+            first, second = head[:GROUP], head[GROUP:]
+            third = routed[i, 16:, :].astype(jnp.float32)
+            parts += [
+                jnp.where(low, first, pltpu.roll(third, 64, 1)),
+                jnp.where(low, second, pltpu.roll(third, 32, 1)),
+                jnp.where(low, pltpu.roll(first, 64, 1), third),
+                jnp.where(low, pltpu.roll(second, 64, 1), pltpu.roll(third, 96, 1)),
+            ]
         rows = jnp.concatenate(parts, axis=0).astype(jnp.bfloat16)
         lit = jnp.dot(basis[...], transfer[...], preferred_element_type=jnp.float32)
         shade = lax.dot_general(
@@ -659,13 +677,6 @@
     directions = basis.shape[0]
     wide = np.zeros((directions, LANES), jnp.bfloat16)
     wide[:, :coeffs] = basis
-    half = LANES // 2
-    unpick = np.zeros((4, 2 * LANES, LANES), np.float32)
-    for q in range(4):
-        for c in range(half):
-            unpick[q, (q // 2) * half + c, c] = 1.0
-        for c in range(32):
-            unpick[q, LANES + q * 32 + c, half + c] = 1.0
     return pl.pallas_call(
         kernel,
         out_shape=jax.ShapeDtypeStruct((coeffs, count), jnp.bfloat16),
@@ -676,19 +687,11 @@
             pl.BlockSpec((directions, coeffs), lambda i: (0, 0)),
             pl.BlockSpec((directions, LANES), lambda i: (0, 0)),
             pl.BlockSpec((coeffs, directions), lambda i: (0, 0)),
-            pl.BlockSpec(unpick.shape, lambda i: (0, 0, 0)),
         ],
         out_specs=pl.BlockSpec((coeffs, block), lambda i: (0, i)),
         compiler_params=pltpu.CompilerParams(vmem_limit_bytes=40 * MIB),
         name="relight",
-    )(
-        transfer,
-        routed,
-        jnp.asarray(basis),
-        jnp.asarray(wide),
-        jnp.asarray(projector),
-        jnp.asarray(unpick.astype(jnp.bfloat16)),
-    )
+    )(transfer, routed, jnp.asarray(basis), jnp.asarray(wide), jnp.asarray(projector))
 
 
 def moves(sizes, steps):
@@ -739,6 +742,7 @@
     index, ordered = prepare(samples, weights, slot, origin, cells, total)
     table, index, ordered, ylo, yhi = lax.optimization_barrier((table, index, ordered, ylo, yhi))
     up, down = cut_corners(ylo, yhi)
+    up, down, table = lax.optimization_barrier((up, down, table))
     clo = shift(up, "gx", ups[0])
     chi = shift(down, "gx", downs[0])
     table, bottoms, tops = add_planes(
@@ -746,12 +750,12 @@
     )
     zhi = lax.ppermute(bottoms, "gz", downs[2])
     zlo = lax.ppermute(tops, "gz", ups[2])
+    bottoms, tops, ordered = lax.optimization_barrier((bottoms, tops, ordered))
+    wide = spread_weights(ordered)
+    zlo, zhi, wide = lax.optimization_barrier((zlo, zhi, wide))
     up, down = cut_ends(zlo, zhi, early, cells_x, cells_y)
-    up, down, ordered = lax.optimization_barrier((up, down, ordered))
     elo = lax.ppermute(up, "gx", ups[0])
     ehi = lax.ppermute(down, "gx", downs[0])
-    wide = spread_weights(ordered)
-    table, wide = lax.optimization_barrier((table, wide))
     sides = [(xlo, 0), (xlo, 1), (xhi, 0), (xhi, 1)]
     table = add_planes(table, sides, (clo, chi), eye, cells_x + 2, total_rows, 0)[0]
     outgoing = gather_rows(

time: 129 us -> 127 us (0.984)
    ppermute x1, waiting for transfers between devices: 0.01 us -> 2.24 us  [halo_step(): zlo = lax.ppermute(tops, 'gz', ups[2])]
    ppermute x6, waiting for transfers between devices: 10.2 us -> 8.6 us  [shift(): lax.ppermute(array, axis, pairs)]
    unnamed x48 -> x50, local copies, waits for them, and re-layouts: 4.34 us -> 4.33 us
  transfers between devices with their start and end apart: 10 -> 10, of which waited for: 1 -> 2; matrix products, arithmetic and copies ran while one was open for 0% -> 0% of each run, Pallas kernels for 28% -> 28%
where the time goes in v8:
time: 127 us
  Pallas kernels  72.5 us (57%)
  blocking collectives  25.1 us (20%)
  starting transfers between devices  13.9 us (11%)
  waiting for transfers between devices  10.8 us (9%)
  local copies, waits for them, and re-layouts  4.33 us (3%)
    all_to_all x1, blocking collectives, halo_step(): lax.all_to_all(outgoing, ('gx', 'gy', 'gz'), split_axis=0, concat_axis=0,...  25.1 us
    pallas_call x1, Pallas kernels, gather_rows(): pl.pallas_call(kernel, out_shape=(pltpu.VMEM(table.shape, jnp.float32), p...  24.9 us
    pallas_call x3, Pallas kernels, add_planes(): pl.pallas_call(kernel, out_shape=shapes, in_specs=[vmem] * len(held) + [h...  15 us
    ppermute x6, starting transfers between devices, shift(): lax.ppermute(array, axis, pairs)  10.9 us
    pallas_call x1, Pallas kernels, prepare(): pl.pallas_call(kernel, out_shape=(jax.ShapeDtypeStruct((count * SAMPLES /...  9.08 us
    ppermute x6, waiting for transfers between devices, shift(): lax.ppermute(array, axis, pairs)  8.6 us
    pallas_call x1, Pallas kernels, spread_weights(): pl.pallas_call(kernel, out_shape=pltpu.HBM((count * SAMPLES, LANES), jnp....  7.68 us
    pallas_call x1, Pallas kernels, relight(): pl.pallas_call(kernel, out_shape=jax.ShapeDtypeStruct((coeffs, count), jn...  7.55 us
  transfers between devices with their start and end apart: 10, of which 2 were waited for; matrix products, arithmetic and copies ran while one was open for 0% of the time, Pallas kernels for 28%

profile of v8, /device:TPU:1, one launch (start us, length us, event | category | flops | bytes accessed | tf_op | source)
XLA Modules:
  0.0 127.0 jit_solution(7082141597630565683)
XLA Ops:
  0.0 0.7 copy-done.7
  0.7 4.6 %cut_faces.1 = (bf16[81,2,16,256]{3,2,1,0:T(8,128)(2,1)}, bf16[81,2,16,256]{3,2,1,0:T(8,128)(2,1)}, bf16[81,16,256]{2,1,0:T(8,128)(2,1)}, bf16[81,16,256]{2,1,0:T(8,128)(2,1)}) custom-call(bf16[81,8,16,256]{3,2,1,0:T(8,128)(2,1)} %field.1, bf16[32,128]{1,0:T(8,128)(2,1)S(1)} %copy-done.7), custom_call_target="tpu_custom_call" | custom-call | tf_op jit(solution)/shard_map/cut_faces/pallas_call | solution.py:143
  5.3 4.2 %collective-permute-start = (bf16[81,16,256]{2,1,0:T(8,128)(2,1)}, bf16[81,16,256]{2,1,0:T(8,128)(2,1)S(1)}, u32[]{:S(2)}, u32[]{:S(2)}) collective-permute-start(bf16[81,16,256]{2,1,0:T(8,128)(2,1)} %get-tuple-element.39), channel_id=1, source_target_pairs={{0,4},{4,8},{8,12},{12,0},{1,5},{5,9},{9,13},{13,1},{2,6},{6,10},{... | collective-permute-start | bytes 1990664 | tf_op jit(solution)/shard_map/ppermute | solution.py:707
  9.5 1.6 %collective-permute-start.6 = (bf16[81,2,16,256]{3,2,1,0:T(8,128)(2,1)}, bf16[81,2,16,256]{3,2,1,0:T(8,128)(2,1)S(1)}, u32[]{:S(2)}, u32[]{:S(2)}) collective-permute-start(bf16[81,2,16,256]{3,2,1,0:T(8,128)(2,1)} %get-tuple-element.58), channel_id=1, source_target_pairs={{0,16},{16,32},{32,48},{48,64},{64,80},{80,96},{96,112},{112,0},{1... | collective-permute-start | bytes 3981320 | tf_op jit(solution)/shard_map/ppermute | solution.py:707
  11.2 2.2 %collective-permute-start.7 = (bf16[81,2,16,256]{3,2,1,0:T(8,128)(2,1)}, bf16[81,2,16,256]{3,2,1,0:T(8,128)(2,1)}, u32[]{:S(2)}, u32[]{:S(2)}) collective-permute-start(bf16[81,2,16,256]{3,2,1,0:T(8,128)(2,1)} %get-tuple-element.59), channel_id=1, source_target_pairs={{0,112},{16,0},{32,16},{48,32},{64,48},{80,64},{96,80},{112,96},{1... | collective-permute-start | bytes 3981320 | tf_op jit(solution)/shard_map/ppermute | solution.py:707
  13.4 6.3 %shard_map.154.refs_0_ = f32[62400,128]{1,0:T(8,128)S(1)} custom-call(bf16[81,8,16,256]{3,2,1,0:T(8,128)(2,1)} %field.1, bf16[256,256]{1,0:T(8,128)(2,1)} %constant.42.clone.refs_1_.eye.refs_3_.refs_5_), custom_call_target="tpu_custom_call" | custom-call | flops 20000000000 | bytes 20000000 | tf_op jit(solution)/shard_map/pallas_call | solution.py:288
  19.8 9.1 %prepare.1 = (s32[256,128]{1,0:T(8,128)S(1)}, f32[4096,128]{1,0:T(8,128)S(1)}) custom-call(s32[3]{0:T(128)S(1)} %pad_add_fusion.origin, s32[4096]{0:T(1024)S(1)} %bitcast.5, s32[3,8,4096]{2,1,0:T(8,128)S(1)} %copy-done.9, f32[8,4096]{1,0:T(8,128)S(1)} %copy-done.10, bf16[256,256]{1,0:T(8,128)(2,1)S(1)} %copy-done.12, bf16[16,128]{1,0:T(8,128)(2,1)S(1)} %copy-done.14), custom_call_target="tpu_custom_call" | custom-call | flops 20000000000 | bytes 3000000 | tf_op jit(solution)/shard_map/prepare/pallas_call | solution.py:437
  28.9 0.7 copy-done.13
  29.6 0.8 copy-done.15
  30.6 3.3 %cut_corners.1 = (bf16[81,8,256]{2,1,0:T(8,128)(2,1)}, bf16[81,8,256]{2,1,0:T(8,128)(2,1)}) custom-call(bf16[81,16,256]{2,1,0:T(8,128)(2,1)} %copy-done.15, bf16[81,16,256]{2,1,0:T(8,128)(2,1)} %copy-done.16, bf16[16,32]{1,0:T(8,128)(2,1)S(1)} %copy-done.8), custom_call_target="tpu_custom_call" | custom-call | tf_op jit(solution)/shard_map/cut_corners/pallas_call | solution.py:183
  34.0 4.1 %shard_map.155 = (f32[62400,128]{1,0:T(8,128)S(1)}, bf16[320,128]{1,0:T(8,128)(2,1)}, bf16[320,128]{1,0:T(8,128)(2,1)}) custom-call(f32[62400,128]{1,0:T(8,128)S(1)} %shard_map.154.refs_0_, bf16[81,16,256]{2,1,0:T(8,128)(2,1)} %copy-done.15, bf16[81,16,256]{2,1,0:T(8,128)(2,1)} %copy-done.16, ...), custom_call_target="tpu_custom_call", output_to_operand_aliasing={{0}: (0, {})} | custom-call | flops 20000000000 | bytes 20000000 | tf_op jit(solution)/shard_map/pallas_call | solution.py:288
  38.1 1.4 %collective-permute-start.2 = (bf16[320,128]{1,0:T(8,128)(2,1)}, bf16[320,128]{1,0:T(8,128)(2,1)S(1)}, u32[]{:S(2)}, u32[]{:S(2)}) collective-permute-start(bf16[320,128]{1,0:T(8,128)(2,1)} %get-tuple-element.48), channel_id=1, source_target_pairs={{0,1},{1,2},{2,3},{3,0},{4,5},{5,6},{6,7},{7,4},{8,9},{9,10},{10,1... | collective-permute-start | bytes 245768 | tf_op jit(solution)/shard_map/ppermute | solution.py:752
  39.5 1.5 %collective-permute-start.3 = (bf16[320,128]{1,0:T(8,128)(2,1)}, bf16[320,128]{1,0:T(8,128)(2,1)S(1)}, u32[]{:S(2)}, u32[]{:S(2)}) collective-permute-start(bf16[320,128]{1,0:T(8,128)(2,1)} %get-tuple-element.49), channel_id=1, source_target_pairs={{0,3},{1,0},{2,1},{3,2},{4,7},{5,4},{6,5},{7,6},{8,11},{9,8},{10,9... | collective-permute-start | bytes 245768 | tf_op jit(solution)/shard_map/ppermute | solution.py:751
  41.0 2.2 %collective-permute-done.2.zlo.refs_0_ = bf16[320,128]{1,0:T(8,128)(2,1)S(1)} collective-permute-done((bf16[320,128]{1,0:T(8,128)(2,1)}, bf16[320,128]{1,0:T(8,128)(2,1)S(1)}, u32[]{:S(2)}, u32[]{:S(2)}) %collective-permute-start.2) | collective-permute-done | bytes 81952 | tf_op jit(solution)/shard_map/ppermute | solution.py:752
  43.2 2.9 %collective-permute-start.9 = (bf16[81,8,256]{2,1,0:T(8,128)(2,1)S(1)}, bf16[81,8,256]{2,1,0:T(8,128)(2,1)S(1)}, u32[]{:S(2)}, u32[]{:S(2)}) collective-permute-start(bf16[81,8,256]{2,1,0:T(8,128)(2,1)S(1)} %copy-done.19), channel_id=1, source_target_pairs={{0,112},{16,0},{32,16},{48,32},{64,48},{80,64},{96,80},{112,96},{1... | collective-permute-start | bytes 995336 | tf_op jit(solution)/shard_map/ppermute | solution.py:707
  46.2 7.7 %spread_weights.1.wide = f32[32768,128]{1,0:T(8,128)} custom-call(f32[4096,128]{1,0:T(8,128)S(1)} %get-tuple-element.51.ordered, bf16[128,1024]{1,0:T(8,128)(2,1)S(1)} %copy-done.11), custom_call_target="tpu_custom_call" | custom-call | flops 10000000000 | bytes 3000000 | tf_op jit(solution)/shard_map/spread_weights/pallas_call | solution.py:482
  54.2 8.6 %collective-permute-done.8.refs_3_ = bf16[81,8,256]{2,1,0:T(8,128)(2,1)S(1)} collective-permute-done((bf16[81,8,256]{2,1,0:T(8,128)(2,1)S(1)}, bf16[81,8,256]{2,1,0:T(8,128)(2,1)S(1)}, u32[]{:S(2)}, u32[]{:S(2)}) %collective-permute-start.8) | collective-permute-done | bytes 331808 | tf_op jit(solution)/shard_map/ppermute | solution.py:707
  62.9 0.7 copy-done.20
  63.7 0.4 copy-done.18
  64.1 4.7 %shard_map.156.refs_4_ = f32[62400,128]{1,0:T(8,128)S(1)} custom-call(f32[62400,128]{1,0:T(8,128)S(1)} %get-tuple-element.57.refs_0_, bf16[81,2,16,256]{3,2,1,0:T(8,128)(2,1)} %copy-done.18, bf16[81,2,16,256]{3,2,1,0:T(8,128)(2,1)} %collective-permute-done.7.refs_2_, bf16[81,8,256]{2,1,0:T(8,128)(2,1)} %copy-done.20, ...), custom_call_target="tpu_custom_call", output_to_operand_aliasing={{}: (0, {})} | custom-call | flops 20000000000 | bytes 20000000 | tf_op jit(solution)/shard_map/pallas_call | solution.py:288
  68.8 0.6 copy-done.23
  69.4 24.9 %gather_rows.1 = (f32[62400,128]{1,0:T(8,128)S(1)}, bf16[128,24,128]{2,1,0:T(8,128)(2,1)}) custom-call(s32[32768]{0:T(1024)} %bitcast.6, f32[32768,128]{1,0:T(8,128)} %spread_weights.1.wide, bf16[3,256,128]{2,1,0:T(8,128)(2,1)} %constant.47.clone.pick, bf16[320,128]{1,0:T(8,128)(2,1)} %copy-done.5, ...), custom_call_target="tpu_custom_call", output_to_operand_aliasing={{0}: (7, {})} | custom-call | flops 40000000000 | bytes 20000000 | tf_op jit(solution)/shard_map/gather_rows/pallas_call | solution.py:621
  94.3 25.1 %all_to_all.5.routed = bf16[128,24,128]{2,1,0:T(8,128)(2,1)S(1)} all-to-all(bf16[128,24,128]{2,1,0:T(8,128)(2,1)} %get-tuple-element.62), channel_id=1, replica_groups=mesh['gx'=8,'gy'=4,'gz'=4] {'gx','gy','gz'}, dimensions={0} | all-to-all | bytes 1572864 | tf_op jit(solution)/shard_map/all_to_all | solution.py:764
  119.5 7.6 %relight.1 = bf16[81,4096]{1,0:T(8,128)(2,1)} custom-call(bf16[81,4096]{1,0:T(8,128)(2,1)S(1)} %copy-done, bf16[128,24,128]{2,1,0:T(8,128)(2,1)S(1)} %all_to_all.5.routed, bf16[1024,81]{1,0:T(8,128)(2,1)S(1)} %copy-done.3, bf16[1024,128]{1,0:T(8,128)(2,1)S(1)} %copy-done.2, bf16[81,1024]{1,0:T(8,128)(2,1)S(1)} %copy-done.4), custom_call_target="tpu_custom_call" | custom-call | tf_op jit(solution)/shard_map/relight/pallas_call | solution.py:680
  (59 shorter events, 0.9 us)
Async XLA Ops:
  0.7 12.6 %copy-start.17 = (s32[2,4096]{1,0:T(2,128)S(1)}, s32[2,4096]{1,0:T(2,128)}, u32[]{:S(2)}) copy-start(s32[2,4096]{1,0:T(2,128)} %param.19) | copy-start | bytes 98308
  5.3 24.2 %collective-permute-start = (bf16[81,16,256]{2,1,0:T(8,128)(2,1)}, bf16[81,16,256]{2,1,0:T(8,128)(2,1)S(1)}, u32[]{:S(2)}, u32[]{:S(2)}) collective-permute-start(bf16[81,16,256]{2,1,0:T(8,128)(2,1)} %get-tuple-element.39), channel_id=1, source_target_pairs={{0,4},{4,8},{8,12},{12,0},{1,5},{5,9},{9,13},{13,1},{2,6},{6,10},{... | collective-permute-start | bytes 1990664 | tf_op jit(solution)/shard_map/ppermute | solution.py:707
  9.5 20.1 %collective-permute-start.1 = (bf16[81,16,256]{2,1,0:T(8,128)(2,1)}, bf16[81,16,256]{2,1,0:T(8,128)(2,1)S(1)}, u32[]{:S(2)}, u32[]{:S(2)}) collective-permute-start(bf16[81,16,256]{2,1,0:T(8,128)(2,1)} %get-tuple-element.40), channel_id=1, source_target_pairs={{0,12},{4,0},{8,4},{12,8},{1,13},{5,1},{9,5},{13,9},{2,14},{6,2},{... | collective-permute-start | bytes 1990664 | tf_op jit(solution)/shard_map/ppermute | solution.py:707
  9.5 53.3 %collective-permute-start.6 = (bf16[81,2,16,256]{3,2,1,0:T(8,128)(2,1)}, bf16[81,2,16,256]{3,2,1,0:T(8,128)(2,1)S(1)}, u32[]{:S(2)}, u32[]{:S(2)}) collective-permute-start(bf16[81,2,16,256]{3,2,1,0:T(8,128)(2,1)} %get-tuple-element.58), channel_id=1, source_target_pairs={{0,16},{16,32},{32,48},{48,64},{64,80},{80,96},{96,112},{112,0},{1... | collective-permute-start | bytes 3981320 | tf_op jit(solution)/shard_map/ppermute | solution.py:707
  11.2 51.7 %collective-permute-start.7 = (bf16[81,2,16,256]{3,2,1,0:T(8,128)(2,1)}, bf16[81,2,16,256]{3,2,1,0:T(8,128)(2,1)}, u32[]{:S(2)}, u32[]{:S(2)}) collective-permute-start(bf16[81,2,16,256]{3,2,1,0:T(8,128)(2,1)} %get-tuple-element.59), channel_id=1, source_target_pairs={{0,112},{16,0},{32,16},{48,32},{64,48},{80,64},{96,80},{112,96},{1... | collective-permute-start | bytes 3981320 | tf_op jit(solution)/shard_map/ppermute | solution.py:707
  13.4 6.3 %copy-start.12 = (bf16[256,256]{1,0:T(8,128)(2,1)S(1)}, bf16[256,256]{1,0:T(8,128)(2,1)}, u32[]{:S(2)}) copy-start(bf16[256,256]{1,0:T(8,128)(2,1)} %constant.42.clone.refs_1_.eye.refs_3_.refs_5_) | copy-start | bytes 393220
  13.4 6.4 %copy-start.14 = (bf16[16,128]{1,0:T(8,128)(2,1)S(1)}, bf16[16,128]{1,0:T(8,128)(2,1)}, u32[]{:S(2)}) copy-start(bf16[16,128]{1,0:T(8,128)(2,1)} %constant.43.clone.join) | copy-start | bytes 12292
  19.8 10.8 %copy-start.8 = (bf16[16,32]{1,0:T(8,128)(2,1)S(1)}, bf16[16,32]{1,0:T(8,128)(2,1)}, u32[]{:S(2)}) copy-start(bf16[16,32]{1,0:T(8,128)(2,1)} %constant.44.clone.pick) | copy-start | bytes 3076
  34.0 7.0 %copy-start.21 = (bf16[81,8,256]{2,1,0:T(8,128)(2,1)S(1)}, bf16[81,8,256]{2,1,0:T(8,128)(2,1)}, u32[]{:S(2)}) copy-start(bf16[81,8,256]{2,1,0:T(8,128)(2,1)} %get-tuple-element.60) | copy-start | bytes 995332
  34.0 9.3 %copy-start.19 = (bf16[81,8,256]{2,1,0:T(8,128)(2,1)S(1)}, bf16[81,8,256]{2,1,0:T(8,128)(2,1)}, u32[]{:S(2)}) copy-start(bf16[81,8,256]{2,1,0:T(8,128)(2,1)} %get-tuple-element.61) | copy-start | bytes 995332
  34.0 12.2 %copy-start.11 = (bf16[128,1024]{1,0:T(8,128)(2,1)S(1)}, bf16[128,1024]{1,0:T(8,128)(2,1)}, u32[]{:S(2)}) copy-start(bf16[128,1024]{1,0:T(8,128)(2,1)} %constant.45.clone.ones) | copy-start | bytes 786436
  38.1 5.2 %collective-permute-start.2 = (bf16[320,128]{1,0:T(8,128)(2,1)}, bf16[320,128]{1,0:T(8,128)(2,1)S(1)}, u32[]{:S(2)}, u32[]{:S(2)}) collective-permute-start(bf16[320,128]{1,0:T(8,128)(2,1)} %get-tuple-element.48), channel_id=1, source_target_pairs={{0,1},{1,2},{2,3},{3,0},{4,5},{5,6},{6,7},{7,4},{8,9},{9,10},{10,1... | collective-permute-start | bytes 245768 | tf_op jit(solution)/shard_map/ppermute | solution.py:752
  39.5 14.4 %copy-start.1 = (bf16[320,640]{1,0:T(8,128)(2,1)S(1)}, bf16[320,640]{1,0:T(8,128)(2,1)}, u32[]{:S(2)}) copy-start(bf16[320,640]{1,0:T(8,128)(2,1)} %constant.46.clone.pick) | copy-start | bytes 1228804
  39.5 14.4 %collective-permute-start.3 = (bf16[320,128]{1,0:T(8,128)(2,1)}, bf16[320,128]{1,0:T(8,128)(2,1)S(1)}, u32[]{:S(2)}, u32[]{:S(2)}) collective-permute-start(bf16[320,128]{1,0:T(8,128)(2,1)} %get-tuple-element.49), channel_id=1, source_target_pairs={{0,3},{1,0},{2,1},{3,2},{4,7},{5,4},{6,5},{7,6},{8,11},{9,8},{10,9... | collective-permute-start | bytes 245768 | tf_op jit(solution)/shard_map/ppermute | solution.py:751
  41.0 21.8 %collective-permute-start.8 = (bf16[81,8,256]{2,1,0:T(8,128)(2,1)S(1)}, bf16[81,8,256]{2,1,0:T(8,128)(2,1)S(1)}, u32[]{:S(2)}, u32[]{:S(2)}) collective-permute-start(bf16[81,8,256]{2,1,0:T(8,128)(2,1)S(1)} %copy-done.21), channel_id=1, source_target_pairs={{0,16},{16,32},{32,48},{48,64},{64,80},{80,96},{96,112},{112,0},{1... | collective-permute-start | bytes 995336 | tf_op jit(solution)/shard_map/ppermute | solution.py:707
  43.2 10.6 %copy-start.5 = (bf16[320,128]{1,0:T(8,128)(2,1)}, bf16[320,128]{1,0:T(8,128)(2,1)S(1)}, u32[]{:S(2)}) copy-start(bf16[320,128]{1,0:T(8,128)(2,1)S(1)} %collective-permute-done.2.zlo.refs_0_) | copy-start | bytes 245764
  43.2 19.6 %collective-permute-start.9 = (bf16[81,8,256]{2,1,0:T(8,128)(2,1)S(1)}, bf16[81,8,256]{2,1,0:T(8,128)(2,1)S(1)}, u32[]{:S(2)}, u32[]{:S(2)}) collective-permute-start(bf16[81,8,256]{2,1,0:T(8,128)(2,1)S(1)} %copy-done.19), channel_id=1, source_target_pairs={{0,112},{16,0},{32,16},{48,32},{64,48},{80,64},{96,80},{112,96},{1... | collective-permute-start | bytes 995336 | tf_op jit(solution)/shard_map/ppermute | solution.py:707
  53.9 14.9 %copy-start.6 = (bf16[320,128]{1,0:T(8,128)(2,1)}, bf16[320,128]{1,0:T(8,128)(2,1)S(1)}, u32[]{:S(2)}) copy-start(bf16[320,128]{1,0:T(8,128)(2,1)S(1)} %collective-permute-done.3.zhi.refs_1_) | copy-start | bytes 245764
  54.1 14.6 %collective-permute-start.4 = (bf16[160,128]{1,0:T(8,128)(2,1)S(1)}, bf16[160,128]{1,0:T(8,128)(2,1)S(1)}, u32[]{:S(2)}, u32[]{:S(2)}) collective-permute-start(bf16[160,128]{1,0:T(8,128)(2,1)S(1)} %get-tuple-element.55), channel_id=1, source_target_pairs={{0,16},{16,32},{32,48},{48,64},{64,80},{80,96},{96,112},{112,0},{1... | collective-permute-start | bytes 122888 | tf_op jit(solution)/shard_map/ppermute | solution.py:757
  62.8 6.0 %collective-permute-start.5 = (bf16[160,128]{1,0:T(8,128)(2,1)S(1)}, bf16[160,128]{1,0:T(8,128)(2,1)S(1)}, u32[]{:S(2)}, u32[]{:S(2)}) collective-permute-start(bf16[160,128]{1,0:T(8,128)(2,1)S(1)} %get-tuple-element.56), channel_id=1, source_target_pairs={{0,112},{16,0},{32,16},{48,32},{64,48},{80,64},{96,80},{112,96},{1... | collective-permute-start | bytes 122888 | tf_op jit(solution)/shard_map/ppermute | solution.py:758
  69.4 50.0 %copy-start = (bf16[81,4096]{1,0:T(8,128)(2,1)S(1)}, bf16[81,4096]{1,0:T(8,128)(2,1)}, u32[]{:S(2)}) copy-start(bf16[81,4096]{1,0:T(8,128)(2,1)} %transfer.1) | copy-start | bytes 1990660
  69.4 50.0 %copy-start.2 = (bf16[1024,128]{1,0:T(8,128)(2,1)S(1)}, bf16[1024,128]{1,0:T(8,128)(2,1)}, u32[]{:S(2)}) copy-start(bf16[1024,128]{1,0:T(8,128)(2,1)} %constant.49.clone.wide) | copy-start | bytes 786436
  69.4 50.0 %copy-start.3 = (bf16[1024,81]{1,0:T(8,128)(2,1)S(1)}, bf16[1024,81]{1,0:T(8,128)(2,1)}, u32[]{:S(2)}) copy-start(bf16[1024,81]{1,0:T(8,128)(2,1)} %constant.48.clone.basis) | copy-start | bytes 497668
  69.4 50.1 %copy-start.4 = (bf16[81,1024]{1,0:T(8,128)(2,1)S(1)}, bf16[81,1024]{1,0:T(8,128)(2,1)}, u32[]{:S(2)}) copy-start(bf16[81,1024]{1,0:T(8,128)(2,1)} %constant.50.clone.projector) | copy-start | bytes 497668
  (11 other events, 20.0 us)

commit v9 on v8

--- a/solution.py
+++ b/solution.py
@@ -208,10 +208,11 @@
             refs.pop(0)
         inputs = [refs.pop(0) for _ in arrays]
         shared = [refs.pop(0) for _ in halves]
-        eye = refs.pop(0)
+        eye_in = refs.pop(0)
         table = refs.pop(0)
         edges = [refs.pop(0) for _ in range(2)] if edge_lines else []
-        buf, sems, spread = refs[:3]
+        eye, eye_sem, buf, sems, spread = refs[:5]
+        refs = refs[2:]
         copies = []
         for p, ((_, at), place) in enumerate(zip(planes, places)):
             ref = inputs[place] if at is None else inputs[place].at[:, at]
@@ -220,6 +221,9 @@
             copies.append(pltpu.make_async_copy(piece, refs[3].at[q], refs[4].at[q]))
         for copy in copies:
             copy.start()
+        eye_copy = pltpu.make_async_copy(eye_in, eye, eye_sem)
+        eye_copy.start()
+        eye_copy.wait()
 
         def turn(p):
             def put(y, block):
@@ -275,6 +279,8 @@
     if edge_lines:
         shapes += [jax.ShapeDtypeStruct((HALO * edge_lines, LANES), jnp.bfloat16)] * 2
     scratch = [
+        pltpu.VMEM(eye.shape, eye.dtype),
+        pltpu.SemaphoreType.DMA(()),
         pltpu.VMEM((count, coeffs, cells_y, cells_z), jnp.bfloat16),
         pltpu.SemaphoreType.DMA((count,)),
         spread_shape(coeffs, cells_y, cells_z),
@@ -288,7 +294,7 @@
     return pl.pallas_call(
         kernel,
         out_shape=shapes,
-        in_specs=[vmem] * len(held) + [hbm] * (len(arrays) + len(halves)) + [vmem],
+        in_specs=[vmem] * len(held) + [hbm] * (len(arrays) + len(halves) + 1),
         out_specs=[vmem] * len(shapes),
         scratch_shapes=scratch,
         input_output_aliases={} if new else {0: 0},
@@ -509,8 +515,10 @@
     pairs = count // 32
     half = LANES // 2
 
-    def kernel(index, wide, pick, *refs):
-        table, out, local, sems, near, near_sems, rows, staged, out_sems = refs[len(edges) + 1 :]
+    def kernel(index, wide, pick_in, *refs):
+        scratch = refs[len(edges) + 1 :]
+        table, out, local, sems, near, near_sems, rows, staged, out_sems = scratch[:9]
+        side_sems, pick, *held = scratch[9:]
         sublane = lax.broadcasted_iota(jnp.int32, (GROUP, LANES), 0)
         masks = [sublane == k for k in range(GROUP)]
         used = lax.broadcasted_iota(jnp.int32, (GROUP, LANES), 1) < coeffs
@@ -557,8 +565,17 @@
         for b in range(STREAM - 1):
             stream(b, b).start()
 
+        sides = [
+            pltpu.make_async_copy(source, target, side_sems.at[i])
+            for i, (source, target) in enumerate(zip(refs[: len(edges)], held))
+        ]
+        sides.append(pltpu.make_async_copy(pick_in, pick, side_sems.at[len(edges)]))
+        for side in sides:
+            side.start()
+        for side in sides:
+            side.wait()
         at = first_edge
-        for edge in refs[: len(edges)]:
+        for edge in held:
             table[pl.ds(at, edge.shape[0]), :] = edge[...].astype(jnp.float32)
             at += edge.shape[0]
 
@@ -624,7 +641,7 @@
             pltpu.VMEM(table.shape, jnp.float32),
             pltpu.HBM((pairs, 24, LANES), jnp.bfloat16),
         ),
-        in_specs=[pl.BlockSpec(memory_space=pl.ANY)] * 2 + [vmem] * (2 + len(edges)),
+        in_specs=[pl.BlockSpec(memory_space=pl.ANY)] * (3 + len(edges)) + [vmem],
         out_specs=(vmem, pl.BlockSpec(memory_space=pl.ANY)),
         scratch_shapes=[
             pltpu.SMEM((RING, CHUNK), jnp.int32),
@@ -634,6 +651,9 @@
             pltpu.VMEM((4, pairs * GROUP, LANES), jnp.float32),
             pltpu.VMEM((pairs, 24, LANES), jnp.bfloat16),
             pltpu.SemaphoreType.DMA((chunks,)),
+            pltpu.SemaphoreType.DMA((len(edges) + 1,)),
+            pltpu.VMEM(pick.shape, jnp.bfloat16),
+            *(pltpu.VMEM(edge.shape, edge.dtype) for edge in edges),
         ],
         input_output_aliases={3 + len(edges): 0},
         compiler_params=pltpu.CompilerParams(vmem_limit_bytes=24 * MIB),

time: 127 us -> 127 us (level)
  no operation moved by 1% of the time
where the time goes in v9:
time: 127 us
  Pallas kernels  72.4 us (57%)
  blocking collectives  25.1 us (20%)
  starting transfers between devices  13.3 us (10%)
  waiting for transfers between devices  11.5 us (9%)
  local copies, waits for them, and re-layouts  4.33 us (3%)
    all_to_all x1, blocking collectives, halo_step(): lax.all_to_all(outgoing, ('gx', 'gy', 'gz'), split_axis=0, concat_axis=0,...  25.1 us
    pallas_call x1, Pallas kernels, gather_rows(): pl.pallas_call(kernel, out_shape=(pltpu.VMEM(table.shape, jnp.float32), p...  25 us
    pallas_call x3, Pallas kernels, add_planes(): pl.pallas_call(kernel, out_shape=shapes, in_specs=[vmem] * len(held) + [h...  14.8 us
    ppermute x6, starting transfers between devices, shift(): lax.ppermute(array, axis, pairs)  10.4 us
    ppermute x6, waiting for transfers between devices, shift(): lax.ppermute(array, axis, pairs)  9.28 us
    pallas_call x1, Pallas kernels, prepare(): pl.pallas_call(kernel, out_shape=(jax.ShapeDtypeStruct((count * SAMPLES /...  9.08 us
    pallas_call x1, Pallas kernels, spread_weights(): pl.pallas_call(kernel, out_shape=pltpu.HBM((count * SAMPLES, LANES), jnp....  7.68 us
    pallas_call x1, Pallas kernels, relight(): pl.pallas_call(kernel, out_shape=jax.ShapeDtypeStruct((coeffs, count), jn...  7.53 us
  transfers between devices with their start and end apart: 10, of which 2 were waited for; matrix products, arithmetic and copies ran while one was open for 0% of the time, Pallas kernels for 28%

profile of v9, /device:TPU:1, one launch (start us, length us, event | category | flops | bytes accessed | tf_op | source)
XLA Modules:
  0.0 127.0 jit_solution(3637389100991792708)
XLA Ops:
  0.0 0.7 copy-done.7
  0.7 4.6 %cut_faces.1 = (bf16[81,2,16,256]{3,2,1,0:T(8,128)(2,1)}, bf16[81,2,16,256]{3,2,1,0:T(8,128)(2,1)}, bf16[81,16,256]{2,1,0:T(8,128)(2,1)}, bf16[81,16,256]{2,1,0:T(8,128)(2,1)}) custom-call(bf16[81,8,16,256]{3,2,1,0:T(8,128)(2,1)} %field.1, bf16[32,128]{1,0:T(8,128)(2,1)S(1)} %copy-done.7), custom_call_target="tpu_custom_call" | custom-call | tf_op jit(solution)/shard_map/cut_faces/pallas_call | solution.py:143
  5.3 4.2 %collective-permute-start = (bf16[81,16,256]{2,1,0:T(8,128)(2,1)}, bf16[81,16,256]{2,1,0:T(8,128)(2,1)S(1)}, u32[]{:S(2)}, u32[]{:S(2)}) collective-permute-start(bf16[81,16,256]{2,1,0:T(8,128)(2,1)} %get-tuple-element.39), channel_id=1, source_target_pairs={{0,4},{4,8},{8,12},{12,0},{1,5},{5,9},{9,13},{13,1},{2,6},{6,10},{... | collective-permute-start | bytes 1990664 | tf_op jit(solution)/shard_map/ppermute | solution.py:727
  9.5 1.6 %collective-permute-start.6 = (bf16[81,2,16,256]{3,2,1,0:T(8,128)(2,1)}, bf16[81,2,16,256]{3,2,1,0:T(8,128)(2,1)S(1)}, u32[]{:S(2)}, u32[]{:S(2)}) collective-permute-start(bf16[81,2,16,256]{3,2,1,0:T(8,128)(2,1)} %get-tuple-element.58), channel_id=1, source_target_pairs={{0,16},{16,32},{32,48},{48,64},{64,80},{80,96},{96,112},{112,0},{1... | collective-permute-start | bytes 3981320 | tf_op jit(solution)/shard_map/ppermute | solution.py:727
  11.2 2.2 %collective-permute-start.7 = (bf16[81,2,16,256]{3,2,1,0:T(8,128)(2,1)}, bf16[81,2,16,256]{3,2,1,0:T(8,128)(2,1)}, u32[]{:S(2)}, u32[]{:S(2)}) collective-permute-start(bf16[81,2,16,256]{3,2,1,0:T(8,128)(2,1)} %get-tuple-element.59), channel_id=1, source_target_pairs={{0,112},{16,0},{32,16},{48,32},{64,48},{80,64},{96,80},{112,96},{1... | collective-permute-start | bytes 3981320 | tf_op jit(solution)/shard_map/ppermute | solution.py:727
  13.4 6.9 %shard_map.154.refs_0_ = f32[62400,128]{1,0:T(8,128)S(1)} custom-call(bf16[81,8,16,256]{3,2,1,0:T(8,128)(2,1)} %field.1, bf16[256,256]{1,0:T(8,128)(2,1)} %constant.42.clone.refs_1_.eye.refs_3_.refs_5_), custom_call_target="tpu_custom_call" | custom-call | flops 20000000000 | bytes 20000000 | tf_op jit(solution)/shard_map/pallas_call | solution.py:294
  20.4 9.1 %prepare.1 = (s32[256,128]{1,0:T(8,128)S(1)}, f32[4096,128]{1,0:T(8,128)S(1)}) custom-call(s32[3]{0:T(128)S(1)} %pad_add_fusion.origin, s32[4096]{0:T(1024)S(1)} %bitcast.5, s32[3,8,4096]{2,1,0:T(8,128)S(1)} %copy-done.9, f32[8,4096]{1,0:T(8,128)S(1)} %copy-done.10, bf16[256,256]{1,0:T(8,128)(2,1)S(1)} %copy-done.12, bf16[16,128]{1,0:T(8,128)(2,1)S(1)} %copy-done.14), custom_call_target="tpu_custom_call" | custom-call | flops 20000000000 | bytes 3000000 | tf_op jit(solution)/shard_map/prepare/pallas_call | solution.py:443
  29.5 0.7 copy-done.13
  30.1 0.8 copy-done.15
  31.2 3.3 %cut_corners.1 = (bf16[81,8,256]{2,1,0:T(8,128)(2,1)}, bf16[81,8,256]{2,1,0:T(8,128)(2,1)}) custom-call(bf16[81,16,256]{2,1,0:T(8,128)(2,1)} %copy-done.15, bf16[81,16,256]{2,1,0:T(8,128)(2,1)} %copy-done.16, bf16[16,32]{1,0:T(8,128)(2,1)S(1)} %copy-done.8), custom_call_target="tpu_custom_call" | custom-call | tf_op jit(solution)/shard_map/cut_corners/pallas_call | solution.py:183
  34.6 3.4 %shard_map.155 = (f32[62400,128]{1,0:T(8,128)S(1)}, bf16[320,128]{1,0:T(8,128)(2,1)}, bf16[320,128]{1,0:T(8,128)(2,1)}) custom-call(f32[62400,128]{1,0:T(8,128)S(1)} %shard_map.154.refs_0_, bf16[81,16,256]{2,1,0:T(8,128)(2,1)} %copy-done.15, bf16[81,16,256]{2,1,0:T(8,128)(2,1)} %copy-done.16, ...), custom_call_target="tpu_custom_call", output_to_operand_aliasing={{0}: (0, {})} | custom-call | flops 20000000000 | bytes 20000000 | tf_op jit(solution)/shard_map/pallas_call | solution.py:294
  38.0 1.4 %collective-permute-start.2 = (bf16[320,128]{1,0:T(8,128)(2,1)}, bf16[320,128]{1,0:T(8,128)(2,1)S(1)}, u32[]{:S(2)}, u32[]{:S(2)}) collective-permute-start(bf16[320,128]{1,0:T(8,128)(2,1)} %get-tuple-element.48), channel_id=1, source_target_pairs={{0,1},{1,2},{2,3},{3,0},{4,5},{5,6},{6,7},{7,4},{8,9},{9,10},{10,1... | collective-permute-start | bytes 245768 | tf_op jit(solution)/shard_map/ppermute | solution.py:772
  39.3 1.5 %collective-permute-start.3 = (bf16[320,128]{1,0:T(8,128)(2,1)}, bf16[320,128]{1,0:T(8,128)(2,1)S(1)}, u32[]{:S(2)}, u32[]{:S(2)}) collective-permute-start(bf16[320,128]{1,0:T(8,128)(2,1)} %get-tuple-element.49), channel_id=1, source_target_pairs={{0,3},{1,0},{2,1},{3,2},{4,7},{5,4},{6,5},{7,6},{8,11},{9,8},{10,9... | collective-permute-start | bytes 245768 | tf_op jit(solution)/shard_map/ppermute | solution.py:771
  40.9 2.2 %collective-permute-done.2.zlo.refs_0_ = bf16[320,128]{1,0:T(8,128)(2,1)S(1)} collective-permute-done((bf16[320,128]{1,0:T(8,128)(2,1)}, bf16[320,128]{1,0:T(8,128)(2,1)S(1)}, u32[]{:S(2)}, u32[]{:S(2)}) %collective-permute-start.2) | collective-permute-done | bytes 81952 | tf_op jit(solution)/shard_map/ppermute | solution.py:772
  43.1 2.4 %collective-permute-start.9 = (bf16[81,8,256]{2,1,0:T(8,128)(2,1)S(1)}, bf16[81,8,256]{2,1,0:T(8,128)(2,1)S(1)}, u32[]{:S(2)}, u32[]{:S(2)}) collective-permute-start(bf16[81,8,256]{2,1,0:T(8,128)(2,1)S(1)} %copy-done.19), channel_id=1, source_target_pairs={{0,112},{16,0},{32,16},{48,32},{64,48},{80,64},{96,80},{112,96},{1... | collective-permute-start | bytes 995336 | tf_op jit(solution)/shard_map/ppermute | solution.py:727
  45.5 7.7 %spread_weights.1.wide = f32[32768,128]{1,0:T(8,128)} custom-call(f32[4096,128]{1,0:T(8,128)S(1)} %get-tuple-element.51.ordered, bf16[128,1024]{1,0:T(8,128)(2,1)S(1)} %copy-done.11), custom_call_target="tpu_custom_call" | custom-call | flops 10000000000 | bytes 3000000 | tf_op jit(solution)/shard_map/spread_weights/pallas_call | solution.py:488
  53.5 9.3 %collective-permute-done.8.refs_3_ = bf16[81,8,256]{2,1,0:T(8,128)(2,1)S(1)} collective-permute-done((bf16[81,8,256]{2,1,0:T(8,128)(2,1)S(1)}, bf16[81,8,256]{2,1,0:T(8,128)(2,1)S(1)}, u32[]{:S(2)}, u32[]{:S(2)}) %collective-permute-start.8) | collective-permute-done | bytes 331808 | tf_op jit(solution)/shard_map/ppermute | solution.py:727
  62.9 0.7 copy-done.20
  63.7 0.4 copy-done.18
  64.1 4.6 %shard_map.156.refs_4_ = f32[62400,128]{1,0:T(8,128)S(1)} custom-call(f32[62400,128]{1,0:T(8,128)S(1)} %get-tuple-element.57.refs_0_, bf16[81,2,16,256]{3,2,1,0:T(8,128)(2,1)} %copy-done.18, bf16[81,2,16,256]{3,2,1,0:T(8,128)(2,1)} %collective-permute-done.7.refs_2_, bf16[81,8,256]{2,1,0:T(8,128)(2,1)} %copy-done.20, ...), custom_call_target="tpu_custom_call", output_to_operand_aliasing={{}: (0, {})} | custom-call | flops 20000000000 | bytes 20000000 | tf_op jit(solution)/shard_map/pallas_call | solution.py:294
  68.7 0.6 copy-done.23
  69.4 25.0 %gather_rows.1 = (f32[62400,128]{1,0:T(8,128)S(1)}, bf16[128,24,128]{2,1,0:T(8,128)(2,1)}) custom-call(s32[32768]{0:T(1024)} %bitcast.6, f32[32768,128]{1,0:T(8,128)} %spread_weights.1.wide, bf16[3,256,128]{2,1,0:T(8,128)(2,1)} %constant.47.clone.pick_in, bf16[320,128]{1,0:T(8,128)(2,1)} %copy-done.5, ...), custom_call_target="tpu_custom_call", output_to_operand_aliasing={{0}: (7, {})} | custom-call | flops 40000000000 | bytes 20000000 | tf_op jit(solution)/shard_map/gather_rows/pallas_call | solution.py:638
  94.3 25.1 %all_to_all.5.routed = bf16[128,24,128]{2,1,0:T(8,128)(2,1)S(1)} all-to-all(bf16[128,24,128]{2,1,0:T(8,128)(2,1)} %get-tuple-element.62), channel_id=1, replica_groups=mesh['gx'=8,'gy'=4,'gz'=4] {'gx','gy','gz'}, dimensions={0} | all-to-all | bytes 1572864 | tf_op jit(solution)/shard_map/all_to_all | solution.py:784
  119.5 7.5 %relight.1 = bf16[81,4096]{1,0:T(8,128)(2,1)} custom-call(bf16[81,4096]{1,0:T(8,128)(2,1)S(1)} %copy-done, bf16[128,24,128]{2,1,0:T(8,128)(2,1)S(1)} %all_to_all.5.routed, bf16[1024,81]{1,0:T(8,128)(2,1)S(1)} %copy-done.3, bf16[1024,128]{1,0:T(8,128)(2,1)S(1)} %copy-done.2, bf16[81,1024]{1,0:T(8,128)(2,1)S(1)} %copy-done.4), custom_call_target="tpu_custom_call" | custom-call | tf_op jit(solution)/shard_map/relight/pallas_call | solution.py:700
  (59 shorter events, 0.9 us)
Async XLA Ops:
  0.7 12.6 %copy-start.17 = (s32[2,4096]{1,0:T(2,128)S(1)}, s32[2,4096]{1,0:T(2,128)}, u32[]{:S(2)}) copy-start(s32[2,4096]{1,0:T(2,128)} %param.19) | copy-start | bytes 98308
  5.3 24.8 %collective-permute-start = (bf16[81,16,256]{2,1,0:T(8,128)(2,1)}, bf16[81,16,256]{2,1,0:T(8,128)(2,1)S(1)}, u32[]{:S(2)}, u32[]{:S(2)}) collective-permute-start(bf16[81,16,256]{2,1,0:T(8,128)(2,1)} %get-tuple-element.39), channel_id=1, source_target_pairs={{0,4},{4,8},{8,12},{12,0},{1,5},{5,9},{9,13},{13,1},{2,6},{6,10},{... | collective-permute-start | bytes 1990664 | tf_op jit(solution)/shard_map/ppermute | solution.py:727
  9.5 20.6 %collective-permute-start.1 = (bf16[81,16,256]{2,1,0:T(8,128)(2,1)}, bf16[81,16,256]{2,1,0:T(8,128)(2,1)S(1)}, u32[]{:S(2)}, u32[]{:S(2)}) collective-permute-start(bf16[81,16,256]{2,1,0:T(8,128)(2,1)} %get-tuple-element.40), channel_id=1, source_target_pairs={{0,12},{4,0},{8,4},{12,8},{1,13},{5,1},{9,5},{13,9},{2,14},{6,2},{... | collective-permute-start | bytes 1990664 | tf_op jit(solution)/shard_map/ppermute | solution.py:727
  9.5 53.3 %collective-permute-start.6 = (bf16[81,2,16,256]{3,2,1,0:T(8,128)(2,1)}, bf16[81,2,16,256]{3,2,1,0:T(8,128)(2,1)S(1)}, u32[]{:S(2)}, u32[]{:S(2)}) collective-permute-start(bf16[81,2,16,256]{3,2,1,0:T(8,128)(2,1)} %get-tuple-element.58), channel_id=1, source_target_pairs={{0,16},{16,32},{32,48},{48,64},{64,80},{80,96},{96,112},{112,0},{1... | collective-permute-start | bytes 3981320 | tf_op jit(solution)/shard_map/ppermute | solution.py:727
  11.2 51.7 %collective-permute-start.7 = (bf16[81,2,16,256]{3,2,1,0:T(8,128)(2,1)}, bf16[81,2,16,256]{3,2,1,0:T(8,128)(2,1)}, u32[]{:S(2)}, u32[]{:S(2)}) collective-permute-start(bf16[81,2,16,256]{3,2,1,0:T(8,128)(2,1)} %get-tuple-element.59), channel_id=1, source_target_pairs={{0,112},{16,0},{32,16},{48,32},{64,48},{80,64},{96,80},{112,96},{1... | collective-permute-start | bytes 3981320 | tf_op jit(solution)/shard_map/ppermute | solution.py:727
  13.4 6.9 %copy-start.10 = (f32[8,4096]{1,0:T(8,128)S(1)}, f32[8,4096]{1,0:T(8,128)}, u32[]{:S(2)}) copy-start(f32[8,4096]{1,0:T(8,128)} %weights.1) | copy-start | bytes 393220
  13.4 6.9 %copy-start.12 = (bf16[256,256]{1,0:T(8,128)(2,1)S(1)}, bf16[256,256]{1,0:T(8,128)(2,1)}, u32[]{:S(2)}) copy-start(bf16[256,256]{1,0:T(8,128)(2,1)} %constant.42.clone.refs_1_.eye.refs_3_.refs_5_) | copy-start | bytes 393220
  13.4 6.9 %copy-start.14 = (bf16[16,128]{1,0:T(8,128)(2,1)S(1)}, bf16[16,128]{1,0:T(8,128)(2,1)}, u32[]{:S(2)}) copy-start(bf16[16,128]{1,0:T(8,128)(2,1)} %constant.43.clone.join) | copy-start | bytes 12292
  20.4 10.8 %copy-start.8 = (bf16[16,32]{1,0:T(8,128)(2,1)S(1)}, bf16[16,32]{1,0:T(8,128)(2,1)}, u32[]{:S(2)}) copy-start(bf16[16,32]{1,0:T(8,128)(2,1)} %constant.44.clone.pick) | copy-start | bytes 3076
  34.5 8.6 %copy-start.19 = (bf16[81,8,256]{2,1,0:T(8,128)(2,1)S(1)}, bf16[81,8,256]{2,1,0:T(8,128)(2,1)}, u32[]{:S(2)}) copy-start(bf16[81,8,256]{2,1,0:T(8,128)(2,1)} %get-tuple-element.61) | copy-start | bytes 995332
  34.5 10.9 %copy-start.11 = (bf16[128,1024]{1,0:T(8,128)(2,1)S(1)}, bf16[128,1024]{1,0:T(8,128)(2,1)}, u32[]{:S(2)}) copy-start(bf16[128,1024]{1,0:T(8,128)(2,1)} %constant.45.clone.ones) | copy-start | bytes 786436
  38.0 5.1 %collective-permute-start.2 = (bf16[320,128]{1,0:T(8,128)(2,1)}, bf16[320,128]{1,0:T(8,128)(2,1)S(1)}, u32[]{:S(2)}, u32[]{:S(2)}) collective-permute-start(bf16[320,128]{1,0:T(8,128)(2,1)} %get-tuple-element.48), channel_id=1, source_target_pairs={{0,1},{1,2},{2,3},{3,0},{4,5},{5,6},{6,7},{7,4},{8,9},{9,10},{10,1... | collective-permute-start | bytes 245768 | tf_op jit(solution)/shard_map/ppermute | solution.py:772
  39.3 13.9 %copy-start.1 = (bf16[320,640]{1,0:T(8,128)(2,1)S(1)}, bf16[320,640]{1,0:T(8,128)(2,1)}, u32[]{:S(2)}) copy-start(bf16[320,640]{1,0:T(8,128)(2,1)} %constant.46.clone.pick) | copy-start | bytes 1228804
  39.3 13.8 %collective-permute-start.3 = (bf16[320,128]{1,0:T(8,128)(2,1)}, bf16[320,128]{1,0:T(8,128)(2,1)S(1)}, u32[]{:S(2)}, u32[]{:S(2)}) collective-permute-start(bf16[320,128]{1,0:T(8,128)(2,1)} %get-tuple-element.49), channel_id=1, source_target_pairs={{0,3},{1,0},{2,1},{3,2},{4,7},{5,4},{6,5},{7,6},{8,11},{9,8},{10,9... | collective-permute-start | bytes 245768 | tf_op jit(solution)/shard_map/ppermute | solution.py:771
  40.9 22.0 %collective-permute-start.8 = (bf16[81,8,256]{2,1,0:T(8,128)(2,1)S(1)}, bf16[81,8,256]{2,1,0:T(8,128)(2,1)S(1)}, u32[]{:S(2)}, u32[]{:S(2)}) collective-permute-start(bf16[81,8,256]{2,1,0:T(8,128)(2,1)S(1)} %copy-done.21), channel_id=1, source_target_pairs={{0,16},{16,32},{32,48},{48,64},{64,80},{80,96},{96,112},{112,0},{1... | collective-permute-start | bytes 995336 | tf_op jit(solution)/shard_map/ppermute | solution.py:727
  43.1 10.1 %copy-start.5 = (bf16[320,128]{1,0:T(8,128)(2,1)}, bf16[320,128]{1,0:T(8,128)(2,1)S(1)}, u32[]{:S(2)}) copy-start(bf16[320,128]{1,0:T(8,128)(2,1)S(1)} %collective-permute-done.2.zlo.refs_0_) | copy-start | bytes 245764
  43.1 19.7 %collective-permute-start.9 = (bf16[81,8,256]{2,1,0:T(8,128)(2,1)S(1)}, bf16[81,8,256]{2,1,0:T(8,128)(2,1)S(1)}, u32[]{:S(2)}, u32[]{:S(2)}) collective-permute-start(bf16[81,8,256]{2,1,0:T(8,128)(2,1)S(1)} %copy-done.19), channel_id=1, source_target_pairs={{0,112},{16,0},{32,16},{48,32},{64,48},{80,64},{96,80},{112,96},{1... | collective-permute-start | bytes 995336 | tf_op jit(solution)/shard_map/ppermute | solution.py:727
  53.2 15.5 %copy-start.6 = (bf16[320,128]{1,0:T(8,128)(2,1)}, bf16[320,128]{1,0:T(8,128)(2,1)S(1)}, u32[]{:S(2)}) copy-start(bf16[320,128]{1,0:T(8,128)(2,1)S(1)} %collective-permute-done.3.zhi.refs_1_) | copy-start | bytes 245764
  53.5 15.2 %collective-permute-start.4 = (bf16[160,128]{1,0:T(8,128)(2,1)S(1)}, bf16[160,128]{1,0:T(8,128)(2,1)S(1)}, u32[]{:S(2)}, u32[]{:S(2)}) collective-permute-start(bf16[160,128]{1,0:T(8,128)(2,1)S(1)} %get-tuple-element.55), channel_id=1, source_target_pairs={{0,16},{16,32},{32,48},{48,64},{64,80},{80,96},{96,112},{112,0},{1... | collective-permute-start | bytes 122888 | tf_op jit(solution)/shard_map/ppermute | solution.py:777
  62.8 5.9 %collective-permute-start.5 = (bf16[160,128]{1,0:T(8,128)(2,1)S(1)}, bf16[160,128]{1,0:T(8,128)(2,1)S(1)}, u32[]{:S(2)}, u32[]{:S(2)}) collective-permute-start(bf16[160,128]{1,0:T(8,128)(2,1)S(1)} %get-tuple-element.56), channel_id=1, source_target_pairs={{0,112},{16,0},{32,16},{48,32},{64,48},{80,64},{96,80},{112,96},{1... | collective-permute-start | bytes 122888 | tf_op jit(solution)/shard_map/ppermute | solution.py:778
  69.3 50.1 %copy-start = (bf16[81,4096]{1,0:T(8,128)(2,1)S(1)}, bf16[81,4096]{1,0:T(8,128)(2,1)}, u32[]{:S(2)}) copy-start(bf16[81,4096]{1,0:T(8,128)(2,1)} %transfer.1) | copy-start | bytes 1990660
  69.3 50.1 %copy-start.2 = (bf16[1024,128]{1,0:T(8,128)(2,1)S(1)}, bf16[1024,128]{1,0:T(8,128)(2,1)}, u32[]{:S(2)}) copy-start(bf16[1024,128]{1,0:T(8,128)(2,1)} %constant.49.clone.wide) | copy-start | bytes 786436
  69.3 50.1 %copy-start.3 = (bf16[1024,81]{1,0:T(8,128)(2,1)S(1)}, bf16[1024,81]{1,0:T(8,128)(2,1)}, u32[]{:S(2)}) copy-start(bf16[1024,81]{1,0:T(8,128)(2,1)} %constant.48.clone.basis) | copy-start | bytes 497668
  69.3 50.1 %copy-start.4 = (bf16[81,1024]{1,0:T(8,128)(2,1)S(1)}, bf16[81,1024]{1,0:T(8,128)(2,1)}, u32[]{:S(2)}) copy-start(bf16[81,1024]{1,0:T(8,128)(2,1)} %constant.50.clone.projector) | copy-start | bytes 497668
  (11 other events, 20.5 us)

commit v10 on v8

--- a/solution.py
+++ b/solution.py
@@ -92,7 +92,9 @@
     per_part = coeffs // parts
     rows = cells_x * HALO
 
-    def kernel(field, pick, last, first, top, bottom, buf, high, low, sems, out_sems):
+    def kernel(field, pick_in, last, first, top, bottom, *scratch):
+        buf, high, low, sems, out_sems, pick, pick_sem = scratch
+
         def load(i):
             here = pl.ds(i * per_part, per_part)
             return pltpu.make_async_copy(field.at[here], buf.at[here], sems.at[i])
@@ -110,8 +112,11 @@
                 ),
             ]
 
+        choice = pltpu.make_async_copy(pick_in, pick, pick_sem)
+        choice.start()
         for i in range(parts):
             load(i).start()
+        choice.wait()
 
         def body(i, _):
             load(i).wait()
@@ -143,7 +148,7 @@
     return pl.pallas_call(
         kernel,
         out_shape=[pltpu.HBM(shape, jnp.bfloat16) for shape in shapes],
-        in_specs=[hbm, pl.BlockSpec(memory_space=pltpu.VMEM)],
+        in_specs=[hbm, hbm],
         out_specs=[hbm] * 4,
         scratch_shapes=[
             pltpu.VMEM(field.shape, jnp.bfloat16),
@@ -151,10 +156,15 @@
             pltpu.VMEM((coeffs, rows, cells_z), jnp.bfloat16),
             pltpu.SemaphoreType.DMA((parts,)),
             pltpu.SemaphoreType.DMA((4, parts)),
+            pltpu.VMEM(pick.shape, jnp.bfloat16),
+            pltpu.SemaphoreType.DMA(()),
         ],
         compiler_params=pltpu.CompilerParams(vmem_limit_bytes=16 * MIB),
         name="cut_faces",
-    )(field, jnp.asarray(pick.astype(jnp.bfloat16)))
+    )(
+        field,
+        pltpu.with_memory_space_constraint(jnp.asarray(pick.astype(jnp.bfloat16)), pltpu.HBM),
+    )
 
 
 def cut_corners(ylo, yhi):
@@ -208,10 +218,11 @@
             refs.pop(0)
         inputs = [refs.pop(0) for _ in arrays]
         shared = [refs.pop(0) for _ in halves]
-        eye = refs.pop(0)
+        eye_in = refs.pop(0)
         table = refs.pop(0)
         edges = [refs.pop(0) for _ in range(2)] if edge_lines else []
-        buf, sems, spread = refs[:3]
+        eye, eye_sem, buf, sems, spread = refs[:5]
+        refs = refs[2:]
         copies = []
         for p, ((_, at), place) in enumerate(zip(planes, places)):
             ref = inputs[place] if at is None else inputs[place].at[:, at]
@@ -220,6 +231,9 @@
             copies.append(pltpu.make_async_copy(piece, refs[3].at[q], refs[4].at[q]))
         for copy in copies:
             copy.start()
+        eye_copy = pltpu.make_async_copy(eye_in, eye, eye_sem)
+        eye_copy.start()
+        eye_copy.wait()
 
         def turn(p):
             def put(y, block):
@@ -275,6 +289,8 @@
     if edge_lines:
         shapes += [jax.ShapeDtypeStruct((HALO * edge_lines, LANES), jnp.bfloat16)] * 2
     scratch = [
+        pltpu.VMEM(eye.shape, eye.dtype),
+        pltpu.SemaphoreType.DMA(()),
         pltpu.VMEM((count, coeffs, cells_y, cells_z), jnp.bfloat16),
         pltpu.SemaphoreType.DMA((count,)),
         spread_shape(coeffs, cells_y, cells_z),
@@ -288,7 +304,7 @@
     return pl.pallas_call(
         kernel,
         out_shape=shapes,
-        in_specs=[vmem] * len(held) + [hbm] * (len(arrays) + len(halves)) + [vmem],
+        in_specs=[vmem] * len(held) + [hbm] * (len(arrays) + len(halves) + 1),
         out_specs=[vmem] * len(shapes),
         scratch_shapes=scratch,
         input_output_aliases={} if new else {0: 0},

time: 127 us -> 127 us (level)
    unnamed x50 -> x48, local copies, waits for them, and re-layouts: 4.33 us -> 3.65 us
where the time goes in v10:
time: 127 us
  Pallas kernels  73 us (57%)
  blocking collectives  25.1 us (20%)
  starting transfers between devices  13.3 us (10%)
  waiting for transfers between devices  11.5 us (9%)
  local copies, waits for them, and re-layouts  3.65 us (3%)
    all_to_all x1, blocking collectives, halo_step(): lax.all_to_all(outgoing, ('gx', 'gy', 'gz'), split_axis=0, concat_axis=0,...  25.1 us
    pallas_call x1, Pallas kernels, gather_rows(): pl.pallas_call(kernel, out_shape=(pltpu.VMEM(table.shape, jnp.float32), p...  24.9 us
    pallas_call x3, Pallas kernels, add_planes(): pl.pallas_call(kernel, out_shape=shapes, in_specs=[vmem] * len(held) + [h...  14.9 us
    ppermute x6, starting transfers between devices, shift(): lax.ppermute(array, axis, pairs)  10.4 us
    ppermute x6, waiting for transfers between devices, shift(): lax.ppermute(array, axis, pairs)  9.23 us
    pallas_call x1, Pallas kernels, prepare(): pl.pallas_call(kernel, out_shape=(jax.ShapeDtypeStruct((count * SAMPLES /...  9.08 us
    pallas_call x1, Pallas kernels, spread_weights(): pl.pallas_call(kernel, out_shape=pltpu.HBM((count * SAMPLES, LANES), jnp....  7.68 us
    pallas_call x1, Pallas kernels, relight(): pl.pallas_call(kernel, out_shape=jax.ShapeDtypeStruct((coeffs, count), jn...  7.55 us
  transfers between devices with their start and end apart: 10, of which 2 were waited for; matrix products, arithmetic and copies ran while one was open for 0% of the time, Pallas kernels for 28%

profile of v10, /device:TPU:1, one launch (start us, length us, event | category | flops | bytes accessed | tf_op | source)
XLA Modules:
  0.0 126.9 jit_solution(14224588600138736734)
XLA Ops:
  0.0 5.3 %cut_faces.1 = (bf16[81,2,16,256]{3,2,1,0:T(8,128)(2,1)}, bf16[81,2,16,256]{3,2,1,0:T(8,128)(2,1)}, bf16[81,16,256]{2,1,0:T(8,128)(2,1)}, bf16[81,16,256]{2,1,0:T(8,128)(2,1)}) custom-call(bf16[81,8,16,256]{3,2,1,0:T(8,128)(2,1)} %field.1, bf16[32,128]{1,0:T(8,128)(2,1)} %constant.41.clone.pick_in), custom_call_target="tpu_custom_call" | custom-call | tf_op jit(solution)/shard_map/cut_faces/pallas_call | solution.py:148
  5.3 4.2 %collective-permute-start = (bf16[81,16,256]{2,1,0:T(8,128)(2,1)}, bf16[81,16,256]{2,1,0:T(8,128)(2,1)S(1)}, u32[]{:S(2)}, u32[]{:S(2)}) collective-permute-start(bf16[81,16,256]{2,1,0:T(8,128)(2,1)} %get-tuple-element.39), channel_id=1, source_target_pairs={{0,4},{4,8},{8,12},{12,0},{1,5},{5,9},{9,13},{13,1},{2,6},{6,10},{... | collective-permute-start | bytes 1990664 | tf_op jit(solution)/shard_map/ppermute | solution.py:723
  9.5 1.6 %collective-permute-start.6 = (bf16[81,2,16,256]{3,2,1,0:T(8,128)(2,1)}, bf16[81,2,16,256]{3,2,1,0:T(8,128)(2,1)S(1)}, u32[]{:S(2)}, u32[]{:S(2)}) collective-permute-start(bf16[81,2,16,256]{3,2,1,0:T(8,128)(2,1)} %get-tuple-element.58), channel_id=1, source_target_pairs={{0,16},{16,32},{32,48},{48,64},{64,80},{80,96},{96,112},{112,0},{1... | collective-permute-start | bytes 3981320 | tf_op jit(solution)/shard_map/ppermute | solution.py:723
  11.1 2.1 %collective-permute-start.7 = (bf16[81,2,16,256]{3,2,1,0:T(8,128)(2,1)}, bf16[81,2,16,256]{3,2,1,0:T(8,128)(2,1)}, u32[]{:S(2)}, u32[]{:S(2)}) collective-permute-start(bf16[81,2,16,256]{3,2,1,0:T(8,128)(2,1)} %get-tuple-element.59), channel_id=1, source_target_pairs={{0,112},{16,0},{32,16},{48,32},{64,48},{80,64},{96,80},{112,96},{1... | collective-permute-start | bytes 3981320 | tf_op jit(solution)/shard_map/ppermute | solution.py:723
  13.4 6.9 %shard_map.154.refs_0_ = f32[62400,128]{1,0:T(8,128)S(1)} custom-call(bf16[81,8,16,256]{3,2,1,0:T(8,128)(2,1)} %field.1, bf16[256,256]{1,0:T(8,128)(2,1)} %constant.42.clone.refs_1_.eye.refs_3_.refs_5_), custom_call_target="tpu_custom_call" | custom-call | flops 20000000000 | bytes 20000000 | tf_op jit(solution)/shard_map/pallas_call | solution.py:304
  20.3 9.1 %prepare.1 = (s32[256,128]{1,0:T(8,128)S(1)}, f32[4096,128]{1,0:T(8,128)S(1)}) custom-call(s32[3]{0:T(128)S(1)} %pad_add_fusion.origin, s32[4096]{0:T(1024)S(1)} %bitcast.5, s32[3,8,4096]{2,1,0:T(8,128)S(1)} %copy-done.8, f32[8,4096]{1,0:T(8,128)S(1)} %copy-done.9, bf16[256,256]{1,0:T(8,128)(2,1)S(1)} %copy-done.11, bf16[16,128]{1,0:T(8,128)(2,1)S(1)} %copy-done.13), custom_call_target="tpu_custom_call" | custom-call | flops 20000000000 | bytes 3000000 | tf_op jit(solution)/shard_map/prepare/pallas_call | solution.py:453
  29.4 0.7 copy-done.12
  30.1 0.8 copy-done.14
  31.2 3.4 %cut_corners.1 = (bf16[81,8,256]{2,1,0:T(8,128)(2,1)}, bf16[81,8,256]{2,1,0:T(8,128)(2,1)}) custom-call(bf16[81,16,256]{2,1,0:T(8,128)(2,1)} %copy-done.14, bf16[81,16,256]{2,1,0:T(8,128)(2,1)} %copy-done.15, bf16[16,32]{1,0:T(8,128)(2,1)S(1)} %copy-done.7), custom_call_target="tpu_custom_call" | custom-call | tf_op jit(solution)/shard_map/cut_corners/pallas_call | solution.py:193
  34.6 3.4 %shard_map.155 = (f32[62400,128]{1,0:T(8,128)S(1)}, bf16[320,128]{1,0:T(8,128)(2,1)}, bf16[320,128]{1,0:T(8,128)(2,1)}) custom-call(f32[62400,128]{1,0:T(8,128)S(1)} %shard_map.154.refs_0_, bf16[81,16,256]{2,1,0:T(8,128)(2,1)} %copy-done.14, bf16[81,16,256]{2,1,0:T(8,128)(2,1)} %copy-done.15, ...), custom_call_target="tpu_custom_call", output_to_operand_aliasing={{0}: (0, {})} | custom-call | flops 20000000000 | bytes 20000000 | tf_op jit(solution)/shard_map/pallas_call | solution.py:304
  38.0 1.4 %collective-permute-start.2 = (bf16[320,128]{1,0:T(8,128)(2,1)}, bf16[320,128]{1,0:T(8,128)(2,1)S(1)}, u32[]{:S(2)}, u32[]{:S(2)}) collective-permute-start(bf16[320,128]{1,0:T(8,128)(2,1)} %get-tuple-element.48), channel_id=1, source_target_pairs={{0,1},{1,2},{2,3},{3,0},{4,5},{5,6},{6,7},{7,4},{8,9},{9,10},{10,1... | collective-permute-start | bytes 245768 | tf_op jit(solution)/shard_map/ppermute | solution.py:768
  39.3 1.5 %collective-permute-start.3 = (bf16[320,128]{1,0:T(8,128)(2,1)}, bf16[320,128]{1,0:T(8,128)(2,1)S(1)}, u32[]{:S(2)}, u32[]{:S(2)}) collective-permute-start(bf16[320,128]{1,0:T(8,128)(2,1)} %get-tuple-element.49), channel_id=1, source_target_pairs={{0,3},{1,0},{2,1},{3,2},{4,7},{5,4},{6,5},{7,6},{8,11},{9,8},{10,9... | collective-permute-start | bytes 245768 | tf_op jit(solution)/shard_map/ppermute | solution.py:767
  40.9 2.2 %collective-permute-done.2.zlo.refs_0_ = bf16[320,128]{1,0:T(8,128)(2,1)S(1)} collective-permute-done((bf16[320,128]{1,0:T(8,128)(2,1)}, bf16[320,128]{1,0:T(8,128)(2,1)S(1)}, u32[]{:S(2)}, u32[]{:S(2)}) %collective-permute-start.2) | collective-permute-done | bytes 81952 | tf_op jit(solution)/shard_map/ppermute | solution.py:768
  43.1 2.4 %collective-permute-start.9 = (bf16[81,8,256]{2,1,0:T(8,128)(2,1)S(1)}, bf16[81,8,256]{2,1,0:T(8,128)(2,1)S(1)}, u32[]{:S(2)}, u32[]{:S(2)}) collective-permute-start(bf16[81,8,256]{2,1,0:T(8,128)(2,1)S(1)} %copy-done.18), channel_id=1, source_target_pairs={{0,112},{16,0},{32,16},{48,32},{64,48},{80,64},{96,80},{112,96},{1... | collective-permute-start | bytes 995336 | tf_op jit(solution)/shard_map/ppermute | solution.py:723
  45.5 7.7 %spread_weights.1.wide = f32[32768,128]{1,0:T(8,128)} custom-call(f32[4096,128]{1,0:T(8,128)S(1)} %get-tuple-element.51.ordered, bf16[128,1024]{1,0:T(8,128)(2,1)S(1)} %copy-done.10), custom_call_target="tpu_custom_call" | custom-call | flops 10000000000 | bytes 3000000 | tf_op jit(solution)/shard_map/spread_weights/pallas_call | solution.py:498
  53.2 0.3 cut_ends.1
  53.6 9.2 %collective-permute-done.8.refs_3_ = bf16[81,8,256]{2,1,0:T(8,128)(2,1)S(1)} collective-permute-done((bf16[81,8,256]{2,1,0:T(8,128)(2,1)S(1)}, bf16[81,8,256]{2,1,0:T(8,128)(2,1)S(1)}, u32[]{:S(2)}, u32[]{:S(2)}) %collective-permute-start.8) | collective-permute-done | bytes 331808 | tf_op jit(solution)/shard_map/ppermute | solution.py:723
  62.8 0.7 copy-done.19
  63.6 0.4 copy-done.17
  64.1 4.6 %shard_map.156.refs_4_ = f32[62400,128]{1,0:T(8,128)S(1)} custom-call(f32[62400,128]{1,0:T(8,128)S(1)} %get-tuple-element.57.refs_0_, bf16[81,2,16,256]{3,2,1,0:T(8,128)(2,1)} %copy-done.17, bf16[81,2,16,256]{3,2,1,0:T(8,128)(2,1)} %collective-permute-done.7.refs_2_, bf16[81,8,256]{2,1,0:T(8,128)(2,1)} %copy-done.19, ...), custom_call_target="tpu_custom_call", output_to_operand_aliasing={{}: (0, {})} | custom-call | flops 20000000000 | bytes 20000000 | tf_op jit(solution)/shard_map/pallas_call | solution.py:304
  68.7 0.6 copy-done.22
  69.3 24.9 %gather_rows.1 = (f32[62400,128]{1,0:T(8,128)S(1)}, bf16[128,24,128]{2,1,0:T(8,128)(2,1)}) custom-call(s32[32768]{0:T(1024)} %bitcast.6, f32[32768,128]{1,0:T(8,128)} %spread_weights.1.wide, bf16[3,256,128]{2,1,0:T(8,128)(2,1)} %constant.47.clone.pick, bf16[320,128]{1,0:T(8,128)(2,1)} %copy-done.5, ...), custom_call_target="tpu_custom_call", output_to_operand_aliasing={{0}: (7, {})} | custom-call | flops 40000000000 | bytes 20000000 | tf_op jit(solution)/shard_map/gather_rows/pallas_call | solution.py:637
  94.2 25.1 %all_to_all.5.routed = bf16[128,24,128]{2,1,0:T(8,128)(2,1)S(1)} all-to-all(bf16[128,24,128]{2,1,0:T(8,128)(2,1)} %get-tuple-element.62), channel_id=1, replica_groups=mesh['gx'=8,'gy'=4,'gz'=4] {'gx','gy','gz'}, dimensions={0} | all-to-all | bytes 1572864 | tf_op jit(solution)/shard_map/all_to_all | solution.py:780
  119.4 7.6 %relight.1 = bf16[81,4096]{1,0:T(8,128)(2,1)} custom-call(bf16[81,4096]{1,0:T(8,128)(2,1)S(1)} %copy-done, bf16[128,24,128]{2,1,0:T(8,128)(2,1)S(1)} %all_to_all.5.routed, bf16[1024,81]{1,0:T(8,128)(2,1)S(1)} %copy-done.3, bf16[1024,128]{1,0:T(8,128)(2,1)S(1)} %copy-done.2, bf16[81,1024]{1,0:T(8,128)(2,1)S(1)} %copy-done.4), custom_call_target="tpu_custom_call" | custom-call | tf_op jit(solution)/shard_map/relight/pallas_call | solution.py:696
  (57 shorter events, 0.7 us)
Async XLA Ops:
  0.0 13.3 %copy-start.16 = (s32[2,4096]{1,0:T(2,128)S(1)}, s32[2,4096]{1,0:T(2,128)}, u32[]{:S(2)}) copy-start(s32[2,4096]{1,0:T(2,128)} %param.19) | copy-start | bytes 98308
  5.3 24.8 %collective-permute-start = (bf16[81,16,256]{2,1,0:T(8,128)(2,1)}, bf16[81,16,256]{2,1,0:T(8,128)(2,1)S(1)}, u32[]{:S(2)}, u32[]{:S(2)}) collective-permute-start(bf16[81,16,256]{2,1,0:T(8,128)(2,1)} %get-tuple-element.39), channel_id=1, source_target_pairs={{0,4},{4,8},{8,12},{12,0},{1,5},{5,9},{9,13},{13,1},{2,6},{6,10},{... | collective-permute-start | bytes 1990664 | tf_op jit(solution)/shard_map/ppermute | solution.py:723
  9.5 20.6 %collective-permute-start.1 = (bf16[81,16,256]{2,1,0:T(8,128)(2,1)}, bf16[81,16,256]{2,1,0:T(8,128)(2,1)S(1)}, u32[]{:S(2)}, u32[]{:S(2)}) collective-permute-start(bf16[81,16,256]{2,1,0:T(8,128)(2,1)} %get-tuple-element.40), channel_id=1, source_target_pairs={{0,12},{4,0},{8,4},{12,8},{1,13},{5,1},{9,5},{13,9},{2,14},{6,2},{... | collective-permute-start | bytes 1990664 | tf_op jit(solution)/shard_map/ppermute | solution.py:723
  9.5 53.3 %collective-permute-start.6 = (bf16[81,2,16,256]{3,2,1,0:T(8,128)(2,1)}, bf16[81,2,16,256]{3,2,1,0:T(8,128)(2,1)S(1)}, u32[]{:S(2)}, u32[]{:S(2)}) collective-permute-start(bf16[81,2,16,256]{3,2,1,0:T(8,128)(2,1)} %get-tuple-element.58), channel_id=1, source_target_pairs={{0,16},{16,32},{32,48},{48,64},{64,80},{80,96},{96,112},{112,0},{1... | collective-permute-start | bytes 3981320 | tf_op jit(solution)/shard_map/ppermute | solution.py:723
  11.1 51.7 %collective-permute-start.7 = (bf16[81,2,16,256]{3,2,1,0:T(8,128)(2,1)}, bf16[81,2,16,256]{3,2,1,0:T(8,128)(2,1)}, u32[]{:S(2)}, u32[]{:S(2)}) collective-permute-start(bf16[81,2,16,256]{3,2,1,0:T(8,128)(2,1)} %get-tuple-element.59), channel_id=1, source_target_pairs={{0,112},{16,0},{32,16},{48,32},{64,48},{80,64},{96,80},{112,96},{1... | collective-permute-start | bytes 3981320 | tf_op jit(solution)/shard_map/ppermute | solution.py:723
  13.4 6.9 %copy-start.9 = (f32[8,4096]{1,0:T(8,128)S(1)}, f32[8,4096]{1,0:T(8,128)}, u32[]{:S(2)}) copy-start(f32[8,4096]{1,0:T(8,128)} %weights.1) | copy-start | bytes 393220
  13.4 6.9 %copy-start.11 = (bf16[256,256]{1,0:T(8,128)(2,1)S(1)}, bf16[256,256]{1,0:T(8,128)(2,1)}, u32[]{:S(2)}) copy-start(bf16[256,256]{1,0:T(8,128)(2,1)} %constant.42.clone.refs_1_.eye.refs_3_.refs_5_) | copy-start | bytes 393220
  13.4 6.9 %copy-start.13 = (bf16[16,128]{1,0:T(8,128)(2,1)S(1)}, bf16[16,128]{1,0:T(8,128)(2,1)}, u32[]{:S(2)}) copy-start(bf16[16,128]{1,0:T(8,128)(2,1)} %constant.43.clone.join) | copy-start | bytes 12292
  20.3 10.9 %copy-start.7 = (bf16[16,32]{1,0:T(8,128)(2,1)S(1)}, bf16[16,32]{1,0:T(8,128)(2,1)}, u32[]{:S(2)}) copy-start(bf16[16,32]{1,0:T(8,128)(2,1)} %constant.44.clone.pick) | copy-start | bytes 3076
  34.5 8.6 %copy-start.18 = (bf16[81,8,256]{2,1,0:T(8,128)(2,1)S(1)}, bf16[81,8,256]{2,1,0:T(8,128)(2,1)}, u32[]{:S(2)}) copy-start(bf16[81,8,256]{2,1,0:T(8,128)(2,1)} %get-tuple-element.61) | copy-start | bytes 995332
  34.5 11.0 %copy-start.10 = (bf16[128,1024]{1,0:T(8,128)(2,1)S(1)}, bf16[128,1024]{1,0:T(8,128)(2,1)}, u32[]{:S(2)}) copy-start(bf16[128,1024]{1,0:T(8,128)(2,1)} %constant.45.clone.ones) | copy-start | bytes 786436
  38.0 5.1 %collective-permute-start.2 = (bf16[320,128]{1,0:T(8,128)(2,1)}, bf16[320,128]{1,0:T(8,128)(2,1)S(1)}, u32[]{:S(2)}, u32[]{:S(2)}) collective-permute-start(bf16[320,128]{1,0:T(8,128)(2,1)} %get-tuple-element.48), channel_id=1, source_target_pairs={{0,1},{1,2},{2,3},{3,0},{4,5},{5,6},{6,7},{7,4},{8,9},{9,10},{10,1... | collective-permute-start | bytes 245768 | tf_op jit(solution)/shard_map/ppermute | solution.py:768
  39.3 13.9 %copy-start.1 = (bf16[320,640]{1,0:T(8,128)(2,1)S(1)}, bf16[320,640]{1,0:T(8,128)(2,1)}, u32[]{:S(2)}) copy-start(bf16[320,640]{1,0:T(8,128)(2,1)} %constant.46.clone.pick) | copy-start | bytes 1228804
  39.3 13.8 %collective-permute-start.3 = (bf16[320,128]{1,0:T(8,128)(2,1)}, bf16[320,128]{1,0:T(8,128)(2,1)S(1)}, u32[]{:S(2)}, u32[]{:S(2)}) collective-permute-start(bf16[320,128]{1,0:T(8,128)(2,1)} %get-tuple-element.49), channel_id=1, source_target_pairs={{0,3},{1,0},{2,1},{3,2},{4,7},{5,4},{6,5},{7,6},{8,11},{9,8},{10,9... | collective-permute-start | bytes 245768 | tf_op jit(solution)/shard_map/ppermute | solution.py:767
  40.9 21.9 %collective-permute-start.8 = (bf16[81,8,256]{2,1,0:T(8,128)(2,1)S(1)}, bf16[81,8,256]{2,1,0:T(8,128)(2,1)S(1)}, u32[]{:S(2)}, u32[]{:S(2)}) collective-permute-start(bf16[81,8,256]{2,1,0:T(8,128)(2,1)S(1)} %copy-done.20), channel_id=1, source_target_pairs={{0,16},{16,32},{32,48},{48,64},{64,80},{80,96},{96,112},{112,0},{1... | collective-permute-start | bytes 995336 | tf_op jit(solution)/shard_map/ppermute | solution.py:723
  43.1 10.1 %copy-start.5 = (bf16[320,128]{1,0:T(8,128)(2,1)}, bf16[320,128]{1,0:T(8,128)(2,1)S(1)}, u32[]{:S(2)}) copy-start(bf16[320,128]{1,0:T(8,128)(2,1)S(1)} %collective-permute-done.2.zlo.refs_0_) | copy-start | bytes 245764
  43.1 19.7 %collective-permute-start.9 = (bf16[81,8,256]{2,1,0:T(8,128)(2,1)S(1)}, bf16[81,8,256]{2,1,0:T(8,128)(2,1)S(1)}, u32[]{:S(2)}, u32[]{:S(2)}) collective-permute-start(bf16[81,8,256]{2,1,0:T(8,128)(2,1)S(1)} %copy-done.18), channel_id=1, source_target_pairs={{0,112},{16,0},{32,16},{48,32},{64,48},{80,64},{96,80},{112,96},{1... | collective-permute-start | bytes 995336 | tf_op jit(solution)/shard_map/ppermute | solution.py:723
  53.2 15.5 %copy-start.6 = (bf16[320,128]{1,0:T(8,128)(2,1)}, bf16[320,128]{1,0:T(8,128)(2,1)S(1)}, u32[]{:S(2)}) copy-start(bf16[320,128]{1,0:T(8,128)(2,1)S(1)} %collective-permute-done.3.zhi.refs_1_) | copy-start | bytes 245764
  53.5 15.2 %collective-permute-start.4 = (bf16[160,128]{1,0:T(8,128)(2,1)S(1)}, bf16[160,128]{1,0:T(8,128)(2,1)S(1)}, u32[]{:S(2)}, u32[]{:S(2)}) collective-permute-start(bf16[160,128]{1,0:T(8,128)(2,1)S(1)} %get-tuple-element.55), channel_id=1, source_target_pairs={{0,16},{16,32},{32,48},{48,64},{64,80},{80,96},{96,112},{112,0},{1... | collective-permute-start | bytes 122888 | tf_op jit(solution)/shard_map/ppermute | solution.py:773
  62.8 5.9 %collective-permute-start.5 = (bf16[160,128]{1,0:T(8,128)(2,1)S(1)}, bf16[160,128]{1,0:T(8,128)(2,1)S(1)}, u32[]{:S(2)}, u32[]{:S(2)}) collective-permute-start(bf16[160,128]{1,0:T(8,128)(2,1)S(1)} %get-tuple-element.56), channel_id=1, source_target_pairs={{0,112},{16,0},{32,16},{48,32},{64,48},{80,64},{96,80},{112,96},{1... | collective-permute-start | bytes 122888 | tf_op jit(solution)/shard_map/ppermute | solution.py:774
  69.3 50.0 %copy-start = (bf16[81,4096]{1,0:T(8,128)(2,1)S(1)}, bf16[81,4096]{1,0:T(8,128)(2,1)}, u32[]{:S(2)}) copy-start(bf16[81,4096]{1,0:T(8,128)(2,1)} %transfer.1) | copy-start | bytes 1990660
  69.3 50.0 %copy-start.2 = (bf16[1024,128]{1,0:T(8,128)(2,1)S(1)}, bf16[1024,128]{1,0:T(8,128)(2,1)}, u32[]{:S(2)}) copy-start(bf16[1024,128]{1,0:T(8,128)(2,1)} %constant.49.clone.wide) | copy-start | bytes 786436
  69.3 50.0 %copy-start.3 = (bf16[1024,81]{1,0:T(8,128)(2,1)S(1)}, bf16[1024,81]{1,0:T(8,128)(2,1)}, u32[]{:S(2)}) copy-start(bf16[1024,81]{1,0:T(8,128)(2,1)} %constant.48.clone.basis) | copy-start | bytes 497668
  69.3 50.0 %copy-start.4 = (bf16[81,1024]{1,0:T(8,128)(2,1)S(1)}, bf16[81,1024]{1,0:T(8,128)(2,1)}, u32[]{:S(2)}) copy-start(bf16[81,1024]{1,0:T(8,128)(2,1)} %constant.50.clone.projector) | copy-start | bytes 497668
  (10 other events, 19.9 us)
